TPU v7x, 32 devices: a whole 2x2x4 slice. The times are simulated.
32 devices in a mesh: dp: 8 (over z, x), mp: 4 (over y, core).
Axes of the slice: x: 2, y: 2, z: 4, core: 2. Of those that a mesh axis runs over, the one named last changes fastest.
Arguments:
- text_in: bfloat16 [7680, 768], P(('dp', 'mp')), may hold values from -6 to 6
- caption_ids: int32 [480, 16], P('dp'), may hold values from 0 to 31999, as said below
- pairing: int32 [480], replicated, may hold values from 0 to 479, each once
- image_low: bfloat16 [19200, 768], P(('dp', 'mp')), may hold values from -6 to 6
- image_high: bfloat16 [13920, 768], P(('dp', 'mp')), may hold values from -6 to 6
- img_gains: float32 [2, 768], replicated, may hold values from 0.5 to 1.5
- img_qkv: bfloat16 [3, 768, 768], P(None, None, 'mp'), may hold values from -0.21875 to 0.21875
- img_out: bfloat16 [768, 768], P('mp'), may hold values from -0.625 to 0.625
- img_fc1: bfloat16 [768, 3072], P(None, 'mp'), may hold values from -0.21875 to 0.21875
- img_fc2: bfloat16 [3072, 768], P('mp'), may hold values from -0.109375 to 0.109375
- txt_qkv: bfloat16 [3, 768, 768], P(None, None, 'mp'), may hold values from -0.21875 to 0.21875
- txt_qv_bias: float32 [2, 768], P(None, 'mp'), may hold values from -3 to 3
- txt_out: bfloat16 [768, 768], P('mp'), may hold values from -0.4375 to 0.4375
- txt_fc1: bfloat16 [768, 3072], P(None, 'mp'), may hold values from -0.21875 to 0.21875
- txt_fc1_bias: float32 [3072], P('mp'), may hold values from -3 to 3
- txt_fc2: bfloat16 [3072, 768], P('mp'), may hold values from -0.109375 to 0.109375
- txt_gains: float32 [2, 768], replicated, may hold values from 0.5 to 1.5
- txt_shifts: float32 [2, 768], replicated, may hold values from -2 to 2
- txt_biases: float32 [2, 768], replicated, may hold values from -2 to 2
Outputs:
- loss: float32 [], replicated
- grad_text_in: float32 [7680, 768], P(('dp', 'mp'))
- grad_qkv: float32 [3, 768, 768], P(None, None, 'mp')
- grad_qv_bias: float32 [2, 768], P(None, 'mp')
- grad_out: float32 [768, 768], P('mp')
- grad_fc1: float32 [768, 3072], P(None, 'mp')
- grad_fc1_bias: float32 [3072], P('mp')
- grad_fc2: float32 [3072, 768], P('mp')
- grad_gains: float32 [2, 768], replicated
- grad_shifts: float32 [2, 768], replicated
- grad_biases: float32 [2, 768], replicated
Inputs may be any that keep to these rules, and one draw needn't show every extreme that they name: `caption_ids`: in each caption the nonzero ids come first and the zeros after; each caption has 4 to 16 nonzero ids. Image i is paired with caption pairing[i]; each caption is paired once.
All inputs are finite; a program needn't handle non-finite values.
Results may differ from a plain program's by a relative error of at most 0.017.
Values may be sent and summed in bfloat16 or wider, within the bound.
A program may use at most 192 MiB of HBM per device.

v0:
```python
import jax
import jax.numpy as jnp
from jax import lax
from jax.sharding import PartitionSpec as P

D = 768
HEAD = 64
L = 16
P_LOW = 50
P_HIGH = 145


EPS = 1e-06
SCALE = 40.0
LOSS_SCALE = 16.0
MASKED = -1e30


def layer_stats(values):
    center = values - jnp.mean(values, -1, keepdims=True)
    inverse = lax.rsqrt(jnp.mean(center * center, -1, keepdims=True) + EPS)
    return (center * inverse, inverse)


def norm_back(grad_out, unit, inverse, gain):
    scaled = grad_out * gain
    return inverse * (
        scaled
        - jnp.mean(scaled, -1, keepdims=True)
        - unit * jnp.mean(scaled * unit, -1, keepdims=True)
    )


def gelu_exact(values):
    return jax.nn.gelu(values, approximate=False)


def score_rows(queries, keys_all, keep):
    scores = (
        jnp.einsum("nqhe,nkhe->nhqk", queries, keys_all, preferred_element_type=jnp.float32) * 0.125
    )
    if keep is not None:
        scores = jnp.where(keep, scores, MASKED)
    return scores


def attention_shares(queries, keys_all, keep):
    scores = score_rows(queries, keys_all, keep)
    highest = jnp.max(scores, -1, keepdims=True)
    raised = jnp.exp(scores - highest)
    totals = jnp.sum(raised, -1, keepdims=True)
    return (raised / totals, highest + jnp.log(totals))


def image_tower(tokens, count, length, gains, weights):
    w_qkv, w_out, w_fc1, w_fc2 = weights
    head_count = D // HEAD
    inputs = tokens.astype(jnp.float32)
    unit, spare = layer_stats(inputs)
    normed = (unit * gains[0]).astype(jnp.bfloat16)
    projected = jnp.einsum("rd,jdw->jrw", normed, w_qkv, preferred_element_type=jnp.float32).astype(
        jnp.bfloat16
    )
    shaped = projected.reshape(3, count, length, head_count, HEAD)
    shares, spare_lse = attention_shares(shaped[0], shaped[1], None)
    context = jnp.einsum(
        "nhqk,nkhe->nqhe",
        shares.astype(jnp.bfloat16),
        shaped[2],
        preferred_element_type=jnp.float32,
    )
    context = context.astype(jnp.bfloat16).reshape(count * length, D)
    middle = inputs + jnp.dot(context, w_out, preferred_element_type=jnp.float32)
    unit2, spare2 = layer_stats(middle)
    normed2 = (unit2 * gains[1]).astype(jnp.bfloat16)
    active = gelu_exact(jnp.dot(normed2, w_fc1, preferred_element_type=jnp.float32)).astype(
        jnp.bfloat16
    )
    result = middle + jnp.dot(active, w_fc2, preferred_element_type=jnp.float32)
    pooled = jnp.mean(result.reshape(count, length, D), 1)
    return (pooled * lax.rsqrt(jnp.sum(pooled * pooled, -1, keepdims=True) + EPS)).astype(
        jnp.bfloat16
    )


def local(
    text_in,
    caption_ids,
    pairing,
    image_low,
    image_high,
    img_gains,
    img_qkv,
    img_out,
    img_fc1,
    img_fc2,
    txt_qkv,
    txt_qv_bias,
    txt_out,
    txt_fc1,
    txt_fc1_bias,
    txt_fc2,
    txt_gains,
    txt_shifts,
    txt_biases,
):
    weights = (
        lax.all_gather(img_qkv, "mp", axis=2, tiled=True),
        lax.all_gather(img_out, "mp", axis=0, tiled=True),
        lax.all_gather(img_fc1, "mp", axis=1, tiled=True),
        lax.all_gather(img_fc2, "mp", axis=0, tiled=True),
    )
    low_count = image_low.shape[0] // P_LOW
    high_count = image_high.shape[0] // P_HIGH
    images16 = jnp.concatenate(
        [
            image_tower(image_low, low_count, P_LOW, img_gains, weights),
            image_tower(image_high, high_count, P_HIGH, img_gains, weights),
        ],
        0,
    )
    width = txt_qkv.shape[2]
    head_count = width // HEAD
    own_rows = text_in.shape[0]
    own_caps = own_rows // L
    group_caps = caption_ids.shape[0]
    group_rows = group_caps * L
    own_ids = lax.dynamic_slice_in_dim(caption_ids, lax.axis_index("mp") * own_caps, own_caps, 0)
    keep = (caption_ids > 0)[:, None, None, :]
    inputs = text_in.astype(jnp.float32)
    unit1, inverse1 = layer_stats(inputs)
    normed1 = (unit1 * txt_gains[0] + txt_shifts[0]).astype(jnp.bfloat16)
    bias_rows = jnp.stack([txt_qv_bias[0], jnp.zeros_like(txt_qv_bias[0]), txt_qv_bias[1]])
    piece = lax.all_gather(normed1, "mp", axis=0, tiled=True)
    made = jnp.einsum("rd,jdw->rjw", piece, txt_qkv, preferred_element_type=jnp.float32) + bias_rows
    joined = jnp.concatenate(
        [piece, made.astype(jnp.bfloat16).reshape(piece.shape[0], 3 * width)], 1
    )
    normed1_all = joined[:, :D]
    triple = joined[:, D:].reshape(group_caps, L, 3, head_count, HEAD)
    queries = triple[:, :, 0]
    keys_all = triple[:, :, 1]
    values_all = triple[:, :, 2]
    shares, log_totals = attention_shares(queries, keys_all, keep)
    context = jnp.einsum(
        "nhqk,nkhe->nqhe",
        shares.astype(jnp.bfloat16),
        values_all,
        preferred_element_type=jnp.float32,
    )
    context = context.astype(jnp.bfloat16).reshape(group_rows, width)
    middle = inputs + (
        lax.psum_scatter(
            jnp.dot(context, txt_out, preferred_element_type=jnp.float32).astype(jnp.bfloat16),
            "mp",
            scatter_dimension=0,
            tiled=True,
        ).astype(jnp.float32)
        + txt_biases[0]
    )
    unit2, inverse2 = layer_stats(middle)
    normed2 = (unit2 * txt_gains[1] + txt_shifts[1]).astype(jnp.bfloat16)
    piece = lax.all_gather(normed2, "mp", axis=0, tiled=True)
    hidden_piece = jnp.dot(piece, txt_fc1, preferred_element_type=jnp.float32) + txt_fc1_bias
    spread = jnp.concatenate([piece.astype(jnp.float32), hidden_piece], 1)
    normed2_all = spread[:, :D].astype(jnp.bfloat16)
    hidden = spread[:, D:]
    active, gelu_pull = jax.vjp(gelu_exact, hidden)
    active16 = active.astype(jnp.bfloat16)
    result = middle + (
        lax.psum_scatter(
            jnp.dot(active16, txt_fc2, preferred_element_type=jnp.float32).astype(jnp.bfloat16),
            "mp",
            scatter_dimension=0,
            tiled=True,
        ).astype(jnp.float32)
        + txt_biases[1]
    )
    present = (own_ids > 0).astype(jnp.float32)
    counts = jnp.sum(present, 1, keepdims=True)
    pooled = jnp.sum(result.reshape(own_caps, L, D) * present[:, :, None], 1) / counts
    inverse_len = lax.rsqrt(jnp.sum(pooled * pooled, -1, keepdims=True) + EPS)
    captions_unit = pooled * inverse_len
    captions16 = captions_unit.astype(jnp.bfloat16)
    total_pairs = pairing.shape[0]
    first_pair = lax.axis_index(("dp", "mp")) * own_caps
    arrived = lax.all_gather(captions16, ("dp", "mp"), axis=0, tiled=True)
    logits = SCALE * jnp.einsum("id,jd->ij", images16, arrived, preferred_element_type=jnp.float32)
    targets = lax.dynamic_slice_in_dim(pairing, first_pair, own_caps, 0)
    matched = (targets[:, None] == jnp.arange(total_pairs)[None, :]).astype(jnp.float32)
    raised = jnp.exp(logits - SCALE)
    local_lse = SCALE + jnp.log(jnp.sum(raised, 1))
    partial_value = jnp.sum(raised, 0)
    own_term = 0.5 * jnp.sum(local_lse) - jnp.sum(matched * logits)
    summed, scalar = lax.psum((partial_value, own_term), ("dp", "mp"))
    other_lse = SCALE + jnp.log(summed)
    total = scalar + 0.5 * jnp.sum(other_lse)
    loss = total / total_pairs
    grads16 = (
        LOSS_SCALE
        * (
            0.5 * jnp.exp(logits - local_lse[:, None])
            + 0.5 * jnp.exp(logits - other_lse[None, :])
            - matched
        )
    ).astype(jnp.bfloat16)
    grad_caps = lax.psum_scatter(
        SCALE * jnp.einsum("ic,id->cd", grads16, images16, preferred_element_type=jnp.float32),
        ("dp", "mp"),
        scatter_dimension=0,
        tiled=True,
    )
    grad_pooled = inverse_len * (
        grad_caps - captions_unit * jnp.sum(captions_unit * grad_caps, -1, keepdims=True)
    )
    grad_result = (grad_pooled[:, None, :] * (present / counts)[:, :, None]).reshape(own_rows, D)
    grad_all = lax.all_gather(grad_result.astype(jnp.bfloat16), "mp", axis=0, tiled=True)
    grad_fc2 = jnp.einsum("gf,gd->fd", active16, grad_all, preferred_element_type=jnp.float32)
    grad_active = jnp.einsum("gd,fd->gf", grad_all, txt_fc2, preferred_element_type=jnp.float32)
    grad_hidden16 = gelu_pull(grad_active)[0].astype(jnp.bfloat16)
    grad_fc1 = jnp.einsum(
        "gd,gf->df", normed2_all, grad_hidden16, preferred_element_type=jnp.float32
    )
    grad_fc1_bias = jnp.sum(grad_hidden16.astype(jnp.float32), 0)
    grad_normed2 = lax.psum_scatter(
        jnp.einsum("gf,df->gd", grad_hidden16, txt_fc1, preferred_element_type=jnp.float32).astype(
            jnp.bfloat16
        ),
        "mp",
        scatter_dimension=0,
        tiled=True,
    ).astype(jnp.float32)
    grad_middle = grad_result + norm_back(grad_normed2, unit2, inverse2, txt_gains[1])
    grad_mid_all = lax.all_gather(grad_middle.astype(jnp.bfloat16), "mp", axis=0, tiled=True)
    grad_out = jnp.einsum("gw,gd->wd", context, grad_mid_all, preferred_element_type=jnp.float32)
    grad_context = jnp.einsum(
        "gd,wd->gw", grad_mid_all, txt_out, preferred_element_type=jnp.float32
    )
    grad_context = grad_context.astype(jnp.bfloat16).reshape(group_caps, L, head_count, HEAD)
    shares_again = jnp.exp(score_rows(queries, keys_all, keep) - log_totals)
    grad_shares = jnp.einsum(
        "nqhe,nkhe->nhqk", grad_context, values_all, preferred_element_type=jnp.float32
    )
    grad_values = jnp.einsum(
        "nhqk,nqhe->nkhe",
        shares_again.astype(jnp.bfloat16),
        grad_context,
        preferred_element_type=jnp.float32,
    ).astype(jnp.bfloat16)
    grad_scores = (
        shares_again * (grad_shares - jnp.sum(grad_shares * shares_again, -1, keepdims=True))
    ).astype(jnp.bfloat16)
    grad_queries = (
        jnp.einsum("nhqk,nkhe->nqhe", grad_scores, keys_all, preferred_element_type=jnp.float32)
        * 0.125
    ).astype(jnp.bfloat16)
    grad_keys = (
        jnp.einsum("nhqk,nqhe->nkhe", grad_scores, queries, preferred_element_type=jnp.float32)
        * 0.125
    ).astype(jnp.bfloat16)
    grad_triple = jnp.stack([grad_queries, grad_keys, grad_values], 0).reshape(3, group_rows, width)
    grad_qkv = jnp.einsum(
        "gd,jgw->jdw", normed1_all, grad_triple, preferred_element_type=jnp.float32
    )
    grad_qv_bias = jnp.stack(
        [
            jnp.sum(grad_triple[0].astype(jnp.float32), 0),
            jnp.sum(grad_triple[2].astype(jnp.float32), 0),
        ]
    )
    grad_normed1 = lax.psum_scatter(
        jnp.einsum("jgw,jdw->gd", grad_triple, txt_qkv, preferred_element_type=jnp.float32).astype(
            jnp.bfloat16
        ),
        "mp",
        scatter_dimension=0,
        tiled=True,
    ).astype(jnp.float32)
    grad_inputs = grad_middle + norm_back(grad_normed1, unit1, inverse1, txt_gains[0])
    summed_grads = lax.psum(
        (grad_qkv, grad_qv_bias, grad_out, grad_fc1, grad_fc1_bias, grad_fc2), "dp"
    )
    small_parts = jnp.stack(
        [
            jnp.sum(grad_normed1 * unit1, 0),
            jnp.sum(grad_normed2 * unit2, 0),
            jnp.sum(grad_normed1, 0),
            jnp.sum(grad_normed2, 0),
            jnp.sum(grad_middle, 0),
            jnp.sum(grad_result, 0),
        ]
    )
    shared = lax.psum(small_parts, ("dp", "mp"))
    return (
        loss,
        grad_inputs,
        summed_grads[0],
        summed_grads[1],
        summed_grads[2],
        summed_grads[3],
        summed_grads[4],
        summed_grads[5],
        shared[0:2],
        shared[2:4],
        shared[4:6],
    )


def solution(mesh):
    placed = (
        P(("dp", "mp"), None),
        P("dp", None),
        P(),
        P(("dp", "mp"), None),
        P(("dp", "mp"), None),
        P(),
        P(None, None, "mp"),
        P("mp", None),
        P(None, "mp"),
        P("mp", None),
        P(None, None, "mp"),
        P(None, "mp"),
        P("mp", None),
        P(None, "mp"),
        P("mp"),
        P("mp", None),
        P(),
        P(),
        P(),
    )
    return jax.shard_map(
        local,
        mesh=mesh,
        in_specs=placed,
        out_specs=(
            P(),
            P(("dp", "mp"), None),
            P(None, None, "mp"),
            P(None, "mp"),
            P("mp", None),
            P(None, "mp"),
            P("mp"),
            P("mp", None),
            P(),
            P(),
            P(),
        ),
        check_vma=False,
    )
```

profile of v0, /device:TPU:0, one launch (start us, length us, event | category | flops | bytes accessed | tf_op | source)
XLA Modules:
  0.0 829.3 jit_solution(6300139161258848959)
XLA Ops:
  11.1 2.0 fusion.104
  14.9 20.2 %all-gather.18.cloned.1.call-done = bf16[960,768]{1,0:T(8,128)(2,1)} async-done(((bf16[240,768]{1,0:T(8,128)(2,1)}), bf16[960,768]{1,0:T(8,128)(2,1)}) %all-gather.18.cloned.1.call-update) | async-done | bytes 1474576 | tf_op jit(solution)/shard_map/all_gather | solution.py:134
  35.1 2.7 fusion.231
  39.0 1.9 copy.127
  40.9 3.0 reshape_reshape.3
  43.9 3.2 fusion.221
  50.4 1.6 convolution_convert_fusion.2
  59.0 20.6 %reduce-scatter.7.cloned.1.call-done = bf16[240,768]{1,0:T(8,128)(2,1)} async-done(((bf16[960,768]{1,0:T(8,128)(2,1)}), bf16[240,768]{1,0:T(8,128)(2,1)}) %reduce-scatter.7.cloned.1.call-update) | async-done | bytes 368656 | tf_op jit(solution)/shard_map/reduce_scatter | solution.py:153
  82.1 1.9 add_convert_fusion.2
  84.2 27.8 %all-gather.10.cloned.1.call-done = bf16[3,768,768]{1,2,0:T(8,128)(2,1)} async-done(((bf16[3,768,192]{1,2,0:T(8,128)(2,1)}), bf16[3,768,768]{1,2,0:T(8,128)(2,1)}) %all-gather.10.cloned.1.call-update) | async-done | bytes 3538960 | tf_op jit(solution)/shard_map/all_gather | solution.py:108
  112.0 4.5 convert_bitcast_fusion
  116.5 1.4 fusion.222
  117.9 4.5 squeeze.30
  122.4 4.1 squeeze.31
  126.5 3.8 fusion.45
  130.3 3.2 fusion.229
  133.5 2.8 squeeze.29
  136.3 4.5 convert_bitcast_fusion.1
  140.9 1.9 copy.118
  142.7 4.2 reshape.220
  146.9 2.7 fusion.230
  150.9 1.9 convert_bitcast_fusion.2
  154.1 2.5 reshape.236
  156.6 3.3 reshape.237
  159.9 2.4 fusion.65
  162.3 3.8 fusion.227
  166.2 2.3 reshape.235
  168.5 4.1 fusion.69
  173.6 2.1 reshape.222
  175.8 2.5 fusion.228
  179.6 29.0 %all-gather.16.cloned.1.call-done = bf16[3072,768]{1,0:T(8,128)(2,1)} async-done(((bf16[768,768]{1,0:T(8,128)(2,1)}), bf16[3072,768]{1,0:T(8,128)(2,1)}) %all-gather.16.cloned.1.call-update) | async-done | bytes 4718608 | tf_op jit(solution)/shard_map/all_gather | solution.py:111
  208.6 25.3 %fusion.58 = f32[600,768]{1,0:T(8,128)S(1)} fusion(f32[600,768]{1,0:T(8,128)} %copy-done.23, bf16[3072,768]{1,0:T(8,128)(2,1)} %all-gather.16.cloned.1.call-done, bf16[768,3072]{1,0:T(8,128)(2,1)} %all-gather.14.cloned.1.call-done, f32[768]{0:T(1024)S(1)} %get-tuple-element.22, f32[600]{0:T(1024)S(1)} %add_rsqrt_fusion, f32[600]{0:T(1024)S(1)} %broadcast_multiply_fusion), kind=kOutput, calls=%fused_computation.102 | convolution fusion | flops 5784422400 | bytes 13131456 | tf_op jit(solution)/shard_map/dot_general | solution.py:79
  234.0 10.1 %multiply_convert_fusion = (bf16[960,768]{1,0:T(8,128)(2,1)S(1)}, f32[960,768]{1,0:T(8,128)}, f32[960,768]{1,0:T(8,128)}) fusion(f32[768]{0:T(1024)S(1)} %copy-done.64, bf16[960,768]{1,0:T(8,128)(2,1)} %all-gather.20.cloned.1.call-done, bf16[768,768]{1,0:T(8,128)(2,1)S(1)} %copy-done), kind=kOutput, calls=%fused_computation.54 | convolution fusion | flops 1181122560 | bytes 10030080 | tf_op jit(solution)/shard_map/dot_general | solution.py:164
  245.3 2.4 convolution_convert_fusion.1
  248.0 20.6 %fusion.62 = f32[435,768]{1,0:T(8,128)} fusion(f32[435,768]{1,0:T(8,128)} %copy-done.25, bf16[3072,768]{1,0:T(8,128)(2,1)} %all-gather.16.cloned.1.call-done, bf16[768,3072]{1,0:T(8,128)(2,1)} %all-gather.14.cloned.1.call-done, f32[768]{0:T(1024)S(1)} %get-tuple-element.22, f32[435]{0:T(512)S(1)} %add_rsqrt_fusion.2, f32[435]{0:T(512)S(1)} %broadcast_multiply_fusion.2), kind=kOutput, calls=%fused_computation.115 | convolution fusion | flops 4193706240 | bytes 12116376 | tf_op jit(solution)/shard_map/dot_general | solution.py:79
  268.5 1.5 reshape.221
  270.1 1.8 reduce_sum.383
  271.9 1.5 reshape.223
  277.0 42.7 %all-gather = bf16[32,15,768]{2,1,0:T(8,128)(2,1)S(1)} all-gather(bf16[1,15,768]{2,1,0:T(8,128)(2,1)S(1)} %fusion.139), channel_id=1, replica_groups=mesh['dp'=8,'mp'=4] {'dp','mp'}, dimensions={0}, use_global_device_ids=true | all-gather | bytes 760320 | tf_op jit(solution)/shard_map/all_gather | solution.py:187
  319.9 1.6 fusion.137
  321.5 36.8 %psum.64 = f32[480]{0:T(512)S(1)} all-reduce(f32[480]{0:T(512)S(1)} %get-tuple-element.19), channel_id=1, replica_groups=mesh['dp'=8,'mp'=4] {'dp','mp'}, use_global_device_ids=true, to_apply=%region_32.33 | all-reduce | flops 480 | bytes 3840 | tf_op jit(solution)/shard_map/psum | solution.py:195
  360.7 77.1 %fusion = f32[16,768]{1,0:T(8,128)S(1)} fusion(f32[480,768]{1,0:T(8,128)S(1)} %convolution_multiply_fusion), kind=kCustom, calls=%all-reduce-scatter | all-reduce-scatter fusion | flops 393217 | bytes 1523712
  445.0 18.3 %all-gather.22.cloned.1.call-done = bf16[960,768]{1,0:T(8,128)(2,1)} async-done(((bf16[240,768]{1,0:T(8,128)(2,1)}), bf16[960,768]{1,0:T(8,128)(2,1)}) %all-gather.22.cloned.1.call-update) | async-done | bytes 1474576 | tf_op jit(solution)/shard_map/all_gather | solution.py:217
  463.3 5.6 convert_reduce_fusion
  470.1 2.5 convolution_convert_fusion
  472.6 27.5 %reduce-scatter.11.cloned.1.call-done = bf16[240,768]{1,0:T(8,128)(2,1)} async-done(((bf16[960,768]{1,0:T(8,128)(2,1)}), bf16[240,768]{1,0:T(8,128)(2,1)}) %reduce-scatter.11.cloned.1.call-update) | async-done | bytes 368656 | tf_op jit(solution)/shard_map/reduce_scatter | solution.py:225
  500.1 1.5 fusion.114
  505.8 18.1 %all-gather.24.cloned.1.call-done = bf16[960,768]{1,0:T(8,128)(2,1)} async-done(((bf16[240,768]{1,0:T(8,128)(2,1)}), bf16[960,768]{1,0:T(8,128)(2,1)}) %all-gather.24.cloned.1.call-update) | async-done | bytes 1474576 | tf_op jit(solution)/shard_map/all_gather | solution.py:234
  523.9 2.8 convolution_convert_fusion.5
  529.0 2.3 multiply_reduce_fusion.3
  537.2 2.0 copy.143
  539.2 1.6 copy.140
  542.1 2.0 copy.144
  545.4 3.9 bitcast_convert_fusion
  549.6 4.8 fusion.234
  554.5 2.8 fusion.233
  558.7 2.3 convolution_bitcast_fusion
  563.4 13.5 %reduce-scatter.13.cloned.1.call-done = bf16[240,768]{1,0:T(8,128)(2,1)} async-done(((bf16[960,768]{1,0:T(8,128)(2,1)}), bf16[240,768]{1,0:T(8,128)(2,1)}) %reduce-scatter.13.cloned.1.call-update) | async-done | bytes 368656 | tf_op jit(solution)/shard_map/reduce_scatter | solution.py:271
  576.9 1.4 fusion.115
  578.4 23.1 %all-reduce.3 = (f32[2,192]{1,0:T(2,128)}, f32[768]{0:T(1024)}) all-reduce(f32[2,192]{1,0:T(2,128)S(1)} %pad_maximum_fusion.7, f32[768]{0:T(1024)S(1)} %get-tuple-element.38), channel_id=1, replica_groups=mesh['dp'=8,'mp'=4] {'dp'}, use_global_device_ids=true, to_apply=%region_46.47 | all-reduce | flops 1152 | bytes 9216 | tf_op jit(solution)/shard_map/psum | solution.py:280
  601.5 41.9 %all-reduce.2 = (f32[]{:T(128)}, f32[6,768]{1,0:T(8,128)S(1)}) all-reduce(f32[]{:T(128)S(6)} %sub.157, f32[6,768]{1,0:T(8,128)S(1)} %stack.59), channel_id=1, replica_groups=mesh['dp'=8,'mp'=4] {'dp','mp'}, use_global_device_ids=true, to_apply=%region_30.31 | all-reduce | flops 4609 | bytes 36872 | tf_op jit(solution)/shard_map/psum | solution.py:195
  644.7 2.2 fusion.107
  646.8 168.1 %all-reduce.7.cloned.1.call-done = (f32[3,768,192]{1,2,0:T(8,128)}, f32[192,768]{1,0:T(8,128)}, f32[768,768]{1,0:T(8,128)}, f32[768,768]{1,0:T(8,128)}) async-done(((f32[3,768,192]{1,2,0:T(8,128)}, f32[192,768]{1,0:T(8,128)}, f32[768,768]{1,0:T(8,128)}, f32[768,768]{1,0:T(8,128)}), (f32[3,768,192]{1,2,0:T(8,128)}, f32[192,768]{1,0:T(8,128)}, f32[768,768]{1,0:T(8,128)}, ...) | async-done | bytes 7077904 | tf_op jit(solution)/shard_map/psum | solution.py:280
  814.9 2.9 copy.205
  (270 shorter events, 61.4 us)
Async XLA Ops:
  7.2 226.8 %copy-start = (bf16[768,768]{1,0:T(8,128)(2,1)S(1)}, bf16[768,768]{1,0:T(8,128)(2,1)}, u32[]{:S(2)}) copy-start(bf16[768,768]{1,0:T(8,128)(2,1)} %param.32) | copy-start | bytes 3538948
  7.2 27.9 %all-gather.18.cloned.1.call-start = ((), (), s32[]{:S(2)}) async-start(), calls=%async_computation.8 | async-start | bytes 1843200 | tf_op jit(solution)/shard_map/all_gather | solution.py:134
  8.5 2.1 copy-start.47
  10.5 71.6 %copy-start.43 = (f32[768]{0:T(1024)}, f32[768]{0:T(1024)S(1)}, u32[]{:S(2)}) copy-start(f32[768]{0:T(1024)S(1)} %get-tuple-element.82) | copy-start | bytes 9220
  13.1 66.5 %reduce-scatter.7.cloned.1.call-start = ((), (), s32[]{:S(2)}) async-start(), calls=%async_computation.9 | async-start | bytes 1843200 | tf_op jit(solution)/shard_map/reduce_scatter | solution.py:153
  52.1 2.6 copy-start.46
  52.1 5.1 copy-start.57
  52.1 5.2 copy-start.58
  52.1 5.8 copy-start.16
  52.1 6.0 copy-start.11
  52.1 59.9 %all-gather.10.cloned.1.call-start = ((), (), s32[]{:S(2)}) async-start(), calls=%async_computation.4 | async-start | bytes 4423680 | tf_op jit(solution)/shard_map/all_gather | solution.py:108
  52.9 26.8 %copy-start.1 = (bf16[240,768]{1,0:T(8,128)(2,1)S(1)}, bf16[240,768]{1,0:T(8,128)(2,1)}, u32[]{:S(2)}) copy-start(bf16[240,768]{1,0:T(8,128)(2,1)} %param.19) | copy-start | bytes 1105924
  52.9 94.1 %all-gather.12.cloned.1.call-start = ((), (), s32[]{:S(2)}) async-start(), calls=%async_computation.5 | async-start | bytes 1474560 | tf_op jit(solution)/shard_map/all_gather | solution.py:109
  53.4 126.2 %all-gather.14.cloned.1.call-start = ((), (), s32[]{:S(2)}) async-start(), calls=%async_computation.6 | async-start | bytes 5898240 | tf_op jit(solution)/shard_map/all_gather | solution.py:110
  54.0 154.6 %all-gather.16.cloned.1.call-start = ((), (), s32[]{:S(2)}) async-start(), calls=%async_computation.7 | async-start | bytes 5898240 | tf_op jit(solution)/shard_map/all_gather | solution.py:111
  54.6 179.4 %all-gather.20.cloned.1.call-start = ((), (), s32[]{:S(2)}) async-start(), calls=%async_computation.10 | async-start | bytes 1843200 | tf_op jit(solution)/shard_map/all_gather | solution.py:163
  57.9 26.2 %copy-start.38 = (f32[768]{0:T(1024)}, f32[768]{0:T(1024)S(1)}, u32[]{:S(2)}) copy-start(f32[768]{0:T(1024)S(1)} %get-tuple-element.25) | copy-start | bytes 9220
  80.8 35.6 %copy-start.49 = (f32[240]{0:T(256)}, f32[240]{0:T(256)S(1)}, u32[]{:S(2)}) copy-start(f32[240]{0:T(256)S(1)} %broadcast_multiply_fusion.8) | copy-start | bytes 2884
  82.1 34.4 %copy-start.54 = (f32[240]{0:T(256)}, f32[240]{0:T(256)S(1)}, u32[]{:S(2)}) copy-start(f32[240]{0:T(256)S(1)} %add_rsqrt_fusion.4) | copy-start | bytes 2884
  84.1 191.2 %reduce-scatter.9.cloned.1.call-start = ((), (), s32[]{:S(2)}) async-start(), calls=%async_computation.11 | async-start | bytes 1843200 | tf_op jit(solution)/shard_map/reduce_scatter | solution.py:171
  146.9 3.9 copy-start.17
  146.9 3.9 copy-start.60
  162.3 3.8 copy-start.19
  172.6 3.2 copy-start.18
  208.6 25.4 %copy-start.64 = (f32[768]{0:T(1024)S(1)}, f32[768]{0:T(1024)}, u32[]{:S(2)}) copy-start(f32[768]{0:T(1024)} %param.33) | copy-start | bytes 9220
  234.0 11.3 %copy-start.63 = (bf16[768,768]{1,0:T(8,128)(2,1)S(1)}, bf16[768,768]{1,0:T(8,128)(2,1)}, u32[]{:S(2)}) copy-start(bf16[768,768]{1,0:T(8,128)(2,1)} %param.34) | copy-start | bytes 3538948
  247.7 215.6 %all-gather.22.cloned.1.call-start = ((), (), s32[]{:S(2)}) async-start(), calls=%async_computation.12 | async-start | bytes 1843200 | tf_op jit(solution)/shard_map/all_gather | solution.py:217
  270.1 5.2 copy-start.2
  270.1 5.2 copy-start.5
  270.1 5.2 copy-start.39
  270.1 5.2 copy-start.56
  271.9 4.6 copy-start.45
  271.9 4.8 copy-start.51
  276.9 42.8 %copy-start.59 = (f32[15]{0:T(128)}, f32[15]{0:T(128)S(1)}, u32[]{:S(2)}) copy-start(f32[15]{0:T(128)S(1)} %add_rsqrt_fusion.6) | copy-start | bytes 184
  437.9 4.3 collective-permute-start
  439.2 3.0 collective-permute-start.1
  444.1 57.5 %copy-start.28 = (f32[15,768]{1,0:T(8,128)}, f32[15,768]{1,0:T(8,128)S(1)}, u32[]{:S(2)}) copy-start(f32[15,768]{1,0:T(8,128)S(1)} %subtract_multiply_fusion.1) | copy-start | bytes 138244
  445.0 55.1 %reduce-scatter.11.cloned.1.call-start = ((), (), s32[]{:S(2)}) async-start(), calls=%async_computation.13 | async-start | bytes 1843200 | tf_op jit(solution)/shard_map/reduce_scatter | solution.py:225
  470.1 30.0 %copy-start.44 = (f32[768]{0:T(1024)S(1)}, f32[768]{0:T(1024)}, u32[]{:S(2)}) copy-start(f32[768]{0:T(1024)} %copy-done.43) | copy-start | bytes 9220
  470.1 30.0 %copy-start.50 = (f32[240]{0:T(256)S(1)}, f32[240]{0:T(256)}, u32[]{:S(2)}) copy-start(f32[240]{0:T(256)} %copy-done.49) | copy-start | bytes 2884
  470.1 30.0 %copy-start.55 = (f32[240]{0:T(256)S(1)}, f32[240]{0:T(256)}, u32[]{:S(2)}) copy-start(f32[240]{0:T(256)} %copy-done.54) | copy-start | bytes 2884
  472.5 32.6 %copy-start.32 = (f32[60,3,16]{2,1,0:T(4,128)S(1)}, f32[60,3,16]{2,1,0:T(4,128)}, u32[]{:S(2)}) copy-start(f32[60,3,16]{2,1,0:T(4,128)} %copy-done.31) | copy-start | bytes 34564
  472.5 32.6 %copy-start.34 = (f32[60,3,16]{2,1,0:T(4,128)S(1)}, f32[60,3,16]{2,1,0:T(4,128)}, u32[]{:S(2)}) copy-start(f32[60,3,16]{2,1,0:T(4,128)} %copy-done.33) | copy-start | bytes 34564
  472.6 51.4 %all-gather.24.cloned.1.call-start = ((), (), s32[]{:S(2)}) async-start(), calls=%async_computation.14 | async-start | bytes 1843200 | tf_op jit(solution)/shard_map/all_gather | solution.py:234
  503.9 25.1 %copy-start.4 = (f32[60,3,16,16]{2,3,1,0:T(8,128)S(1)}, f32[60,3,16,16]{2,3,1,0:T(8,128)}, u32[]{:S(2)}) copy-start(f32[60,3,16,16]{2,3,1,0:T(8,128)} %copy-done.3) | copy-start | bytes 552964
  504.7 72.2 %reduce-scatter.13.cloned.1.call-start = ((), (), s32[]{:S(2)}) async-start(), calls=%async_computation.15 | async-start | bytes 1843200 | tf_op jit(solution)/shard_map/reduce_scatter | solution.py:271
  529.0 2.3 copy-start.8
  529.0 2.3 copy-start.22
  535.9 8.2 copy-start.15
  549.4 265.5 %all-reduce.7.cloned.1.call-start = ((), (), s32[]{:S(2)}) async-start(), calls=%async_computation.16 | async-start | bytes 14155776 | tf_op jit(solution)/shard_map/psum | solution.py:280
  549.6 4.8 copy-start.62
  549.6 4.8 copy-start.67
  554.4 2.9 copy-start.10
  554.4 2.9 copy-start.24
  554.5 4.2 copy-start.35
  554.5 4.2 copy-start.36
  554.5 4.2 copy-start.61
  561.0 15.9 %copy-start.42 = (f32[768]{0:T(1024)S(1)}, f32[768]{0:T(1024)}, u32[]{:S(2)}) copy-start(f32[768]{0:T(1024)} %copy-done.41) | copy-start | bytes 9220
  561.0 15.9 %copy-start.48 = (f32[240]{0:T(256)S(1)}, f32[240]{0:T(256)}, u32[]{:S(2)}) copy-start(f32[240]{0:T(256)} %copy-done.47) | copy-start | bytes 2884
  561.0 15.9 %copy-start.53 = (f32[240]{0:T(256)S(1)}, f32[240]{0:T(256)}, u32[]{:S(2)}) copy-start(f32[240]{0:T(256)} %copy-done.52) | copy-start | bytes 2884
  561.0 83.7 %copy-start.7 = (f32[240,768]{1,0:T(8,128)S(1)}, f32[240,768]{1,0:T(8,128)}, u32[]{:S(2)}) copy-start(f32[240,768]{1,0:T(8,128)} %copy-done.6) | copy-start | bytes 2211844
  814.9 3.0 copy-start.30
  814.9 3.8 copy-start.21
  817.8 2.2 copy-start.20
  (19 other events, 25.8 us)
Sparse Core Ops, SparseCore 0:
  13.2 21.7 all-gather.17
  52.2 27.3 reduce-scatter.6
  81.2 30.7 all-gather.9
  113.4 17.4 all-gather.11
  132.3 37.4 all-gather.13
  171.2 37.4 all-gather.15
  210.8 19.0 all-gather.19
  247.9 27.3 reduce-scatter.8
  445.1 18.2 all-gather.21
  472.7 27.3 reduce-scatter.10
  504.8 19.0 all-gather.23
  549.5 27.3 reduce-scatter.12
  581.9 232.9 all-reduce.6
where the time goes:
time: 839 us; the launch traced here: 829 us
  waiting for transfers between devices  347 us (41%)
  blocking collectives  222 us (26%)
  matrix products  125 us (15%)
  local copies, waits for them, and re-layouts  74.8 us (9%)
  other arithmetic  38.1 us (5%)
  between operations  18.9 us (2%)
    psum x1, waiting for transfers between devices, local(): lax.psum((grad_qkv, grad_qv_bias, grad_out, grad_fc1, grad_fc1_bias, grad...  168 us
    psum x2, blocking collectives, local(): summed, scalar = lax.psum((partial_value, own_term), ('dp', 'mp'))  78.7 us
    unnamed x1, blocking collectives  77.1 us
    dot_general x2, matrix products, image_tower(): result = middle + jnp.dot(active, w_fc2, preferred_element_type=jnp.float32)  45.9 us
    all_gather x1, blocking collectives, local(): arrived = lax.all_gather(captions16, ('dp', 'mp'), axis=0, tiled=True)  42.7 us
    all_gather x1, waiting for transfers between devices, local(): lax.all_gather(img_fc2, 'mp', axis=0, tiled=True)  29 us
    all_gather x1, waiting for transfers between devices, local(): lax.all_gather(img_qkv, 'mp', axis=2, tiled=True)  27.8 us
    reduce_scatter x1, waiting for transfers between devices, local(): lax.psum_scatter(jnp.einsum('gf,df->gd', grad_hidden16, txt_fc1, preferre...  27.5 us
  transfers between devices with their start and end apart: 15, of which 11 were waited for; matrix products, arithmetic and copies ran while one was open for 18% of the time, Pallas kernels for 0%

commit v1 on v0

--- a/solution.py
+++ b/solution.py
@@ -119,6 +119,7 @@
         ],
         0,
     )
+    images_all = lax.all_gather(images16, ("dp", "mp"), axis=0, tiled=True)
     width = txt_qkv.shape[2]
     head_count = width // HEAD
     own_rows = text_in.shape[0]
@@ -185,30 +186,26 @@
     total_pairs = pairing.shape[0]
     first_pair = lax.axis_index(("dp", "mp")) * own_caps
     arrived = lax.all_gather(captions16, ("dp", "mp"), axis=0, tiled=True)
-    logits = SCALE * jnp.einsum("id,jd->ij", images16, arrived, preferred_element_type=jnp.float32)
-    targets = lax.dynamic_slice_in_dim(pairing, first_pair, own_caps, 0)
-    matched = (targets[:, None] == jnp.arange(total_pairs)[None, :]).astype(jnp.float32)
+    logits = SCALE * jnp.einsum("id,jd->ij", images_all, arrived, preferred_element_type=jnp.float32)
+    matched = (pairing[:, None] == jnp.arange(total_pairs)[None, :]).astype(jnp.float32)
     raised = jnp.exp(logits - SCALE)
-    local_lse = SCALE + jnp.log(jnp.sum(raised, 1))
-    partial_value = jnp.sum(raised, 0)
-    own_term = 0.5 * jnp.sum(local_lse) - jnp.sum(matched * logits)
-    summed, scalar = lax.psum((partial_value, own_term), ("dp", "mp"))
-    other_lse = SCALE + jnp.log(summed)
-    total = scalar + 0.5 * jnp.sum(other_lse)
+    row_lse = SCALE + jnp.log(jnp.sum(raised, 1))
+    col_lse = SCALE + jnp.log(jnp.sum(raised, 0))
+    total = 0.5 * jnp.sum(row_lse) + 0.5 * jnp.sum(col_lse) - jnp.sum(matched * logits)
     loss = total / total_pairs
+    own_logits = lax.dynamic_slice_in_dim(logits, first_pair, own_caps, 1)
+    own_col_lse = lax.dynamic_slice_in_dim(col_lse, first_pair, own_caps, 0)
+    own_matched = lax.dynamic_slice_in_dim(matched, first_pair, own_caps, 1)
     grads16 = (
         LOSS_SCALE
         * (
-            0.5 * jnp.exp(logits - local_lse[:, None])
-            + 0.5 * jnp.exp(logits - other_lse[None, :])
-            - matched
+            0.5 * jnp.exp(own_logits - row_lse[:, None])
+            + 0.5 * jnp.exp(own_logits - own_col_lse[None, :])
+            - own_matched
         )
     ).astype(jnp.bfloat16)
-    grad_caps = lax.psum_scatter(
-        SCALE * jnp.einsum("ic,id->cd", grads16, images16, preferred_element_type=jnp.float32),
-        ("dp", "mp"),
-        scatter_dimension=0,
-        tiled=True,
+    grad_caps = SCALE * jnp.einsum(
+        "ic,id->cd", grads16, images_all, preferred_element_type=jnp.float32
     )
     grad_pooled = inverse_len * (
         grad_caps - captions_unit * jnp.sum(captions_unit * grad_caps, -1, keepdims=True)
@@ -277,8 +274,17 @@
         tiled=True,
     ).astype(jnp.float32)
     grad_inputs = grad_middle + norm_back(grad_normed1, unit1, inverse1, txt_gains[0])
-    summed_grads = lax.psum(
-        (grad_qkv, grad_qv_bias, grad_out, grad_fc1, grad_fc1_bias, grad_fc2), "dp"
+    summed16 = lax.psum(
+        tuple(g.astype(jnp.bfloat16) for g in (grad_qkv, grad_out, grad_fc1, grad_fc2)), "dp"
+    )
+    summed_bias = lax.psum((grad_qv_bias, grad_fc1_bias), "dp")
+    summed_grads = (
+        summed16[0].astype(jnp.float32),
+        summed_bias[0],
+        summed16[1].astype(jnp.float32),
+        summed16[2].astype(jnp.float32),
+        summed_bias[1],
+        summed16[3].astype(jnp.float32),
     )
     small_parts = jnp.stack(
         [

time: 839 us -> 664 us (0.79)
  waiting for transfers between devices: 347 us -> 243 us
  blocking collectives: 222 us -> 145 us
    unnamed x1 -> x0, blocking collectives: 77.1 us -> none
    psum x1, waiting for transfers between devices: 168 us -> 91 us  [local(): lax.psum(tuple((g.astype(jnp.bfloat16) for g in (grad_qkv, grad_out, grad...]
    all_gather x0 -> x1, blocking collectives: none -> 42.8 us  [local(): images_all = lax.all_gather(images16, ('dp', 'mp'), axis=0, tiled=True)]
    psum x3 -> x2, blocking collectives: 102 us -> 63.4 us  [the longest x1 41.2 us: local(): shared = lax.psum(small_parts, ('dp', 'mp'))]
    all_gather x1, waiting for transfers between devices: 29 us -> 0.02 us  [local(): lax.all_gather(img_fc2, 'mp', axis=0, tiled=True)]
    all_gather x1, waiting for transfers between devices: 0.02 us -> 18.5 us  [local(): lax.all_gather(img_fc1, 'mp', axis=1, tiled=True)]
    reduce_scatter x1, waiting for transfers between devices: 13.5 us -> 0.01 us  [local(): lax.psum_scatter(jnp.einsum('jgw,jdw->gd', grad_triple, txt_qkv, preferre...]
    squeeze x4, local copies, waits for them, and re-layouts: 14.5 us -> 25.5 us  [image_tower(): shares, spare_lse = attention_shares(shaped[0], shaped[1], None)]
  transfers between devices with their start and end apart: 15 -> 13, of which waited for: 11 -> 8; matrix products, arithmetic and copies ran while one was open for 18% -> 24% of each run, Pallas kernels for 0% -> 0%
where the time goes in v1:
time: 664 us; the launch traced here: 655 us
  waiting for transfers between devices  243 us (37%)
  blocking collectives  145 us (22%)
  matrix products  124 us (19%)
  local copies, waits for them, and re-layouts  81.4 us (12%)
  other arithmetic  42.8 us (6%)
  between operations  18.2 us (3%)
    psum x1, waiting for transfers between devices, local(): lax.psum(tuple((g.astype(jnp.bfloat16) for g in (grad_qkv, grad_out, grad...  91 us
    dot_general x2, matrix products, image_tower(): result = middle + jnp.dot(active, w_fc2, preferred_element_type=jnp.float32)  46.4 us
    all_gather x1, blocking collectives, local(): images_all = lax.all_gather(images16, ('dp', 'mp'), axis=0, tiled=True)  42.8 us
    psum x1, blocking collectives, local(): shared = lax.psum(small_parts, ('dp', 'mp'))  41.2 us
    all_gather x1, blocking collectives, local(): arrived = lax.all_gather(captions16, ('dp', 'mp'), axis=0, tiled=True)  38.8 us
    all_gather x1, waiting for transfers between devices, local(): lax.all_gather(img_qkv, 'mp', axis=2, tiled=True)  27.8 us
    reduce_scatter x1, waiting for transfers between devices, local(): lax.psum_scatter(jnp.einsum('gf,df->gd', grad_hidden16, txt_fc1, preferre...  27.5 us
    squeeze x4, local copies, waits for them, and re-layouts, image_tower(): shares, spare_lse = attention_shares(shaped[0], shaped[1], None)  25.5 us
  transfers between devices with their start and end apart: 13, of which 8 were waited for; matrix products, arithmetic and copies ran while one was open for 24% of the time, Pallas kernels for 0%

profile of v1, /device:TPU:0, one launch (start us, length us, event | category | flops | bytes accessed | tf_op | source)
XLA Modules:
  0.0 655.0 jit_solution(13765450852409297696)
XLA Ops:
  11.8 2.0 fusion.112
  15.6 20.2 %all-gather.19.cloned.1.call-done = bf16[960,768]{1,0:T(8,128)(2,1)} async-done(((bf16[240,768]{1,0:T(8,128)(2,1)}), bf16[960,768]{1,0:T(8,128)(2,1)}) %all-gather.19.cloned.1.call-update) | async-done | bytes 1474576 | tf_op jit(solution)/shard_map/all_gather | solution.py:135
  35.8 2.7 fusion.235
  39.7 1.9 copy.94
  41.6 3.0 reshape_reshape.3
  44.6 3.2 fusion.225
  52.0 1.7 convolution_convert_fusion.2
  60.5 20.8 %reduce-scatter.5.cloned.1.call-done = bf16[240,768]{1,0:T(8,128)(2,1)} async-done(((bf16[960,768]{1,0:T(8,128)(2,1)}), bf16[240,768]{1,0:T(8,128)(2,1)}) %reduce-scatter.5.cloned.1.call-update) | async-done | bytes 368656 | tf_op jit(solution)/shard_map/reduce_scatter | solution.py:154
  83.7 1.9 add_convert_fusion.2
  85.7 27.8 %all-gather.11.cloned.1.call-done = bf16[3,768,768]{1,2,0:T(8,128)(2,1)} async-done(((bf16[3,768,192]{1,2,0:T(8,128)(2,1)}), bf16[3,768,768]{1,2,0:T(8,128)(2,1)}) %all-gather.11.cloned.1.call-update) | async-done | bytes 3538960 | tf_op jit(solution)/shard_map/all_gather | solution.py:108
  113.6 3.9 convert_bitcast_fusion.2
  118.8 14.1 %reshape.239 = bf16[3,145,12,64]{3,2,1,0:T(8,128)(2,1)S(1)} reshape(bf16[1,435,768]{2,1,0:T(8,128)(2,1)} %get-tuple-element.51) | data formatting | bytes 1336320 | tf_op jit(solution)/shard_map/squeeze | solution.py:65
  132.9 3.3 reshape.238
  136.2 2.4 fusion.68
  138.7 4.1 fusion.230
  142.7 2.3 reshape.237
  145.0 4.1 fusion.72
  150.2 2.0 reshape.222
  152.1 2.5 fusion.231
  155.7 2.5 convert_bitcast_fusion
  158.2 1.4 fusion.226
  159.6 4.1 squeeze.31
  163.7 4.1 squeeze.30
  167.8 3.7 fusion.44
  171.4 3.1 fusion.232
  174.6 2.8 squeeze.29
  177.3 4.8 convert_bitcast_fusion.1
  182.1 1.8 copy.85
  184.0 3.9 reshape.220
  187.8 2.2 fusion.233
  191.7 18.5 %all-gather.15.cloned.1.call-done = bf16[768,3072]{1,0:T(8,128)(2,1)} async-done(((bf16[768,768]{1,0:T(8,128)(2,1)}), bf16[768,3072]{1,0:T(8,128)(2,1)}) %all-gather.15.cloned.1.call-update) | async-done | bytes 4718608 | tf_op jit(solution)/shard_map/all_gather | solution.py:110
  210.2 26.3 %fusion.57 = f32[600,768]{1,0:T(8,128)} fusion(f32[600,768]{1,0:T(8,128)} %copy-done.21, bf16[3072,768]{1,0:T(8,128)(2,1)} %all-gather.17.cloned.1.call-done, bf16[768,3072]{1,0:T(8,128)(2,1)} %all-gather.15.cloned.1.call-done, f32[768]{0:T(1024)S(1)} %get-tuple-element.28, f32[600]{0:T(1024)S(1)} %add_rsqrt_fusion, f32[600]{0:T(1024)S(1)} %broadcast_multiply_fusion), kind=kOutput, calls=%fused_computation.103 | convolution fusion | flops 5784422400 | bytes 13131456 | tf_op jit(solution)/shard_map/dot_general | solution.py:79
  236.5 10.0 %multiply_convert_fusion = (bf16[960,768]{1,0:T(8,128)(2,1)S(1)}, f32[960,768]{1,0:T(8,128)}, f32[960,768]{1,0:T(8,128)}) fusion(f32[768]{0:T(1024)S(1)} %copy-done.68, bf16[960,768]{1,0:T(8,128)(2,1)} %all-gather.21.cloned.1.call-done, bf16[768,768]{1,0:T(8,128)(2,1)S(1)} %copy-done), kind=kOutput, calls=%fused_computation.54 | convolution fusion | flops 1181122560 | bytes 10030080 | tf_op jit(solution)/shard_map/dot_general | solution.py:165
  247.6 2.4 convolution_convert_fusion.1
  250.4 20.1 %fusion.65 = f32[435,768]{1,0:T(8,128)} fusion(f32[435,768]{1,0:T(8,128)S(1)} %copy-done.23, bf16[3072,768]{1,0:T(8,128)(2,1)} %all-gather.17.cloned.1.call-done, bf16[768,3072]{1,0:T(8,128)(2,1)} %all-gather.15.cloned.1.call-done, f32[768]{0:T(1024)S(1)} %get-tuple-element.28, f32[435]{0:T(512)S(1)} %add_rsqrt_fusion.2, f32[435]{0:T(512)S(1)} %broadcast_multiply_fusion.2), kind=kOutput, calls=%fused_computation.117 | convolution fusion | flops 4193706240 | bytes 12116376 | tf_op jit(solution)/shard_map/dot_general | solution.py:79
  270.4 1.5 reshape.223
  272.0 2.7 reshape.221
  274.8 1.8 reduce_sum.383
  277.1 42.8 %all-gather = bf16[32,15,768]{2,1,0:T(8,128)(2,1)S(1)} all-gather(bf16[1,15,768]{2,1,0:T(8,128)(2,1)S(1)} %maximum_bitcast_fusion), channel_id=1, replica_groups=mesh['dp'=8,'mp'=4] {'dp','mp'}, dimensions={0}, use_global_device_ids=true | all-gather | bytes 760320 | tf_op jit(solution)/shard_map/all_gather | solution.py:122
  321.8 38.8 %all-gather.1 = bf16[32,15,768]{2,1,0:T(8,128)(2,1)S(1)} all-gather(bf16[1,15,768]{2,1,0:T(8,128)(2,1)S(1)} %fusion.145), channel_id=1, replica_groups=mesh['dp'=8,'mp'=4] {'dp','mp'}, dimensions={0}, use_global_device_ids=true | all-gather | bytes 760320 | tf_op jit(solution)/shard_map/all_gather | solution.py:188
  361.7 2.6 select_reduce_fusion
  367.1 16.7 %all-gather.23.cloned.1.call-done = bf16[960,768]{1,0:T(8,128)(2,1)} async-done(((bf16[240,768]{1,0:T(8,128)(2,1)}), bf16[960,768]{1,0:T(8,128)(2,1)}) %all-gather.23.cloned.1.call-update) | async-done | bytes 1474576 | tf_op jit(solution)/shard_map/all_gather | solution.py:214
  383.8 5.6 convert_reduce_fusion
  390.5 2.5 convolution_convert_fusion
  393.0 27.5 %reduce-scatter.9.cloned.1.call-done = bf16[240,768]{1,0:T(8,128)(2,1)} async-done(((bf16[960,768]{1,0:T(8,128)(2,1)}), bf16[240,768]{1,0:T(8,128)(2,1)}) %reduce-scatter.9.cloned.1.call-update) | async-done | bytes 368656 | tf_op jit(solution)/shard_map/reduce_scatter | solution.py:222
  420.5 1.5 fusion.122
  426.1 18.3 %all-gather.25.cloned.1.call-done = bf16[960,768]{1,0:T(8,128)(2,1)} async-done(((bf16[240,768]{1,0:T(8,128)(2,1)}), bf16[960,768]{1,0:T(8,128)(2,1)}) %all-gather.25.cloned.1.call-update) | async-done | bytes 1474576 | tf_op jit(solution)/shard_map/all_gather | solution.py:231
  444.3 2.8 convolution_convert_fusion.7
  449.4 2.0 convert_reduce_fusion.3
  457.1 2.0 copy.112
  461.2 1.6 copy.106
  463.7 3.8 bitcast_convert_fusion
  467.6 4.4 convolution_convert_fusion.4
  472.0 2.5 convolution_convert_fusion.3
  475.7 2.0 fusion.78
  480.8 22.2 %all-reduce = (f32[2,192]{1,0:T(2,128)}, f32[768]{0:T(1024)}) all-reduce(f32[2,192]{1,0:T(2,128)S(1)} %pad_maximum_fusion.4, f32[768]{0:T(1024)S(1)} %get-tuple-element.38), channel_id=1, replica_groups=mesh['dp'=8,'mp'=4] {'dp'}, use_global_device_ids=true, to_apply=%region_43.44 | all-reduce | flops 1152 | bytes 9216 | tf_op jit(solution)/shard_map/psum | solution.py:280
  503.0 1.4 fusion.123
  504.5 41.2 %psum.55 = f32[6,768]{1,0:T(8,128)S(1)} all-reduce(f32[6,768]{1,0:T(8,128)S(1)} %stack.59), channel_id=1, replica_groups=mesh['dp'=8,'mp'=4] {'dp','mp'}, use_global_device_ids=true, to_apply=%region_55.56 | all-reduce | flops 4608 | bytes 36864 | tf_op jit(solution)/shard_map/psum | solution.py:299
  546.4 2.2 fusion.115
  548.5 91.0 %all-reduce.4.cloned.1.call-done = (bf16[3,768,192]{1,2,0:T(8,128)(2,1)}, bf16[192,768]{1,0:T(8,128)(2,1)}, bf16[768,768]{1,0:T(8,128)(2,1)}, bf16[768,768]{1,0:T(8,128)(2,1)}) async-done(((bf16[3,768,192]{1,2,0:T(8,128)(2,1)}, bf16[192,768]{1,0:T(8,128)(2,1)}, bf16[768,768]{1,0:T(8,128)(2,1)}, bf16[768,768]{1,0:T(8,128)(2,1)}), (bf16[3,768,192]{1,2,0:T(8,128)(2,1)}, bf16[192,768]{1,0:T(8,128)(2,1)}, ...) | async-done | bytes 3538960 | tf_op jit(solution)/shard_map/psum | solution.py:277
  639.5 2.7 convert_element_type.252
  642.2 1.8 convert_element_type.256
  644.0 1.6 convert_element_type.258
  645.6 1.6 convert_element_type.261
  (273 shorter events, 52.6 us)
Async XLA Ops:
  7.2 229.3 %copy-start = (bf16[768,768]{1,0:T(8,128)(2,1)S(1)}, bf16[768,768]{1,0:T(8,128)(2,1)}, u32[]{:S(2)}) copy-start(bf16[768,768]{1,0:T(8,128)(2,1)} %param.32) | copy-start | bytes 3538948
  7.2 28.6 %all-gather.19.cloned.1.call-start = ((), (), s32[]{:S(2)}) async-start(), calls=%async_computation.8 | async-start | bytes 1843200 | tf_op jit(solution)/shard_map/all_gather | solution.py:135
  8.8 2.4 copy-start.41
  8.9 74.8 %copy-start.43 = (f32[768]{0:T(1024)}, f32[768]{0:T(1024)S(1)}, u32[]{:S(2)}) copy-start(f32[768]{0:T(1024)S(1)} %get-tuple-element.25) | copy-start | bytes 9220
  13.8 67.4 %reduce-scatter.5.cloned.1.call-start = ((), (), s32[]{:S(2)}) async-start(), calls=%async_computation.9 | async-start | bytes 1843200 | tf_op jit(solution)/shard_map/reduce_scatter | solution.py:154
  53.6 2.6 copy-start.46
  53.6 4.1 copy-start.59
  53.7 4.2 copy-start.60
  53.7 4.8 copy-start.15
  53.7 4.9 copy-start.9
  53.7 59.9 %all-gather.11.cloned.1.call-start = ((), (), s32[]{:S(2)}) async-start(), calls=%async_computation.4 | async-start | bytes 4423680 | tf_op jit(solution)/shard_map/all_gather | solution.py:108
  54.4 5.2 copy-start.61
  54.4 97.7 %all-gather.13.cloned.1.call-start = ((), (), s32[]{:S(2)}) async-start(), calls=%async_computation.5 | async-start | bytes 1474560 | tf_op jit(solution)/shard_map/all_gather | solution.py:109
  55.0 26.2 %copy-start.1 = (bf16[240,768]{1,0:T(8,128)(2,1)S(1)}, bf16[240,768]{1,0:T(8,128)(2,1)}, u32[]{:S(2)}) copy-start(bf16[240,768]{1,0:T(8,128)(2,1)} %param.19) | copy-start | bytes 1105924
  55.0 136.7 %all-gather.17.cloned.1.call-start = ((), (), s32[]{:S(2)}) async-start(), calls=%async_computation.7 | async-start | bytes 5898240 | tf_op jit(solution)/shard_map/all_gather | solution.py:111
  55.6 154.6 %all-gather.15.cloned.1.call-start = ((), (), s32[]{:S(2)}) async-start(), calls=%async_computation.6 | async-start | bytes 5898240 | tf_op jit(solution)/shard_map/all_gather | solution.py:110
  56.2 180.3 %all-gather.21.cloned.1.call-start = ((), (), s32[]{:S(2)}) async-start(), calls=%async_computation.10 | async-start | bytes 1843200 | tf_op jit(solution)/shard_map/all_gather | solution.py:164
  56.4 29.3 %copy-start.51 = (f32[15]{0:T(128)}, f32[15]{0:T(128)S(1)}, u32[]{:S(2)}) copy-start(f32[15]{0:T(128)S(1)} %get-tuple-element.40) | copy-start | bytes 184
  58.4 27.2 %copy-start.37 = (f32[768]{0:T(1024)}, f32[768]{0:T(1024)S(1)}, u32[]{:S(2)}) copy-start(f32[768]{0:T(1024)S(1)} %get-tuple-element.23) | copy-start | bytes 9220
  82.4 35.0 %copy-start.49 = (f32[240]{0:T(256)}, f32[240]{0:T(256)S(1)}, u32[]{:S(2)}) copy-start(f32[240]{0:T(256)S(1)} %broadcast_multiply_fusion.8) | copy-start | bytes 2884
  83.7 33.8 %copy-start.55 = (f32[240]{0:T(256)}, f32[240]{0:T(256)S(1)}, u32[]{:S(2)}) copy-start(f32[240]{0:T(256)S(1)} %add_rsqrt_fusion.4) | copy-start | bytes 2884
  85.7 234.4 %reduce-scatter.7.cloned.1.call-start = ((), (), s32[]{:S(2)}) async-start(), calls=%async_computation.11 | async-start | bytes 1843200 | tf_op jit(solution)/shard_map/reduce_scatter | solution.py:172
  138.6 4.1 copy-start.17
  149.1 3.0 copy-start.16
  152.1 3.6 copy-start.10
  152.1 3.6 copy-start.63
  210.2 26.3 %copy-start.68 = (f32[768]{0:T(1024)S(1)}, f32[768]{0:T(1024)}, u32[]{:S(2)}) copy-start(f32[768]{0:T(1024)} %param.33) | copy-start | bytes 9220
  236.5 11.1 %copy-start.67 = (bf16[768,768]{1,0:T(8,128)(2,1)S(1)}, bf16[768,768]{1,0:T(8,128)(2,1)}, u32[]{:S(2)}) copy-start(bf16[768,768]{1,0:T(8,128)(2,1)} %param.34) | copy-start | bytes 3538948
  247.6 2.7 copy-start.23
  250.1 133.7 %all-gather.23.cloned.1.call-start = ((), (), s32[]{:S(2)}) async-start(), calls=%async_computation.12 | async-start | bytes 1843200 | tf_op jit(solution)/shard_map/all_gather | solution.py:214
  274.8 45.3 %copy-start.2 = (bf16[240,768]{1,0:T(8,128)(2,1)S(1)}, bf16[240,768]{1,0:T(8,128)(2,1)}, u32[]{:S(2)}) copy-start(bf16[240,768]{1,0:T(8,128)(2,1)} %param.19) | copy-start | bytes 1105924
  274.8 45.3 %copy-start.5 = (bf16[240,768]{1,0:T(8,128)(2,1)S(1)}, bf16[240,768]{1,0:T(8,128)(2,1)}, u32[]{:S(2)}) copy-start(bf16[240,768]{1,0:T(8,128)(2,1)} %reduce-scatter.5.cloned.1.call-done) | copy-start | bytes 1105924
  274.8 45.4 %copy-start.38 = (f32[768]{0:T(1024)S(1)}, f32[768]{0:T(1024)}, u32[]{:S(2)}) copy-start(f32[768]{0:T(1024)} %copy-done.37) | copy-start | bytes 9220
  274.8 45.4 %copy-start.57 = (f32[768]{0:T(1024)S(1)}, f32[768]{0:T(1024)}, u32[]{:S(2)}) copy-start(f32[768]{0:T(1024)} %get-tuple-element.22) | copy-start | bytes 9220
  274.8 46.5 %copy-start.45 = (f32[15,16]{1,0:T(8,128)S(1)}, f32[15,16]{1,0:T(8,128)}, u32[]{:S(2)}) copy-start(f32[15,16]{1,0:T(8,128)} %copy.101) | copy-start | bytes 2884
  276.6 44.9 %copy-start.52 = (f32[15]{0:T(128)S(1)}, f32[15]{0:T(128)}, u32[]{:S(2)}) copy-start(f32[15]{0:T(128)} %copy-done.51) | copy-start | bytes 184
  319.8 41.9 %copy-start.62 = (s32[480]{0:T(512)S(1)}, s32[480]{0:T(512)}, u32[]{:S(2)}) copy-start(s32[480]{0:T(512)} %param.21) | copy-start | bytes 5764
  361.7 4.5 copy-start.58
  366.2 55.9 %copy-start.28 = (f32[15,768]{1,0:T(8,128)}, f32[15,768]{1,0:T(8,128)S(1)}, u32[]{:S(2)}) copy-start(f32[15,768]{1,0:T(8,128)S(1)} %subtract_multiply_fusion.1) | copy-start | bytes 138244
  367.0 53.5 %reduce-scatter.9.cloned.1.call-start = ((), (), s32[]{:S(2)}) async-start(), calls=%async_computation.13 | async-start | bytes 1843200 | tf_op jit(solution)/shard_map/reduce_scatter | solution.py:222
  390.5 30.0 %copy-start.44 = (f32[768]{0:T(1024)S(1)}, f32[768]{0:T(1024)}, u32[]{:S(2)}) copy-start(f32[768]{0:T(1024)} %copy-done.43) | copy-start | bytes 9220
  390.5 30.0 %copy-start.50 = (f32[240]{0:T(256)S(1)}, f32[240]{0:T(256)}, u32[]{:S(2)}) copy-start(f32[240]{0:T(256)} %copy-done.49) | copy-start | bytes 2884
  390.5 30.0 %copy-start.56 = (f32[240]{0:T(256)S(1)}, f32[240]{0:T(256)}, u32[]{:S(2)}) copy-start(f32[240]{0:T(256)} %copy-done.55) | copy-start | bytes 2884
  393.0 32.4 %copy-start.31 = (f32[60,3,16]{2,1,0:T(4,128)S(1)}, f32[60,3,16]{2,1,0:T(4,128)}, u32[]{:S(2)}) copy-start(f32[60,3,16]{2,1,0:T(4,128)} %copy-done.30) | copy-start | bytes 34564
  393.0 32.4 %copy-start.33 = (f32[60,3,16]{2,1,0:T(4,128)S(1)}, f32[60,3,16]{2,1,0:T(4,128)}, u32[]{:S(2)}) copy-start(f32[60,3,16]{2,1,0:T(4,128)} %copy-done.32) | copy-start | bytes 34564
  393.0 51.4 %all-gather.25.cloned.1.call-start = ((), (), s32[]{:S(2)}) async-start(), calls=%async_computation.14 | async-start | bytes 1843200 | tf_op jit(solution)/shard_map/all_gather | solution.py:231
  424.3 25.1 %copy-start.4 = (f32[60,3,16,16]{2,3,1,0:T(8,128)S(1)}, f32[60,3,16,16]{2,3,1,0:T(8,128)}, u32[]{:S(2)}) copy-start(f32[60,3,16,16]{2,3,1,0:T(8,128)} %copy-done.3) | copy-start | bytes 552964
  425.1 77.9 %reduce-scatter.11.cloned.1.call-start = ((), (), s32[]{:S(2)}) async-start(), calls=%async_computation.15 | async-start | bytes 1843200 | tf_op jit(solution)/shard_map/reduce_scatter | solution.py:268
  449.4 2.0 copy-start.12
  449.4 2.0 copy-start.20
  459.6 4.1 copy-start.34
  467.5 172.1 %all-reduce.4.cloned.1.call-start = ((), (), s32[]{:S(2)}) async-start(), calls=%async_computation.16 | async-start | bytes 7077888 | tf_op jit(solution)/shard_map/psum | solution.py:277
  467.5 4.4 copy-start.65
  467.5 4.4 copy-start.70
  472.0 2.5 copy-start.19
  472.0 2.5 copy-start.66
  472.0 3.7 copy-start.35
  472.0 3.7 copy-start.64
  477.7 25.3 %copy-start.42 = (f32[768]{0:T(1024)S(1)}, f32[768]{0:T(1024)}, u32[]{:S(2)}) copy-start(f32[768]{0:T(1024)} %copy-done.41) | copy-start | bytes 9220
  477.7 25.3 %copy-start.48 = (f32[240]{0:T(256)S(1)}, f32[240]{0:T(256)}, u32[]{:S(2)}) copy-start(f32[240]{0:T(256)} %copy-done.47) | copy-start | bytes 2884
  477.7 25.3 %copy-start.54 = (f32[240]{0:T(256)S(1)}, f32[240]{0:T(256)}, u32[]{:S(2)}) copy-start(f32[240]{0:T(256)} %copy-done.53) | copy-start | bytes 2884
  477.7 68.6 %copy-start.7 = (f32[240,768]{1,0:T(8,128)S(1)}, f32[240,768]{1,0:T(8,128)}, u32[]{:S(2)}) copy-start(f32[240,768]{1,0:T(8,128)} %copy-done.6) | copy-start | bytes 2211844
  639.5 4.5 copy-start.25
  639.5 6.1 copy-start.24
  (21 other events, 26.5 us)
Sparse Core Ops, SparseCore 0:
  13.9 21.7 all-gather.18
  53.8 27.3 reduce-scatter.4
  82.8 30.7 all-gather.10
  115.0 17.4 all-gather.12
  133.9 37.4 all-gather.16
  172.7 37.4 all-gather.14
  212.3 19.0 all-gather.20
  250.2 27.4 reduce-scatter.6
  367.2 16.5 all-gather.22
  393.1 27.3 reduce-scatter.8
  425.2 19.0 all-gather.24
  467.6 27.4 reduce-scatter.10
  499.6 139.8 all-reduce.3

commit v2 on v1

--- a/solution.py
+++ b/solution.py
@@ -119,26 +119,25 @@
         ],
         0,
     )
-    images_all = lax.all_gather(images16, ("dp", "mp"), axis=0, tiled=True)
     width = txt_qkv.shape[2]
     head_count = width // HEAD
     own_rows = text_in.shape[0]
     own_caps = own_rows // L
     group_caps = caption_ids.shape[0]
     group_rows = group_caps * L
-    own_ids = lax.dynamic_slice_in_dim(caption_ids, lax.axis_index("mp") * own_caps, own_caps, 0)
+    mp_index = lax.axis_index("mp")
+    present = (caption_ids > 0).astype(jnp.float32)
     keep = (caption_ids > 0)[:, None, None, :]
-    inputs = text_in.astype(jnp.float32)
+    counts = jnp.sum(present, 1, keepdims=True)
+    inputs = lax.all_gather(text_in, "mp", axis=0, tiled=True).astype(jnp.float32)
     unit1, inverse1 = layer_stats(inputs)
-    normed1 = (unit1 * txt_gains[0] + txt_shifts[0]).astype(jnp.bfloat16)
+    normed1_all = (unit1 * txt_gains[0] + txt_shifts[0]).astype(jnp.bfloat16)
     bias_rows = jnp.stack([txt_qv_bias[0], jnp.zeros_like(txt_qv_bias[0]), txt_qv_bias[1]])
-    piece = lax.all_gather(normed1, "mp", axis=0, tiled=True)
-    made = jnp.einsum("rd,jdw->rjw", piece, txt_qkv, preferred_element_type=jnp.float32) + bias_rows
-    joined = jnp.concatenate(
-        [piece, made.astype(jnp.bfloat16).reshape(piece.shape[0], 3 * width)], 1
-    )
-    normed1_all = joined[:, :D]
-    triple = joined[:, D:].reshape(group_caps, L, 3, head_count, HEAD)
+    made = (
+        jnp.einsum("rd,jdw->rjw", normed1_all, txt_qkv, preferred_element_type=jnp.float32)
+        + bias_rows
+    )
+    triple = made.astype(jnp.bfloat16).reshape(group_caps, L, 3, head_count, HEAD)
     queries = triple[:, :, 0]
     keys_all = triple[:, :, 1]
     values_all = triple[:, :, 2]
@@ -151,41 +150,38 @@
     )
     context = context.astype(jnp.bfloat16).reshape(group_rows, width)
     middle = inputs + (
-        lax.psum_scatter(
+        lax.psum(
             jnp.dot(context, txt_out, preferred_element_type=jnp.float32).astype(jnp.bfloat16),
             "mp",
-            scatter_dimension=0,
-            tiled=True,
         ).astype(jnp.float32)
         + txt_biases[0]
     )
     unit2, inverse2 = layer_stats(middle)
-    normed2 = (unit2 * txt_gains[1] + txt_shifts[1]).astype(jnp.bfloat16)
-    piece = lax.all_gather(normed2, "mp", axis=0, tiled=True)
-    hidden_piece = jnp.dot(piece, txt_fc1, preferred_element_type=jnp.float32) + txt_fc1_bias
-    spread = jnp.concatenate([piece.astype(jnp.float32), hidden_piece], 1)
-    normed2_all = spread[:, :D].astype(jnp.bfloat16)
-    hidden = spread[:, D:]
+    normed2_all = (unit2 * txt_gains[1] + txt_shifts[1]).astype(jnp.bfloat16)
+    hidden = jnp.dot(normed2_all, txt_fc1, preferred_element_type=jnp.float32) + txt_fc1_bias
     active, gelu_pull = jax.vjp(gelu_exact, hidden)
     active16 = active.astype(jnp.bfloat16)
-    result = middle + (
-        lax.psum_scatter(
-            jnp.dot(active16, txt_fc2, preferred_element_type=jnp.float32).astype(jnp.bfloat16),
-            "mp",
-            scatter_dimension=0,
-            tiled=True,
-        ).astype(jnp.float32)
-        + txt_biases[1]
-    )
-    present = (own_ids > 0).astype(jnp.float32)
-    counts = jnp.sum(present, 1, keepdims=True)
-    pooled = jnp.sum(result.reshape(own_caps, L, D) * present[:, :, None], 1) / counts
+    ffn_part = jnp.dot(active16, txt_fc2, preferred_element_type=jnp.float32)
+    ffn_pooled = jnp.sum(ffn_part.reshape(group_caps, L, D) * present[:, :, None], 1)
+    image_slots = lax.dynamic_update_slice_in_dim(
+        jnp.zeros((group_caps, D), jnp.float32),
+        images16.astype(jnp.float32),
+        mp_index * own_caps,
+        0,
+    )
+    both = lax.psum(jnp.concatenate([ffn_pooled, image_slots], 0), "mp")
+    mid_pooled = jnp.sum(middle.reshape(group_caps, L, D) * present[:, :, None], 1)
+    pooled = (mid_pooled + both[:group_caps]) / counts + txt_biases[1]
     inverse_len = lax.rsqrt(jnp.sum(pooled * pooled, -1, keepdims=True) + EPS)
     captions_unit = pooled * inverse_len
     captions16 = captions_unit.astype(jnp.bfloat16)
+    gathered = lax.all_gather(
+        jnp.concatenate([captions16, both[group_caps:].astype(jnp.bfloat16)], 0), "dp", axis=0
+    )
+    arrived = gathered[:, :group_caps].reshape(-1, D)
+    images_all = gathered[:, group_caps:].reshape(-1, D)
     total_pairs = pairing.shape[0]
-    first_pair = lax.axis_index(("dp", "mp")) * own_caps
-    arrived = lax.all_gather(captions16, ("dp", "mp"), axis=0, tiled=True)
+    first_pair = lax.axis_index("dp") * group_caps
     logits = SCALE * jnp.einsum("id,jd->ij", images_all, arrived, preferred_element_type=jnp.float32)
     matched = (pairing[:, None] == jnp.arange(total_pairs)[None, :]).astype(jnp.float32)
     raised = jnp.exp(logits - SCALE)
@@ -193,9 +189,9 @@
     col_lse = SCALE + jnp.log(jnp.sum(raised, 0))
     total = 0.5 * jnp.sum(row_lse) + 0.5 * jnp.sum(col_lse) - jnp.sum(matched * logits)
     loss = total / total_pairs
-    own_logits = lax.dynamic_slice_in_dim(logits, first_pair, own_caps, 1)
-    own_col_lse = lax.dynamic_slice_in_dim(col_lse, first_pair, own_caps, 0)
-    own_matched = lax.dynamic_slice_in_dim(matched, first_pair, own_caps, 1)
+    own_logits = lax.dynamic_slice_in_dim(logits, first_pair, group_caps, 1)
+    own_col_lse = lax.dynamic_slice_in_dim(col_lse, first_pair, group_caps, 0)
+    own_matched = lax.dynamic_slice_in_dim(matched, first_pair, group_caps, 1)
     grads16 = (
         LOSS_SCALE
         * (
@@ -210,8 +206,8 @@
     grad_pooled = inverse_len * (
         grad_caps - captions_unit * jnp.sum(captions_unit * grad_caps, -1, keepdims=True)
     )
-    grad_result = (grad_pooled[:, None, :] * (present / counts)[:, :, None]).reshape(own_rows, D)
-    grad_all = lax.all_gather(grad_result.astype(jnp.bfloat16), "mp", axis=0, tiled=True)
+    grad_result = (grad_pooled[:, None, :] * (present / counts)[:, :, None]).reshape(group_rows, D)
+    grad_all = grad_result.astype(jnp.bfloat16)
     grad_fc2 = jnp.einsum("gf,gd->fd", active16, grad_all, preferred_element_type=jnp.float32)
     grad_active = jnp.einsum("gd,fd->gf", grad_all, txt_fc2, preferred_element_type=jnp.float32)
     grad_hidden16 = gelu_pull(grad_active)[0].astype(jnp.bfloat16)
@@ -219,16 +215,14 @@
         "gd,gf->df", normed2_all, grad_hidden16, preferred_element_type=jnp.float32
     )
     grad_fc1_bias = jnp.sum(grad_hidden16.astype(jnp.float32), 0)
-    grad_normed2 = lax.psum_scatter(
+    grad_normed2 = lax.psum(
         jnp.einsum("gf,df->gd", grad_hidden16, txt_fc1, preferred_element_type=jnp.float32).astype(
             jnp.bfloat16
         ),
         "mp",
-        scatter_dimension=0,
-        tiled=True,
     ).astype(jnp.float32)
     grad_middle = grad_result + norm_back(grad_normed2, unit2, inverse2, txt_gains[1])
-    grad_mid_all = lax.all_gather(grad_middle.astype(jnp.bfloat16), "mp", axis=0, tiled=True)
+    grad_mid_all = grad_middle.astype(jnp.bfloat16)
     grad_out = jnp.einsum("gw,gd->wd", context, grad_mid_all, preferred_element_type=jnp.float32)
     grad_context = jnp.einsum(
         "gd,wd->gw", grad_mid_all, txt_out, preferred_element_type=jnp.float32
@@ -273,39 +267,39 @@
         scatter_dimension=0,
         tiled=True,
     ).astype(jnp.float32)
-    grad_inputs = grad_middle + norm_back(grad_normed1, unit1, inverse1, txt_gains[0])
+
+    def own(values):
+        return lax.dynamic_slice_in_dim(values, mp_index * own_rows, own_rows, 0)
+
+    unit1_own = own(unit1)
+    grad_normed2_own = own(grad_normed2)
+    unit2_own = own(unit2)
+    grad_middle_own = own(grad_middle)
+    grad_inputs = grad_middle_own + norm_back(grad_normed1, unit1_own, own(inverse1), txt_gains[0])
     summed16 = lax.psum(
         tuple(g.astype(jnp.bfloat16) for g in (grad_qkv, grad_out, grad_fc1, grad_fc2)), "dp"
     )
     summed_bias = lax.psum((grad_qv_bias, grad_fc1_bias), "dp")
-    summed_grads = (
+    small_parts = jnp.stack(
+        [
+            jnp.sum(grad_normed1 * unit1_own, 0),
+            jnp.sum(grad_normed2_own * unit2_own, 0),
+            jnp.sum(grad_normed1, 0),
+            jnp.sum(grad_normed2_own, 0),
+            jnp.sum(grad_middle_own, 0),
+            jnp.sum(own(grad_result), 0),
+        ]
+    )
+    shared = lax.psum(small_parts, ("dp", "mp"))
+    return (
+        loss,
+        grad_inputs,
         summed16[0].astype(jnp.float32),
         summed_bias[0],
         summed16[1].astype(jnp.float32),
         summed16[2].astype(jnp.float32),
         summed_bias[1],
         summed16[3].astype(jnp.float32),
-    )
-    small_parts = jnp.stack(
-        [
-            jnp.sum(grad_normed1 * unit1, 0),
-            jnp.sum(grad_normed2 * unit2, 0),
-            jnp.sum(grad_normed1, 0),
-            jnp.sum(grad_normed2, 0),
-            jnp.sum(grad_middle, 0),
-            jnp.sum(grad_result, 0),
-        ]
-    )
-    shared = lax.psum(small_parts, ("dp", "mp"))
-    return (
-        loss,
-        grad_inputs,
-        summed_grads[0],
-        summed_grads[1],
-        summed_grads[2],
-        summed_grads[3],
-        summed_grads[4],
-        summed_grads[5],
         shared[0:2],
         shared[2:4],
         shared[4:6],

time: 664 us -> 639 us (0.962)
  blocking collectives: 145 us -> 63.6 us
  waiting for transfers between devices: 243 us -> 304 us
  other arithmetic: 42.8 us -> 57.2 us
  matrix products: 124 us -> 110 us
    psum x0 -> x3, waiting for transfers between devices: none -> 106 us  [the longest x1 40 us: local(): lax.psum(jnp.einsum('gf,df->gd', grad_hidden16, txt_fc1, preferred_elemen...]
    all_gather x2 -> x0, blocking collectives: 81.5 us -> none  [the longest x1 42.8 us: local(): images_all = lax.all_gather(images16, ('dp', 'mp'), axis=0, tiled=True)]
    reduce_scatter x3 -> x0, waiting for transfers between devices: 48.3 us -> none  [the longest x1 27.5 us: local(): lax.psum_scatter(jnp.einsum('gf,df->gd', grad_hidden16, txt_fc1, preferre...]
    all_gather x1, waiting for transfers between devices: 27.8 us -> 14.7 us  [local(): lax.all_gather(img_qkv, 'mp', axis=2, tiled=True)]
    squeeze x4, local copies, waits for them, and re-layouts: 25.5 us -> 12.7 us  [image_tower(): shares, spare_lse = attention_shares(shaped[0], shaped[1], None)]
    all_gather x1, waiting for transfers between devices: 18.5 us -> 29.6 us  [local(): lax.all_gather(img_fc1, 'mp', axis=1, tiled=True)]
    reshape x0 -> x3, local copies, waits for them, and re-layouts: none -> 8.44 us  [the longest x1 6.44 us: local(): made.astype(jnp.bfloat16).reshape(group_caps, L, 3, head_count, HEAD)]
    all_gather x4 -> x2, waiting for transfers between devices: 55.2 us -> 63 us  [the longest x1 43.4 us: local(): lax.all_gather(jnp.concatenate([captions16, both[group_caps:].astype(jnp....]
  transfers between devices with their start and end apart: 13 -> 11, of which waited for: 8 -> 8; matrix products, arithmetic and copies ran while one was open for 24% -> 17% of each run, Pallas kernels for 0% -> 0%
where the time goes in v2:
time: 639 us; the launch traced here: 629 us
  waiting for transfers between devices  304 us (48%)
  matrix products  110 us (17%)
  local copies, waits for them, and re-layouts  75.8 us (12%)
  blocking collectives  63.6 us (10%)
  other arithmetic  57.2 us (9%)
  between operations  18.5 us (3%)
    psum x1, waiting for transfers between devices, local(): lax.psum(tuple((g.astype(jnp.bfloat16) for g in (grad_qkv, grad_out, grad...  87.9 us
    dot_general x2, matrix products, image_tower(): result = middle + jnp.dot(active, w_fc2, preferred_element_type=jnp.float32)  46.5 us
    all_gather x1, waiting for transfers between devices, local(): lax.all_gather(jnp.concatenate([captions16, both[group_caps:].astype(jnp....  43.4 us
    psum x1, blocking collectives, local(): shared = lax.psum(small_parts, ('dp', 'mp'))  41.5 us
    psum x1, waiting for transfers between devices, local(): lax.psum(jnp.einsum('gf,df->gd', grad_hidden16, txt_fc1, preferred_elemen...  40 us
    psum x1, waiting for transfers between devices, local(): lax.psum(jnp.dot(context, txt_out, preferred_element_type=jnp.float32).as...  33.7 us
    psum x1, waiting for transfers between devices, local(): both = lax.psum(jnp.concatenate([ffn_pooled, image_slots], 0), 'mp')  32 us
    all_gather x1, waiting for transfers between devices, local(): lax.all_gather(img_fc1, 'mp', axis=1, tiled=True)  29.6 us
  transfers between devices with their start and end apart: 11, of which 8 were waited for; matrix products, arithmetic and copies ran while one was open for 17% of the time, Pallas kernels for 0%

profile of v2, /device:TPU:0, one launch (start us, length us, event | category | flops | bytes accessed | tf_op | source)
XLA Modules:
  0.0 629.2 jit_solution(6522583633254543920)
XLA Ops:
  11.9 19.5 %all-gather.8.cloned.1.call-done = bf16[960,768]{1,0:T(8,128)(2,1)} async-done(((bf16[240,768]{1,0:T(8,128)(2,1)}), bf16[960,768]{1,0:T(8,128)(2,1)}) %all-gather.8.cloned.1.call-update) | async-done | bytes 1474576 | tf_op jit(solution)/shard_map/all_gather | solution.py:132
  31.4 1.8 convert_reduce_fusion
  33.2 2.0 fusion.32
  37.8 2.5 copy.47
  40.2 6.4 %reshape.242 = bf16[60,16,3,3,64]{4,3,1,0,2:T(4,128)(2,1)} reshape(bf16[960,3,192]{2,0,1:T(8,128)(2,1)} %copy.47) | data formatting | bytes 2211840 | tf_op jit(solution)/shard_map/reshape | solution.py:140
  46.7 3.2 fusion.216
  52.1 1.4 copy.53
  53.5 2.4 reshape.243
  56.0 1.6 convolution_convert_fusion.1
  61.6 1.4 fusion.79
  63.0 1.4 convert_reduce_fusion.2
  65.6 33.7 %all-reduce.7.cloned.1.call-done = bf16[960,768]{1,0:T(8,128)(2,1)} async-done(((bf16[960,768]{1,0:T(8,128)(2,1)}), bf16[960,768]{1,0:T(8,128)(2,1)}) %all-reduce.7.cloned.1.call-update) | async-done | bytes 1474576 | tf_op jit(solution)/shard_map/psum | solution.py:153
  99.3 4.0 fusion.215
  104.8 8.8 %multiply_convert_fusion = (bf16[960,768]{1,0:T(8,128)(2,1)S(1)}, f32[960,768]{1,0:T(8,128)}, f32[960,768]{1,0:T(8,128)}) fusion(f32[768]{0:T(1024)S(1)} %copy-done.73, bf16[768,768]{1,0:T(8,128)(2,1)S(1)} %copy-done, f32[960,768]{1,0:T(8,128)S(1)} %subtract_multiply_fusion, f32[768]{0:T(1024)S(1)} %get-tuple-element.28, f32[768]{0:T(1024)S(1)} %get-tuple-element.26), kind=kOutput, calls=%fused_computation.64 | convolution fusion | flops 1183334400 | bytes 11510784 | tf_op jit(solution)/shard_map/dot_general | solution.py:161
  115.0 2.0 multiply_reduce_fusion.5
  117.0 14.7 %all-gather.10.cloned.1.call-done = bf16[3,768,768]{1,2,0:T(8,128)(2,1)} async-done(((bf16[3,768,192]{1,2,0:T(8,128)(2,1)}), bf16[3,768,768]{1,2,0:T(8,128)(2,1)}) %all-gather.10.cloned.1.call-update) | async-done | bytes 3538960 | tf_op jit(solution)/shard_map/all_gather | solution.py:108
  131.6 3.9 convert_bitcast_fusion.2
  136.9 2.5 reshape.262
  139.4 3.3 reshape.261
  142.7 3.3 reshape.260
  146.0 2.4 fusion.72
  148.4 5.2 fusion.222
  155.7 2.2 reshape.248
  157.8 5.2 convert_bitcast_fusion
  164.2 4.1 squeeze.34
  168.2 2.8 squeeze.33
  171.0 2.8 squeeze.32
  173.9 3.8 fusion.48
  177.7 6.8 %fusion.224 = (f32[12,12,50]{2,1,0:T(8,128)S(1)}, f32[12,12,50,50]{2,3,1,0:T(8,128)S(1)}) fusion(f32[12,12,50,50]{2,3,1,0:T(8,128)S(1)} %fusion.48), kind=kOutput, calls=%fused_computation.340 | output fusion | flops 1440049 | bytes 2908800 | tf_op jit(solution)/shard_map/sub | solution.py:50
  185.7 1.8 copy.59
  187.5 4.6 reshape.246
  192.2 2.5 fusion.223
  198.7 29.6 %all-gather.14.cloned.1.call-done = bf16[768,3072]{1,0:T(8,128)(2,1)} async-done(((bf16[768,768]{1,0:T(8,128)(2,1)}), bf16[768,3072]{1,0:T(8,128)(2,1)}) %all-gather.14.cloned.1.call-update) | async-done | bytes 4718608 | tf_op jit(solution)/shard_map/all_gather | solution.py:110
  228.3 19.8 %fusion.69 = f32[435,768]{1,0:T(8,128)} fusion(f32[435,768]{1,0:T(8,128)S(1)} %copy-done.31, bf16[3072,768]{1,0:T(8,128)(2,1)} %all-gather.16.cloned.1.call-done, bf16[768,3072]{1,0:T(8,128)(2,1)} %all-gather.14.cloned.1.call-done, f32[768]{0:T(1024)S(1)} %get-tuple-element.30, f32[435]{0:T(512)S(1)} %add_rsqrt_fusion.4, f32[435]{0:T(512)S(1)} %broadcast_multiply_fusion.6), kind=kOutput, calls=%fused_computation.133 | convolution fusion | flops 4193706240 | bytes 12116376 | tf_op jit(solution)/shard_map/dot_general | solution.py:79
  248.1 1.5 reshape.249
  249.8 26.8 %fusion.61 = f32[600,768]{1,0:T(8,128)} fusion(f32[600,768]{1,0:T(8,128)} %copy-done.26, bf16[3072,768]{1,0:T(8,128)(2,1)} %all-gather.16.cloned.1.call-done, bf16[768,3072]{1,0:T(8,128)(2,1)} %all-gather.14.cloned.1.call-done, f32[768]{0:T(1024)S(1)} %get-tuple-element.30, f32[600]{0:T(1024)S(1)} %add_rsqrt_fusion, f32[600]{0:T(1024)S(1)} %broadcast_multiply_fusion), kind=kOutput, calls=%fused_computation.119 | convolution fusion | flops 5784422400 | bytes 13131456 | tf_op jit(solution)/shard_map/dot_general | solution.py:79
  276.6 1.6 reshape.247
  279.1 1.7 pad_maximum_fusion.3
  280.9 32.0 %all-reduce.9.cloned.1.call-done = f32[120,768]{1,0:T(8,128)} async-done(((f32[120,768]{1,0:T(8,128)}), f32[120,768]{1,0:T(8,128)}) %all-reduce.9.cloned.1.call-update) | async-done | bytes 368656 | tf_op jit(solution)/shard_map/psum | solution.py:172
  316.3 43.4 %all-gather.18.cloned.1.call-done = bf16[960,768]{1,0:T(8,128)(2,1)} async-done(((bf16[120,768]{1,0:T(8,128)(2,1)}), bf16[960,768]{1,0:T(8,128)(2,1)}) %all-gather.18.cloned.1.call-update) | async-done | bytes 1474576 | tf_op jit(solution)/shard_map/all_gather | solution.py:178
  359.7 1.6 fusion.219
  363.3 3.0 select_reduce_fusion
  367.8 2.1 convert_reduce_fusion.1
  371.0 2.5 convolution_convert_fusion
  373.7 40.0 %all-reduce.11.cloned.1.call-done = bf16[960,768]{1,0:T(8,128)(2,1)} async-done(((bf16[960,768]{1,0:T(8,128)(2,1)}), bf16[960,768]{1,0:T(8,128)(2,1)}) %all-reduce.11.cloned.1.call-update) | async-done | bytes 1474576 | tf_op jit(solution)/shard_map/psum | solution.py:218
  413.7 3.4 multiply_reduce_fusion.6
  417.3 2.6 bitcast_multiply_fusion
  419.9 1.6 copy-done.3
  421.5 1.4 convolution_convert_fusion.6
  425.4 1.9 convert_reduce_fusion.4
  434.6 1.6 copy.72
  437.8 3.9 bitcast_convert_fusion
  441.8 4.0 convolution_convert_fusion.2
  445.8 2.5 convolution_convert_fusion.3
  450.1 2.3 fusion.82
  457.4 22.1 %all-reduce = (f32[2,192]{1,0:T(2,128)}, f32[768]{0:T(1024)}) all-reduce(f32[2,192]{1,0:T(2,128)S(1)} %pad_maximum_fusion.6, f32[768]{0:T(1024)S(1)} %get-tuple-element.38), channel_id=1, replica_groups=mesh['dp'=8,'mp'=4] {'dp'}, use_global_device_ids=true, to_apply=%region_44.45 | all-reduce | flops 1152 | bytes 9216 | tf_op jit(solution)/shard_map/psum | solution.py:282
  479.6 1.6 fusion.112
  481.2 2.5 dynamic-slice_reduce_fusion.2
  483.8 41.5 %psum.79 = f32[6,768]{1,0:T(8,128)S(1)} all-reduce(f32[6,768]{1,0:T(8,128)S(1)} %stack.59), channel_id=1, replica_groups=mesh['dp'=8,'mp'=4] {'dp','mp'}, use_global_device_ids=true, to_apply=%region_56.57 | all-reduce | flops 4608 | bytes 36864 | tf_op jit(solution)/shard_map/psum | solution.py:293
  525.9 87.9 %all-reduce.13.cloned.1.call-done = (bf16[3,768,192]{1,2,0:T(8,128)(2,1)}, bf16[192,768]{1,0:T(8,128)(2,1)}, bf16[768,768]{1,0:T(8,128)(2,1)}, bf16[768,768]{1,0:T(8,128)(2,1)}) async-done(((bf16[3,768,192]{1,2,0:T(8,128)(2,1)}, bf16[192,768]{1,0:T(8,128)(2,1)}, bf16[768,768]{1,0:T(8,128)(2,1)}, bf16[768,768]{1,0:T(8,128)(2,1)}), (bf16[3,768,192]{1,2,0:T(8,128)(2,1)}, bf16[192,768]{1,0:T(8,128)(2,1)}, ...) | async-done | bytes 3538960 | tf_op jit(solution)/shard_map/psum | solution.py:279
  613.7 2.7 convert_element_type.247
  616.4 1.8 convert_element_type.251
  618.2 1.6 convert_element_type.253
  619.8 1.6 convert_element_type.256
  (287 shorter events, 52.8 us)
Async XLA Ops:
  7.2 97.6 %copy-start = (bf16[768,768]{1,0:T(8,128)(2,1)S(1)}, bf16[768,768]{1,0:T(8,128)(2,1)}, u32[]{:S(2)}) copy-start(bf16[768,768]{1,0:T(8,128)(2,1)} %param.32) | copy-start | bytes 3538948
  7.2 24.2 %all-gather.8.cloned.1.call-start = ((), (), s32[]{:S(2)}) async-start(), calls=%async_computation.1 | async-start | bytes 1843200 | tf_op jit(solution)/shard_map/all_gather | solution.py:132
  7.9 91.3 %all-reduce.7.cloned.1.call-start = ((), (), s32[]{:S(2)}) async-start(), calls=%async_computation.2 | async-start | bytes 2949120 | tf_op jit(solution)/shard_map/psum | solution.py:153
  9.2 51.0 %copy-start.56 = (pred[60,16]{0,1:T(8,128)(4,1)}, pred[60,16]{0,1:T(8,128)(4,1)S(1)}, u32[]{:S(2)}) copy-start(pred[60,16]{0,1:T(8,128)(4,1)S(1)} %get-tuple-element.43) | copy-start | bytes 2884
  10.2 26.4 %copy-start.64 = (f32[768]{0:T(1024)}, f32[768]{0:T(1024)S(1)}, u32[]{:S(2)}) copy-start(f32[768]{0:T(1024)S(1)} %get-tuple-element.29) | copy-start | bytes 9220
  10.2 94.6 %copy-start.66 = (f32[768]{0:T(1024)}, f32[768]{0:T(1024)S(1)}, u32[]{:S(2)}) copy-start(f32[768]{0:T(1024)S(1)} %get-tuple-element.28) | copy-start | bytes 9220
  11.0 25.6 %copy-start.50 = (f32[768]{0:T(1024)}, f32[768]{0:T(1024)S(1)}, u32[]{:S(2)}) copy-start(f32[768]{0:T(1024)S(1)} %get-tuple-element.27) | copy-start | bytes 9220
  11.0 93.7 %copy-start.52 = (f32[768]{0:T(1024)}, f32[768]{0:T(1024)S(1)}, u32[]{:S(2)}) copy-start(f32[768]{0:T(1024)S(1)} %get-tuple-element.26) | copy-start | bytes 9220
  31.4 3.8 copy-start.9
  31.4 3.8 copy-start.72
  33.2 66.0 %copy-start.54 = (f32[960]{0:T(1024)}, f32[960]{0:T(1024)S(1)}, u32[]{:S(2)}) copy-start(f32[960]{0:T(1024)S(1)} %broadcast_multiply_fusion.5) | copy-start | bytes 11524
  35.2 64.1 %copy-start.58 = (f32[960]{0:T(1024)}, f32[960]{0:T(1024)S(1)}, u32[]{:S(2)}) copy-start(f32[960]{0:T(1024)S(1)} %add_rsqrt_fusion.3) | copy-start | bytes 11524
  52.1 3.9 copy-start.32
  56.0 3.6 copy-start.14
  57.6 2.6 copy-start.61
  57.6 74.0 %all-gather.10.cloned.1.call-start = ((), (), s32[]{:S(2)}) async-start(), calls=%async_computation.3 | async-start | bytes 4423680 | tf_op jit(solution)/shard_map/all_gather | solution.py:108
  58.4 6.5 %copy-start.62 = (f32[2,768]{1,0:T(2,128)S(1)}, f32[2,768]{1,0:T(2,128)}, u32[]{:S(2)}) copy-start(f32[2,768]{1,0:T(2,128)} %param.37) | copy-start | bytes 18436
  58.4 133.8 %all-gather.12.cloned.1.call-start = ((), (), s32[]{:S(2)}) async-start(), calls=%async_computation.4 | async-start | bytes 1474560 | tf_op jit(solution)/shard_map/all_gather | solution.py:109
  59.0 139.7 %all-gather.16.cloned.1.call-start = ((), (), s32[]{:S(2)}) async-start(), calls=%async_computation.6 | async-start | bytes 5898240 | tf_op jit(solution)/shard_map/all_gather | solution.py:111
  59.6 168.7 %all-gather.14.cloned.1.call-start = ((), (), s32[]{:S(2)}) async-start(), calls=%async_computation.5 | async-start | bytes 5898240 | tf_op jit(solution)/shard_map/all_gather | solution.py:110
  60.1 252.8 %all-reduce.9.cloned.1.call-start = ((), (), s32[]{:S(2)}) async-start(), calls=%async_computation.7 | async-start | bytes 737280 | tf_op jit(solution)/shard_map/psum | solution.py:172
  60.2 4.3 copy-start.16
  103.3 11.7 %copy-start.1 = (f32[960,768]{1,0:T(8,128)}, f32[960,768]{1,0:T(8,128)S(1)}, u32[]{:S(2)}) copy-start(f32[960,768]{1,0:T(8,128)S(1)} %get-tuple-element.47) | copy-start | bytes 8847364
  104.7 8.9 %copy-start.12 = (f32[960,768]{1,0:T(8,128)}, f32[960,768]{1,0:T(8,128)S(1)}, u32[]{:S(2)}) copy-start(f32[960,768]{1,0:T(8,128)S(1)} %subtract_multiply_fusion) | copy-start | bytes 8847364
  104.8 8.9 %copy-start.69 = (bf16[768,768]{1,0:T(8,128)(2,1)S(1)}, bf16[768,768]{1,0:T(8,128)(2,1)}, u32[]{:S(2)}) copy-start(bf16[768,768]{1,0:T(8,128)(2,1)} %param.34) | copy-start | bytes 3538948
  115.0 16.7 %copy-start.23 = (bf16[435,768]{1,0:T(8,128)(2,1)S(1)}, bf16[435,768]{1,0:T(8,128)(2,1)}, u32[]{:S(2)}) copy-start(bf16[435,768]{1,0:T(8,128)(2,1)} %param.23) | copy-start | bytes 2004484
  148.4 5.2 copy-start.27
  177.6 6.8 %copy-start.25 = (bf16[12,50,12,64]{3,2,1,0:T(8,128)(2,1)S(1)}, bf16[12,50,12,64]{3,2,1,0:T(8,128)(2,1)}, u32[]{:S(2)}) copy-start(bf16[12,50,12,64]{3,2,1,0:T(8,128)(2,1)} %squeeze.32) | copy-start | bytes 2764804
  185.7 6.5 %copy-start.24 = (bf16[435,768]{1,0:T(8,128)(2,1)S(1)}, bf16[435,768]{1,0:T(8,128)(2,1)}, u32[]{:S(2)}) copy-start(bf16[435,768]{1,0:T(8,128)(2,1)} %param.23) | copy-start | bytes 2004484
  192.1 3.9 copy-start.17
  192.2 3.9 copy-start.38
  192.2 3.9 copy-start.71
  196.1 32.2 %copy-start.31 = (f32[435,768]{1,0:T(8,128)S(1)}, f32[435,768]{1,0:T(8,128)}, u32[]{:S(2)}) copy-start(f32[435,768]{1,0:T(8,128)} %copy-done.30) | copy-start | bytes 4008964
  276.6 36.3 %copy-start.39 = (f32[60,768]{1,0:T(8,128)S(1)}, f32[60,768]{1,0:T(8,128)}, u32[]{:S(2)}) copy-start(f32[60,768]{1,0:T(8,128)} %get-tuple-element.22) | copy-start | bytes 552964
  276.6 36.3 %copy-start.60 = (f32[768]{0:T(1024)S(1)}, f32[768]{0:T(1024)}, u32[]{:S(2)}) copy-start(f32[768]{0:T(1024)} %get-tuple-element.24) | copy-start | bytes 9220
  276.6 36.4 %copy-start.63 = (f32[60]{0:T(128)S(1)}, f32[60]{0:T(128)}, u32[]{:S(2)}) copy-start(f32[60]{0:T(128)} %get-tuple-element.42) | copy-start | bytes 724
  278.2 37.7 %copy-start.57 = (pred[60,16]{0,1:T(8,128)(4,1)S(1)}, pred[60,16]{0,1:T(8,128)(4,1)}, u32[]{:S(2)}) copy-start(pred[60,16]{0,1:T(8,128)(4,1)} %copy-done.56) | copy-start | bytes 2884
  278.2 37.9 %copy-start.68 = (s32[480]{0:T(512)S(1)}, s32[480]{0:T(512)}, u32[]{:S(2)}) copy-start(s32[480]{0:T(512)} %param.21) | copy-start | bytes 5764
  280.9 78.9 %all-gather.18.cloned.1.call-start = ((), (), s32[]{:S(2)}) async-start(), calls=%async_computation.10 | async-start | bytes 1658880 | tf_op jit(solution)/shard_map/all_gather | solution.py:178
  315.9 97.8 %all-reduce.11.cloned.1.call-start = ((), (), s32[]{:S(2)}) async-start(), calls=%async_computation.8 | async-start | bytes 2949120 | tf_op jit(solution)/shard_map/psum | solution.py:218
  362.3 4.7 copy-start.22
  363.3 4.4 copy-start.70
  363.3 4.4 copy-start.74
  363.3 4.4 copy-start.76
  363.3 4.4 copy-start.77
  371.0 2.6 copy-start.41
  371.0 2.6 copy-start.43
  371.0 42.7 %copy-start.47 = (f32[960]{0:T(1024)S(1)}, f32[960]{0:T(1024)}, u32[]{:S(2)}) copy-start(f32[960]{0:T(1024)} %copy-done.46) | copy-start | bytes 11524
  371.0 42.7 %copy-start.49 = (f32[960]{0:T(1024)S(1)}, f32[960]{0:T(1024)}, u32[]{:S(2)}) copy-start(f32[960]{0:T(1024)} %copy-done.48) | copy-start | bytes 11524
  371.0 42.7 %copy-start.53 = (f32[768]{0:T(1024)S(1)}, f32[768]{0:T(1024)}, u32[]{:S(2)}) copy-start(f32[768]{0:T(1024)} %copy-done.52) | copy-start | bytes 9220
  373.5 106.0 %reduce-scatter.2.cloned.1.call-start = ((), (), s32[]{:S(2)}) async-start(), calls=%async_computation.9 | async-start | bytes 1843200 | tf_op jit(solution)/shard_map/reduce_scatter | solution.py:262
  413.7 3.4 copy-start.2
  413.7 3.6 copy-start.7
  417.3 4.2 copy-start.33
  421.5 3.9 copy-start.6
  433.8 4.0 copy-start.44
  437.8 4.0 copy-start.29
  441.7 4.1 copy-start.67
  441.7 172.0 %all-reduce.13.cloned.1.call-start = ((), (), s32[]{:S(2)}) async-start(), calls=%async_computation.11 | async-start | bytes 7077888 | tf_op jit(solution)/shard_map/psum | solution.py:279
  441.8 4.0 copy-start.13
  441.8 4.0 copy-start.79
  445.8 2.5 copy-start.4
  613.7 4.5 copy-start.35
  613.7 6.1 copy-start.34
  (27 other events, 42.8 us)
Sparse Core Ops, SparseCore 0:
  9.6 21.7 all-gather.7
  57.8 41.4 all-reduce.6
  100.8 30.7 all-gather.9
  133.1 17.4 all-gather.11
  151.9 37.4 all-gather.15
  190.8 37.4 all-gather.13
  281.0 31.9 all-reduce.8
  316.0 43.6 all-gather.17
  373.7 39.9 all-reduce.10
  441.8 27.4 reduce-scatter.1
  473.8 139.8 all-reduce.12

commit v3 on v2

--- a/solution.py
+++ b/solution.py
@@ -50,6 +50,47 @@
     raised = jnp.exp(scores - highest)
     totals = jnp.sum(raised, -1, keepdims=True)
     return (raised / totals, highest + jnp.log(totals))
+
+
+def axis_bits(axis):
+    count = lax.axis_size(axis)
+    bits = count.bit_length() - 1
+    assert 1 << bits == count
+    return count, list(reversed(range(bits)))
+
+
+def exchange(values, axis, count, bit):
+    return lax.ppermute(values, axis, [(i, i ^ (1 << bit)) for i in range(count)])
+
+
+def gather_stacked(values, axis):
+    count, bits = axis_bits(axis)
+    data = values[None]
+    for bit in bits:
+        data = jnp.concatenate([data, exchange(data, axis, count, bit)], 0)
+    return data
+
+
+def gather_ordered(values, axis):
+    count, bits = axis_bits(axis)
+    index = lax.axis_index(axis)
+    data = values
+    done = []
+    for bit in bits:
+        other = exchange(data, axis, count, bit)
+        upper = ((index >> bit) & 1) == 1
+        data = jnp.stack([jnp.where(upper, other, data), jnp.where(upper, data, other)], 0)
+        done.insert(0, bit)
+    order = sorted(range(len(done)), key=lambda a: -done[a])
+    data = data.transpose(order + list(range(len(done), data.ndim)))
+    return data.reshape((count,) + values.shape)
+
+
+def sum_exchanged(values, axis):
+    count, bits = axis_bits(axis)
+    for bit in reversed(bits):
+        values = values + exchange(values, axis, count, bit)
+    return values
 
 
 def image_tower(tokens, count, length, gains, weights):
@@ -104,11 +145,13 @@
     txt_shifts,
     txt_biases,
 ):
+    qkv_parts = gather_stacked(img_qkv, "mp")
+    fc1_parts = gather_stacked(img_fc1, "mp")
     weights = (
-        lax.all_gather(img_qkv, "mp", axis=2, tiled=True),
-        lax.all_gather(img_out, "mp", axis=0, tiled=True),
-        lax.all_gather(img_fc1, "mp", axis=1, tiled=True),
-        lax.all_gather(img_fc2, "mp", axis=0, tiled=True),
+        qkv_parts.transpose(1, 2, 0, 3).reshape(3, D, -1),
+        gather_stacked(img_out, "mp").reshape(-1, D),
+        fc1_parts.transpose(1, 0, 2).reshape(D, -1),
+        gather_stacked(img_fc2, "mp").reshape(-1, D),
     )
     low_count = image_low.shape[0] // P_LOW
     high_count = image_high.shape[0] // P_HIGH
@@ -169,14 +212,14 @@
         mp_index * own_caps,
         0,
     )
-    both = lax.psum(jnp.concatenate([ffn_pooled, image_slots], 0), "mp")
+    both = sum_exchanged(jnp.concatenate([ffn_pooled, image_slots], 0), "mp")
     mid_pooled = jnp.sum(middle.reshape(group_caps, L, D) * present[:, :, None], 1)
     pooled = (mid_pooled + both[:group_caps]) / counts + txt_biases[1]
     inverse_len = lax.rsqrt(jnp.sum(pooled * pooled, -1, keepdims=True) + EPS)
     captions_unit = pooled * inverse_len
     captions16 = captions_unit.astype(jnp.bfloat16)
-    gathered = lax.all_gather(
-        jnp.concatenate([captions16, both[group_caps:].astype(jnp.bfloat16)], 0), "dp", axis=0
+    gathered = gather_ordered(
+        jnp.concatenate([captions16, both[group_caps:].astype(jnp.bfloat16)], 0), "dp"
     )
     arrived = gathered[:, :group_caps].reshape(-1, D)
     images_all = gathered[:, group_caps:].reshape(-1, D)

time: 639 us -> 609 us (0.953)
  waiting for transfers between devices: 304 us -> 228 us
  other arithmetic: 57.2 us -> 75.9 us
  starting transfers between devices: 0.44 us -> 13.6 us
  local copies, waits for them, and re-layouts: 75.8 us -> 84.8 us
    ppermute x0 -> x13, waiting for transfers between devices: none -> 96.1 us  [exchange(): return lax.ppermute(values, axis, [(i, i ^ 1 << bit) for i in range(count)])]
    all_gather x5 -> x0, waiting for transfers between devices: 87.7 us -> none  [the longest x1 43.4 us: local(): lax.all_gather(jnp.concatenate([captions16, both[group_caps:].astype(jnp....]
    psum x1, waiting for transfers between devices: 33.7 us -> 0.02 us  [local(): lax.psum(jnp.dot(context, txt_out, preferred_element_type=jnp.float32).as...]
    psum x1 -> x0, waiting for transfers between devices: 32 us -> none  [local(): both = lax.psum(jnp.concatenate([ffn_pooled, image_slots], 0), 'mp')]
    all_gather x1, waiting for transfers between devices: 19.5 us -> 0.01 us  [local(): lax.all_gather(text_in, 'mp', axis=0, tiled=True).astype(jnp.float32)]
    concatenate x1 -> x9, other arithmetic: 1.69 us -> 20.9 us  [the longest x8 20.8 us: gather_stacked(): data = jnp.concatenate([data, exchange(data, axis, count, bit)], 0)]
    ppermute x0 -> x13, starting transfers between devices: none -> 13.2 us  [exchange(): return lax.ppermute(values, axis, [(i, i ^ 1 << bit) for i in range(count)])]
  transfers between devices with their start and end apart: 11 -> 18, of which waited for: 8 -> 10; matrix products, arithmetic and copies ran while one was open for 17% -> 28% of each run, Pallas kernels for 0% -> 0%
where the time goes in v3:
time: 609 us; the launch traced here: 600 us
  waiting for transfers between devices  228 us (37%)
  matrix products  115 us (19%)
  local copies, waits for them, and re-layouts  84.8 us (14%)
  other arithmetic  75.9 us (12%)
  blocking collectives  63.5 us (10%)
  between operations  18.8 us (3%)
  starting transfers between devices  13.6 us (2%)
    ppermute x13, waiting for transfers between devices, exchange(): return lax.ppermute(values, axis, [(i, i ^ 1 << bit) for i in range(count)])  96.1 us
    psum x1, waiting for transfers between devices, local(): lax.psum(tuple((g.astype(jnp.bfloat16) for g in (grad_qkv, grad_out, grad...  87.8 us
    dot_general x2, matrix products, image_tower(): result = middle + jnp.dot(active, w_fc2, preferred_element_type=jnp.float32)  45.7 us
    psum x1, waiting for transfers between devices, local(): lax.psum(jnp.einsum('gf,df->gd', grad_hidden16, txt_fc1, preferred_elemen...  44.3 us
    psum x1, blocking collectives, local(): shared = lax.psum(small_parts, ('dp', 'mp'))  41.4 us
    psum x1, blocking collectives, local(): summed_bias = lax.psum((grad_qv_bias, grad_fc1_bias), 'dp')  22.1 us
    concatenate x8, other arithmetic, gather_stacked(): data = jnp.concatenate([data, exchange(data, axis, count, bit)], 0)  20.8 us
    squeeze x4, local copies, waits for them, and re-layouts, image_tower(): shares, spare_lse = attention_shares(shaped[0], shaped[1], None)  14.7 us
  transfers between devices with their start and end apart: 18, of which 10 were waited for; matrix products, arithmetic and copies ran while one was open for 28% of the time, Pallas kernels for 0%

profile of v3, /device:TPU:0, one launch (start us, length us, event | category | flops | bytes accessed | tf_op | source)
XLA Modules:
  0.0 599.7 jit_solution(7105411776497436561)
XLA Ops:
  7.2 3.1 collective-permute-start
  10.4 1.9 collective-permute-start.6
  17.4 2.0 fusion.79
  20.8 2.2 fusion.55
  29.3 16.0 %collective-permute-done.2 = bf16[1,192,768]{2,1,0:T(8,128)(2,1)} collective-permute-done((bf16[1,192,768]{2,1,0:T(8,128)(2,1)}, bf16[1,192,768]{2,1,0:T(8,128)(2,1)}, u32[]{:S(2)}, u32[]{:S(2)}) %collective-permute-start.2) | collective-permute-done | bytes 294944 | tf_op jit(solution)/shard_map/ppermute | solution.py:63
  49.1 2.9 pad_maximum_fusion.5
  52.5 2.1 pad_maximum_fusion.6
  54.6 16.0 %collective-permute-done.6 = bf16[1,768,768]{2,1,0:T(8,128)(2,1)} collective-permute-done((bf16[1,768,768]{2,1,0:T(8,128)(2,1)}, bf16[1,768,768]{2,1,0:T(8,128)(2,1)}, u32[]{:S(2)}, u32[]{:S(2)}) %collective-permute-start.6) | collective-permute-done | bytes 1179680 | tf_op jit(solution)/shard_map/ppermute | solution.py:63
  70.6 2.9 pad_maximum_fusion.4
  73.5 21.4 %collective-permute-done.4 = bf16[1,768,768]{1,2,0:T(8,128)(2,1)S(1)} collective-permute-done((bf16[1,768,768]{1,2,0:T(8,128)(2,1)S(1)}, bf16[1,768,768]{1,2,0:T(8,128)(2,1)S(1)}, u32[]{:S(2)}, u32[]{:S(2)}) %collective-permute-start.4) | collective-permute-done | bytes 1179680 | tf_op jit(solution)/shard_map/ppermute | solution.py:63
  98.5 2.0 fusion.32
  100.6 2.5 fusion.134
  104.2 2.5 copy.48
  106.7 6.4 %reshape.257 = bf16[60,16,3,3,64]{4,3,1,0,2:T(4,128)(2,1)} reshape(bf16[960,3,192]{2,0,1:T(8,128)(2,1)} %copy.48) | data formatting | bytes 2211840 | tf_op jit(solution)/shard_map/reshape | solution.py:183
  113.2 3.2 fusion.216
  120.0 2.4 reshape.258
  124.4 2.2 pad_maximum_fusion.2
  126.7 1.9 convert_bitcast_fusion.2
  129.8 3.3 reshape.281
  133.1 3.3 reshape.280
  136.4 3.0 fusion.72
  139.4 3.9 fusion.222
  143.2 2.3 reshape.279
  145.6 4.1 fusion.76
  149.7 2.2 copy.71
  151.9 4.4 reshape.267
  156.3 3.5 fusion.223
  159.8 2.5 convert_bitcast_fusion
  163.9 4.1 squeeze.34
  168.0 4.1 squeeze.33
  172.0 3.8 fusion.48
  175.8 3.1 fusion.224
  178.9 4.1 squeeze.32
  183.0 4.2 convert_bitcast_fusion.1
  189.0 4.3 reshape.262
  193.4 2.9 fusion.225
  198.0 4.0 fusion.215
  203.5 8.7 %multiply_convert_fusion = (bf16[960,768]{1,0:T(8,128)(2,1)S(1)}, f32[960,768]{1,0:T(8,128)}, f32[960,768]{1,0:T(8,128)}) fusion(f32[768]{0:T(1024)S(1)} %copy-done.85, bf16[768,768]{1,0:T(8,128)(2,1)S(1)} %copy-done, f32[960,768]{1,0:T(8,128)S(1)} %subtract_multiply_fusion, f32[768]{0:T(1024)S(1)} %copy-done.75, f32[768]{0:T(1024)S(1)} %get-tuple-element.26), kind=kOutput, calls=%fused_computation.67 | convolution fusion | flops 1183334400 | bytes 11510784 | tf_op jit(solution)/shard_map/dot_general | solution.py:204
  213.6 1.9 multiply_reduce_fusion.5
  215.5 3.9 pad_maximum_fusion.1
  219.4 4.0 pad_maximum_fusion
  223.4 19.8 %fusion.69 = f32[435,768]{1,0:T(8,128)} fusion(f32[435,768]{1,0:T(8,128)S(1)} %copy-done.35, bf16[3072,768]{1,0:T(8,128)(2,1)} %bitcast.136, bf16[768,3072]{0,1:T(8,128)(2,1)} %bitcast.138, f32[768]{0:T(1024)S(1)} %copy-done.77, f32[435]{0:T(512)S(1)} %add_rsqrt_fusion.4, f32[435]{0:T(512)S(1)} %broadcast_multiply_fusion.6), kind=kOutput, calls=%fused_computation.140 | convolution fusion | flops 4193706240 | bytes 12116376 | tf_op jit(solution)/shard_map/dot_general | solution.py:120
  245.0 26.0 %fusion.61 = f32[600,768]{1,0:T(8,128)} fusion(f32[600,768]{1,0:T(8,128)} %copy-done.31, bf16[3072,768]{1,0:T(8,128)(2,1)} %bitcast.137, bf16[768,3072]{0,1:T(8,128)(2,1)} %bitcast.139, f32[768]{0:T(1024)S(1)} %copy-done.77, f32[600]{0:T(1024)S(1)} %add_rsqrt_fusion, f32[600]{0:T(1024)S(1)} %broadcast_multiply_fusion), kind=kOutput, calls=%fused_computation.125 | convolution fusion | flops 5784422400 | bytes 13131456 | tf_op jit(solution)/shard_map/dot_general | solution.py:120
  277.2 9.2 %collective-permute-done.9 = f32[120,768]{1,0:T(8,128)S(1)} collective-permute-done((f32[120,768]{1,0:T(8,128)S(1)}, f32[120,768]{1,0:T(8,128)S(1)}, u32[]{:S(2)}, u32[]{:S(2)}) %collective-permute-start.9) | collective-permute-done | bytes 368672 | tf_op jit(solution)/shard_map/ppermute | solution.py:63
  286.9 2.8 collective-permute-start.10
  289.7 8.3 %collective-permute-done.10 = bf16[120,768]{1,0:T(8,128)(2,1)S(1)} collective-permute-done((bf16[120,768]{1,0:T(8,128)(2,1)S(1)}, bf16[120,768]{1,0:T(8,128)(2,1)S(1)}, u32[]{:S(2)}, u32[]{:S(2)}) %collective-permute-start.10) | collective-permute-done | bytes 184352 | tf_op jit(solution)/shard_map/ppermute | solution.py:63
  298.9 8.8 %collective-permute-done.11 = bf16[2,120,768]{2,1,0:T(8,128)(2,1)S(1)} collective-permute-done((bf16[2,120,768]{2,1,0:T(8,128)(2,1)S(1)}, bf16[2,120,768]{2,1,0:T(8,128)(2,1)S(1)}, u32[]{:S(2)}, u32[]{:S(2)}) %collective-permute-start.11) | collective-permute-done | bytes 368672 | tf_op jit(solution)/shard_map/ppermute | solution.py:63
  310.6 15.1 %collective-permute-done.12 = bf16[2,2,120,768]{3,2,1,0:T(8,128)(2,1)S(1)} collective-permute-done((bf16[2,2,120,768]{3,2,1,0:T(8,128)(2,1)}, bf16[2,2,120,768]{3,2,1,0:T(8,128)(2,1)S(1)}, u32[]{:S(2)}, u32[]{:S(2)}) %collective-permute-start.12) | collective-permute-done | bytes 737312 | tf_op jit(solution)/shard_map/ppermute | solution.py:63
  329.4 2.7 select_reduce_fusion
  333.6 2.1 convert_reduce_fusion.1
  336.9 2.5 convolution_convert_fusion
  339.5 44.3 %all-reduce.8.cloned.1.call-done = bf16[960,768]{1,0:T(8,128)(2,1)} async-done(((bf16[960,768]{1,0:T(8,128)(2,1)}), bf16[960,768]{1,0:T(8,128)(2,1)}) %all-reduce.8.cloned.1.call-update) | async-done | bytes 1474576 | tf_op jit(solution)/shard_map/psum | solution.py:261
  383.9 3.4 multiply_reduce_fusion.6
  387.5 2.7 bitcast_multiply_fusion
  395.7 1.9 convert_reduce_fusion.4
  408.1 3.9 bitcast_convert_fusion
  412.1 4.0 convolution_convert_fusion.2
  416.1 2.5 convolution_convert_fusion.3
  420.4 2.3 fusion.82
  427.8 22.1 %all-reduce = (f32[2,192]{1,0:T(2,128)}, f32[768]{0:T(1024)}) all-reduce(f32[2,192]{1,0:T(2,128)S(1)} %pad_maximum_fusion.16, f32[768]{0:T(1024)S(1)} %get-tuple-element.38), channel_id=1, replica_groups=mesh['dp'=8,'mp'=4] {'dp'}, use_global_device_ids=true, to_apply=%region_43.44 | all-reduce | flops 1152 | bytes 9216 | tf_op jit(solution)/shard_map/psum | solution.py:325
  451.5 2.5 dynamic-slice_reduce_fusion.2
  454.1 41.4 %psum.71 = f32[6,768]{1,0:T(8,128)S(1)} all-reduce(f32[6,768]{1,0:T(8,128)S(1)} %stack.95), channel_id=1, replica_groups=mesh['dp'=8,'mp'=4] {'dp','mp'}, use_global_device_ids=true, to_apply=%region_55.56 | all-reduce | flops 4608 | bytes 36864 | tf_op jit(solution)/shard_map/psum | solution.py:336
  496.1 87.8 %all-reduce.10.cloned.1.call-done = (bf16[3,768,192]{1,2,0:T(8,128)(2,1)}, bf16[192,768]{1,0:T(8,128)(2,1)}, bf16[768,768]{1,0:T(8,128)(2,1)}, bf16[768,768]{1,0:T(8,128)(2,1)}) async-done(((bf16[3,768,192]{1,2,0:T(8,128)(2,1)}, bf16[192,768]{1,0:T(8,128)(2,1)}, bf16[768,768]{1,0:T(8,128)(2,1)}, bf16[768,768]{1,0:T(8,128)(2,1)}), (bf16[3,768,192]{1,2,0:T(8,128)(2,1)}, bf16[192,768]{1,0:T(8,128)(2,1)}, ...) | async-done | bytes 3538960 | tf_op jit(solution)/shard_map/psum | solution.py:322
  583.9 2.7 convert_element_type.247
  (337 shorter events, 83.1 us)
Async XLA Ops:
  7.2 196.3 %copy-start = (bf16[768,768]{1,0:T(8,128)(2,1)S(1)}, bf16[768,768]{1,0:T(8,128)(2,1)}, u32[]{:S(2)}) copy-start(bf16[768,768]{1,0:T(8,128)(2,1)} %param.32) | copy-start | bytes 3538948
  7.2 89.6 %all-gather.2.cloned.1.call-start = ((), (), s32[]{:S(2)}) async-start(), calls=%async_computation.1 | async-start | bytes 1843200 | tf_op jit(solution)/shard_map/all_gather | solution.py:175
  7.2 41.9 %collective-permute-start = (bf16[1,3,768,192]{2,3,0,1:T(8,128)(2,1)}, bf16[1,3,768,192]{2,3,0,1:T(8,128)(2,1)}, u32[]{:S(2)}, u32[]{:S(2)}) collective-permute-start(bf16[1,3,768,192]{2,3,0,1:T(8,128)(2,1)} %bitcast.140), channel_id=1, source_target_pairs={{0,2},{1,3},{2,0},{3,1},{4,6},{5,7},{6,4},{7,5},{8,10},{9,11},{10,... | collective-permute-start | bytes 2654216 | tf_op jit(solution)/shard_map/ppermute | solution.py:63
  10.3 35.0 %collective-permute-start.2 = (bf16[1,192,768]{2,1,0:T(8,128)(2,1)}, bf16[1,192,768]{2,1,0:T(8,128)(2,1)}, u32[]{:S(2)}, u32[]{:S(2)}) collective-permute-start(bf16[1,192,768]{2,1,0:T(8,128)(2,1)} %bitcast.147), channel_id=1, source_target_pairs={{0,2},{1,3},{2,0},{3,1},{4,6},{5,7},{6,4},{7,5},{8,10},{9,11},{10,... | collective-permute-start | bytes 884744 | tf_op jit(solution)/shard_map/ppermute | solution.py:63
  10.4 12.7 %copy-start.81 = (f32[2,192]{1,0:T(2,128)S(1)}, f32[2,192]{1,0:T(2,128)}, u32[]{:S(2)}) copy-start(f32[2,192]{1,0:T(2,128)} %param.30) | copy-start | bytes 4612
  10.4 13.4 %copy-start.72 = (s32[60,16]{0,1:T(8,128)S(1)}, s32[60,16]{0,1:T(8,128)}, u32[]{:S(2)}) copy-start(s32[60,16]{0,1:T(8,128)} %param.20) | copy-start | bytes 11524
  10.4 60.2 %collective-permute-start.6 = (bf16[1,768,768]{2,1,0:T(8,128)(2,1)}, bf16[1,768,768]{2,1,0:T(8,128)(2,1)}, u32[]{:S(2)}, u32[]{:S(2)}) collective-permute-start(bf16[1,768,768]{2,1,0:T(8,128)(2,1)} %bitcast.133), channel_id=1, source_target_pairs={{0,2},{1,3},{2,0},{3,1},{4,6},{5,7},{6,4},{7,5},{8,10},{9,11},{10,... | collective-permute-start | bytes 3538952 | tf_op jit(solution)/shard_map/ppermute | solution.py:63
  13.9 81.0 %copy-start.11 = (bf16[768,768]{0,1:T(8,128)(2,1)}, bf16[768,768]{0,1:T(8,128)(2,1)S(1)}, u32[]{:S(2)}) copy-start(bf16[768,768]{0,1:T(8,128)(2,1)S(1)} %copy.62) | copy-start | bytes 3538948
  13.9 81.0 %collective-permute-start.4 = (bf16[1,768,768]{1,2,0:T(8,128)(2,1)S(1)}, bf16[1,768,768]{1,2,0:T(8,128)(2,1)S(1)}, u32[]{:S(2)}, u32[]{:S(2)}) collective-permute-start(bf16[1,768,768]{1,2,0:T(8,128)(2,1)S(1)} %bitcast.129), channel_id=1, source_target_pairs={{0,2},{1,3},{2,0},{3,1},{4,6},{5,7},{6,4},{7,5},{8,10},{9,11},{10,... | collective-permute-start | bytes 3538952 | tf_op jit(solution)/shard_map/ppermute | solution.py:63
  14.1 183.9 %all-reduce.6.cloned.1.call-start = ((), (), s32[]{:S(2)}) async-start(), calls=%async_computation.2 | async-start | bytes 2949120 | tf_op jit(solution)/shard_map/psum | solution.py:196
  24.3 30.3 %copy-start.61 = (pred[60,16]{0,1:T(8,128)(4,1)}, pred[60,16]{0,1:T(8,128)(4,1)S(1)}, u32[]{:S(2)}) copy-start(pred[60,16]{0,1:T(8,128)(4,1)S(1)} %get-tuple-element.43) | copy-start | bytes 2884
  28.5 24.0 %copy-start.40 = (bf16[192,768]{1,0:T(8,128)(2,1)S(1)}, bf16[192,768]{1,0:T(8,128)(2,1)}, u32[]{:S(2)}) copy-start(bf16[192,768]{1,0:T(8,128)(2,1)} %param.26) | copy-start | bytes 884740
  29.3 71.2 %copy-start.55 = (f32[768]{0:T(1024)}, f32[768]{0:T(1024)S(1)}, u32[]{:S(2)}) copy-start(f32[768]{0:T(1024)S(1)} %get-tuple-element.27) | copy-start | bytes 9220
  29.3 174.2 %copy-start.57 = (f32[768]{0:T(1024)}, f32[768]{0:T(1024)S(1)}, u32[]{:S(2)}) copy-start(f32[768]{0:T(1024)S(1)} %get-tuple-element.26) | copy-start | bytes 9220
  46.4 6.0 %collective-permute-start.3 = (bf16[2,192,768]{2,1,0:T(8,128)(2,1)S(1)}, bf16[2,192,768]{2,1,0:T(8,128)(2,1)S(1)}, u32[]{:S(2)}, u32[]{:S(2)}) collective-permute-start(bf16[2,192,768]{2,1,0:T(8,128)(2,1)S(1)} %pad_maximum_fusion.9), channel_id=1, source_target_pairs={{0,1},{1,0},{2,3},{3,2},{4,5},{5,4},{6,7},{7,6},{8,9},{9,8},{10,11... | collective-permute-start | bytes 1769480 | tf_op jit(solution)/shard_map/ppermute | solution.py:63
  49.1 21.5 %copy-start.14 = (bf16[768,768]{1,0:T(8,128)(2,1)S(1)}, bf16[768,768]{1,0:T(8,128)(2,1)}, u32[]{:S(2)}) copy-start(bf16[768,768]{1,0:T(8,128)(2,1)} %param.28) | copy-start | bytes 3538948
  52.0 72.4 %collective-permute-start.1 = (bf16[2,3,768,192]{2,3,0,1:T(8,128)(2,1)}, bf16[2,3,768,192]{2,3,0,1:T(8,128)(2,1)}, u32[]{:S(2)}, u32[]{:S(2)}) collective-permute-start(bf16[2,3,768,192]{2,3,0,1:T(8,128)(2,1)} %pad_maximum_fusion.5), channel_id=1, source_target_pairs={{0,1},{1,0},{2,3},{3,2},{4,5},{5,4},{6,7},{7,6},{8,9},{9,8},{10,11... | collective-permute-start | bytes 5308424 | tf_op jit(solution)/shard_map/ppermute | solution.py:63
  73.5 142.0 %collective-permute-start.7 = (bf16[2,768,768]{2,1,0:T(8,128)(2,1)}, bf16[2,768,768]{2,1,0:T(8,128)(2,1)}, u32[]{:S(2)}, u32[]{:S(2)}) collective-permute-start(bf16[2,768,768]{2,1,0:T(8,128)(2,1)} %pad_maximum_fusion.4), channel_id=1, source_target_pairs={{0,1},{1,0},{2,3},{3,2},{4,5},{5,4},{6,7},{7,6},{8,9},{9,8},{10,11... | collective-permute-start | bytes 7077896 | tf_op jit(solution)/shard_map/ppermute | solution.py:63
  96.7 122.7 %collective-permute-start.5 = (bf16[2,768,768]{1,2,0:T(8,128)(2,1)}, bf16[2,768,768]{1,2,0:T(8,128)(2,1)}, u32[]{:S(2)}, u32[]{:S(2)}) collective-permute-start(bf16[2,768,768]{1,2,0:T(8,128)(2,1)} %pad_maximum_fusion.3), channel_id=1, source_target_pairs={{0,1},{1,0},{2,3},{3,2},{4,5},{5,4},{6,7},{7,6},{8,9},{9,8},{10,11... | collective-permute-start | bytes 7077896 | tf_op jit(solution)/shard_map/ppermute | solution.py:63
  96.8 3.8 copy-start.9
  98.5 99.5 %copy-start.59 = (f32[960]{0:T(1024)}, f32[960]{0:T(1024)S(1)}, u32[]{:S(2)}) copy-start(f32[960]{0:T(1024)S(1)} %broadcast_multiply_fusion.5) | copy-start | bytes 11524
  100.5 97.5 %copy-start.63 = (f32[960]{0:T(1024)}, f32[960]{0:T(1024)S(1)}, u32[]{:S(2)}) copy-start(f32[960]{0:T(1024)S(1)} %add_rsqrt_fusion.3) | copy-start | bytes 11524
  118.5 3.9 copy-start.36
  122.4 4.2 copy-start.20
  124.1 259.7 %all-reduce.8.cloned.1.call-start = ((), (), s32[]{:S(2)}) async-start(), calls=%async_computation.3 | async-start | bytes 2949120 | tf_op jit(solution)/shard_map/psum | solution.py:261
  149.7 6.5 %copy-start.30 = (bf16[435,768]{1,0:T(8,128)(2,1)S(1)}, bf16[435,768]{1,0:T(8,128)(2,1)}, u32[]{:S(2)}) copy-start(bf16[435,768]{1,0:T(8,128)(2,1)} %param.23) | copy-start | bytes 2004484
  156.2 3.5 copy-start.22
  156.2 3.5 copy-start.24
  202.0 11.5 %copy-start.1 = (f32[960,768]{1,0:T(8,128)}, f32[960,768]{1,0:T(8,128)S(1)}, u32[]{:S(2)}) copy-start(f32[960,768]{1,0:T(8,128)S(1)} %get-tuple-element.47) | copy-start | bytes 8847364
  203.5 8.7 %copy-start.18 = (f32[960,768]{1,0:T(8,128)}, f32[960,768]{1,0:T(8,128)S(1)}, u32[]{:S(2)}) copy-start(f32[960,768]{1,0:T(8,128)S(1)} %subtract_multiply_fusion) | copy-start | bytes 8847364
  203.5 8.7 %copy-start.83 = (bf16[768,768]{1,0:T(8,128)(2,1)S(1)}, bf16[768,768]{1,0:T(8,128)(2,1)}, u32[]{:S(2)}) copy-start(bf16[768,768]{1,0:T(8,128)(2,1)} %param.34) | copy-start | bytes 3538948
  215.5 4.0 copy-start.12
  215.5 4.0 copy-start.17
  219.4 4.0 copy-start.35
  219.4 4.0 copy-start.77
  272.5 14.1 %copy-start.65 = (f32[768]{0:T(1024)S(1)}, f32[768]{0:T(1024)}, u32[]{:S(2)}) copy-start(f32[768]{0:T(1024)} %get-tuple-element.24) | copy-start | bytes 9220
  272.5 14.1 %copy-start.73 = (f32[60]{0:T(128)S(1)}, f32[60]{0:T(128)}, u32[]{:S(2)}) copy-start(f32[60]{0:T(128)} %get-tuple-element.42) | copy-start | bytes 724
  272.7 13.9 %copy-start.43 = (f32[60,768]{1,0:T(8,128)S(1)}, f32[60,768]{1,0:T(8,128)}, u32[]{:S(2)}) copy-start(f32[60,768]{1,0:T(8,128)} %get-tuple-element.22) | copy-start | bytes 552964
  273.7 1.8 collective-permute-start.8
  275.5 10.9 %collective-permute-start.9 = (f32[120,768]{1,0:T(8,128)S(1)}, f32[120,768]{1,0:T(8,128)S(1)}, u32[]{:S(2)}, u32[]{:S(2)}) collective-permute-start(f32[120,768]{1,0:T(8,128)S(1)} %fusion.259), channel_id=1, source_target_pairs={{0,2},{1,3},{2,0},{3,1},{4,6},{5,7},{6,4},{7,5},{8,10},{9,11},{10,... | collective-permute-start | bytes 1105928 | tf_op jit(solution)/shard_map/ppermute | solution.py:63
  286.5 23.8 %copy-start.62 = (pred[60,16]{0,1:T(8,128)(4,1)S(1)}, pred[60,16]{0,1:T(8,128)(4,1)}, u32[]{:S(2)}) copy-start(pred[60,16]{0,1:T(8,128)(4,1)} %copy-done.61) | copy-start | bytes 2884
  286.5 23.9 %copy-start.80 = (s32[480]{0:T(512)S(1)}, s32[480]{0:T(512)}, u32[]{:S(2)}) copy-start(s32[480]{0:T(512)} %param.21) | copy-start | bytes 5764
  286.9 11.1 %collective-permute-start.10 = (bf16[120,768]{1,0:T(8,128)(2,1)S(1)}, bf16[120,768]{1,0:T(8,128)(2,1)S(1)}, u32[]{:S(2)}, u32[]{:S(2)}) collective-permute-start(bf16[120,768]{1,0:T(8,128)(2,1)S(1)} %pad_maximum_fusion.14), channel_id=1, source_target_pairs={{0,16},{4,20},{8,24},{12,28},{16,0},{20,4},{24,8},{28,12},{1,17},{... | collective-permute-start | bytes 552968 | tf_op jit(solution)/shard_map/ppermute | solution.py:63
  298.1 9.6 %collective-permute-start.11 = (bf16[2,120,768]{2,1,0:T(8,128)(2,1)S(1)}, bf16[2,120,768]{2,1,0:T(8,128)(2,1)S(1)}, u32[]{:S(2)}, u32[]{:S(2)}) collective-permute-start(bf16[2,120,768]{2,1,0:T(8,128)(2,1)S(1)} %pad_maximum_fusion.13), channel_id=1, source_target_pairs={{0,8},{4,12},{8,0},{12,4},{16,24},{20,28},{24,16},{28,20},{1,9},{5... | collective-permute-start | bytes 1105928 | tf_op jit(solution)/shard_map/ppermute | solution.py:63
  308.6 17.0 %collective-permute-start.12 = (bf16[2,2,120,768]{3,2,1,0:T(8,128)(2,1)}, bf16[2,2,120,768]{3,2,1,0:T(8,128)(2,1)S(1)}, u32[]{:S(2)}, u32[]{:S(2)}) collective-permute-start(bf16[2,2,120,768]{3,2,1,0:T(8,128)(2,1)} %pad_maximum_fusion.8), channel_id=1, source_target_pairs={{0,4},{4,0},{8,12},{12,8},{16,20},{20,16},{24,28},{28,24},{1,5},{5... | collective-permute-start | bytes 2211848 | tf_op jit(solution)/shard_map/ppermute | solution.py:63
  329.4 4.2 copy-start.84
  329.4 4.2 copy-start.86
  329.4 4.2 copy-start.88
  329.4 4.2 copy-start.89
  336.9 47.0 %copy-start.52 = (f32[960]{0:T(1024)S(1)}, f32[960]{0:T(1024)}, u32[]{:S(2)}) copy-start(f32[960]{0:T(1024)} %copy-done.51) | copy-start | bytes 11524
  336.9 47.0 %copy-start.54 = (f32[960]{0:T(1024)S(1)}, f32[960]{0:T(1024)}, u32[]{:S(2)}) copy-start(f32[960]{0:T(1024)} %copy-done.53) | copy-start | bytes 11524
  336.9 47.0 %copy-start.58 = (f32[768]{0:T(1024)S(1)}, f32[768]{0:T(1024)}, u32[]{:S(2)}) copy-start(f32[768]{0:T(1024)} %copy-done.57) | copy-start | bytes 9220
  339.4 110.5 %reduce-scatter.2.cloned.1.call-start = ((), (), s32[]{:S(2)}) async-start(), calls=%async_computation.4 | async-start | bytes 1843200 | tf_op jit(solution)/shard_map/reduce_scatter | solution.py:305
  383.9 3.6 copy-start.7
  387.5 4.3 copy-start.37
  391.8 4.0 copy-start.6
  404.1 4.0 copy-start.48
  408.1 4.0 copy-start.33
  412.0 4.1 copy-start.76
  412.0 171.9 %all-reduce.10.cloned.1.call-start = ((), (), s32[]{:S(2)}) async-start(), calls=%async_computation.5 | async-start | bytes 7077888 | tf_op jit(solution)/shard_map/psum | solution.py:322
  412.1 4.0 copy-start.19
  412.1 4.0 copy-start.91
  583.9 4.5 copy-start.39
  583.9 6.1 %copy-start.38 = (bf16[768,768]{1,0:T(8,128)(2,1)S(1)}, bf16[768,768]{1,0:T(8,128)(2,1)}, u32[]{:S(2)}) copy-start(bf16[768,768]{1,0:T(8,128)(2,1)} %get-tuple-element.37) | copy-start | bytes 3538948
  (46 other events, 89.8 us)
Sparse Core Ops, SparseCore 0:
  14.2 28.7 all-gather.1
  124.2 42.9 all-reduce.5
  339.5 44.2 all-reduce.7
  412.2 27.4 reduce-scatter.1
  444.0 139.8 all-reduce.9

commit v4 on v3

--- a/solution.py
+++ b/solution.py
@@ -91,6 +91,24 @@
     for bit in reversed(bits):
         values = values + exchange(values, axis, count, bit)
     return values
+
+
+def scatter_exchanged(values, axis):
+    count, bits = axis_bits(axis)
+    index = lax.axis_index(axis)
+    data = values.reshape((2,) * len(bits) + (values.shape[0] // count,) + values.shape[1:])
+    for bit in reversed(bits):
+        place = len(bits) - 1 - bit
+        mine = (index >> bit) & 1
+        kept = lax.dynamic_index_in_dim(data, mine, place, keepdims=False)
+        sent = lax.dynamic_index_in_dim(data, 1 - mine, place, keepdims=False)
+        data = kept + exchange(sent.astype(jnp.bfloat16), axis, count, bit).astype(jnp.float32)
+    return data
+
+
+def reduce_exchanged(values, axis):
+    part = scatter_exchanged(values, axis).astype(jnp.bfloat16)
+    return gather_ordered(part, axis).reshape(values.shape)
 
 
 def image_tower(tokens, count, length, gains, weights):
@@ -258,11 +276,9 @@
         "gd,gf->df", normed2_all, grad_hidden16, preferred_element_type=jnp.float32
     )
     grad_fc1_bias = jnp.sum(grad_hidden16.astype(jnp.float32), 0)
-    grad_normed2 = lax.psum(
-        jnp.einsum("gf,df->gd", grad_hidden16, txt_fc1, preferred_element_type=jnp.float32).astype(
-            jnp.bfloat16
-        ),
-        "mp",
+    fc_sums = lax.psum((grad_fc1.astype(jnp.bfloat16), grad_fc2.astype(jnp.bfloat16)), "dp")
+    grad_normed2 = reduce_exchanged(
+        jnp.einsum("gf,df->gd", grad_hidden16, txt_fc1, preferred_element_type=jnp.float32), "mp"
     ).astype(jnp.float32)
     grad_middle = grad_result + norm_back(grad_normed2, unit2, inverse2, txt_gains[1])
     grad_mid_all = grad_middle.astype(jnp.bfloat16)
@@ -302,14 +318,13 @@
             jnp.sum(grad_triple[2].astype(jnp.float32), 0),
         ]
     )
-    grad_normed1 = lax.psum_scatter(
-        jnp.einsum("jgw,jdw->gd", grad_triple, txt_qkv, preferred_element_type=jnp.float32).astype(
-            jnp.bfloat16
-        ),
-        "mp",
-        scatter_dimension=0,
-        tiled=True,
-    ).astype(jnp.float32)
+    fc_sums, attn_parts = lax.optimization_barrier(
+        (fc_sums, (grad_qkv.astype(jnp.bfloat16), grad_out.astype(jnp.bfloat16)))
+    )
+    attn_sums = lax.psum(attn_parts, "dp")
+    grad_normed1 = scatter_exchanged(
+        jnp.einsum("jgw,jdw->gd", grad_triple, txt_qkv, preferred_element_type=jnp.float32), "mp"
+    )
 
     def own(values):
         return lax.dynamic_slice_in_dim(values, mp_index * own_rows, own_rows, 0)
@@ -319,10 +334,6 @@
     unit2_own = own(unit2)
     grad_middle_own = own(grad_middle)
     grad_inputs = grad_middle_own + norm_back(grad_normed1, unit1_own, own(inverse1), txt_gains[0])
-    summed16 = lax.psum(
-        tuple(g.astype(jnp.bfloat16) for g in (grad_qkv, grad_out, grad_fc1, grad_fc2)), "dp"
-    )
-    summed_bias = lax.psum((grad_qv_bias, grad_fc1_bias), "dp")
     small_parts = jnp.stack(
         [
             jnp.sum(grad_normed1 * unit1_own, 0),
@@ -333,16 +344,18 @@
             jnp.sum(own(grad_result), 0),
         ]
     )
-    shared = lax.psum(small_parts, ("dp", "mp"))
+    shared, summed_bias = lax.psum(
+        (sum_exchanged(small_parts, "mp"), (grad_qv_bias, grad_fc1_bias)), "dp"
+    )
     return (
         loss,
         grad_inputs,
-        summed16[0].astype(jnp.float32),
+        attn_sums[0].astype(jnp.float32),
         summed_bias[0],
-        summed16[1].astype(jnp.float32),
-        summed16[2].astype(jnp.float32),
+        attn_sums[1].astype(jnp.float32),
+        fc_sums[0].astype(jnp.float32),
         summed_bias[1],
-        summed16[3].astype(jnp.float32),
+        fc_sums[1].astype(jnp.float32),
         shared[0:2],
         shared[2:4],
         shared[4:6],

time: 609 us -> 589 us (0.967)
  blocking collectives: 63.5 us -> 35.4 us
  waiting for transfers between devices: 228 us -> 204 us
  local copies, waits for them, and re-layouts: 84.8 us -> 97.8 us
  other arithmetic: 75.9 us -> 86.2 us
  starting transfers between devices: 13.6 us -> 20.4 us
    psum x2, waiting for transfers between devices: 132 us -> 89.5 us  [the longest x1 57.3 us: local(): lax.psum((grad_fc1.astype(jnp.bfloat16), grad_fc2.astype(jnp.bfloat16)),...]
    psum x2 -> x1, blocking collectives: 63.5 us -> 35.4 us  [local(): lax.psum((sum_exchanged(small_parts, 'mp'), (grad_qv_bias, grad_fc1_bias)...]
    ppermute x13 -> x21, waiting for transfers between devices: 96.1 us -> 115 us  [exchange(): return lax.ppermute(values, axis, [(i, i ^ 1 << bit) for i in range(count)])]
    ppermute x13 -> x21, starting transfers between devices: 13.2 us -> 20 us  [exchange(): return lax.ppermute(values, axis, [(i, i ^ 1 << bit) for i in range(count)])]
  transfers between devices with their start and end apart: 18 -> 25, of which waited for: 10 -> 13; matrix products, arithmetic and copies ran while one was open for 28% -> 37% of each run, Pallas kernels for 0% -> 0%
where the time goes in v4:
time: 589 us; the launch traced here: 579 us
  waiting for transfers between devices  204 us (35%)
  matrix products  117 us (20%)
  local copies, waits for them, and re-layouts  97.8 us (17%)
  other arithmetic  86.2 us (15%)
  blocking collectives  35.4 us (6%)
  starting transfers between devices  20.4 us (3%)
  between operations  18.6 us (3%)
    ppermute x21, waiting for transfers between devices, exchange(): return lax.ppermute(values, axis, [(i, i ^ 1 << bit) for i in range(count)])  115 us
    psum x1, waiting for transfers between devices, local(): lax.psum((grad_fc1.astype(jnp.bfloat16), grad_fc2.astype(jnp.bfloat16)),...  57.3 us
    dot_general x2, matrix products, image_tower(): result = middle + jnp.dot(active, w_fc2, preferred_element_type=jnp.float32)  45.7 us
    psum x1, blocking collectives, local(): lax.psum((sum_exchanged(small_parts, 'mp'), (grad_qv_bias, grad_fc1_bias)...  35.4 us
    psum x1, waiting for transfers between devices, local(): attn_sums = lax.psum(attn_parts, 'dp')  32.2 us
    concatenate x8, other arithmetic, gather_stacked(): data = jnp.concatenate([data, exchange(data, axis, count, bit)], 0)  20.8 us
    ppermute x21, starting transfers between devices, exchange(): return lax.ppermute(values, axis, [(i, i ^ 1 << bit) for i in range(count)])  20 us
    squeeze x4, local copies, waits for them, and re-layouts, image_tower(): shares, spare_lse = attention_shares(shaped[0], shaped[1], None)  14.7 us
  transfers between devices with their start and end apart: 25, of which 13 were waited for; matrix products, arithmetic and copies ran while one was open for 37% of the time, Pallas kernels for 0%

profile of v4, /device:TPU:0, one launch (start us, length us, event | category | flops | bytes accessed | tf_op | source)
XLA Modules:
  0.0 579.3 jit_solution(4800949990628811830)
XLA Ops:
  7.2 3.1 collective-permute-start
  20.8 2.2 fusion.55
  29.3 16.0 %collective-permute-done.2 = bf16[1,192,768]{2,1,0:T(8,128)(2,1)} collective-permute-done((bf16[1,192,768]{2,1,0:T(8,128)(2,1)}, bf16[1,192,768]{2,1,0:T(8,128)(2,1)}, u32[]{:S(2)}, u32[]{:S(2)}) %collective-permute-start.2) | collective-permute-done | bytes 294944 | tf_op jit(solution)/shard_map/ppermute | solution.py:63
  49.1 2.9 pad_maximum_fusion.5
  54.6 16.0 %collective-permute-done.6 = bf16[1,768,768]{2,1,0:T(8,128)(2,1)} collective-permute-done((bf16[1,768,768]{2,1,0:T(8,128)(2,1)}, bf16[1,768,768]{2,1,0:T(8,128)(2,1)}, u32[]{:S(2)}, u32[]{:S(2)}) %collective-permute-start.6) | collective-permute-done | bytes 1179680 | tf_op jit(solution)/shard_map/ppermute | solution.py:63
  70.6 2.9 pad_maximum_fusion.4
  73.5 21.4 %collective-permute-done.4 = bf16[1,768,768]{1,2,0:T(8,128)(2,1)S(1)} collective-permute-done((bf16[1,768,768]{1,2,0:T(8,128)(2,1)S(1)}, bf16[1,768,768]{1,2,0:T(8,128)(2,1)S(1)}, u32[]{:S(2)}, u32[]{:S(2)}) %collective-permute-start.4) | collective-permute-done | bytes 1179680 | tf_op jit(solution)/shard_map/ppermute | solution.py:63
  100.6 2.5 fusion.132
  104.2 2.5 copy.51
  106.7 6.4 %reshape.279 = bf16[60,16,3,3,64]{4,3,1,0,2:T(4,128)(2,1)} reshape(bf16[960,3,192]{2,0,1:T(8,128)(2,1)} %copy.51) | data formatting | bytes 2211840 | tf_op jit(solution)/shard_map/reshape | solution.py:201
  113.2 3.2 fusion.215
  120.0 2.4 reshape.280
  124.4 2.2 pad_maximum_fusion.2
  129.8 3.3 reshape.306
  133.1 3.3 reshape.305
  136.4 3.0 fusion.72
  139.4 3.9 fusion.221
  143.3 2.3 reshape.304
  145.6 4.1 fusion.76
  149.7 2.2 copy.74
  151.9 4.4 reshape.289
  156.3 3.5 fusion.222
  159.8 2.5 convert_bitcast_fusion
  163.9 4.1 squeeze.52
  168.0 4.1 squeeze.51
  172.0 3.8 fusion.48
  175.8 3.1 fusion.223
  178.9 4.1 squeeze.50
  183.0 4.2 convert_bitcast_fusion.1
  189.0 4.3 reshape.284
  193.4 2.9 fusion.224
  198.0 4.0 fusion.214
  203.5 8.7 %multiply_convert_fusion = (bf16[960,768]{1,0:T(8,128)(2,1)S(1)}, f32[960,768]{1,0:T(8,128)}, f32[960,768]{1,0:T(8,128)}) fusion(f32[768]{0:T(1024)S(1)} %copy-done.86, bf16[768,768]{1,0:T(8,128)(2,1)S(1)} %copy-done, f32[960,768]{1,0:T(8,128)S(1)} %subtract_multiply_fusion, f32[768]{0:T(1024)S(1)} %copy-done.75, f32[768]{0:T(1024)S(1)} %get-tuple-element.32), kind=kOutput, calls=%fused_computation.67 | convolution fusion | flops 1183334400 | bytes 11510784 | tf_op jit(solution)/shard_map/dot_general | solution.py:222
  215.5 3.9 pad_maximum_fusion.1
  219.5 4.0 pad_maximum_fusion
  223.5 19.8 %fusion.69 = f32[435,768]{1,0:T(8,128)} fusion(f32[435,768]{1,0:T(8,128)S(1)} %copy-done.39, bf16[3072,768]{1,0:T(8,128)(2,1)} %bitcast.191, bf16[768,3072]{0,1:T(8,128)(2,1)} %bitcast.193, f32[768]{0:T(1024)S(1)} %copy-done.78, f32[435]{0:T(512)S(1)} %add_rsqrt_fusion.4, f32[435]{0:T(512)S(1)} %broadcast_multiply_fusion.5), kind=kOutput, calls=%fused_computation.144 | convolution fusion | flops 4193706240 | bytes 12116376 | tf_op jit(solution)/shard_map/dot_general | solution.py:138
  245.0 26.0 %fusion.61 = f32[600,768]{1,0:T(8,128)} fusion(f32[600,768]{1,0:T(8,128)} %copy-done.29, bf16[3072,768]{1,0:T(8,128)(2,1)} %bitcast.192, bf16[768,3072]{0,1:T(8,128)(2,1)} %bitcast.194, f32[768]{0:T(1024)S(1)} %copy-done.78, f32[600]{0:T(1024)S(1)} %add_rsqrt_fusion, f32[600]{0:T(1024)S(1)} %broadcast_multiply_fusion), kind=kOutput, calls=%fused_computation.124 | convolution fusion | flops 5784422400 | bytes 13131456 | tf_op jit(solution)/shard_map/dot_general | solution.py:138
  277.3 9.2 %collective-permute-done.9 = f32[120,768]{1,0:T(8,128)S(1)} collective-permute-done((f32[120,768]{1,0:T(8,128)S(1)}, f32[120,768]{1,0:T(8,128)S(1)}, u32[]{:S(2)}, u32[]{:S(2)}) %collective-permute-start.9) | collective-permute-done | bytes 368672 | tf_op jit(solution)/shard_map/ppermute | solution.py:63
  287.0 2.9 collective-permute-start.10
  289.9 8.3 %collective-permute-done.10 = bf16[120,768]{1,0:T(8,128)(2,1)S(1)} collective-permute-done((bf16[120,768]{1,0:T(8,128)(2,1)S(1)}, bf16[120,768]{1,0:T(8,128)(2,1)S(1)}, u32[]{:S(2)}, u32[]{:S(2)}) %collective-permute-start.10) | collective-permute-done | bytes 184352 | tf_op jit(solution)/shard_map/ppermute | solution.py:63
  299.0 8.8 %collective-permute-done.11 = bf16[2,120,768]{2,1,0:T(8,128)(2,1)S(1)} collective-permute-done((bf16[2,120,768]{2,1,0:T(8,128)(2,1)S(1)}, bf16[2,120,768]{2,1,0:T(8,128)(2,1)S(1)}, u32[]{:S(2)}, u32[]{:S(2)}) %collective-permute-start.11) | collective-permute-done | bytes 368672 | tf_op jit(solution)/shard_map/ppermute | solution.py:63
  310.6 15.0 %collective-permute-done.12 = bf16[2,2,120,768]{3,2,1,0:T(8,128)(2,1)S(1)} collective-permute-done((bf16[2,2,120,768]{3,2,1,0:T(8,128)(2,1)}, bf16[2,2,120,768]{3,2,1,0:T(8,128)(2,1)S(1)}, u32[]{:S(2)}, u32[]{:S(2)}) %collective-permute-start.12) | collective-permute-done | bytes 737312 | tf_op jit(solution)/shard_map/ppermute | solution.py:63
  329.4 2.7 select_reduce_fusion
  333.6 2.7 convert_reduce_fusion.1
  339.5 2.3 collective-permute-done.13
  345.2 9.2 %collective-permute-done.14 = bf16[240,768]{1,0:T(8,128)(2,1)} collective-permute-done((bf16[240,768]{1,0:T(8,128)(2,1)S(1)}, bf16[240,768]{1,0:T(8,128)(2,1)}, u32[]{:S(2)}, u32[]{:S(2)}) %collective-permute-start.14) | collective-permute-done | bytes 368672 | tf_op jit(solution)/shard_map/ppermute | solution.py:63
  358.2 7.1 %collective-permute-done.15 = bf16[240,768]{1,0:T(8,128)(2,1)S(1)} collective-permute-done((bf16[240,768]{1,0:T(8,128)(2,1)S(1)}, bf16[240,768]{1,0:T(8,128)(2,1)S(1)}, u32[]{:S(2)}, u32[]{:S(2)}) %collective-permute-start.15) | collective-permute-done | bytes 368672 | tf_op jit(solution)/shard_map/ppermute | solution.py:63
  366.4 2.5 convolution_convert_fusion.1
  368.9 2.5 convolution_convert_fusion.2
  372.2 2.3 copy-done.2
  375.3 5.4 bitcast_multiply_fusion
  386.3 2.5 convert_reduce_fusion.4
  388.8 2.5 multiply_reduce_fusion.8
  392.8 2.4 stack.108
  400.6 2.3 convert_reduce_fusion.5
  406.1 2.1 dot_general.129
  408.3 2.9 convolution_bitcast_fusion
  416.7 3.1 convolution_convert_fusion.6
  423.6 2.3 fusion.82
  426.0 57.3 %all-reduce.11.cloned.1.call-done = (bf16[768,768]{1,0:T(8,128)(2,1)}, bf16[768,768]{1,0:T(8,128)(2,1)}) async-done(((bf16[768,768]{1,0:T(8,128)(2,1)}, bf16[768,768]{1,0:T(8,128)(2,1)}), (bf16[768,768]{1,0:T(8,128)(2,1)}, bf16[768,768]{1,0:T(8,128)(2,1)})) %all-reduce.11.cloned.1.call-update) | async-done | bytes 2359312 | tf_op jit(solution)/shard_map/psum | solution.py:279
  486.0 2.5 dynamic-slice_reduce_fusion.2
  498.7 35.4 %all-reduce = (f32[2,192]{1,0:T(2,128)}, f32[768]{0:T(1024)}, f32[6,768]{1,0:T(8,128)S(1)}) all-reduce(f32[2,192]{1,0:T(2,128)S(1)} %pad_maximum_fusion.16, f32[768]{0:T(1024)S(1)} %copy-done.77, f32[6,768]{1,0:T(8,128)S(1)} %add.316), channel_id=1, replica_groups=mesh['dp'=8,'mp'=4] {'dp'}, use_global_device_ids=true, to_apply=%region_43.44 | all-reduce | flops 5760 | bytes 46080 | tf_op jit(solution)/shard_map/psum | solution.py:347
  534.7 32.2 %all-reduce.9.cloned.1.call-done = (bf16[3,768,192]{1,2,0:T(8,128)(2,1)}, bf16[192,768]{1,0:T(8,128)(2,1)}) async-done(((bf16[3,768,192]{1,2,0:T(8,128)(2,1)}, bf16[192,768]{1,0:T(8,128)(2,1)}), (bf16[3,768,192]{1,2,0:T(8,128)(2,1)}, bf16[192,768]{1,0:T(8,128)(2,1)})) %all-reduce.9.cloned.1.call-update) | async-done | bytes 1179664 | tf_op jit(solution)/shard_map/psum | solution.py:324
  566.9 2.5 convert_element_type.303
  (369 shorter events, 116.8 us)
Async XLA Ops:
  7.2 196.3 %copy-start = (bf16[768,768]{1,0:T(8,128)(2,1)S(1)}, bf16[768,768]{1,0:T(8,128)(2,1)}, u32[]{:S(2)}) copy-start(bf16[768,768]{1,0:T(8,128)(2,1)} %param.32) | copy-start | bytes 3538948
  7.2 89.6 %all-gather.2.cloned.1.call-start = ((), (), s32[]{:S(2)}) async-start(), calls=%async_computation | async-start | bytes 1843200 | tf_op jit(solution)/shard_map/all_gather | solution.py:193
  7.2 41.9 %collective-permute-start = (bf16[1,3,768,192]{2,3,0,1:T(8,128)(2,1)}, bf16[1,3,768,192]{2,3,0,1:T(8,128)(2,1)}, u32[]{:S(2)}, u32[]{:S(2)}) collective-permute-start(bf16[1,3,768,192]{2,3,0,1:T(8,128)(2,1)} %bitcast.195), channel_id=1, source_target_pairs={{0,2},{1,3},{2,0},{3,1},{4,6},{5,7},{6,4},{7,5},{8,10},{9,11},{10,... | collective-permute-start | bytes 2654216 | tf_op jit(solution)/shard_map/ppermute | solution.py:63
  10.3 35.0 %collective-permute-start.2 = (bf16[1,192,768]{2,1,0:T(8,128)(2,1)}, bf16[1,192,768]{2,1,0:T(8,128)(2,1)}, u32[]{:S(2)}, u32[]{:S(2)}) collective-permute-start(bf16[1,192,768]{2,1,0:T(8,128)(2,1)} %bitcast.204), channel_id=1, source_target_pairs={{0,2},{1,3},{2,0},{3,1},{4,6},{5,7},{6,4},{7,5},{8,10},{9,11},{10,... | collective-permute-start | bytes 884744 | tf_op jit(solution)/shard_map/ppermute | solution.py:63
  10.4 12.7 %copy-start.82 = (f32[2,192]{1,0:T(2,128)S(1)}, f32[2,192]{1,0:T(2,128)}, u32[]{:S(2)}) copy-start(f32[2,192]{1,0:T(2,128)} %param.30) | copy-start | bytes 4612
  10.4 13.4 %copy-start.72 = (s32[60,16]{0,1:T(8,128)S(1)}, s32[60,16]{0,1:T(8,128)}, u32[]{:S(2)}) copy-start(s32[60,16]{0,1:T(8,128)} %param.20) | copy-start | bytes 11524
  10.4 60.2 %collective-permute-start.6 = (bf16[1,768,768]{2,1,0:T(8,128)(2,1)}, bf16[1,768,768]{2,1,0:T(8,128)(2,1)}, u32[]{:S(2)}, u32[]{:S(2)}) collective-permute-start(bf16[1,768,768]{2,1,0:T(8,128)(2,1)} %bitcast.188), channel_id=1, source_target_pairs={{0,2},{1,3},{2,0},{3,1},{4,6},{5,7},{6,4},{7,5},{8,10},{9,11},{10,... | collective-permute-start | bytes 3538952 | tf_op jit(solution)/shard_map/ppermute | solution.py:63
  13.9 81.0 %copy-start.9 = (bf16[768,768]{0,1:T(8,128)(2,1)}, bf16[768,768]{0,1:T(8,128)(2,1)S(1)}, u32[]{:S(2)}) copy-start(bf16[768,768]{0,1:T(8,128)(2,1)S(1)} %copy.65) | copy-start | bytes 3538948
  13.9 81.0 %collective-permute-start.4 = (bf16[1,768,768]{1,2,0:T(8,128)(2,1)S(1)}, bf16[1,768,768]{1,2,0:T(8,128)(2,1)S(1)}, u32[]{:S(2)}, u32[]{:S(2)}) collective-permute-start(bf16[1,768,768]{1,2,0:T(8,128)(2,1)S(1)} %bitcast.184), channel_id=1, source_target_pairs={{0,2},{1,3},{2,0},{3,1},{4,6},{5,7},{6,4},{7,5},{8,10},{9,11},{10,... | collective-permute-start | bytes 3538952 | tf_op jit(solution)/shard_map/ppermute | solution.py:63
  14.1 183.9 %all-reduce.7.cloned.1.call-start = ((), (), s32[]{:S(2)}) async-start(), calls=%async_computation.1 | async-start | bytes 2949120 | tf_op jit(solution)/shard_map/psum | solution.py:214
  24.3 30.3 %copy-start.61 = (pred[60,16]{0,1:T(8,128)(4,1)}, pred[60,16]{0,1:T(8,128)(4,1)S(1)}, u32[]{:S(2)}) copy-start(pred[60,16]{0,1:T(8,128)(4,1)S(1)} %get-tuple-element.51) | copy-start | bytes 2884
  28.5 24.0 %copy-start.44 = (bf16[192,768]{1,0:T(8,128)(2,1)S(1)}, bf16[192,768]{1,0:T(8,128)(2,1)}, u32[]{:S(2)}) copy-start(bf16[192,768]{1,0:T(8,128)(2,1)} %param.26) | copy-start | bytes 884740
  29.3 71.2 %copy-start.57 = (f32[768]{0:T(1024)}, f32[768]{0:T(1024)S(1)}, u32[]{:S(2)}) copy-start(f32[768]{0:T(1024)S(1)} %get-tuple-element.33) | copy-start | bytes 9220
  29.3 174.2 %copy-start.53 = (f32[768]{0:T(1024)}, f32[768]{0:T(1024)S(1)}, u32[]{:S(2)}) copy-start(f32[768]{0:T(1024)S(1)} %get-tuple-element.32) | copy-start | bytes 9220
  46.4 6.0 %collective-permute-start.3 = (bf16[2,192,768]{2,1,0:T(8,128)(2,1)S(1)}, bf16[2,192,768]{2,1,0:T(8,128)(2,1)S(1)}, u32[]{:S(2)}, u32[]{:S(2)}) collective-permute-start(bf16[2,192,768]{2,1,0:T(8,128)(2,1)S(1)} %pad_maximum_fusion.10), channel_id=1, source_target_pairs={{0,1},{1,0},{2,3},{3,2},{4,5},{5,4},{6,7},{7,6},{8,9},{9,8},{10,11... | collective-permute-start | bytes 1769480 | tf_op jit(solution)/shard_map/ppermute | solution.py:63
  49.1 21.5 %copy-start.12 = (bf16[768,768]{1,0:T(8,128)(2,1)S(1)}, bf16[768,768]{1,0:T(8,128)(2,1)}, u32[]{:S(2)}) copy-start(bf16[768,768]{1,0:T(8,128)(2,1)} %param.28) | copy-start | bytes 3538948
  52.0 72.4 %collective-permute-start.1 = (bf16[2,3,768,192]{2,3,0,1:T(8,128)(2,1)}, bf16[2,3,768,192]{2,3,0,1:T(8,128)(2,1)}, u32[]{:S(2)}, u32[]{:S(2)}) collective-permute-start(bf16[2,3,768,192]{2,3,0,1:T(8,128)(2,1)} %pad_maximum_fusion.5), channel_id=1, source_target_pairs={{0,1},{1,0},{2,3},{3,2},{4,5},{5,4},{6,7},{7,6},{8,9},{9,8},{10,11... | collective-permute-start | bytes 5308424 | tf_op jit(solution)/shard_map/ppermute | solution.py:63
  73.5 142.0 %collective-permute-start.7 = (bf16[2,768,768]{2,1,0:T(8,128)(2,1)}, bf16[2,768,768]{2,1,0:T(8,128)(2,1)}, u32[]{:S(2)}, u32[]{:S(2)}) collective-permute-start(bf16[2,768,768]{2,1,0:T(8,128)(2,1)} %pad_maximum_fusion.4), channel_id=1, source_target_pairs={{0,1},{1,0},{2,3},{3,2},{4,5},{5,4},{6,7},{7,6},{8,9},{9,8},{10,11... | collective-permute-start | bytes 7077896 | tf_op jit(solution)/shard_map/ppermute | solution.py:63
  96.7 122.7 %collective-permute-start.5 = (bf16[2,768,768]{1,2,0:T(8,128)(2,1)}, bf16[2,768,768]{1,2,0:T(8,128)(2,1)}, u32[]{:S(2)}, u32[]{:S(2)}) collective-permute-start(bf16[2,768,768]{1,2,0:T(8,128)(2,1)} %pad_maximum_fusion.3), channel_id=1, source_target_pairs={{0,1},{1,0},{2,3},{3,2},{4,5},{5,4},{6,7},{7,6},{8,9},{9,8},{10,11... | collective-permute-start | bytes 7077896 | tf_op jit(solution)/shard_map/ppermute | solution.py:63
  98.5 99.5 %copy-start.59 = (f32[960]{0:T(1024)}, f32[960]{0:T(1024)S(1)}, u32[]{:S(2)}) copy-start(f32[960]{0:T(1024)S(1)} %broadcast_multiply_fusion.4) | copy-start | bytes 11524
  100.5 97.5 %copy-start.63 = (f32[960]{0:T(1024)}, f32[960]{0:T(1024)S(1)}, u32[]{:S(2)}) copy-start(f32[960]{0:T(1024)S(1)} %add_rsqrt_fusion.3) | copy-start | bytes 11524
  122.4 4.2 copy-start.18
  124.1 359.1 %all-reduce.11.cloned.1.call-start = ((), (), s32[]{:S(2)}) async-start(), calls=%async_computation.3 | async-start | bytes 4718592 | tf_op jit(solution)/shard_map/psum | solution.py:279
  149.7 6.5 %copy-start.28 = (bf16[435,768]{1,0:T(8,128)(2,1)S(1)}, bf16[435,768]{1,0:T(8,128)(2,1)}, u32[]{:S(2)}) copy-start(bf16[435,768]{1,0:T(8,128)(2,1)} %param.23) | copy-start | bytes 2004484
  202.0 11.5 %copy-start.1 = (f32[960,768]{1,0:T(8,128)}, f32[960,768]{1,0:T(8,128)S(1)}, u32[]{:S(2)}) copy-start(f32[960,768]{1,0:T(8,128)S(1)} %get-tuple-element.55) | copy-start | bytes 8847364
  203.5 8.7 %copy-start.16 = (f32[960,768]{1,0:T(8,128)}, f32[960,768]{1,0:T(8,128)S(1)}, u32[]{:S(2)}) copy-start(f32[960,768]{1,0:T(8,128)S(1)} %subtract_multiply_fusion) | copy-start | bytes 8847364
  203.5 8.7 %copy-start.84 = (bf16[768,768]{1,0:T(8,128)(2,1)S(1)}, bf16[768,768]{1,0:T(8,128)(2,1)}, u32[]{:S(2)}) copy-start(bf16[768,768]{1,0:T(8,128)(2,1)} %param.34) | copy-start | bytes 3538948
  215.5 4.0 copy-start.10
  215.5 4.0 copy-start.15
  219.4 4.0 copy-start.39
  219.4 4.0 copy-start.78
  272.5 14.1 %copy-start.65 = (f32[768]{0:T(1024)S(1)}, f32[768]{0:T(1024)}, u32[]{:S(2)}) copy-start(f32[768]{0:T(1024)} %get-tuple-element.30) | copy-start | bytes 9220
  272.5 14.1 %copy-start.73 = (f32[60]{0:T(128)S(1)}, f32[60]{0:T(128)}, u32[]{:S(2)}) copy-start(f32[60]{0:T(128)} %get-tuple-element.50) | copy-start | bytes 724
  272.7 13.9 %copy-start.46 = (f32[60,768]{1,0:T(8,128)S(1)}, f32[60,768]{1,0:T(8,128)}, u32[]{:S(2)}) copy-start(f32[60,768]{1,0:T(8,128)} %get-tuple-element.28) | copy-start | bytes 552964
  273.7 1.8 collective-permute-start.8
  275.5 10.9 %collective-permute-start.9 = (f32[120,768]{1,0:T(8,128)S(1)}, f32[120,768]{1,0:T(8,128)S(1)}, u32[]{:S(2)}, u32[]{:S(2)}) collective-permute-start(f32[120,768]{1,0:T(8,128)S(1)} %fusion.258), channel_id=1, source_target_pairs={{0,2},{1,3},{2,0},{3,1},{4,6},{5,7},{6,4},{7,5},{8,10},{9,11},{10,... | collective-permute-start | bytes 1105928 | tf_op jit(solution)/shard_map/ppermute | solution.py:63
  286.5 23.8 %copy-start.62 = (pred[60,16]{0,1:T(8,128)(4,1)S(1)}, pred[60,16]{0,1:T(8,128)(4,1)}, u32[]{:S(2)}) copy-start(pred[60,16]{0,1:T(8,128)(4,1)} %copy-done.61) | copy-start | bytes 2884
  286.6 23.9 %copy-start.81 = (s32[480]{0:T(512)S(1)}, s32[480]{0:T(512)}, u32[]{:S(2)}) copy-start(s32[480]{0:T(512)} %param.21) | copy-start | bytes 5764
  287.0 11.2 %collective-permute-start.10 = (bf16[120,768]{1,0:T(8,128)(2,1)S(1)}, bf16[120,768]{1,0:T(8,128)(2,1)S(1)}, u32[]{:S(2)}, u32[]{:S(2)}) collective-permute-start(bf16[120,768]{1,0:T(8,128)(2,1)S(1)} %pad_maximum_fusion.14), channel_id=1, source_target_pairs={{0,16},{4,20},{8,24},{12,28},{16,0},{20,4},{24,8},{28,12},{1,17},{... | collective-permute-start | bytes 552968 | tf_op jit(solution)/shard_map/ppermute | solution.py:63
  298.3 9.5 %collective-permute-start.11 = (bf16[2,120,768]{2,1,0:T(8,128)(2,1)S(1)}, bf16[2,120,768]{2,1,0:T(8,128)(2,1)S(1)}, u32[]{:S(2)}, u32[]{:S(2)}) collective-permute-start(bf16[2,120,768]{2,1,0:T(8,128)(2,1)S(1)} %pad_maximum_fusion.13), channel_id=1, source_target_pairs={{0,8},{4,12},{8,0},{12,4},{16,24},{20,28},{24,16},{28,20},{1,9},{5... | collective-permute-start | bytes 1105928 | tf_op jit(solution)/shard_map/ppermute | solution.py:63
  308.8 16.9 %collective-permute-start.12 = (bf16[2,2,120,768]{3,2,1,0:T(8,128)(2,1)}, bf16[2,2,120,768]{3,2,1,0:T(8,128)(2,1)S(1)}, u32[]{:S(2)}, u32[]{:S(2)}) collective-permute-start(bf16[2,2,120,768]{3,2,1,0:T(8,128)(2,1)} %pad_maximum_fusion.8), channel_id=1, source_target_pairs={{0,4},{4,0},{8,12},{12,8},{16,20},{20,16},{24,28},{28,24},{1,5},{5... | collective-permute-start | bytes 2211848 | tf_op jit(solution)/shard_map/ppermute | solution.py:63
  329.4 4.2 copy-start.85
  329.4 4.2 copy-start.87
  329.4 4.2 copy-start.92
  329.4 4.2 copy-start.93
  339.4 2.4 collective-permute-start.13
  339.5 17.6 %copy-start.48 = (f32[60,3,16]{2,1,0:T(4,128)S(1)}, f32[60,3,16]{2,1,0:T(4,128)}, u32[]{:S(2)}) copy-start(f32[60,3,16]{2,1,0:T(4,128)} %copy-done.47) | copy-start | bytes 34564
  343.6 10.8 %collective-permute-start.14 = (bf16[240,768]{1,0:T(8,128)(2,1)S(1)}, bf16[240,768]{1,0:T(8,128)(2,1)}, u32[]{:S(2)}, u32[]{:S(2)}) collective-permute-start(bf16[240,768]{1,0:T(8,128)(2,1)S(1)} %fusion.134), channel_id=1, source_target_pairs={{0,2},{1,3},{2,0},{3,1},{4,6},{5,7},{6,4},{7,5},{8,10},{9,11},{10,... | collective-permute-start | bytes 1105928 | tf_op jit(solution)/shard_map/ppermute | solution.py:63
  355.4 9.8 %collective-permute-start.15 = (bf16[240,768]{1,0:T(8,128)(2,1)S(1)}, bf16[240,768]{1,0:T(8,128)(2,1)S(1)}, u32[]{:S(2)}, u32[]{:S(2)}) collective-permute-start(bf16[240,768]{1,0:T(8,128)(2,1)S(1)} %fusion.110), channel_id=1, source_target_pairs={{0,2},{1,3},{2,0},{3,1},{4,6},{5,7},{6,4},{7,5},{8,10},{9,11},{10,... | collective-permute-start | bytes 1105928 | tf_op jit(solution)/shard_map/ppermute | solution.py:63
  357.1 9.3 %copy-start.37 = (bf16[960,768]{1,0:T(8,128)(2,1)S(1)}, bf16[960,768]{1,0:T(8,128)(2,1)}, u32[]{:S(2)}) copy-start(bf16[960,768]{1,0:T(8,128)(2,1)} %copy-done.36) | copy-start | bytes 4423684
  357.1 9.3 %copy-start.89 = (bf16[960,768]{1,0:T(8,128)(2,1)S(1)}, bf16[960,768]{1,0:T(8,128)(2,1)}, u32[]{:S(2)}) copy-start(bf16[960,768]{1,0:T(8,128)(2,1)} %copy-done.88) | copy-start | bytes 4423684
  366.3 5.2 collective-permute-start.16
  371.4 195.5 %all-reduce.9.cloned.1.call-start = ((), (), s32[]{:S(2)}) async-start(), calls=%async_computation.2 | async-start | bytes 2359296 | tf_op jit(solution)/shard_map/psum | solution.py:324
  375.3 7.0 %copy-start.41 = (bf16[192,768]{1,0:T(8,128)(2,1)S(1)}, bf16[192,768]{1,0:T(8,128)(2,1)}, u32[]{:S(2)}) copy-start(bf16[192,768]{1,0:T(8,128)(2,1)} %param.31) | copy-start | bytes 884740
  382.4 4.0 copy-start.6
  408.3 5.1 copy-start.64
  412.8 4.0 copy-start.19
  412.8 7.0 %collective-permute-start.17 = (bf16[2,240,768]{2,1,0:T(8,128)(2,1)S(1)}, bf16[2,240,768]{2,1,0:T(8,128)(2,1)}, u32[]{:S(2)}, u32[]{:S(2)}) collective-permute-start(bf16[2,240,768]{2,1,0:T(8,128)(2,1)S(1)} %fusion.109), channel_id=1, source_target_pairs={{0,1},{1,0},{2,3},{3,2},{4,5},{5,4},{6,7},{7,6},{8,9},{9,8},{10,11... | collective-permute-start | bytes 2211848 | tf_op jit(solution)/shard_map/ppermute | solution.py:63
  413.9 5.9 %copy-start.31 = (f32[2,2,240,768]{3,2,1,0:T(8,128)S(1)}, f32[2,2,240,768]{3,2,1,0:T(8,128)}, u32[]{:S(2)}) copy-start(f32[2,2,240,768]{3,2,1,0:T(8,128)} %copy-done.30) | copy-start | bytes 8847364
  422.0 61.2 %collective-permute-start.18 = (bf16[240,768]{1,0:T(8,128)(2,1)}, bf16[240,768]{1,0:T(8,128)(2,1)}, u32[]{:S(2)}, u32[]{:S(2)}) collective-permute-start(bf16[240,768]{1,0:T(8,128)(2,1)} %fusion.135), channel_id=1, source_target_pairs={{0,2},{1,3},{2,0},{3,1},{4,6},{5,7},{6,4},{7,5},{8,10},{9,11},{10,... | collective-permute-start | bytes 1105928 | tf_op jit(solution)/shard_map/ppermute | solution.py:63
  484.9 10.6 %copy-start.43 = (bf16[768,768]{1,0:T(8,128)(2,1)S(1)}, bf16[768,768]{1,0:T(8,128)(2,1)}, u32[]{:S(2)}) copy-start(bf16[768,768]{1,0:T(8,128)(2,1)} %get-tuple-element.17) | copy-start | bytes 3538948
  486.0 11.0 %copy-start.42 = (bf16[768,768]{1,0:T(8,128)(2,1)S(1)}, bf16[768,768]{1,0:T(8,128)(2,1)}, u32[]{:S(2)}) copy-start(bf16[768,768]{1,0:T(8,128)(2,1)} %get-tuple-element.18) | copy-start | bytes 3538948
  489.9 3.3 collective-permute-start.19
  494.0 4.7 collective-permute-start.20
  (55 other events, 131.3 us)
Sparse Core Ops, SparseCore 0:
  14.2 28.7 all-gather.1
  124.2 43.0 all-reduce.6
  371.5 111.7 all-reduce.10
  487.2 79.6 all-reduce.8

commit v5 on v4

--- a/solution.py
+++ b/solution.py
@@ -276,7 +276,7 @@
         "gd,gf->df", normed2_all, grad_hidden16, preferred_element_type=jnp.float32
     )
     grad_fc1_bias = jnp.sum(grad_hidden16.astype(jnp.float32), 0)
-    fc_sums = lax.psum((grad_fc1.astype(jnp.bfloat16), grad_fc2.astype(jnp.bfloat16)), "dp")
+    fc_sums = reduce_exchanged(jnp.concatenate([grad_fc1, grad_fc2], 0), "dp")
     grad_normed2 = reduce_exchanged(
         jnp.einsum("gf,df->gd", grad_hidden16, txt_fc1, preferred_element_type=jnp.float32), "mp"
     ).astype(jnp.float32)
@@ -318,10 +318,7 @@
             jnp.sum(grad_triple[2].astype(jnp.float32), 0),
         ]
     )
-    fc_sums, attn_parts = lax.optimization_barrier(
-        (fc_sums, (grad_qkv.astype(jnp.bfloat16), grad_out.astype(jnp.bfloat16)))
-    )
-    attn_sums = lax.psum(attn_parts, "dp")
+    attn_sums = reduce_exchanged(jnp.concatenate([grad_qkv.reshape(-1, D), grad_out], 0), "dp")
     grad_normed1 = scatter_exchanged(
         jnp.einsum("jgw,jdw->gd", grad_triple, txt_qkv, preferred_element_type=jnp.float32), "mp"
     )
@@ -344,18 +341,21 @@
             jnp.sum(own(grad_result), 0),
         ]
     )
-    shared, summed_bias = lax.psum(
-        (sum_exchanged(small_parts, "mp"), (grad_qv_bias, grad_fc1_bias)), "dp"
-    )
+    bias_rows = jnp.stack(
+        [jnp.concatenate([grad_qv_bias.reshape(-1), jnp.zeros_like(grad_qv_bias.reshape(-1))]), grad_fc1_bias]
+    )
+    shared = sum_exchanged(jnp.concatenate([sum_exchanged(small_parts, "mp"), bias_rows], 0), "dp")
+    qv_count = grad_qv_bias.size
+    fc1_rows = grad_fc1.shape[0]
     return (
         loss,
         grad_inputs,
-        attn_sums[0].astype(jnp.float32),
-        summed_bias[0],
-        attn_sums[1].astype(jnp.float32),
-        fc_sums[0].astype(jnp.float32),
-        summed_bias[1],
-        fc_sums[1].astype(jnp.float32),
+        attn_sums[: grad_qkv.size // D].astype(jnp.float32).reshape(grad_qkv.shape),
+        shared[6, :qv_count].reshape(grad_qv_bias.shape),
+        attn_sums[grad_qkv.size // D :].astype(jnp.float32),
+        fc_sums[:fc1_rows].astype(jnp.float32),
+        shared[7],
+        fc_sums[fc1_rows:].astype(jnp.float32),
         shared[0:2],
         shared[2:4],
         shared[4:6],

time: 589 us -> 578 us (0.981)
  blocking collectives: 35.4 us -> 0 us
  starting transfers between devices: 20.4 us -> 44.9 us
  local copies, waits for them, and re-layouts: 97.8 us -> 115 us
  waiting for transfers between devices: 204 us -> 187 us
  other arithmetic: 86.2 us -> 93.4 us
    psum x2 -> x0, waiting for transfers between devices: 89.5 us -> none  [the longest x1 57.3 us: local(): lax.psum((grad_fc1.astype(jnp.bfloat16), grad_fc2.astype(jnp.bfloat16)),...]
    ppermute x21 -> x36, waiting for transfers between devices: 115 us -> 187 us  [exchange(): return lax.ppermute(values, axis, [(i, i ^ 1 << bit) for i in range(count)])]
    psum x1 -> x0, blocking collectives: 35.4 us -> none  [local(): lax.psum((sum_exchanged(small_parts, 'mp'), (grad_qv_bias, grad_fc1_bias)...]
    ppermute x21 -> x36, starting transfers between devices: 20 us -> 44.8 us  [exchange(): return lax.ppermute(values, axis, [(i, i ^ 1 << bit) for i in range(count)])]
    another operation x8 -> x18, other arithmetic: 2.38 us -> 9.03 us  [gather_ordered(): jnp.stack([jnp.where(upper, other, data), jnp.where(upper, data, other)], 0)]
    convert_element_type x4 -> x2, other arithmetic: 7.49 us -> 1.27 us  [the longest x1 0.85 us: local(): attn_sums[grad_qkv.size // D:].astype(jnp.float32)]
    unnamed x189 -> x194, local copies, waits for them, and re-layouts: 11.3 us -> 15.8 us
  transfers between devices with their start and end apart: 25 -> 38, of which waited for: 13 -> 22; matrix products, arithmetic and copies ran while one was open for 37% -> 40% of each run, Pallas kernels for 0% -> 0%
where the time goes in v5:
time: 578 us; the launch traced here: 572 us
  waiting for transfers between devices  187 us (32%)
  local copies, waits for them, and re-layouts  115 us (20%)
  matrix products  112 us (19%)
  other arithmetic  93.4 us (16%)
  starting transfers between devices  44.9 us (8%)
  between operations  19 us (3%)
    ppermute x36, waiting for transfers between devices, exchange(): return lax.ppermute(values, axis, [(i, i ^ 1 << bit) for i in range(count)])  187 us
    dot_general x2, matrix products, image_tower(): result = middle + jnp.dot(active, w_fc2, preferred_element_type=jnp.float32)  45.7 us
    ppermute x36, starting transfers between devices, exchange(): return lax.ppermute(values, axis, [(i, i ^ 1 << bit) for i in range(count)])  44.8 us
    concatenate x8, other arithmetic, gather_stacked(): data = jnp.concatenate([data, exchange(data, axis, count, bit)], 0)  21.1 us
    unnamed x194, local copies, waits for them, and re-layouts  15.8 us
    squeeze x4, local copies, waits for them, and re-layouts, image_tower(): shares, spare_lse = attention_shares(shaped[0], shaped[1], None)  15.3 us
  transfers between devices with their start and end apart: 38, of which 22 were waited for; matrix products, arithmetic and copies ran while one was open for 40% of the time, Pallas kernels for 0%

profile of v5, /device:TPU:0, one launch (start us, length us, event | category | flops | bytes accessed | tf_op | source)
XLA Modules:
  0.0 571.7 jit_solution(11973229836223849111)
XLA Ops:
  7.2 3.1 collective-permute-start
  20.8 2.2 fusion.55
  29.2 16.1 %collective-permute-done.2 = bf16[1,192,768]{2,1,0:T(8,128)(2,1)} collective-permute-done((bf16[1,192,768]{2,1,0:T(8,128)(2,1)}, bf16[1,192,768]{2,1,0:T(8,128)(2,1)}, u32[]{:S(2)}, u32[]{:S(2)}) %collective-permute-start.2) | collective-permute-done | bytes 294944 | tf_op jit(solution)/shard_map/ppermute | solution.py:63
  49.1 2.9 pad_maximum_fusion.7
  54.6 16.0 %collective-permute-done.6 = bf16[1,768,768]{2,1,0:T(8,128)(2,1)} collective-permute-done((bf16[1,768,768]{2,1,0:T(8,128)(2,1)}, bf16[1,768,768]{2,1,0:T(8,128)(2,1)}, u32[]{:S(2)}, u32[]{:S(2)}) %collective-permute-start.6) | collective-permute-done | bytes 1179680 | tf_op jit(solution)/shard_map/ppermute | solution.py:63
  70.6 2.9 pad_maximum_fusion.5
  73.5 21.4 %collective-permute-done.4 = bf16[1,768,768]{1,2,0:T(8,128)(2,1)S(1)} collective-permute-done((bf16[1,768,768]{1,2,0:T(8,128)(2,1)S(1)}, bf16[1,768,768]{1,2,0:T(8,128)(2,1)S(1)}, u32[]{:S(2)}, u32[]{:S(2)}) %collective-permute-start.4) | collective-permute-done | bytes 1179680 | tf_op jit(solution)/shard_map/ppermute | solution.py:63
  100.6 2.5 fusion.130
  104.3 2.8 copy.99
  107.1 6.5 %reshape.309 = bf16[60,16,3,3,64]{4,3,1,0,2:T(4,128)(2,1)} reshape(bf16[960,3,192]{2,0,1:T(8,128)(2,1)} %copy.99) | data formatting | bytes 2211840 | tf_op jit(solution)/shard_map/reshape | solution.py:201
  113.5 3.2 fusion.218
  120.4 2.4 reshape.310
  124.5 2.2 pad_maximum_fusion.3
  129.9 3.3 reshape.346
  133.2 3.8 reshape.345
  137.0 3.0 fusion.68
  140.0 3.9 fusion.224
  143.9 2.3 reshape.344
  146.2 4.1 fusion.72
  152.5 4.0 reshape.319
  156.5 3.5 fusion.225
  160.0 2.5 convert_bitcast_fusion
  164.1 4.1 squeeze.85
  168.2 4.2 squeeze.84
  172.4 3.8 fusion.48
  176.2 3.1 fusion.226
  179.3 4.0 squeeze.83
  183.3 4.2 convert_bitcast_fusion.1
  189.4 4.2 reshape.314
  193.6 2.9 fusion.227
  198.2 4.0 fusion.217
  203.7 8.7 %multiply_convert_fusion = (bf16[960,768]{1,0:T(8,128)(2,1)S(1)}, f32[960,768]{1,0:T(8,128)}, f32[960,768]{1,0:T(8,128)}) fusion(f32[768]{0:T(1024)S(1)} %copy-done.90, bf16[768,768]{1,0:T(8,128)(2,1)S(1)} %copy-done, f32[960,768]{1,0:T(8,128)S(1)} %subtract_multiply_fusion, f32[768]{0:T(1024)S(1)} %copy-done.80, f32[768]{0:T(1024)S(1)} %get-tuple-element.46), kind=kOutput, calls=%fused_computation.68 | convolution fusion | flops 1183334400 | bytes 11510784 | tf_op jit(solution)/shard_map/dot_general | solution.py:222
  215.7 4.0 pad_maximum_fusion.1
  219.7 4.1 pad_maximum_fusion
  223.9 19.5 %fusion.65 = f32[435,768]{1,0:T(8,128)} fusion(f32[435,768]{1,0:T(8,128)S(1)} %copy-done.43, bf16[3072,768]{1,0:T(8,128)(2,1)} %bitcast.252, bf16[768,3072]{0,1:T(8,128)(2,1)} %bitcast.254, f32[768]{0:T(1024)S(1)} %copy-done.82, f32[435]{0:T(512)S(1)} %add_rsqrt_fusion.4, f32[435]{0:T(512)S(1)} %broadcast_multiply_fusion.5), kind=kOutput, calls=%fused_computation.146 | convolution fusion | flops 4193706240 | bytes 12116376 | tf_op jit(solution)/shard_map/dot_general | solution.py:138
  245.2 26.2 %fusion.61 = f32[600,768]{1,0:T(8,128)} fusion(f32[600,768]{1,0:T(8,128)} %copy-done.35, bf16[3072,768]{1,0:T(8,128)(2,1)} %bitcast.253, bf16[768,3072]{0,1:T(8,128)(2,1)} %bitcast.255, f32[768]{0:T(1024)S(1)} %copy-done.82, f32[600]{0:T(1024)S(1)} %add_rsqrt_fusion, f32[600]{0:T(1024)S(1)} %broadcast_multiply_fusion), kind=kOutput, calls=%fused_computation.128 | convolution fusion | flops 5784422400 | bytes 13131456 | tf_op jit(solution)/shard_map/dot_general | solution.py:138
  277.5 9.2 %collective-permute-done.9 = f32[120,768]{1,0:T(8,128)S(1)} collective-permute-done((f32[120,768]{1,0:T(8,128)S(1)}, f32[120,768]{1,0:T(8,128)S(1)}, u32[]{:S(2)}, u32[]{:S(2)}) %collective-permute-start.9) | collective-permute-done | bytes 368672 | tf_op jit(solution)/shard_map/ppermute | solution.py:63
  287.1 2.9 collective-permute-start.10
  290.0 8.3 %collective-permute-done.10 = bf16[120,768]{1,0:T(8,128)(2,1)S(1)} collective-permute-done((bf16[120,768]{1,0:T(8,128)(2,1)S(1)}, bf16[120,768]{1,0:T(8,128)(2,1)S(1)}, u32[]{:S(2)}, u32[]{:S(2)}) %collective-permute-start.10) | collective-permute-done | bytes 184352 | tf_op jit(solution)/shard_map/ppermute | solution.py:63
  299.1 8.9 %collective-permute-done.11 = bf16[2,120,768]{2,1,0:T(8,128)(2,1)S(1)} collective-permute-done((bf16[2,120,768]{2,1,0:T(8,128)(2,1)S(1)}, bf16[2,120,768]{2,1,0:T(8,128)(2,1)S(1)}, u32[]{:S(2)}, u32[]{:S(2)}) %collective-permute-start.11) | collective-permute-done | bytes 368672 | tf_op jit(solution)/shard_map/ppermute | solution.py:63
  311.1 14.9 %collective-permute-done.12 = bf16[2,2,120,768]{3,2,1,0:T(8,128)(2,1)S(1)} collective-permute-done((bf16[2,2,120,768]{3,2,1,0:T(8,128)(2,1)}, bf16[2,2,120,768]{3,2,1,0:T(8,128)(2,1)S(1)}, u32[]{:S(2)}, u32[]{:S(2)}) %collective-permute-start.12) | collective-permute-done | bytes 737312 | tf_op jit(solution)/shard_map/ppermute | solution.py:63
  329.8 2.7 select_reduce_fusion
  334.7 2.7 convert_reduce_fusion.1
  351.4 8.8 %collective-permute-done.14 = bf16[240,768]{1,0:T(8,128)(2,1)S(1)} collective-permute-done((bf16[240,768]{1,0:T(8,128)(2,1)S(1)}, bf16[240,768]{1,0:T(8,128)(2,1)S(1)}, u32[]{:S(2)}, u32[]{:S(2)}) %collective-permute-start.14) | collective-permute-done | bytes 368672 | tf_op jit(solution)/shard_map/ppermute | solution.py:63
  362.3 12.5 %collective-permute-done.30 = bf16[2,2,192,768]{3,2,1,0:T(8,128)(2,1)} collective-permute-done((bf16[2,2,192,768]{3,2,1,0:T(8,128)(2,1)}, bf16[2,2,192,768]{3,2,1,0:T(8,128)(2,1)}, u32[]{:S(2)}, u32[]{:S(2)}) %collective-permute-start.30) | collective-permute-done | bytes 1179680 | tf_op jit(solution)/shard_map/ppermute | solution.py:63
  374.8 2.3 bitcast_add_fusion
  378.0 2.3 collective-permute-start.31
  382.6 10.5 %collective-permute-done.31 = bf16[2,192,768]{2,1,0:T(8,128)(2,1)} collective-permute-done((bf16[2,192,768]{2,1,0:T(8,128)(2,1)}, bf16[2,192,768]{2,1,0:T(8,128)(2,1)}, u32[]{:S(2)}, u32[]{:S(2)}) %collective-permute-start.31) | collective-permute-done | bytes 589856 | tf_op jit(solution)/shard_map/ppermute | solution.py:63
  395.3 3.7 collective-permute-start.32
  403.3 7.3 %collective-permute-done.32 = bf16[192,768]{1,0:T(8,128)(2,1)S(1)} collective-permute-done((bf16[192,768]{1,0:T(8,128)(2,1)S(1)}, bf16[192,768]{1,0:T(8,128)(2,1)S(1)}, u32[]{:S(2)}, u32[]{:S(2)}) %collective-permute-start.32) | collective-permute-done | bytes 294944 | tf_op jit(solution)/shard_map/ppermute | solution.py:63
  414.5 2.3 copy-done.2
  417.7 5.4 bitcast_multiply_fusion
  446.3 4.6 convolution_bitcast_fusion
  450.9 2.6 convolution_bitcast_fusion.1
  462.1 2.3 fusion.103
  471.7 4.1 collective-permute-start.34
  477.1 4.1 collective-permute-start.20
  484.1 6.0 %collective-permute-done.34 = bf16[2,192,768]{2,1,0:T(8,128)(2,1)S(1)} collective-permute-done((bf16[2,192,768]{2,1,0:T(8,128)(2,1)S(1)}, bf16[2,192,768]{2,1,0:T(8,128)(2,1)S(1)}, u32[]{:S(2)}, u32[]{:S(2)}) %collective-permute-start.34) | collective-permute-done | bytes 589856 | tf_op jit(solution)/shard_map/ppermute | solution.py:63
  490.1 6.1 %collective-permute-done.20 = bf16[2,96,768]{2,1,0:T(8,128)(2,1)S(1)} collective-permute-done((bf16[2,96,768]{2,1,0:T(8,128)(2,1)S(1)}, bf16[2,96,768]{2,1,0:T(8,128)(2,1)S(1)}, u32[]{:S(2)}, u32[]{:S(2)}) %collective-permute-start.20) | collective-permute-done | bytes 294944 | tf_op jit(solution)/shard_map/ppermute | solution.py:63
  496.7 2.2 dynamic-slice_reduce_fusion.2
  505.2 4.3 collective-permute-done.21
  509.6 22.0 %collective-permute-done.27 = f32[8,768]{1,0:T(8,128)S(1)} collective-permute-done((f32[8,768]{1,0:T(8,128)S(1)}, f32[8,768]{1,0:T(8,128)S(1)}, u32[]{:S(2)}, u32[]{:S(2)}) %collective-permute-start.27) | collective-permute-done | bytes 24608 | tf_op jit(solution)/shard_map/ppermute | solution.py:63
  542.2 2.2 collective-permute-done.23
  550.1 6.9 %collective-permute-done.24 = bf16[2,2,96,768]{3,2,1,0:T(8,128)(2,1)S(1)} collective-permute-done((bf16[2,2,96,768]{3,2,1,0:T(8,128)(2,1)S(1)}, bf16[2,2,96,768]{3,2,1,0:T(8,128)(2,1)S(1)}, u32[]{:S(2)}, u32[]{:S(2)}) %collective-permute-start.24) | collective-permute-done | bytes 589856 | tf_op jit(solution)/shard_map/ppermute | solution.py:63
  (439 shorter events, 169.1 us)
Async XLA Ops:
  7.2 196.5 %copy-start = (bf16[768,768]{1,0:T(8,128)(2,1)S(1)}, bf16[768,768]{1,0:T(8,128)(2,1)}, u32[]{:S(2)}) copy-start(bf16[768,768]{1,0:T(8,128)(2,1)} %param.32) | copy-start | bytes 3538948
  7.2 89.6 %all-gather.2.cloned.1.call-start = ((), (), s32[]{:S(2)}) async-start(), calls=%async_computation | async-start | bytes 1843200 | tf_op jit(solution)/shard_map/all_gather | solution.py:193
  7.2 41.9 %collective-permute-start = (bf16[1,3,768,192]{2,3,0,1:T(8,128)(2,1)}, bf16[1,3,768,192]{2,3,0,1:T(8,128)(2,1)}, u32[]{:S(2)}, u32[]{:S(2)}) collective-permute-start(bf16[1,3,768,192]{2,3,0,1:T(8,128)(2,1)} %bitcast.258), channel_id=1, source_target_pairs={{0,2},{1,3},{2,0},{3,1},{4,6},{5,7},{6,4},{7,5},{8,10},{9,11},{10,... | collective-permute-start | bytes 2654216 | tf_op jit(solution)/shard_map/ppermute | solution.py:63
  10.3 35.0 %collective-permute-start.2 = (bf16[1,192,768]{2,1,0:T(8,128)(2,1)}, bf16[1,192,768]{2,1,0:T(8,128)(2,1)}, u32[]{:S(2)}, u32[]{:S(2)}) collective-permute-start(bf16[1,192,768]{2,1,0:T(8,128)(2,1)} %bitcast.269), channel_id=1, source_target_pairs={{0,2},{1,3},{2,0},{3,1},{4,6},{5,7},{6,4},{7,5},{8,10},{9,11},{10,... | collective-permute-start | bytes 884744 | tf_op jit(solution)/shard_map/ppermute | solution.py:63
  10.4 12.7 %copy-start.86 = (f32[2,192]{1,0:T(2,128)S(1)}, f32[2,192]{1,0:T(2,128)}, u32[]{:S(2)}) copy-start(f32[2,192]{1,0:T(2,128)} %param.30) | copy-start | bytes 4612
  10.4 13.3 %copy-start.76 = (s32[60,16]{0,1:T(8,128)S(1)}, s32[60,16]{0,1:T(8,128)}, u32[]{:S(2)}) copy-start(s32[60,16]{0,1:T(8,128)} %param.20) | copy-start | bytes 11524
  10.4 60.2 %collective-permute-start.6 = (bf16[1,768,768]{2,1,0:T(8,128)(2,1)}, bf16[1,768,768]{2,1,0:T(8,128)(2,1)}, u32[]{:S(2)}, u32[]{:S(2)}) collective-permute-start(bf16[1,768,768]{2,1,0:T(8,128)(2,1)} %bitcast.249), channel_id=1, source_target_pairs={{0,2},{1,3},{2,0},{3,1},{4,6},{5,7},{6,4},{7,5},{8,10},{9,11},{10,... | collective-permute-start | bytes 3538952 | tf_op jit(solution)/shard_map/ppermute | solution.py:63
  13.9 81.0 %copy-start.11 = (bf16[768,768]{0,1:T(8,128)(2,1)}, bf16[768,768]{0,1:T(8,128)(2,1)S(1)}, u32[]{:S(2)}) copy-start(bf16[768,768]{0,1:T(8,128)(2,1)S(1)} %copy.113) | copy-start | bytes 3538948
  13.9 81.0 %collective-permute-start.4 = (bf16[1,768,768]{1,2,0:T(8,128)(2,1)S(1)}, bf16[1,768,768]{1,2,0:T(8,128)(2,1)S(1)}, u32[]{:S(2)}, u32[]{:S(2)}) collective-permute-start(bf16[1,768,768]{1,2,0:T(8,128)(2,1)S(1)} %bitcast.243), channel_id=1, source_target_pairs={{0,2},{1,3},{2,0},{3,1},{4,6},{5,7},{6,4},{7,5},{8,10},{9,11},{10,... | collective-permute-start | bytes 3538952 | tf_op jit(solution)/shard_map/ppermute | solution.py:63
  14.1 184.1 %all-reduce.3.cloned.1.call-start = ((), (), s32[]{:S(2)}) async-start(), calls=%async_computation.1 | async-start | bytes 2949120 | tf_op jit(solution)/shard_map/psum | solution.py:214
  24.3 30.3 %copy-start.63 = (pred[60,16]{0,1:T(8,128)(4,1)}, pred[60,16]{0,1:T(8,128)(4,1)S(1)}, u32[]{:S(2)}) copy-start(pred[60,16]{0,1:T(8,128)(4,1)S(1)} %get-tuple-element.58) | copy-start | bytes 2884
  28.4 24.1 %copy-start.46 = (bf16[192,768]{1,0:T(8,128)(2,1)S(1)}, bf16[192,768]{1,0:T(8,128)(2,1)}, u32[]{:S(2)}) copy-start(bf16[192,768]{1,0:T(8,128)(2,1)} %param.26) | copy-start | bytes 884740
  29.2 71.3 %copy-start.59 = (f32[768]{0:T(1024)}, f32[768]{0:T(1024)S(1)}, u32[]{:S(2)}) copy-start(f32[768]{0:T(1024)S(1)} %get-tuple-element.47) | copy-start | bytes 9220
  29.2 174.5 %copy-start.55 = (f32[768]{0:T(1024)}, f32[768]{0:T(1024)S(1)}, u32[]{:S(2)}) copy-start(f32[768]{0:T(1024)S(1)} %get-tuple-element.46) | copy-start | bytes 9220
  46.4 6.0 %collective-permute-start.3 = (bf16[2,192,768]{2,1,0:T(8,128)(2,1)S(1)}, bf16[2,192,768]{2,1,0:T(8,128)(2,1)S(1)}, u32[]{:S(2)}, u32[]{:S(2)}) collective-permute-start(bf16[2,192,768]{2,1,0:T(8,128)(2,1)S(1)} %pad_maximum_fusion.13), channel_id=1, source_target_pairs={{0,1},{1,0},{2,3},{3,2},{4,5},{5,4},{6,7},{7,6},{8,9},{9,8},{10,11... | collective-permute-start | bytes 1769480 | tf_op jit(solution)/shard_map/ppermute | solution.py:63
  49.1 21.5 %copy-start.15 = (bf16[768,768]{1,0:T(8,128)(2,1)S(1)}, bf16[768,768]{1,0:T(8,128)(2,1)}, u32[]{:S(2)}) copy-start(bf16[768,768]{1,0:T(8,128)(2,1)} %param.28) | copy-start | bytes 3538948
  52.0 72.5 %collective-permute-start.1 = (bf16[2,3,768,192]{2,3,0,1:T(8,128)(2,1)}, bf16[2,3,768,192]{2,3,0,1:T(8,128)(2,1)}, u32[]{:S(2)}, u32[]{:S(2)}) collective-permute-start(bf16[2,3,768,192]{2,3,0,1:T(8,128)(2,1)} %pad_maximum_fusion.7), channel_id=1, source_target_pairs={{0,1},{1,0},{2,3},{3,2},{4,5},{5,4},{6,7},{7,6},{8,9},{9,8},{10,11... | collective-permute-start | bytes 5308424 | tf_op jit(solution)/shard_map/ppermute | solution.py:63
  73.5 142.2 %collective-permute-start.7 = (bf16[2,768,768]{2,1,0:T(8,128)(2,1)}, bf16[2,768,768]{2,1,0:T(8,128)(2,1)}, u32[]{:S(2)}, u32[]{:S(2)}) collective-permute-start(bf16[2,768,768]{2,1,0:T(8,128)(2,1)} %pad_maximum_fusion.5), channel_id=1, source_target_pairs={{0,1},{1,0},{2,3},{3,2},{4,5},{5,4},{6,7},{7,6},{8,9},{9,8},{10,11... | collective-permute-start | bytes 7077896 | tf_op jit(solution)/shard_map/ppermute | solution.py:63
  96.7 123.0 %collective-permute-start.5 = (bf16[2,768,768]{1,2,0:T(8,128)(2,1)}, bf16[2,768,768]{1,2,0:T(8,128)(2,1)}, u32[]{:S(2)}, u32[]{:S(2)}) collective-permute-start(bf16[2,768,768]{1,2,0:T(8,128)(2,1)} %pad_maximum_fusion.4), channel_id=1, source_target_pairs={{0,1},{1,0},{2,3},{3,2},{4,5},{5,4},{6,7},{7,6},{8,9},{9,8},{10,11... | collective-permute-start | bytes 7077896 | tf_op jit(solution)/shard_map/ppermute | solution.py:63
  98.5 99.6 %copy-start.61 = (f32[960]{0:T(1024)}, f32[960]{0:T(1024)S(1)}, u32[]{:S(2)}) copy-start(f32[960]{0:T(1024)S(1)} %broadcast_multiply_fusion.4) | copy-start | bytes 11524
  100.5 97.7 %copy-start.65 = (f32[960]{0:T(1024)}, f32[960]{0:T(1024)S(1)}, u32[]{:S(2)}) copy-start(f32[960]{0:T(1024)S(1)} %add_rsqrt_fusion.3) | copy-start | bytes 11524
  150.3 6.1 %copy-start.34 = (bf16[435,768]{1,0:T(8,128)(2,1)S(1)}, bf16[435,768]{1,0:T(8,128)(2,1)}, u32[]{:S(2)}) copy-start(bf16[435,768]{1,0:T(8,128)(2,1)} %param.23) | copy-start | bytes 2004484
  202.2 11.5 %copy-start.1 = (f32[960,768]{1,0:T(8,128)}, f32[960,768]{1,0:T(8,128)S(1)}, u32[]{:S(2)}) copy-start(f32[960,768]{1,0:T(8,128)S(1)} %get-tuple-element.62) | copy-start | bytes 8847364
  203.7 8.7 %copy-start.19 = (f32[960,768]{1,0:T(8,128)}, f32[960,768]{1,0:T(8,128)S(1)}, u32[]{:S(2)}) copy-start(f32[960,768]{1,0:T(8,128)S(1)} %subtract_multiply_fusion) | copy-start | bytes 8847364
  203.7 8.7 %copy-start.88 = (bf16[768,768]{1,0:T(8,128)(2,1)S(1)}, bf16[768,768]{1,0:T(8,128)(2,1)}, u32[]{:S(2)}) copy-start(bf16[768,768]{1,0:T(8,128)(2,1)} %param.34) | copy-start | bytes 3538948
  272.9 13.8 %copy-start.67 = (f32[768]{0:T(1024)S(1)}, f32[768]{0:T(1024)}, u32[]{:S(2)}) copy-start(f32[768]{0:T(1024)} %get-tuple-element.44) | copy-start | bytes 9220
  272.9 13.8 %copy-start.77 = (f32[60]{0:T(128)S(1)}, f32[60]{0:T(128)}, u32[]{:S(2)}) copy-start(f32[60]{0:T(128)} %get-tuple-element.57) | copy-start | bytes 724
  273.1 13.7 %copy-start.49 = (f32[60,768]{1,0:T(8,128)S(1)}, f32[60,768]{1,0:T(8,128)}, u32[]{:S(2)}) copy-start(f32[60,768]{1,0:T(8,128)} %get-tuple-element.42) | copy-start | bytes 552964
  273.9 1.8 collective-permute-start.8
  275.7 10.9 %collective-permute-start.9 = (f32[120,768]{1,0:T(8,128)S(1)}, f32[120,768]{1,0:T(8,128)S(1)}, u32[]{:S(2)}, u32[]{:S(2)}) collective-permute-start(f32[120,768]{1,0:T(8,128)S(1)} %fusion.263), channel_id=1, source_target_pairs={{0,2},{1,3},{2,0},{3,1},{4,6},{5,7},{6,4},{7,5},{8,10},{9,11},{10,... | collective-permute-start | bytes 1105928 | tf_op jit(solution)/shard_map/ppermute | solution.py:63
  286.7 24.0 %copy-start.64 = (pred[60,16]{0,1:T(8,128)(4,1)S(1)}, pred[60,16]{0,1:T(8,128)(4,1)}, u32[]{:S(2)}) copy-start(pred[60,16]{0,1:T(8,128)(4,1)} %copy-done.63) | copy-start | bytes 2884
  286.8 24.2 %copy-start.85 = (s32[480]{0:T(512)S(1)}, s32[480]{0:T(512)}, u32[]{:S(2)}) copy-start(s32[480]{0:T(512)} %param.21) | copy-start | bytes 5764
  287.1 11.2 %collective-permute-start.10 = (bf16[120,768]{1,0:T(8,128)(2,1)S(1)}, bf16[120,768]{1,0:T(8,128)(2,1)S(1)}, u32[]{:S(2)}, u32[]{:S(2)}) collective-permute-start(bf16[120,768]{1,0:T(8,128)(2,1)S(1)} %pad_maximum_fusion.20), channel_id=1, source_target_pairs={{0,16},{4,20},{8,24},{12,28},{16,0},{20,4},{24,8},{28,12},{1,17},{... | collective-permute-start | bytes 552968 | tf_op jit(solution)/shard_map/ppermute | solution.py:63
  298.4 9.6 %collective-permute-start.11 = (bf16[2,120,768]{2,1,0:T(8,128)(2,1)S(1)}, bf16[2,120,768]{2,1,0:T(8,128)(2,1)S(1)}, u32[]{:S(2)}, u32[]{:S(2)}) collective-permute-start(bf16[2,120,768]{2,1,0:T(8,128)(2,1)S(1)} %pad_maximum_fusion.18), channel_id=1, source_target_pairs={{0,8},{4,12},{8,0},{12,4},{16,24},{20,28},{24,16},{28,20},{1,9},{5... | collective-permute-start | bytes 1105928 | tf_op jit(solution)/shard_map/ppermute | solution.py:63
  309.0 16.9 %collective-permute-start.12 = (bf16[2,2,120,768]{3,2,1,0:T(8,128)(2,1)}, bf16[2,2,120,768]{3,2,1,0:T(8,128)(2,1)S(1)}, u32[]{:S(2)}, u32[]{:S(2)}) collective-permute-start(bf16[2,2,120,768]{3,2,1,0:T(8,128)(2,1)} %pad_maximum_fusion.11), channel_id=1, source_target_pairs={{0,4},{4,0},{8,12},{12,8},{16,20},{20,16},{24,28},{28,24},{1,5},{5... | collective-permute-start | bytes 2211848 | tf_op jit(solution)/shard_map/ppermute | solution.py:63
  329.8 4.9 copy-start.95
  341.0 7.5 %collective-permute-start.13 = (bf16[2,240,768]{2,1,0:T(8,128)(2,1)S(1)}, bf16[2,240,768]{2,1,0:T(8,128)(2,1)S(1)}, u32[]{:S(2)}, u32[]{:S(2)}) collective-permute-start(bf16[2,240,768]{2,1,0:T(8,128)(2,1)S(1)} %fusion.102), channel_id=1, source_target_pairs={{0,1},{1,0},{2,3},{3,2},{4,5},{5,4},{6,7},{7,6},{8,9},{9,8},{10,11... | collective-permute-start | bytes 2211848 | tf_op jit(solution)/shard_map/ppermute | solution.py:63
  346.8 28.0 %collective-permute-start.30 = (bf16[2,2,192,768]{3,2,1,0:T(8,128)(2,1)}, bf16[2,2,192,768]{3,2,1,0:T(8,128)(2,1)}, u32[]{:S(2)}, u32[]{:S(2)}) collective-permute-start(bf16[2,2,192,768]{3,2,1,0:T(8,128)(2,1)} %fusion.83), channel_id=1, source_target_pairs={{0,4},{4,0},{8,12},{12,8},{16,20},{20,16},{24,28},{28,24},{1,5},{5... | collective-permute-start | bytes 3538952 | tf_op jit(solution)/shard_map/ppermute | solution.py:63
  350.1 10.1 %collective-permute-start.14 = (bf16[240,768]{1,0:T(8,128)(2,1)S(1)}, bf16[240,768]{1,0:T(8,128)(2,1)S(1)}, u32[]{:S(2)}, u32[]{:S(2)}) collective-permute-start(bf16[240,768]{1,0:T(8,128)(2,1)S(1)} %fusion.133), channel_id=1, source_target_pairs={{0,2},{1,3},{2,0},{3,1},{4,6},{5,7},{6,4},{7,5},{8,10},{9,11},{10,... | collective-permute-start | bytes 1105928 | tf_op jit(solution)/shard_map/ppermute | solution.py:63
  361.0 19.3 %collective-permute-start.15 = (bf16[240,768]{1,0:T(8,128)(2,1)}, bf16[240,768]{1,0:T(8,128)(2,1)}, u32[]{:S(2)}, u32[]{:S(2)}) collective-permute-start(bf16[240,768]{1,0:T(8,128)(2,1)} %fusion.104), channel_id=1, source_target_pairs={{0,2},{1,3},{2,0},{3,1},{4,6},{5,7},{6,4},{7,5},{8,10},{9,11},{10,... | collective-permute-start | bytes 1105928 | tf_op jit(solution)/shard_map/ppermute | solution.py:63
  378.0 15.1 %collective-permute-start.31 = (bf16[2,192,768]{2,1,0:T(8,128)(2,1)}, bf16[2,192,768]{2,1,0:T(8,128)(2,1)}, u32[]{:S(2)}, u32[]{:S(2)}) collective-permute-start(bf16[2,192,768]{2,1,0:T(8,128)(2,1)} %fusion.124), channel_id=1, source_target_pairs={{0,8},{4,12},{8,0},{12,4},{16,24},{20,28},{24,16},{28,20},{1,9},{5... | collective-permute-start | bytes 1769480 | tf_op jit(solution)/shard_map/ppermute | solution.py:63
  380.3 18.7 %copy-start.66 = (f32[960]{0:T(1024)S(1)}, f32[960]{0:T(1024)}, u32[]{:S(2)}) copy-start(f32[960]{0:T(1024)} %copy-done.65) | copy-start | bytes 11524
  382.5 29.9 %collective-permute-start.16 = (bf16[2,240,768]{2,1,0:T(8,128)(2,1)}, bf16[2,240,768]{2,1,0:T(8,128)(2,1)}, u32[]{:S(2)}, u32[]{:S(2)}) collective-permute-start(bf16[2,240,768]{2,1,0:T(8,128)(2,1)} %pad_maximum_fusion.12), channel_id=1, source_target_pairs={{0,1},{1,0},{2,3},{3,2},{4,5},{5,4},{6,7},{7,6},{8,9},{9,8},{10,11... | collective-permute-start | bytes 2211848 | tf_op jit(solution)/shard_map/ppermute | solution.py:63
  395.3 15.3 %collective-permute-start.32 = (bf16[192,768]{1,0:T(8,128)(2,1)S(1)}, bf16[192,768]{1,0:T(8,128)(2,1)S(1)}, u32[]{:S(2)}, u32[]{:S(2)}) collective-permute-start(bf16[192,768]{1,0:T(8,128)(2,1)S(1)} %fusion.136), channel_id=1, source_target_pairs={{0,16},{4,20},{8,24},{12,28},{16,0},{20,4},{24,8},{28,12},{1,17},{... | collective-permute-start | bytes 884744 | tf_op jit(solution)/shard_map/ppermute | solution.py:63
  412.4 58.0 %collective-permute-start.33 = (bf16[192,768]{1,0:T(8,128)(2,1)}, bf16[192,768]{1,0:T(8,128)(2,1)}, u32[]{:S(2)}, u32[]{:S(2)}) collective-permute-start(bf16[192,768]{1,0:T(8,128)(2,1)} %fusion.125), channel_id=1, source_target_pairs={{0,16},{4,20},{8,24},{12,28},{16,0},{20,4},{24,8},{28,12},{1,17},{... | collective-permute-start | bytes 884744 | tf_op jit(solution)/shard_map/ppermute | solution.py:63
  417.7 7.0 %copy-start.45 = (bf16[192,768]{1,0:T(8,128)(2,1)S(1)}, bf16[192,768]{1,0:T(8,128)(2,1)}, u32[]{:S(2)}) copy-start(bf16[192,768]{1,0:T(8,128)(2,1)} %param.31) | copy-start | bytes 884740
  460.6 15.3 %collective-permute-start.19 = (bf16[2,2,96,768]{3,2,1,0:T(8,128)(2,1)}, bf16[2,2,96,768]{3,2,1,0:T(8,128)(2,1)}, u32[]{:S(2)}, u32[]{:S(2)}) collective-permute-start(bf16[2,2,96,768]{3,2,1,0:T(8,128)(2,1)} %fusion.123), channel_id=1, source_target_pairs={{0,4},{4,0},{8,12},{12,8},{16,20},{20,16},{24,28},{28,24},{1,5},{5... | collective-permute-start | bytes 1769480 | tf_op jit(solution)/shard_map/ppermute | solution.py:63
  464.4 16.8 %collective-permute-start.17 = (bf16[2,240,768]{2,1,0:T(8,128)(2,1)}, bf16[2,240,768]{2,1,0:T(8,128)(2,1)}, u32[]{:S(2)}, u32[]{:S(2)}) collective-permute-start(bf16[2,240,768]{2,1,0:T(8,128)(2,1)} %fusion.103), channel_id=1, source_target_pairs={{0,1},{1,0},{2,3},{3,2},{4,5},{5,4},{6,7},{7,6},{8,9},{9,8},{10,11... | collective-permute-start | bytes 2211848 | tf_op jit(solution)/shard_map/ppermute | solution.py:63
  470.4 10.8 %copy-start.38 = (f32[2,2,240,768]{3,2,1,0:T(8,128)S(1)}, f32[2,2,240,768]{3,2,1,0:T(8,128)}, u32[]{:S(2)}) copy-start(f32[2,2,240,768]{3,2,1,0:T(8,128)} %convolution_bitcast_fusion) | copy-start | bytes 8847364
  471.7 18.3 %collective-permute-start.34 = (bf16[2,192,768]{2,1,0:T(8,128)(2,1)S(1)}, bf16[2,192,768]{2,1,0:T(8,128)(2,1)S(1)}, u32[]{:S(2)}, u32[]{:S(2)}) collective-permute-start(bf16[2,192,768]{2,1,0:T(8,128)(2,1)S(1)} %pad_maximum_fusion.15), channel_id=1, source_target_pairs={{0,8},{4,12},{8,0},{12,4},{16,24},{20,28},{24,16},{28,20},{1,9},{5... | collective-permute-start | bytes 1769480 | tf_op jit(solution)/shard_map/ppermute | solution.py:63
  477.1 19.1 %collective-permute-start.20 = (bf16[2,96,768]{2,1,0:T(8,128)(2,1)S(1)}, bf16[2,96,768]{2,1,0:T(8,128)(2,1)S(1)}, u32[]{:S(2)}, u32[]{:S(2)}) collective-permute-start(bf16[2,96,768]{2,1,0:T(8,128)(2,1)S(1)} %fusion.135), channel_id=1, source_target_pairs={{0,8},{4,12},{8,0},{12,4},{16,24},{20,28},{24,16},{28,20},{1,9},{5... | collective-permute-start | bytes 884744 | tf_op jit(solution)/shard_map/ppermute | solution.py:63
  482.5 13.8 %copy-start.13 = (f32[960,768]{1,0:T(8,128)S(1)}, f32[960,768]{1,0:T(8,128)}, u32[]{:S(2)}) copy-start(f32[960,768]{1,0:T(8,128)} %get-tuple-element.78) | copy-start | bytes 8847364
  482.6 14.2 %copy-start.78 = (f32[240]{0:T(256)S(1)}, f32[240]{0:T(256)}, u32[]{:S(2)}) copy-start(f32[240]{0:T(256)} %dynamic-slice.3) | copy-start | bytes 2884
  482.6 13.7 %collective-permute-start.18 = (bf16[240,768]{1,0:T(8,128)(2,1)S(1)}, bf16[240,768]{1,0:T(8,128)(2,1)S(1)}, u32[]{:S(2)}, u32[]{:S(2)}) collective-permute-start(bf16[240,768]{1,0:T(8,128)(2,1)S(1)} %fusion.134), channel_id=1, source_target_pairs={{0,2},{1,3},{2,0},{3,1},{4,6},{5,7},{6,4},{7,5},{8,10},{9,11},{10,... | collective-permute-start | bytes 1105928 | tf_op jit(solution)/shard_map/ppermute | solution.py:63
  499.0 1.3 collective-permute-start.25
  499.1 10.4 %collective-permute-start.21 = (bf16[96,768]{1,0:T(8,128)(2,1)S(1)}, bf16[96,768]{1,0:T(8,128)(2,1)S(1)}, u32[]{:S(2)}, u32[]{:S(2)}) collective-permute-start(bf16[96,768]{1,0:T(8,128)(2,1)S(1)} %fusion.140), channel_id=1, source_target_pairs={{0,16},{4,20},{8,24},{12,28},{16,0},{20,4},{24,8},{28,12},{1,17},{... | collective-permute-start | bytes 442376 | tf_op jit(solution)/shard_map/ppermute | solution.py:63
  500.2 3.8 collective-permute-start.26
  503.1 41.8 %collective-permute-start.35 = (bf16[2,2,192,768]{3,2,1,0:T(8,128)(2,1)}, bf16[2,2,192,768]{3,2,1,0:T(8,128)(2,1)}, u32[]{:S(2)}, u32[]{:S(2)}) collective-permute-start(bf16[2,2,192,768]{3,2,1,0:T(8,128)(2,1)} %pad_maximum_fusion.10), channel_id=1, source_target_pairs={{0,4},{4,0},{8,12},{12,8},{16,20},{20,16},{24,28},{28,24},{1,5},{5... | collective-permute-start | bytes 3538952 | tf_op jit(solution)/shard_map/ppermute | solution.py:63
  504.1 27.4 %collective-permute-start.27 = (f32[8,768]{1,0:T(8,128)S(1)}, f32[8,768]{1,0:T(8,128)S(1)}, u32[]{:S(2)}, u32[]{:S(2)}) collective-permute-start(f32[8,768]{1,0:T(8,128)S(1)} %pad_maximum_fusion.21), channel_id=1, source_target_pairs={{0,4},{4,0},{8,12},{12,8},{16,20},{20,16},{24,28},{28,24},{1,5},{5... | collective-permute-start | bytes 73736 | tf_op jit(solution)/shard_map/ppermute | solution.py:63
  509.5 23.9 %collective-permute-start.22 = (bf16[96,768]{1,0:T(8,128)(2,1)S(1)}, bf16[96,768]{1,0:T(8,128)(2,1)S(1)}, u32[]{:S(2)}, u32[]{:S(2)}) collective-permute-start(bf16[96,768]{1,0:T(8,128)(2,1)S(1)} %fusion.137), channel_id=1, source_target_pairs={{0,16},{4,20},{8,24},{12,28},{16,0},{20,4},{24,8},{28,12},{1,17},{... | collective-permute-start | bytes 442376 | tf_op jit(solution)/shard_map/ppermute | solution.py:63
  531.6 3.9 collective-permute-start.28
  535.5 4.8 collective-permute-start.29
  537.4 7.0 %collective-permute-start.23 = (bf16[2,96,768]{2,1,0:T(8,128)(2,1)S(1)}, bf16[2,96,768]{2,1,0:T(8,128)(2,1)S(1)}, u32[]{:S(2)}, u32[]{:S(2)}) collective-permute-start(bf16[2,96,768]{2,1,0:T(8,128)(2,1)S(1)} %pad_maximum_fusion.19), channel_id=1, source_target_pairs={{0,8},{4,12},{8,0},{12,4},{16,24},{20,28},{24,16},{28,20},{1,9},{5... | collective-permute-start | bytes 884744 | tf_op jit(solution)/shard_map/ppermute | solution.py:63
  544.5 12.4 %collective-permute-start.24 = (bf16[2,2,96,768]{3,2,1,0:T(8,128)(2,1)S(1)}, bf16[2,2,96,768]{3,2,1,0:T(8,128)(2,1)S(1)}, u32[]{:S(2)}, u32[]{:S(2)}) collective-permute-start(bf16[2,2,96,768]{3,2,1,0:T(8,128)(2,1)S(1)} %pad_maximum_fusion.14), channel_id=1, source_target_pairs={{0,4},{4,0},{8,12},{12,8},{16,20},{20,16},{24,28},{28,24},{1,5},{5... | collective-permute-start | bytes 1769480 | tf_op jit(solution)/shard_map/ppermute | solution.py:63
  (70 other events, 178.8 us)
Sparse Core Ops, SparseCore 0:
  14.2 28.7 all-gather.1
  124.6 43.0 all-reduce.2

commit v6 on v5

--- a/solution.py
+++ b/solution.py
@@ -113,15 +113,20 @@
 
 def image_tower(tokens, count, length, gains, weights):
     w_qkv, w_out, w_fc1, w_fc2 = weights
+    _, middle = image_attention(tokens, count, length, gains, w_qkv, w_out)
+    return image_ffn(middle, count, length, gains, w_fc1, w_fc2)
+
+
+def image_attention(tokens, count, length, gains, w_qkv, w_out):
     head_count = D // HEAD
     inputs = tokens.astype(jnp.float32)
-    unit, spare = layer_stats(inputs)
+    unit, _ = layer_stats(inputs)
     normed = (unit * gains[0]).astype(jnp.bfloat16)
     projected = jnp.einsum("rd,jdw->jrw", normed, w_qkv, preferred_element_type=jnp.float32).astype(
         jnp.bfloat16
     )
     shaped = projected.reshape(3, count, length, head_count, HEAD)
-    shares, spare_lse = attention_shares(shaped[0], shaped[1], None)
+    shares, _ = attention_shares(shaped[0], shaped[1], None)
     context = jnp.einsum(
         "nhqk,nkhe->nqhe",
         shares.astype(jnp.bfloat16),
@@ -130,19 +135,25 @@
     )
     context = context.astype(jnp.bfloat16).reshape(count * length, D)
     middle = inputs + jnp.dot(context, w_out, preferred_element_type=jnp.float32)
-    unit2, spare2 = layer_stats(middle)
+    return inputs, middle
+
+
+def image_ffn(middle, count, length, gains, w_fc1, w_fc2):
+    unit2, _ = layer_stats(middle)
     normed2 = (unit2 * gains[1]).astype(jnp.bfloat16)
     active = gelu_exact(jnp.dot(normed2, w_fc1, preferred_element_type=jnp.float32)).astype(
         jnp.bfloat16
     )
-    result = middle + jnp.dot(active, w_fc2, preferred_element_type=jnp.float32)
-    pooled = jnp.mean(result.reshape(count, length, D), 1)
+    mean_active = jnp.mean(active.astype(jnp.float32).reshape(count, length, -1), 1)
+    pooled = jnp.mean(middle.reshape(count, length, D), 1) + jnp.dot(
+        mean_active, w_fc2.astype(jnp.float32), precision=lax.Precision.HIGHEST
+    )
     return (pooled * lax.rsqrt(jnp.sum(pooled * pooled, -1, keepdims=True) + EPS)).astype(
         jnp.bfloat16
     )
 
 
-def local(
+def local_body(
     text_in,
     caption_ids,
     pairing,
@@ -385,7 +396,7 @@
         P(),
     )
     return jax.shard_map(
-        local,
+        local_body,
         mesh=mesh,
         in_specs=placed,
         out_specs=(

time: 578 us -> 623 us (1.078)
  local copies, waits for them, and re-layouts: 115 us -> 134 us
  waiting for transfers between devices: 187 us -> 198 us
  other arithmetic: 93.4 us -> 103 us
    reshape x12 -> x14, local copies, waits for them, and re-layouts: 28 us -> 43.4 us  [the longest x2 13 us: image_ffn(): active.astype(jnp.float32).reshape(count, length, -1)]
    reduce_sum x11, other arithmetic: 8.35 us -> 19.8 us  [the longest x2 8.04 us: image_ffn(): jnp.mean(active.astype(jnp.float32).reshape(count, length, -1), 1)]
    ppermute x36, waiting for transfers between devices: 187 us -> 198 us  [exchange(): return lax.ppermute(values, axis, [(i, i ^ 1 << bit) for i in range(count)])]
    dot_general x26 -> x28, matrix products: 102 us -> 106 us  [the longest x2 39 us: image_ffn(): jnp.dot(normed2, w_fc1, preferred_element_type=jnp.float32)]
    unnamed x194 -> x204, local copies, waits for them, and re-layouts: 15.8 us -> 19.2 us
  transfers between devices with their start and end apart: 38 -> 38, of which waited for: 22 -> 20; matrix products, arithmetic and copies ran while one was open for 40% -> 44% of each run, Pallas kernels for 0% -> 0%
where the time goes in v6:
time: 623 us; the launch traced here: 616 us
  waiting for transfers between devices  198 us (32%)
  local copies, waits for them, and re-layouts  134 us (22%)
  matrix products  116 us (19%)
  other arithmetic  103 us (17%)
  starting transfers between devices  45.8 us (7%)
  between operations  19 us (3%)
    ppermute x36, waiting for transfers between devices, exchange(): return lax.ppermute(values, axis, [(i, i ^ 1 << bit) for i in range(count)])  198 us
    ppermute x36, starting transfers between devices, exchange(): return lax.ppermute(values, axis, [(i, i ^ 1 << bit) for i in range(count)])  45.7 us
    dot_general x2, matrix products, image_ffn(): jnp.dot(normed2, w_fc1, preferred_element_type=jnp.float32)  39 us
    unnamed x204, local copies, waits for them, and re-layouts  19.2 us
    concatenate x8, other arithmetic, gather_stacked(): data = jnp.concatenate([data, exchange(data, axis, count, bit)], 0)  17.2 us
    squeeze x4, local copies, waits for them, and re-layouts, image_attention(): shares, _ = attention_shares(shaped[0], shaped[1], None)  15 us
    reshape x2, local copies, waits for them, and re-layouts, image_ffn(): active.astype(jnp.float32).reshape(count, length, -1)  13 us
  transfers between devices with their start and end apart: 38, of which 20 were waited for; matrix products, arithmetic and copies ran while one was open for 44% of the time, Pallas kernels for 0%

profile of v6, /device:TPU:0, one launch (start us, length us, event | category | flops | bytes accessed | tf_op | source)
XLA Modules:
  0.0 616.2 jit_solution(10972739681208004114)
XLA Ops:
  7.2 3.1 collective-permute-start.6
  29.4 65.6 %collective-permute-done.2 = bf16[1,192,768]{2,1,0:T(8,128)(2,1)} collective-permute-done((bf16[1,192,768]{2,1,0:T(8,128)(2,1)}, bf16[1,192,768]{2,1,0:T(8,128)(2,1)}, u32[]{:S(2)}, u32[]{:S(2)}) %collective-permute-start.2) | collective-permute-done | bytes 294944 | tf_op jit(solution)/shard_map/ppermute | solution.py:63
  98.1 2.9 pad_maximum_fusion.7
  105.4 2.9 pad_maximum_fusion.4
  112.6 2.5 fusion.116
  116.3 3.0 copy.99
  119.3 6.5 %reshape.321 = bf16[60,16,3,3,64]{4,3,1,0,2:T(4,128)(2,1)} reshape(bf16[960,3,192]{2,0,1:T(8,128)(2,1)} %copy.99) | data formatting | bytes 2211840 | tf_op jit(solution)/shard_map/reshape | solution.py:212
  125.8 3.2 fusion.150
  132.6 2.4 reshape.322
  142.2 3.3 reshape.366
  145.5 3.4 reshape.365
  148.9 3.0 fusion.60
  151.9 3.9 fusion.156
  155.8 2.3 reshape.364
  158.2 4.1 fusion.64
  164.4 4.0 reshape.333
  168.4 3.3 fusion.157
  171.7 2.6 reshape.334
  175.8 4.7 convert_bitcast_fusion
  182.1 4.0 squeeze.85
  186.2 4.2 squeeze.84
  190.4 3.7 fusion.46
  194.1 3.1 fusion.158
  197.2 4.1 squeeze.83
  201.3 4.2 convert_bitcast_fusion.1
  207.3 4.2 reshape.326
  211.5 3.9 fusion.159
  215.5 2.8 reshape.328
  218.2 2.4 reduce_sum.415
  224.7 4.1 fusion.149
  230.3 9.0 %multiply_convert_fusion = (bf16[960,768]{1,0:T(8,128)(2,1)S(1)}, f32[960,768]{1,0:T(8,128)}, f32[960,768]{1,0:T(8,128)}) fusion(f32[768]{0:T(1024)S(1)} %copy-done.95, bf16[768,768]{1,0:T(8,128)(2,1)S(1)} %copy-done, f32[960,768]{1,0:T(8,128)S(1)} %subtract_multiply_fusion, f32[768]{0:T(1024)S(1)} %copy-done.84, f32[768]{0:T(1024)S(1)} %get-tuple-element.46), kind=kOutput, calls=%fused_computation.68 | convolution fusion | flops 1183334400 | bytes 11510784 | tf_op jit(solution)/shard_map/dot_general | solution.py:233
  242.7 2.3 pad_maximum_fusion
  247.2 17.4 %fusion.40 = f32[435,3072]{1,0:T(8,128)} fusion(bf16[768,3072]{0,1:T(8,128)(2,1)S(1)} %bitcast.254, f32[435,768]{1,0:T(8,128)S(1)} %copy-done.17, f32[768]{0:T(1024)S(1)} %copy-done.86, f32[435]{0:T(512)S(1)} %add_rsqrt_fusion.4, f32[435]{0:T(512)S(1)} %broadcast_multiply_fusion.5), kind=kOutput, calls=%fused_computation.93 | convolution fusion | flops 2142120960 | bytes 11406744 | tf_op jit(solution)/shard_map/dot_general | solution.py:144
  264.6 5.5 reshape.351
  270.2 3.7 reduce_sum.426
  280.2 21.6 %fusion.25 = f32[600,3072]{1,0:T(8,128)} fusion(bf16[768,3072]{0,1:T(8,128)(2,1)} %bitcast.255, f32[600,768]{1,0:T(8,128)S(1)} %copy-done.14, f32[768]{0:T(1024)S(1)} %copy-done.87, f32[600]{0:T(1024)S(1)} %copy-done.90, f32[600]{0:T(1024)S(1)} %copy-done.72), kind=kOutput, calls=%fused_computation.53 | convolution fusion | flops 2954649600 | bytes 13942464 | tf_op jit(solution)/shard_map/dot_general | solution.py:144
  301.7 7.4 %reshape.349 = f32[12,50,3072]{2,1,0:T(8,128)} reshape(f32[600,3072]{1,0:T(8,128)} %fusion.25) | data formatting | bytes 14745600 | tf_op jit(solution)/shard_map/reshape | solution.py:147
  309.2 4.3 reduce_sum.418
  313.6 4.4 multiply_reduce_fusion.16
  322.4 8.9 %collective-permute-done.9 = f32[120,768]{1,0:T(8,128)S(1)} collective-permute-done((f32[120,768]{1,0:T(8,128)S(1)}, f32[120,768]{1,0:T(8,128)S(1)}, u32[]{:S(2)}, u32[]{:S(2)}) %collective-permute-start.9) | collective-permute-done | bytes 368672 | tf_op jit(solution)/shard_map/ppermute | solution.py:63
  331.8 2.9 collective-permute-start.10
  334.7 8.0 %collective-permute-done.10 = bf16[120,768]{1,0:T(8,128)(2,1)S(1)} collective-permute-done((bf16[120,768]{1,0:T(8,128)(2,1)S(1)}, bf16[120,768]{1,0:T(8,128)(2,1)S(1)}, u32[]{:S(2)}, u32[]{:S(2)}) %collective-permute-start.10) | collective-permute-done | bytes 184352 | tf_op jit(solution)/shard_map/ppermute | solution.py:63
  343.6 8.8 %collective-permute-done.11 = bf16[2,120,768]{2,1,0:T(8,128)(2,1)S(1)} collective-permute-done((bf16[2,120,768]{2,1,0:T(8,128)(2,1)S(1)}, bf16[2,120,768]{2,1,0:T(8,128)(2,1)S(1)}, u32[]{:S(2)}, u32[]{:S(2)}) %collective-permute-start.11) | collective-permute-done | bytes 368672 | tf_op jit(solution)/shard_map/ppermute | solution.py:63
  355.1 15.3 %collective-permute-done.12 = bf16[2,2,120,768]{3,2,1,0:T(8,128)(2,1)S(1)} collective-permute-done((bf16[2,2,120,768]{3,2,1,0:T(8,128)(2,1)}, bf16[2,2,120,768]{3,2,1,0:T(8,128)(2,1)S(1)}, u32[]{:S(2)}, u32[]{:S(2)}) %collective-permute-start.12) | collective-permute-done | bytes 737312 | tf_op jit(solution)/shard_map/ppermute | solution.py:63
  374.4 2.7 select_reduce_fusion
  379.2 2.7 convert_reduce_fusion.1
  395.9 8.4 %collective-permute-done.14 = bf16[240,768]{1,0:T(8,128)(2,1)S(1)} collective-permute-done((bf16[240,768]{1,0:T(8,128)(2,1)S(1)}, bf16[240,768]{1,0:T(8,128)(2,1)S(1)}, u32[]{:S(2)}, u32[]{:S(2)}) %collective-permute-start.14) | collective-permute-done | bytes 368672 | tf_op jit(solution)/shard_map/ppermute | solution.py:63
  406.8 12.5 %collective-permute-done.30 = bf16[2,2,192,768]{3,2,1,0:T(8,128)(2,1)} collective-permute-done((bf16[2,2,192,768]{3,2,1,0:T(8,128)(2,1)}, bf16[2,2,192,768]{3,2,1,0:T(8,128)(2,1)}, u32[]{:S(2)}, u32[]{:S(2)}) %collective-permute-start.30) | collective-permute-done | bytes 1179680 | tf_op jit(solution)/shard_map/ppermute | solution.py:63
  422.5 2.5 collective-permute-start.31
  427.2 10.5 %collective-permute-done.31 = bf16[2,192,768]{2,1,0:T(8,128)(2,1)} collective-permute-done((bf16[2,192,768]{2,1,0:T(8,128)(2,1)}, bf16[2,192,768]{2,1,0:T(8,128)(2,1)}, u32[]{:S(2)}, u32[]{:S(2)}) %collective-permute-start.31) | collective-permute-done | bytes 589856 | tf_op jit(solution)/shard_map/ppermute | solution.py:63
  440.0 3.7 collective-permute-start.32
  448.0 7.3 %collective-permute-done.32 = bf16[192,768]{1,0:T(8,128)(2,1)S(1)} collective-permute-done((bf16[192,768]{1,0:T(8,128)(2,1)S(1)}, bf16[192,768]{1,0:T(8,128)(2,1)S(1)}, u32[]{:S(2)}, u32[]{:S(2)}) %collective-permute-start.32) | collective-permute-done | bytes 294944 | tf_op jit(solution)/shard_map/ppermute | solution.py:63
  459.2 2.3 copy-done.2
  462.4 5.4 bitcast_multiply_fusion
  491.2 4.6 convolution_bitcast_fusion
  495.8 2.6 convolution_bitcast_fusion.1
  506.8 2.3 fusion.92
  516.4 4.2 collective-permute-start.34
  521.8 4.3 collective-permute-start.20
  528.9 5.8 collective-permute-done.34
  534.8 6.1 collective-permute-done.20
  549.8 4.3 collective-permute-done.21
  554.3 21.9 %collective-permute-done.27 = f32[8,768]{1,0:T(8,128)S(1)} collective-permute-done((f32[8,768]{1,0:T(8,128)S(1)}, f32[8,768]{1,0:T(8,128)S(1)}, u32[]{:S(2)}, u32[]{:S(2)}) %collective-permute-start.27) | collective-permute-done | bytes 24608 | tf_op jit(solution)/shard_map/ppermute | solution.py:63
  594.9 6.7 %collective-permute-done.24 = bf16[2,2,96,768]{3,2,1,0:T(8,128)(2,1)S(1)} collective-permute-done((bf16[2,2,96,768]{3,2,1,0:T(8,128)(2,1)S(1)}, bf16[2,2,96,768]{3,2,1,0:T(8,128)(2,1)S(1)}, u32[]{:S(2)}, u32[]{:S(2)}) %collective-permute-start.24) | collective-permute-done | bytes 589856 | tf_op jit(solution)/shard_map/ppermute | solution.py:63
  (453 shorter events, 189.3 us)
Async XLA Ops:
  7.2 223.1 %copy-start = (bf16[768,768]{1,0:T(8,128)(2,1)S(1)}, bf16[768,768]{1,0:T(8,128)(2,1)}, u32[]{:S(2)}) copy-start(bf16[768,768]{1,0:T(8,128)(2,1)} %param.32) | copy-start | bytes 3538948
  7.2 101.6 %all-gather.2.cloned.1.call-start = ((), (), s32[]{:S(2)}) async-start(), calls=%async_computation | async-start | bytes 1843200 | tf_op jit(solution)/shard_map/all_gather | solution.py:204
  7.2 16.7 %copy-start.79 = (s32[60,16]{0,1:T(8,128)S(1)}, s32[60,16]{0,1:T(8,128)}, u32[]{:S(2)}) copy-start(s32[60,16]{0,1:T(8,128)} %param.20) | copy-start | bytes 11524
  7.2 96.4 %collective-permute-start.6 = (bf16[1,768,768]{2,1,0:T(8,128)(2,1)}, bf16[1,768,768]{2,1,0:T(8,128)(2,1)S(1)}, u32[]{:S(2)}, u32[]{:S(2)}) collective-permute-start(bf16[1,768,768]{2,1,0:T(8,128)(2,1)} %bitcast.251), channel_id=1, source_target_pairs={{0,2},{1,3},{2,0},{3,1},{4,6},{5,7},{6,4},{7,5},{8,10},{9,11},{10,... | collective-permute-start | bytes 3538952 | tf_op jit(solution)/shard_map/ppermute | solution.py:63
  11.9 93.6 %copy-start.12 = (bf16[768,768]{0,1:T(8,128)(2,1)}, bf16[768,768]{0,1:T(8,128)(2,1)S(1)}, u32[]{:S(2)}) copy-start(bf16[768,768]{0,1:T(8,128)(2,1)S(1)} %copy.113) | copy-start | bytes 3538948
  11.9 93.6 %collective-permute-start.4 = (bf16[1,768,768]{1,2,0:T(8,128)(2,1)S(1)}, bf16[1,768,768]{1,2,0:T(8,128)(2,1)}, u32[]{:S(2)}, u32[]{:S(2)}) collective-permute-start(bf16[1,768,768]{1,2,0:T(8,128)(2,1)S(1)} %bitcast.245), channel_id=1, source_target_pairs={{0,2},{1,3},{2,0},{3,1},{4,6},{5,7},{6,4},{7,5},{8,10},{9,11},{10,... | collective-permute-start | bytes 3538952 | tf_op jit(solution)/shard_map/ppermute | solution.py:63
  12.0 86.1 %collective-permute-start = (bf16[1,3,768,192]{2,3,0,1:T(8,128)(2,1)}, bf16[1,3,768,192]{2,3,0,1:T(8,128)(2,1)}, u32[]{:S(2)}, u32[]{:S(2)}) collective-permute-start(bf16[1,3,768,192]{2,3,0,1:T(8,128)(2,1)} %bitcast.258), channel_id=1, source_target_pairs={{0,2},{1,3},{2,0},{3,1},{4,6},{5,7},{6,4},{7,5},{8,10},{9,11},{10,... | collective-permute-start | bytes 2654216 | tf_op jit(solution)/shard_map/ppermute | solution.py:63
  14.0 81.1 %collective-permute-start.2 = (bf16[1,192,768]{2,1,0:T(8,128)(2,1)}, bf16[1,192,768]{2,1,0:T(8,128)(2,1)}, u32[]{:S(2)}, u32[]{:S(2)}) collective-permute-start(bf16[1,192,768]{2,1,0:T(8,128)(2,1)} %bitcast.269), channel_id=1, source_target_pairs={{0,2},{1,3},{2,0},{3,1},{4,6},{5,7},{6,4},{7,5},{8,10},{9,11},{10,... | collective-permute-start | bytes 884744 | tf_op jit(solution)/shard_map/ppermute | solution.py:63
  14.1 210.6 %all-reduce.3.cloned.1.call-start = ((), (), s32[]{:S(2)}) async-start(), calls=%async_computation.1 | async-start | bytes 2949120 | tf_op jit(solution)/shard_map/psum | solution.py:225
  24.5 79.2 %copy-start.63 = (pred[60,16]{0,1:T(8,128)(4,1)}, pred[60,16]{0,1:T(8,128)(4,1)S(1)}, u32[]{:S(2)}) copy-start(pred[60,16]{0,1:T(8,128)(4,1)S(1)} %get-tuple-element.58) | copy-start | bytes 2884
  28.6 72.9 %copy-start.46 = (bf16[192,768]{1,0:T(8,128)(2,1)S(1)}, bf16[192,768]{1,0:T(8,128)(2,1)}, u32[]{:S(2)}) copy-start(bf16[192,768]{1,0:T(8,128)(2,1)} %param.26) | copy-start | bytes 884740
  29.4 83.2 %copy-start.59 = (f32[768]{0:T(1024)}, f32[768]{0:T(1024)S(1)}, u32[]{:S(2)}) copy-start(f32[768]{0:T(1024)S(1)} %get-tuple-element.47) | copy-start | bytes 9220
  96.2 5.4 collective-permute-start.3
  98.1 5.5 copy-start.18
  101.0 35.8 %collective-permute-start.1 = (bf16[2,3,768,192]{2,3,0,1:T(8,128)(2,1)}, bf16[2,3,768,192]{2,3,0,1:T(8,128)(2,1)}, u32[]{:S(2)}, u32[]{:S(2)}) collective-permute-start(bf16[2,3,768,192]{2,3,0,1:T(8,128)(2,1)} %pad_maximum_fusion.7), channel_id=1, source_target_pairs={{0,1},{1,0},{2,3},{3,2},{4,5},{5,4},{6,7},{7,6},{8,9},{9,8},{10,11... | collective-permute-start | bytes 5308424 | tf_op jit(solution)/shard_map/ppermute | solution.py:63
  105.4 7.2 %copy-start.82 = (f32[768]{0:T(1024)S(1)}, f32[768]{0:T(1024)}, u32[]{:S(2)}) copy-start(f32[768]{0:T(1024)} %get-tuple-element.49) | copy-start | bytes 9220
  105.4 168.4 %collective-permute-start.7 = (bf16[2,768,768]{2,1,0:T(8,128)(2,1)}, bf16[2,768,768]{2,1,0:T(8,128)(2,1)}, u32[]{:S(2)}, u32[]{:S(2)}) collective-permute-start(bf16[2,768,768]{2,1,0:T(8,128)(2,1)} %pad_maximum_fusion.5), channel_id=1, source_target_pairs={{0,1},{1,0},{2,3},{3,2},{4,5},{5,4},{6,7},{7,6},{8,9},{9,8},{10,11... | collective-permute-start | bytes 7077896 | tf_op jit(solution)/shard_map/ppermute | solution.py:63
  108.3 134.4 %collective-permute-start.5 = (bf16[2,768,768]{1,2,0:T(8,128)(2,1)}, bf16[2,768,768]{1,2,0:T(8,128)(2,1)}, u32[]{:S(2)}, u32[]{:S(2)}) collective-permute-start(bf16[2,768,768]{1,2,0:T(8,128)(2,1)} %pad_maximum_fusion.4), channel_id=1, source_target_pairs={{0,1},{1,0},{2,3},{3,2},{4,5},{5,4},{6,7},{7,6},{8,9},{9,8},{10,11... | collective-permute-start | bytes 7077896 | tf_op jit(solution)/shard_map/ppermute | solution.py:63
  110.6 114.1 %copy-start.61 = (f32[960]{0:T(1024)}, f32[960]{0:T(1024)S(1)}, u32[]{:S(2)}) copy-start(f32[960]{0:T(1024)S(1)} %broadcast_multiply_fusion.4) | copy-start | bytes 11524
  112.6 112.1 %copy-start.65 = (f32[960]{0:T(1024)}, f32[960]{0:T(1024)S(1)}, u32[]{:S(2)}) copy-start(f32[960]{0:T(1024)S(1)} %add_rsqrt_fusion.3) | copy-start | bytes 11524
  162.3 6.1 copy-start.36
  215.5 6.8 %copy-start.71 = (f32[600]{0:T(1024)}, f32[600]{0:T(1024)S(1)}, u32[]{:S(2)}) copy-start(f32[600]{0:T(1024)S(1)} %broadcast_multiply_fusion) | copy-start | bytes 7204
  218.2 6.4 %copy-start.68 = (f32[768]{0:T(1024)S(1)}, f32[768]{0:T(1024)}, u32[]{:S(2)}) copy-start(f32[768]{0:T(1024)} %get-tuple-element.45) | copy-start | bytes 9220
  228.8 11.9 %copy-start.1 = (f32[960,768]{1,0:T(8,128)}, f32[960,768]{1,0:T(8,128)S(1)}, u32[]{:S(2)}) copy-start(f32[960,768]{1,0:T(8,128)S(1)} %get-tuple-element.62) | copy-start | bytes 8847364
  230.3 9.1 %copy-start.23 = (f32[960,768]{1,0:T(8,128)}, f32[960,768]{1,0:T(8,128)S(1)}, u32[]{:S(2)}) copy-start(f32[960,768]{1,0:T(8,128)S(1)} %subtract_multiply_fusion) | copy-start | bytes 8847364
  230.3 9.1 %copy-start.93 = (bf16[768,768]{1,0:T(8,128)(2,1)S(1)}, bf16[768,768]{1,0:T(8,128)(2,1)}, u32[]{:S(2)}) copy-start(bf16[768,768]{1,0:T(8,128)(2,1)} %param.34) | copy-start | bytes 3538948
  318.0 13.4 %copy-start.49 = (f32[60,768]{1,0:T(8,128)S(1)}, f32[60,768]{1,0:T(8,128)}, u32[]{:S(2)}) copy-start(f32[60,768]{1,0:T(8,128)} %get-tuple-element.42) | copy-start | bytes 552964
  318.0 13.4 %copy-start.67 = (f32[768]{0:T(1024)S(1)}, f32[768]{0:T(1024)}, u32[]{:S(2)}) copy-start(f32[768]{0:T(1024)} %get-tuple-element.44) | copy-start | bytes 9220
  318.0 13.4 %copy-start.80 = (f32[60]{0:T(128)S(1)}, f32[60]{0:T(128)}, u32[]{:S(2)}) copy-start(f32[60]{0:T(128)} %get-tuple-element.57) | copy-start | bytes 724
  318.7 1.8 collective-permute-start.8
  320.5 10.8 %collective-permute-start.9 = (f32[120,768]{1,0:T(8,128)S(1)}, f32[120,768]{1,0:T(8,128)S(1)}, u32[]{:S(2)}, u32[]{:S(2)}) collective-permute-start(f32[120,768]{1,0:T(8,128)S(1)} %fusion.195), channel_id=1, source_target_pairs={{0,2},{1,3},{2,0},{3,1},{4,6},{5,7},{6,4},{7,5},{8,10},{9,11},{10,... | collective-permute-start | bytes 1105928 | tf_op jit(solution)/shard_map/ppermute | solution.py:63
  331.4 23.4 %copy-start.64 = (pred[60,16]{0,1:T(8,128)(4,1)S(1)}, pred[60,16]{0,1:T(8,128)(4,1)}, u32[]{:S(2)}) copy-start(pred[60,16]{0,1:T(8,128)(4,1)} %copy-done.63) | copy-start | bytes 2884
  331.4 23.5 %copy-start.91 = (s32[480]{0:T(512)S(1)}, s32[480]{0:T(512)}, u32[]{:S(2)}) copy-start(s32[480]{0:T(512)} %param.21) | copy-start | bytes 5764
  331.8 10.9 %collective-permute-start.10 = (bf16[120,768]{1,0:T(8,128)(2,1)S(1)}, bf16[120,768]{1,0:T(8,128)(2,1)S(1)}, u32[]{:S(2)}, u32[]{:S(2)}) collective-permute-start(bf16[120,768]{1,0:T(8,128)(2,1)S(1)} %pad_maximum_fusion.20), channel_id=1, source_target_pairs={{0,16},{4,20},{8,24},{12,28},{16,0},{20,4},{24,8},{28,12},{1,17},{... | collective-permute-start | bytes 552968 | tf_op jit(solution)/shard_map/ppermute | solution.py:63
  342.8 9.6 %collective-permute-start.11 = (bf16[2,120,768]{2,1,0:T(8,128)(2,1)S(1)}, bf16[2,120,768]{2,1,0:T(8,128)(2,1)S(1)}, u32[]{:S(2)}, u32[]{:S(2)}) collective-permute-start(bf16[2,120,768]{2,1,0:T(8,128)(2,1)S(1)} %pad_maximum_fusion.18), channel_id=1, source_target_pairs={{0,8},{4,12},{8,0},{12,4},{16,24},{20,28},{24,16},{28,20},{1,9},{5... | collective-permute-start | bytes 1105928 | tf_op jit(solution)/shard_map/ppermute | solution.py:63
  353.4 17.0 %collective-permute-start.12 = (bf16[2,2,120,768]{3,2,1,0:T(8,128)(2,1)}, bf16[2,2,120,768]{3,2,1,0:T(8,128)(2,1)S(1)}, u32[]{:S(2)}, u32[]{:S(2)}) collective-permute-start(bf16[2,2,120,768]{3,2,1,0:T(8,128)(2,1)} %pad_maximum_fusion.11), channel_id=1, source_target_pairs={{0,4},{4,0},{8,12},{12,8},{16,20},{20,16},{24,28},{28,24},{1,5},{5... | collective-permute-start | bytes 2211848 | tf_op jit(solution)/shard_map/ppermute | solution.py:63
  385.5 7.2 %collective-permute-start.13 = (bf16[2,240,768]{2,1,0:T(8,128)(2,1)S(1)}, bf16[2,240,768]{2,1,0:T(8,128)(2,1)S(1)}, u32[]{:S(2)}, u32[]{:S(2)}) collective-permute-start(bf16[2,240,768]{2,1,0:T(8,128)(2,1)S(1)} %fusion.91), channel_id=1, source_target_pairs={{0,1},{1,0},{2,3},{3,2},{4,5},{5,4},{6,7},{7,6},{8,9},{9,8},{10,11... | collective-permute-start | bytes 2211848 | tf_op jit(solution)/shard_map/ppermute | solution.py:63
  391.3 28.0 %collective-permute-start.30 = (bf16[2,2,192,768]{3,2,1,0:T(8,128)(2,1)}, bf16[2,2,192,768]{3,2,1,0:T(8,128)(2,1)}, u32[]{:S(2)}, u32[]{:S(2)}) collective-permute-start(bf16[2,2,192,768]{3,2,1,0:T(8,128)(2,1)} %fusion.75), channel_id=1, source_target_pairs={{0,4},{4,0},{8,12},{12,8},{16,20},{20,16},{24,28},{28,24},{1,5},{5... | collective-permute-start | bytes 3538952 | tf_op jit(solution)/shard_map/ppermute | solution.py:63
  394.3 10.1 %collective-permute-start.14 = (bf16[240,768]{1,0:T(8,128)(2,1)S(1)}, bf16[240,768]{1,0:T(8,128)(2,1)S(1)}, u32[]{:S(2)}, u32[]{:S(2)}) collective-permute-start(bf16[240,768]{1,0:T(8,128)(2,1)S(1)} %fusion.119), channel_id=1, source_target_pairs={{0,2},{1,3},{2,0},{3,1},{4,6},{5,7},{6,4},{7,5},{8,10},{9,11},{10,... | collective-permute-start | bytes 1105928 | tf_op jit(solution)/shard_map/ppermute | solution.py:63
  405.2 19.8 %collective-permute-start.15 = (bf16[240,768]{1,0:T(8,128)(2,1)}, bf16[240,768]{1,0:T(8,128)(2,1)}, u32[]{:S(2)}, u32[]{:S(2)}) collective-permute-start(bf16[240,768]{1,0:T(8,128)(2,1)} %fusion.93), channel_id=1, source_target_pairs={{0,2},{1,3},{2,0},{3,1},{4,6},{5,7},{6,4},{7,5},{8,10},{9,11},{10,... | collective-permute-start | bytes 1105928 | tf_op jit(solution)/shard_map/ppermute | solution.py:63
  422.5 15.3 %collective-permute-start.31 = (bf16[2,192,768]{2,1,0:T(8,128)(2,1)}, bf16[2,192,768]{2,1,0:T(8,128)(2,1)}, u32[]{:S(2)}, u32[]{:S(2)}) collective-permute-start(bf16[2,192,768]{2,1,0:T(8,128)(2,1)} %fusion.110), channel_id=1, source_target_pairs={{0,8},{4,12},{8,0},{12,4},{16,24},{20,28},{24,16},{28,20},{1,9},{5... | collective-permute-start | bytes 1769480 | tf_op jit(solution)/shard_map/ppermute | solution.py:63
  425.0 18.7 %copy-start.66 = (f32[960]{0:T(1024)S(1)}, f32[960]{0:T(1024)}, u32[]{:S(2)}) copy-start(f32[960]{0:T(1024)} %copy-done.65) | copy-start | bytes 11524
  427.2 29.9 %collective-permute-start.16 = (bf16[2,240,768]{2,1,0:T(8,128)(2,1)}, bf16[2,240,768]{2,1,0:T(8,128)(2,1)}, u32[]{:S(2)}, u32[]{:S(2)}) collective-permute-start(bf16[2,240,768]{2,1,0:T(8,128)(2,1)} %pad_maximum_fusion.12), channel_id=1, source_target_pairs={{0,1},{1,0},{2,3},{3,2},{4,5},{5,4},{6,7},{7,6},{8,9},{9,8},{10,11... | collective-permute-start | bytes 2211848 | tf_op jit(solution)/shard_map/ppermute | solution.py:63
  440.0 15.3 %collective-permute-start.32 = (bf16[192,768]{1,0:T(8,128)(2,1)S(1)}, bf16[192,768]{1,0:T(8,128)(2,1)S(1)}, u32[]{:S(2)}, u32[]{:S(2)}) collective-permute-start(bf16[192,768]{1,0:T(8,128)(2,1)S(1)} %fusion.122), channel_id=1, source_target_pairs={{0,16},{4,20},{8,24},{12,28},{16,0},{20,4},{24,8},{28,12},{1,17},{... | collective-permute-start | bytes 884744 | tf_op jit(solution)/shard_map/ppermute | solution.py:63
  457.1 58.0 %collective-permute-start.33 = (bf16[192,768]{1,0:T(8,128)(2,1)}, bf16[192,768]{1,0:T(8,128)(2,1)}, u32[]{:S(2)}, u32[]{:S(2)}) collective-permute-start(bf16[192,768]{1,0:T(8,128)(2,1)} %fusion.111), channel_id=1, source_target_pairs={{0,16},{4,20},{8,24},{12,28},{16,0},{20,4},{24,8},{28,12},{1,17},{... | collective-permute-start | bytes 884744 | tf_op jit(solution)/shard_map/ppermute | solution.py:63
  462.4 7.1 %copy-start.45 = (bf16[192,768]{1,0:T(8,128)(2,1)S(1)}, bf16[192,768]{1,0:T(8,128)(2,1)}, u32[]{:S(2)}) copy-start(bf16[192,768]{1,0:T(8,128)(2,1)} %param.31) | copy-start | bytes 884740
  505.4 15.2 %collective-permute-start.19 = (bf16[2,2,96,768]{3,2,1,0:T(8,128)(2,1)}, bf16[2,2,96,768]{3,2,1,0:T(8,128)(2,1)}, u32[]{:S(2)}, u32[]{:S(2)}) collective-permute-start(bf16[2,2,96,768]{3,2,1,0:T(8,128)(2,1)} %fusion.109), channel_id=1, source_target_pairs={{0,4},{4,0},{8,12},{12,8},{16,20},{20,16},{24,28},{28,24},{1,5},{5... | collective-permute-start | bytes 1769480 | tf_op jit(solution)/shard_map/ppermute | solution.py:63
  509.1 17.0 %collective-permute-start.17 = (bf16[2,240,768]{2,1,0:T(8,128)(2,1)}, bf16[2,240,768]{2,1,0:T(8,128)(2,1)}, u32[]{:S(2)}, u32[]{:S(2)}) collective-permute-start(bf16[2,240,768]{2,1,0:T(8,128)(2,1)} %fusion.92), channel_id=1, source_target_pairs={{0,1},{1,0},{2,3},{3,2},{4,5},{5,4},{6,7},{7,6},{8,9},{9,8},{10,11... | collective-permute-start | bytes 2211848 | tf_op jit(solution)/shard_map/ppermute | solution.py:63
  515.1 11.0 %copy-start.40 = (f32[2,2,240,768]{3,2,1,0:T(8,128)S(1)}, f32[2,2,240,768]{3,2,1,0:T(8,128)}, u32[]{:S(2)}) copy-start(f32[2,2,240,768]{3,2,1,0:T(8,128)} %convolution_bitcast_fusion) | copy-start | bytes 8847364
  516.4 18.3 %collective-permute-start.34 = (bf16[2,192,768]{2,1,0:T(8,128)(2,1)S(1)}, bf16[2,192,768]{2,1,0:T(8,128)(2,1)S(1)}, u32[]{:S(2)}, u32[]{:S(2)}) collective-permute-start(bf16[2,192,768]{2,1,0:T(8,128)(2,1)S(1)} %pad_maximum_fusion.15), channel_id=1, source_target_pairs={{0,8},{4,12},{8,0},{12,4},{16,24},{20,28},{24,16},{28,20},{1,9},{5... | collective-permute-start | bytes 1769480 | tf_op jit(solution)/shard_map/ppermute | solution.py:63
  521.8 19.1 %collective-permute-start.20 = (bf16[2,96,768]{2,1,0:T(8,128)(2,1)S(1)}, bf16[2,96,768]{2,1,0:T(8,128)(2,1)S(1)}, u32[]{:S(2)}, u32[]{:S(2)}) collective-permute-start(bf16[2,96,768]{2,1,0:T(8,128)(2,1)S(1)} %fusion.121), channel_id=1, source_target_pairs={{0,8},{4,12},{8,0},{12,4},{16,24},{20,28},{24,16},{28,20},{1,9},{5... | collective-permute-start | bytes 884744 | tf_op jit(solution)/shard_map/ppermute | solution.py:63
  527.3 13.6 %copy-start.15 = (f32[960,768]{1,0:T(8,128)S(1)}, f32[960,768]{1,0:T(8,128)}, u32[]{:S(2)}) copy-start(f32[960,768]{1,0:T(8,128)} %get-tuple-element.78) | copy-start | bytes 8847364
  527.4 14.0 %copy-start.81 = (f32[240]{0:T(256)S(1)}, f32[240]{0:T(256)}, u32[]{:S(2)}) copy-start(f32[240]{0:T(256)} %dynamic-slice.3) | copy-start | bytes 2884
  527.4 13.6 %collective-permute-start.18 = (bf16[240,768]{1,0:T(8,128)(2,1)S(1)}, bf16[240,768]{1,0:T(8,128)(2,1)S(1)}, u32[]{:S(2)}, u32[]{:S(2)}) collective-permute-start(bf16[240,768]{1,0:T(8,128)(2,1)S(1)} %fusion.120), channel_id=1, source_target_pairs={{0,2},{1,3},{2,0},{3,1},{4,6},{5,7},{6,4},{7,5},{8,10},{9,11},{10,... | collective-permute-start | bytes 1105928 | tf_op jit(solution)/shard_map/ppermute | solution.py:63
  543.7 1.3 collective-permute-start.25
  543.8 10.4 %collective-permute-start.21 = (bf16[96,768]{1,0:T(8,128)(2,1)S(1)}, bf16[96,768]{1,0:T(8,128)(2,1)S(1)}, u32[]{:S(2)}, u32[]{:S(2)}) collective-permute-start(bf16[96,768]{1,0:T(8,128)(2,1)S(1)} %fusion.127), channel_id=1, source_target_pairs={{0,16},{4,20},{8,24},{12,28},{16,0},{20,4},{24,8},{28,12},{1,17},{... | collective-permute-start | bytes 442376 | tf_op jit(solution)/shard_map/ppermute | solution.py:63
  544.9 3.8 collective-permute-start.26
  547.7 42.0 %collective-permute-start.35 = (bf16[2,2,192,768]{3,2,1,0:T(8,128)(2,1)}, bf16[2,2,192,768]{3,2,1,0:T(8,128)(2,1)}, u32[]{:S(2)}, u32[]{:S(2)}) collective-permute-start(bf16[2,2,192,768]{3,2,1,0:T(8,128)(2,1)} %pad_maximum_fusion.10), channel_id=1, source_target_pairs={{0,4},{4,0},{8,12},{12,8},{16,20},{20,16},{24,28},{28,24},{1,5},{5... | collective-permute-start | bytes 3538952 | tf_op jit(solution)/shard_map/ppermute | solution.py:63
  548.8 27.4 %collective-permute-start.27 = (f32[8,768]{1,0:T(8,128)S(1)}, f32[8,768]{1,0:T(8,128)S(1)}, u32[]{:S(2)}, u32[]{:S(2)}) collective-permute-start(f32[8,768]{1,0:T(8,128)S(1)} %pad_maximum_fusion.21), channel_id=1, source_target_pairs={{0,4},{4,0},{8,12},{12,8},{16,20},{20,16},{24,28},{28,24},{1,5},{5... | collective-permute-start | bytes 73736 | tf_op jit(solution)/shard_map/ppermute | solution.py:63
  554.2 23.8 %collective-permute-start.22 = (bf16[96,768]{1,0:T(8,128)(2,1)S(1)}, bf16[96,768]{1,0:T(8,128)(2,1)S(1)}, u32[]{:S(2)}, u32[]{:S(2)}) collective-permute-start(bf16[96,768]{1,0:T(8,128)(2,1)S(1)} %fusion.123), channel_id=1, source_target_pairs={{0,16},{4,20},{8,24},{12,28},{16,0},{20,4},{24,8},{28,12},{1,17},{... | collective-permute-start | bytes 442376 | tf_op jit(solution)/shard_map/ppermute | solution.py:63
  576.2 3.9 collective-permute-start.28
  580.1 4.8 collective-permute-start.29
  582.1 7.0 %collective-permute-start.23 = (bf16[2,96,768]{2,1,0:T(8,128)(2,1)S(1)}, bf16[2,96,768]{2,1,0:T(8,128)(2,1)S(1)}, u32[]{:S(2)}, u32[]{:S(2)}) collective-permute-start(bf16[2,96,768]{2,1,0:T(8,128)(2,1)S(1)} %pad_maximum_fusion.19), channel_id=1, source_target_pairs={{0,8},{4,12},{8,0},{12,4},{16,24},{20,28},{24,16},{28,20},{1,9},{5... | collective-permute-start | bytes 884744 | tf_op jit(solution)/shard_map/ppermute | solution.py:63
  589.2 12.4 %collective-permute-start.24 = (bf16[2,2,96,768]{3,2,1,0:T(8,128)(2,1)S(1)}, bf16[2,2,96,768]{3,2,1,0:T(8,128)(2,1)S(1)}, u32[]{:S(2)}, u32[]{:S(2)}) collective-permute-start(bf16[2,2,96,768]{3,2,1,0:T(8,128)(2,1)S(1)} %pad_maximum_fusion.14), channel_id=1, source_target_pairs={{0,4},{4,0},{8,12},{12,8},{16,20},{20,16},{24,28},{28,24},{1,5},{5... | collective-permute-start | bytes 1769480 | tf_op jit(solution)/shard_map/ppermute | solution.py:63
  (75 other events, 210.2 us)
Sparse Core Ops, SparseCore 0:
  14.2 28.7 all-gather.1
  136.9 42.9 all-reduce.2

commit v7 on v6

--- a/solution.py
+++ b/solution.py
@@ -144,10 +144,8 @@
     active = gelu_exact(jnp.dot(normed2, w_fc1, preferred_element_type=jnp.float32)).astype(
         jnp.bfloat16
     )
-    mean_active = jnp.mean(active.astype(jnp.float32).reshape(count, length, -1), 1)
-    pooled = jnp.mean(middle.reshape(count, length, D), 1) + jnp.dot(
-        mean_active, w_fc2.astype(jnp.float32), precision=lax.Precision.HIGHEST
-    )
+    result = middle + jnp.dot(active, w_fc2, preferred_element_type=jnp.float32)
+    pooled = jnp.mean(result.reshape(count, length, D), 1)
     return (pooled * lax.rsqrt(jnp.sum(pooled * pooled, -1, keepdims=True) + EPS)).astype(
         jnp.bfloat16
     )
@@ -287,7 +285,7 @@
         "gd,gf->df", normed2_all, grad_hidden16, preferred_element_type=jnp.float32
     )
     grad_fc1_bias = jnp.sum(grad_hidden16.astype(jnp.float32), 0)
-    fc_sums = reduce_exchanged(jnp.concatenate([grad_fc1, grad_fc2], 0), "dp")
+    fc_sums = lax.psum(jnp.concatenate([grad_fc1, grad_fc2], 0).astype(jnp.bfloat16), "dp")
     grad_normed2 = reduce_exchanged(
         jnp.einsum("gf,df->gd", grad_hidden16, txt_fc1, preferred_element_type=jnp.float32), "mp"
     ).astype(jnp.float32)

time: 623 us -> 604 us (0.970)
  waiting for transfers between devices: 198 us -> 236 us
  local copies, waits for them, and re-layouts: 134 us -> 105 us
  other arithmetic: 103 us -> 86 us
  starting transfers between devices: 45.8 us -> 35.2 us
    psum x0 -> x1, waiting for transfers between devices: none -> 76.5 us  [local_body(): lax.psum(jnp.concatenate([grad_fc1, grad_fc2], 0).astype(jnp.bfloat16), '...]
    ppermute x36 -> x30, waiting for transfers between devices: 198 us -> 159 us  [exchange(): return lax.ppermute(values, axis, [(i, i ^ 1 << bit) for i in range(count)])]
    reshape x4 -> x2, local copies, waits for them, and re-layouts: 18.4 us -> 3.03 us  [image_ffn(): pooled = jnp.mean(result.reshape(count, length, D), 1)]
    reduce_sum x4, other arithmetic: 11.9 us -> 0.51 us  [the longest x2 0.27 us: image_ffn(): pooled = jnp.mean(result.reshape(count, length, D), 1)]
    ppermute x36 -> x30, starting transfers between devices: 45.7 us -> 34.6 us  [exchange(): return lax.ppermute(values, axis, [(i, i ^ 1 << bit) for i in range(count)])]
    unnamed x204 -> x194, local copies, waits for them, and re-layouts: 19.2 us -> 12.2 us
    another operation x18 -> x13, other arithmetic: 9.04 us -> 2.61 us  [gather_ordered(): jnp.stack([jnp.where(upper, other, data), jnp.where(upper, data, other)], 0)]
    dot_general x4 -> x2, matrix products: 45.5 us -> 45.5 us  [image_ffn(): result = middle + jnp.dot(active, w_fc2, preferred_element_type=jnp.float32)]
  transfers between devices with their start and end apart: 38 -> 33, of which waited for: 20 -> 20; matrix products, arithmetic and copies ran while one was open for 44% -> 29% of each run, Pallas kernels for 0% -> 0%
where the time goes in v7:
time: 604 us; the launch traced here: 594 us
  waiting for transfers between devices  236 us (39%)
  matrix products  113 us (19%)
  local copies, waits for them, and re-layouts  105 us (17%)
  other arithmetic  86 us (14%)
  starting transfers between devices  35.2 us (6%)
  between operations  18.9 us (3%)
    ppermute x30, waiting for transfers between devices, exchange(): return lax.ppermute(values, axis, [(i, i ^ 1 << bit) for i in range(count)])  159 us
    psum x1, waiting for transfers between devices, local_body(): lax.psum(jnp.concatenate([grad_fc1, grad_fc2], 0).astype(jnp.bfloat16), '...  76.5 us
    dot_general x2, matrix products, image_ffn(): result = middle + jnp.dot(active, w_fc2, preferred_element_type=jnp.float32)  45.5 us
    ppermute x30, starting transfers between devices, exchange(): return lax.ppermute(values, axis, [(i, i ^ 1 << bit) for i in range(count)])  34.6 us
    concatenate x8, other arithmetic, gather_stacked(): data = jnp.concatenate([data, exchange(data, axis, count, bit)], 0)  21 us
    squeeze x4, local copies, waits for them, and re-layouts, image_attention(): shares, _ = attention_shares(shaped[0], shaped[1], None)  14.7 us
    unnamed x194, local copies, waits for them, and re-layouts  12.2 us
  transfers between devices with their start and end apart: 33, of which 20 were waited for; matrix products, arithmetic and copies ran while one was open for 29% of the time, Pallas kernels for 0%

profile of v7, /device:TPU:0, one launch (start us, length us, event | category | flops | bytes accessed | tf_op | source)
XLA Modules:
  0.0 594.5 jit_solution(12369038301493511616)
XLA Ops:
  7.2 3.1 collective-permute-start
  20.8 2.2 fusion.55
  29.3 16.1 %collective-permute-done.2 = bf16[1,192,768]{2,1,0:T(8,128)(2,1)} collective-permute-done((bf16[1,192,768]{2,1,0:T(8,128)(2,1)}, bf16[1,192,768]{2,1,0:T(8,128)(2,1)}, u32[]{:S(2)}, u32[]{:S(2)}) %collective-permute-start.2) | collective-permute-done | bytes 294944 | tf_op jit(solution)/shard_map/ppermute | solution.py:63
  49.1 2.9 pad_maximum_fusion.7
  54.6 16.0 %collective-permute-done.6 = bf16[1,768,768]{2,1,0:T(8,128)(2,1)} collective-permute-done((bf16[1,768,768]{2,1,0:T(8,128)(2,1)}, bf16[1,768,768]{2,1,0:T(8,128)(2,1)}, u32[]{:S(2)}, u32[]{:S(2)}) %collective-permute-start.6) | collective-permute-done | bytes 1179680 | tf_op jit(solution)/shard_map/ppermute | solution.py:63
  70.6 2.9 pad_maximum_fusion.4
  73.5 21.4 %collective-permute-done.4 = bf16[1,768,768]{1,2,0:T(8,128)(2,1)S(1)} collective-permute-done((bf16[1,768,768]{1,2,0:T(8,128)(2,1)S(1)}, bf16[1,768,768]{1,2,0:T(8,128)(2,1)S(1)}, u32[]{:S(2)}, u32[]{:S(2)}) %collective-permute-start.4) | collective-permute-done | bytes 1179680 | tf_op jit(solution)/shard_map/ppermute | solution.py:63
  100.5 2.5 fusion.127
  104.2 2.5 copy.95
  106.7 6.4 %reshape.297 = bf16[60,16,3,3,64]{4,3,1,0,2:T(4,128)(2,1)} reshape(bf16[960,3,192]{2,0,1:T(8,128)(2,1)} %copy.95) | data formatting | bytes 2211840 | tf_op jit(solution)/shard_map/reshape | solution.py:210
  113.2 3.2 fusion.213
  120.0 2.4 reshape.298
  124.7 2.2 pad_maximum_fusion.2
  130.0 3.3 reshape.331
  133.4 3.3 reshape.330
  136.7 3.0 fusion.68
  139.6 3.9 fusion.219
  143.5 2.3 reshape.329
  145.8 4.1 fusion.72
  152.1 4.1 reshape.307
  156.3 3.5 fusion.220
  159.8 2.5 convert_bitcast_fusion
  163.9 4.0 squeeze.70
  168.0 4.0 squeeze.69
  172.0 3.7 fusion.48
  175.7 3.1 fusion.221
  178.8 4.1 squeeze.68
  182.9 4.2 convert_bitcast_fusion.1
  188.9 4.4 reshape.302
  193.3 2.9 fusion.222
  197.9 4.0 fusion.212
  203.4 8.7 %multiply_convert_fusion = (bf16[960,768]{1,0:T(8,128)(2,1)S(1)}, f32[960,768]{1,0:T(8,128)}, f32[960,768]{1,0:T(8,128)}) fusion(f32[768]{0:T(1024)S(1)} %copy-done.89, bf16[768,768]{1,0:T(8,128)(2,1)S(1)} %copy-done, f32[960,768]{1,0:T(8,128)S(1)} %subtract_multiply_fusion, f32[768]{0:T(1024)S(1)} %copy-done.76, f32[768]{0:T(1024)S(1)} %get-tuple-element.46), kind=kOutput, calls=%fused_computation.67 | convolution fusion | flops 1183334400 | bytes 11510784 | tf_op jit(solution)/shard_map/dot_general | solution.py:231
  215.4 3.9 pad_maximum_fusion.1
  219.4 4.2 pad_maximum_fusion
  223.6 19.5 %fusion.65 = f32[435,768]{1,0:T(8,128)} fusion(f32[435,768]{1,0:T(8,128)S(1)} %copy-done.36, bf16[3072,768]{1,0:T(8,128)(2,1)} %bitcast.219, bf16[768,3072]{0,1:T(8,128)(2,1)} %bitcast.221, f32[768]{0:T(1024)S(1)} %copy-done.78, f32[435]{0:T(512)S(1)} %add_rsqrt_fusion.4, f32[435]{0:T(512)S(1)} %broadcast_multiply_fusion.5), kind=kOutput, calls=%fused_computation.145 | convolution fusion | flops 4193706240 | bytes 12116376 | tf_op jit(solution)/shard_map/dot_general | solution.py:147
  244.8 26.0 %fusion.61 = f32[600,768]{1,0:T(8,128)} fusion(f32[600,768]{1,0:T(8,128)} %copy-done.29, bf16[3072,768]{1,0:T(8,128)(2,1)} %bitcast.220, bf16[768,3072]{0,1:T(8,128)(2,1)} %bitcast.222, f32[768]{0:T(1024)S(1)} %copy-done.78, f32[600]{0:T(1024)S(1)} %add_rsqrt_fusion, f32[600]{0:T(1024)S(1)} %broadcast_multiply_fusion), kind=kOutput, calls=%fused_computation.127 | convolution fusion | flops 5784422400 | bytes 13131456 | tf_op jit(solution)/shard_map/dot_general | solution.py:147
  277.5 9.1 %collective-permute-done.9 = f32[120,768]{1,0:T(8,128)S(1)} collective-permute-done((f32[120,768]{1,0:T(8,128)S(1)}, f32[120,768]{1,0:T(8,128)S(1)}, u32[]{:S(2)}, u32[]{:S(2)}) %collective-permute-start.9) | collective-permute-done | bytes 368672 | tf_op jit(solution)/shard_map/ppermute | solution.py:63
  287.1 3.0 collective-permute-start.10
  290.1 8.3 %collective-permute-done.10 = bf16[120,768]{1,0:T(8,128)(2,1)S(1)} collective-permute-done((bf16[120,768]{1,0:T(8,128)(2,1)S(1)}, bf16[120,768]{1,0:T(8,128)(2,1)S(1)}, u32[]{:S(2)}, u32[]{:S(2)}) %collective-permute-start.10) | collective-permute-done | bytes 184352 | tf_op jit(solution)/shard_map/ppermute | solution.py:63
  299.3 8.8 %collective-permute-done.11 = bf16[2,120,768]{2,1,0:T(8,128)(2,1)S(1)} collective-permute-done((bf16[2,120,768]{2,1,0:T(8,128)(2,1)S(1)}, bf16[2,120,768]{2,1,0:T(8,128)(2,1)S(1)}, u32[]{:S(2)}, u32[]{:S(2)}) %collective-permute-start.11) | collective-permute-done | bytes 368672 | tf_op jit(solution)/shard_map/ppermute | solution.py:63
  310.9 15.0 %collective-permute-done.12 = bf16[2,2,120,768]{3,2,1,0:T(8,128)(2,1)S(1)} collective-permute-done((bf16[2,2,120,768]{3,2,1,0:T(8,128)(2,1)}, bf16[2,2,120,768]{3,2,1,0:T(8,128)(2,1)S(1)}, u32[]{:S(2)}, u32[]{:S(2)}) %collective-permute-start.12) | collective-permute-done | bytes 737312 | tf_op jit(solution)/shard_map/ppermute | solution.py:63
  329.7 2.7 select_reduce_fusion
  334.0 2.7 convert_reduce_fusion.1
  339.8 2.3 collective-permute-done.13
  345.7 9.1 %collective-permute-done.14 = bf16[240,768]{1,0:T(8,128)(2,1)} collective-permute-done((bf16[240,768]{1,0:T(8,128)(2,1)S(1)}, bf16[240,768]{1,0:T(8,128)(2,1)}, u32[]{:S(2)}, u32[]{:S(2)}) %collective-permute-start.14) | collective-permute-done | bytes 368672 | tf_op jit(solution)/shard_map/ppermute | solution.py:63
  357.5 8.2 %collective-permute-done.15 = bf16[240,768]{1,0:T(8,128)(2,1)S(1)} collective-permute-done((bf16[240,768]{1,0:T(8,128)(2,1)S(1)}, bf16[240,768]{1,0:T(8,128)(2,1)S(1)}, u32[]{:S(2)}, u32[]{:S(2)}) %collective-permute-start.15) | collective-permute-done | bytes 368672 | tf_op jit(solution)/shard_map/ppermute | solution.py:63
  367.4 4.7 convolution_convert_fusion.2
  372.9 2.3 copy-done.2
  376.0 5.5 bitcast_multiply_fusion
  387.0 2.5 convert_reduce_fusion.4
  402.6 2.3 fusion.126
  405.0 6.1 %dot_general.129 = bf16[2,2,240,3,192]{2,1,0,4,3:T(2,128)(2,1)} reshape(bf16[960,3,192]{0,2,1:T(8,128)(2,1)} %fusion.126) | data formatting | bytes 2211840 | tf_op jit(solution)/shard_map/jgw,jdw->gd/dot_general | solution.py:332
  411.1 3.6 convolution_bitcast_fusion.1
  426.0 10.9 %collective-permute-done.19 = bf16[2,2,96,768]{3,2,1,0:T(8,128)(2,1)S(1)} collective-permute-done((bf16[2,2,96,768]{3,2,1,0:T(8,128)(2,1)S(1)}, bf16[2,2,96,768]{3,2,1,0:T(8,128)(2,1)S(1)}, u32[]{:S(2)}, u32[]{:S(2)}) %collective-permute-start.19) | collective-permute-done | bytes 589856 | tf_op jit(solution)/shard_map/ppermute | solution.py:63
  437.1 2.5 collective-permute-start.20
  442.1 4.3 collective-permute-done.20
  446.5 3.7 collective-permute-start.21
  458.1 2.4 dynamic-slice_reduce_fusion.2
  465.7 9.9 %collective-permute-done.22 = bf16[96,768]{1,0:T(8,128)(2,1)S(1)} collective-permute-done((bf16[96,768]{1,0:T(8,128)(2,1)S(1)}, bf16[96,768]{1,0:T(8,128)(2,1)S(1)}, u32[]{:S(2)}, u32[]{:S(2)}) %collective-permute-start.22) | collective-permute-done | bytes 147488 | tf_op jit(solution)/shard_map/ppermute | solution.py:63
  477.5 2.2 collective-permute-done.27
  483.8 11.4 %collective-permute-done.28 = f32[8,768]{1,0:T(8,128)S(1)} collective-permute-done((f32[8,768]{1,0:T(8,128)S(1)}, f32[8,768]{1,0:T(8,128)S(1)}, u32[]{:S(2)}, u32[]{:S(2)}) %collective-permute-start.28) | collective-permute-done | bytes 24608 | tf_op jit(solution)/shard_map/ppermute | solution.py:63
  497.6 76.5 %all-reduce.6.cloned.1.call-done = bf16[1536,768]{1,0:T(8,128)(2,1)} async-done(((bf16[1536,768]{1,0:T(8,128)(2,1)}), bf16[1536,768]{1,0:T(8,128)(2,1)}) %all-reduce.6.cloned.1.call-update) | async-done | bytes 2359312 | tf_op jit(solution)/shard_map/psum | solution.py:288
  574.0 4.2 slice_convert_fusion
  582.6 2.2 reshape.321
  (416 shorter events, 138.7 us)
Async XLA Ops:
  7.2 196.2 %copy-start = (bf16[768,768]{1,0:T(8,128)(2,1)S(1)}, bf16[768,768]{1,0:T(8,128)(2,1)}, u32[]{:S(2)}) copy-start(bf16[768,768]{1,0:T(8,128)(2,1)} %param.32) | copy-start | bytes 3538948
  7.2 89.5 %all-gather.2.cloned.1.call-start = ((), (), s32[]{:S(2)}) async-start(), calls=%async_computation | async-start | bytes 1843200 | tf_op jit(solution)/shard_map/all_gather | solution.py:202
  7.2 41.9 %collective-permute-start = (bf16[1,3,768,192]{2,3,0,1:T(8,128)(2,1)}, bf16[1,3,768,192]{2,3,0,1:T(8,128)(2,1)}, u32[]{:S(2)}, u32[]{:S(2)}) collective-permute-start(bf16[1,3,768,192]{2,3,0,1:T(8,128)(2,1)} %bitcast.225), channel_id=1, source_target_pairs={{0,2},{1,3},{2,0},{3,1},{4,6},{5,7},{6,4},{7,5},{8,10},{9,11},{10,... | collective-permute-start | bytes 2654216 | tf_op jit(solution)/shard_map/ppermute | solution.py:63
  10.3 35.0 %collective-permute-start.2 = (bf16[1,192,768]{2,1,0:T(8,128)(2,1)}, bf16[1,192,768]{2,1,0:T(8,128)(2,1)}, u32[]{:S(2)}, u32[]{:S(2)}) collective-permute-start(bf16[1,192,768]{2,1,0:T(8,128)(2,1)} %bitcast.234), channel_id=1, source_target_pairs={{0,2},{1,3},{2,0},{3,1},{4,6},{5,7},{6,4},{7,5},{8,10},{9,11},{10,... | collective-permute-start | bytes 884744 | tf_op jit(solution)/shard_map/ppermute | solution.py:63
  10.4 12.7 %copy-start.84 = (f32[2,192]{1,0:T(2,128)S(1)}, f32[2,192]{1,0:T(2,128)}, u32[]{:S(2)}) copy-start(f32[2,192]{1,0:T(2,128)} %param.30) | copy-start | bytes 4612
  10.4 13.4 %copy-start.71 = (s32[60,16]{0,1:T(8,128)S(1)}, s32[60,16]{0,1:T(8,128)}, u32[]{:S(2)}) copy-start(s32[60,16]{0,1:T(8,128)} %param.20) | copy-start | bytes 11524
  10.4 60.2 %collective-permute-start.6 = (bf16[1,768,768]{2,1,0:T(8,128)(2,1)}, bf16[1,768,768]{2,1,0:T(8,128)(2,1)}, u32[]{:S(2)}, u32[]{:S(2)}) collective-permute-start(bf16[1,768,768]{2,1,0:T(8,128)(2,1)} %bitcast.216), channel_id=1, source_target_pairs={{0,2},{1,3},{2,0},{3,1},{4,6},{5,7},{6,4},{7,5},{8,10},{9,11},{10,... | collective-permute-start | bytes 3538952 | tf_op jit(solution)/shard_map/ppermute | solution.py:63
  13.9 81.0 %copy-start.10 = (bf16[768,768]{0,1:T(8,128)(2,1)}, bf16[768,768]{0,1:T(8,128)(2,1)S(1)}, u32[]{:S(2)}) copy-start(bf16[768,768]{0,1:T(8,128)(2,1)S(1)} %copy.109) | copy-start | bytes 3538948
  13.9 81.0 %collective-permute-start.4 = (bf16[1,768,768]{1,2,0:T(8,128)(2,1)S(1)}, bf16[1,768,768]{1,2,0:T(8,128)(2,1)S(1)}, u32[]{:S(2)}, u32[]{:S(2)}) collective-permute-start(bf16[1,768,768]{1,2,0:T(8,128)(2,1)S(1)} %bitcast.210), channel_id=1, source_target_pairs={{0,2},{1,3},{2,0},{3,1},{4,6},{5,7},{6,4},{7,5},{8,10},{9,11},{10,... | collective-permute-start | bytes 3538952 | tf_op jit(solution)/shard_map/ppermute | solution.py:63
  14.1 183.8 %all-reduce.4.cloned.1.call-start = ((), (), s32[]{:S(2)}) async-start(), calls=%async_computation.1 | async-start | bytes 2949120 | tf_op jit(solution)/shard_map/psum | solution.py:223
  24.3 30.3 %copy-start.60 = (pred[60,16]{0,1:T(8,128)(4,1)}, pred[60,16]{0,1:T(8,128)(4,1)S(1)}, u32[]{:S(2)}) copy-start(pred[60,16]{0,1:T(8,128)(4,1)S(1)} %get-tuple-element.58) | copy-start | bytes 2884
  28.5 24.0 %copy-start.39 = (bf16[192,768]{1,0:T(8,128)(2,1)S(1)}, bf16[192,768]{1,0:T(8,128)(2,1)}, u32[]{:S(2)}) copy-start(bf16[192,768]{1,0:T(8,128)(2,1)} %param.26) | copy-start | bytes 884740
  29.3 71.2 %copy-start.56 = (f32[768]{0:T(1024)}, f32[768]{0:T(1024)S(1)}, u32[]{:S(2)}) copy-start(f32[768]{0:T(1024)S(1)} %get-tuple-element.47) | copy-start | bytes 9220
  29.3 174.1 %copy-start.52 = (f32[768]{0:T(1024)}, f32[768]{0:T(1024)S(1)}, u32[]{:S(2)}) copy-start(f32[768]{0:T(1024)S(1)} %get-tuple-element.46) | copy-start | bytes 9220
  46.4 6.0 %collective-permute-start.3 = (bf16[2,192,768]{2,1,0:T(8,128)(2,1)S(1)}, bf16[2,192,768]{2,1,0:T(8,128)(2,1)S(1)}, u32[]{:S(2)}, u32[]{:S(2)}) collective-permute-start(bf16[2,192,768]{2,1,0:T(8,128)(2,1)S(1)} %pad_maximum_fusion.12), channel_id=1, source_target_pairs={{0,1},{1,0},{2,3},{3,2},{4,5},{5,4},{6,7},{7,6},{8,9},{9,8},{10,11... | collective-permute-start | bytes 1769480 | tf_op jit(solution)/shard_map/ppermute | solution.py:63
  49.1 21.5 %copy-start.13 = (bf16[768,768]{1,0:T(8,128)(2,1)S(1)}, bf16[768,768]{1,0:T(8,128)(2,1)}, u32[]{:S(2)}) copy-start(bf16[768,768]{1,0:T(8,128)(2,1)} %param.28) | copy-start | bytes 3538948
  52.0 72.7 %collective-permute-start.1 = (bf16[2,3,768,192]{2,3,0,1:T(8,128)(2,1)}, bf16[2,3,768,192]{2,3,0,1:T(8,128)(2,1)}, u32[]{:S(2)}, u32[]{:S(2)}) collective-permute-start(bf16[2,3,768,192]{2,3,0,1:T(8,128)(2,1)} %pad_maximum_fusion.7), channel_id=1, source_target_pairs={{0,1},{1,0},{2,3},{3,2},{4,5},{5,4},{6,7},{7,6},{8,9},{9,8},{10,11... | collective-permute-start | bytes 5308424 | tf_op jit(solution)/shard_map/ppermute | solution.py:63
  73.5 141.9 %collective-permute-start.7 = (bf16[2,768,768]{2,1,0:T(8,128)(2,1)}, bf16[2,768,768]{2,1,0:T(8,128)(2,1)}, u32[]{:S(2)}, u32[]{:S(2)}) collective-permute-start(bf16[2,768,768]{2,1,0:T(8,128)(2,1)} %pad_maximum_fusion.4), channel_id=1, source_target_pairs={{0,1},{1,0},{2,3},{3,2},{4,5},{5,4},{6,7},{7,6},{8,9},{9,8},{10,11... | collective-permute-start | bytes 7077896 | tf_op jit(solution)/shard_map/ppermute | solution.py:63
  96.7 122.6 %collective-permute-start.5 = (bf16[2,768,768]{1,2,0:T(8,128)(2,1)}, bf16[2,768,768]{1,2,0:T(8,128)(2,1)}, u32[]{:S(2)}, u32[]{:S(2)}) collective-permute-start(bf16[2,768,768]{1,2,0:T(8,128)(2,1)} %pad_maximum_fusion.3), channel_id=1, source_target_pairs={{0,1},{1,0},{2,3},{3,2},{4,5},{5,4},{6,7},{7,6},{8,9},{9,8},{10,11... | collective-permute-start | bytes 7077896 | tf_op jit(solution)/shard_map/ppermute | solution.py:63
  98.5 99.4 %copy-start.58 = (f32[960]{0:T(1024)}, f32[960]{0:T(1024)S(1)}, u32[]{:S(2)}) copy-start(f32[960]{0:T(1024)S(1)} %broadcast_multiply_fusion.4) | copy-start | bytes 11524
  100.5 97.4 %copy-start.62 = (f32[960]{0:T(1024)}, f32[960]{0:T(1024)S(1)}, u32[]{:S(2)}) copy-start(f32[960]{0:T(1024)S(1)} %add_rsqrt_fusion.3) | copy-start | bytes 11524
  124.1 449.9 %all-reduce.6.cloned.1.call-start = ((), (), s32[]{:S(2)}) async-start(), calls=%async_computation.2 | async-start | bytes 4718592 | tf_op jit(solution)/shard_map/psum | solution.py:288
  201.9 11.5 %copy-start.1 = (f32[960,768]{1,0:T(8,128)}, f32[960,768]{1,0:T(8,128)S(1)}, u32[]{:S(2)}) copy-start(f32[960,768]{1,0:T(8,128)S(1)} %get-tuple-element.62) | copy-start | bytes 8847364
  203.4 8.7 %copy-start.17 = (f32[960,768]{1,0:T(8,128)}, f32[960,768]{1,0:T(8,128)S(1)}, u32[]{:S(2)}) copy-start(f32[960,768]{1,0:T(8,128)S(1)} %subtract_multiply_fusion) | copy-start | bytes 8847364
  203.4 8.7 %copy-start.86 = (bf16[768,768]{1,0:T(8,128)(2,1)S(1)}, bf16[768,768]{1,0:T(8,128)(2,1)}, u32[]{:S(2)}) copy-start(bf16[768,768]{1,0:T(8,128)(2,1)} %param.34) | copy-start | bytes 3538948
  272.4 14.4 %copy-start.64 = (f32[768]{0:T(1024)S(1)}, f32[768]{0:T(1024)}, u32[]{:S(2)}) copy-start(f32[768]{0:T(1024)} %get-tuple-element.44) | copy-start | bytes 9220
  272.4 14.4 %copy-start.73 = (f32[60]{0:T(128)S(1)}, f32[60]{0:T(128)}, u32[]{:S(2)}) copy-start(f32[60]{0:T(128)} %get-tuple-element.57) | copy-start | bytes 724
  272.6 14.2 %copy-start.44 = (f32[60,768]{1,0:T(8,128)S(1)}, f32[60,768]{1,0:T(8,128)}, u32[]{:S(2)}) copy-start(f32[60,768]{1,0:T(8,128)} %get-tuple-element.42) | copy-start | bytes 552964
  273.8 1.8 collective-permute-start.8
  275.7 11.0 %collective-permute-start.9 = (f32[120,768]{1,0:T(8,128)S(1)}, f32[120,768]{1,0:T(8,128)S(1)}, u32[]{:S(2)}, u32[]{:S(2)}) collective-permute-start(f32[120,768]{1,0:T(8,128)S(1)} %fusion.257), channel_id=1, source_target_pairs={{0,2},{1,3},{2,0},{3,1},{4,6},{5,7},{6,4},{7,5},{8,10},{9,11},{10,... | collective-permute-start | bytes 1105928 | tf_op jit(solution)/shard_map/ppermute | solution.py:63
  286.7 23.9 %copy-start.61 = (pred[60,16]{0,1:T(8,128)(4,1)S(1)}, pred[60,16]{0,1:T(8,128)(4,1)}, u32[]{:S(2)}) copy-start(pred[60,16]{0,1:T(8,128)(4,1)} %copy-done.60) | copy-start | bytes 2884
  286.8 24.0 %copy-start.82 = (s32[480]{0:T(512)S(1)}, s32[480]{0:T(512)}, u32[]{:S(2)}) copy-start(s32[480]{0:T(512)} %param.21) | copy-start | bytes 5764
  287.1 11.2 %collective-permute-start.10 = (bf16[120,768]{1,0:T(8,128)(2,1)S(1)}, bf16[120,768]{1,0:T(8,128)(2,1)S(1)}, u32[]{:S(2)}, u32[]{:S(2)}) collective-permute-start(bf16[120,768]{1,0:T(8,128)(2,1)S(1)} %pad_maximum_fusion.18), channel_id=1, source_target_pairs={{0,16},{4,20},{8,24},{12,28},{16,0},{20,4},{24,8},{28,12},{1,17},{... | collective-permute-start | bytes 552968 | tf_op jit(solution)/shard_map/ppermute | solution.py:63
  298.5 9.5 %collective-permute-start.11 = (bf16[2,120,768]{2,1,0:T(8,128)(2,1)S(1)}, bf16[2,120,768]{2,1,0:T(8,128)(2,1)S(1)}, u32[]{:S(2)}, u32[]{:S(2)}) collective-permute-start(bf16[2,120,768]{2,1,0:T(8,128)(2,1)S(1)} %pad_maximum_fusion.16), channel_id=1, source_target_pairs={{0,8},{4,12},{8,0},{12,4},{16,24},{20,28},{24,16},{28,20},{1,9},{5... | collective-permute-start | bytes 1105928 | tf_op jit(solution)/shard_map/ppermute | solution.py:63
  309.0 16.9 %collective-permute-start.12 = (bf16[2,2,120,768]{3,2,1,0:T(8,128)(2,1)}, bf16[2,2,120,768]{3,2,1,0:T(8,128)(2,1)S(1)}, u32[]{:S(2)}, u32[]{:S(2)}) collective-permute-start(bf16[2,2,120,768]{3,2,1,0:T(8,128)(2,1)} %pad_maximum_fusion.10), channel_id=1, source_target_pairs={{0,4},{4,0},{8,12},{12,8},{16,20},{20,16},{24,28},{28,24},{1,5},{5... | collective-permute-start | bytes 2211848 | tf_op jit(solution)/shard_map/ppermute | solution.py:63
  339.7 2.4 collective-permute-start.13
  343.9 22.8 %copy-start.63 = (f32[960]{0:T(1024)S(1)}, f32[960]{0:T(1024)}, u32[]{:S(2)}) copy-start(f32[960]{0:T(1024)} %copy-done.62) | copy-start | bytes 11524
  343.9 23.4 %copy-start.46 = (f32[60,3,16]{2,1,0:T(4,128)S(1)}, f32[60,3,16]{2,1,0:T(4,128)}, u32[]{:S(2)}) copy-start(f32[60,3,16]{2,1,0:T(4,128)} %copy-done.45) | copy-start | bytes 34564
  343.9 23.4 %copy-start.48 = (f32[60,3,16]{2,1,0:T(4,128)S(1)}, f32[60,3,16]{2,1,0:T(4,128)}, u32[]{:S(2)}) copy-start(f32[60,3,16]{2,1,0:T(4,128)} %copy-done.47) | copy-start | bytes 34564
  343.9 23.5 %copy-start.53 = (f32[768]{0:T(1024)S(1)}, f32[768]{0:T(1024)}, u32[]{:S(2)}) copy-start(f32[768]{0:T(1024)} %copy-done.52) | copy-start | bytes 9220
  343.9 23.5 %copy-start.77 = (f32[768]{0:T(1024)S(1)}, f32[768]{0:T(1024)}, u32[]{:S(2)}) copy-start(f32[768]{0:T(1024)} %get-tuple-element.48) | copy-start | bytes 9220
  344.0 10.8 %collective-permute-start.14 = (bf16[240,768]{1,0:T(8,128)(2,1)S(1)}, bf16[240,768]{1,0:T(8,128)(2,1)}, u32[]{:S(2)}, u32[]{:S(2)}) collective-permute-start(bf16[240,768]{1,0:T(8,128)(2,1)S(1)} %fusion.129), channel_id=1, source_target_pairs={{0,2},{1,3},{2,0},{3,1},{4,6},{5,7},{6,4},{7,5},{8,10},{9,11},{10,... | collective-permute-start | bytes 1105928 | tf_op jit(solution)/shard_map/ppermute | solution.py:63
  355.9 9.8 %collective-permute-start.15 = (bf16[240,768]{1,0:T(8,128)(2,1)S(1)}, bf16[240,768]{1,0:T(8,128)(2,1)S(1)}, u32[]{:S(2)}, u32[]{:S(2)}) collective-permute-start(bf16[240,768]{1,0:T(8,128)(2,1)S(1)} %fusion.103), channel_id=1, source_target_pairs={{0,2},{1,3},{2,0},{3,1},{4,6},{5,7},{6,4},{7,5},{8,10},{9,11},{10,... | collective-permute-start | bytes 1105928 | tf_op jit(solution)/shard_map/ppermute | solution.py:63
  366.7 5.4 collective-permute-start.16
  376.0 7.1 %copy-start.38 = (bf16[192,768]{1,0:T(8,128)(2,1)S(1)}, bf16[192,768]{1,0:T(8,128)(2,1)}, u32[]{:S(2)}) copy-start(bf16[192,768]{1,0:T(8,128)(2,1)} %param.31) | copy-start | bytes 884740
  401.7 9.4 %copy-start.9 = (bf16[960,768]{1,0:T(8,128)(2,1)S(1)}, bf16[960,768]{1,0:T(8,128)(2,1)}, u32[]{:S(2)}) copy-start(bf16[960,768]{1,0:T(8,128)(2,1)} %all-gather.2.cloned.1.call-done) | copy-start | bytes 4423684
  401.7 9.4 %copy-start.57 = (f32[768]{0:T(1024)S(1)}, f32[768]{0:T(1024)}, u32[]{:S(2)}) copy-start(f32[768]{0:T(1024)} %copy-done.56) | copy-start | bytes 9220
  401.7 9.4 %copy-start.59 = (f32[960]{0:T(1024)S(1)}, f32[960]{0:T(1024)}, u32[]{:S(2)}) copy-start(f32[960]{0:T(1024)} %copy-done.58) | copy-start | bytes 11524
  401.7 9.4 %copy-start.75 = (f32[768]{0:T(1024)S(1)}, f32[768]{0:T(1024)}, u32[]{:S(2)}) copy-start(f32[768]{0:T(1024)} %get-tuple-element.49) | copy-start | bytes 9220
  402.6 8.4 %copy-start.32 = (bf16[1,960,192]{1,2,0:T(8,128)(2,1)S(1)}, bf16[1,960,192]{1,2,0:T(8,128)(2,1)}, u32[]{:S(2)}) copy-start(bf16[1,960,192]{1,2,0:T(8,128)(2,1)} %copy.131) | copy-start | bytes 1105924
  421.1 15.8 %collective-permute-start.19 = (bf16[2,2,96,768]{3,2,1,0:T(8,128)(2,1)S(1)}, bf16[2,2,96,768]{3,2,1,0:T(8,128)(2,1)S(1)}, u32[]{:S(2)}, u32[]{:S(2)}) collective-permute-start(bf16[2,2,96,768]{3,2,1,0:T(8,128)(2,1)S(1)} %fusion.122), channel_id=1, source_target_pairs={{0,4},{4,0},{8,12},{12,8},{16,20},{20,16},{24,28},{28,24},{1,5},{5... | collective-permute-start | bytes 1769480 | tf_op jit(solution)/shard_map/ppermute | solution.py:63
  424.2 15.4 %collective-permute-start.17 = (bf16[2,240,768]{2,1,0:T(8,128)(2,1)S(1)}, bf16[2,240,768]{2,1,0:T(8,128)(2,1)S(1)}, u32[]{:S(2)}, u32[]{:S(2)}) collective-permute-start(bf16[2,240,768]{2,1,0:T(8,128)(2,1)S(1)} %fusion.102), channel_id=1, source_target_pairs={{0,1},{1,0},{2,3},{3,2},{4,5},{5,4},{6,7},{7,6},{8,9},{9,8},{10,11... | collective-permute-start | bytes 2211848 | tf_op jit(solution)/shard_map/ppermute | solution.py:63
  437.1 13.2 %copy-start.41 = (bf16[768,768]{1,0:T(8,128)(2,1)S(1)}, bf16[768,768]{1,0:T(8,128)(2,1)}, u32[]{:S(2)}) copy-start(bf16[768,768]{1,0:T(8,128)(2,1)} %convolution_convert_fusion.2) | copy-start | bytes 3538948
  437.1 9.4 %collective-permute-start.20 = (bf16[2,96,768]{2,1,0:T(8,128)(2,1)S(1)}, bf16[2,96,768]{2,1,0:T(8,128)(2,1)S(1)}, u32[]{:S(2)}, u32[]{:S(2)}) collective-permute-start(bf16[2,96,768]{2,1,0:T(8,128)(2,1)S(1)} %fusion.131), channel_id=1, source_target_pairs={{0,8},{4,12},{8,0},{12,4},{16,24},{20,28},{24,16},{28,20},{1,9},{5... | collective-permute-start | bytes 884744 | tf_op jit(solution)/shard_map/ppermute | solution.py:63
  440.5 15.9 %collective-permute-start.18 = (bf16[240,768]{1,0:T(8,128)(2,1)}, bf16[240,768]{1,0:T(8,128)(2,1)}, u32[]{:S(2)}, u32[]{:S(2)}) collective-permute-start(bf16[240,768]{1,0:T(8,128)(2,1)} %fusion.130), channel_id=1, source_target_pairs={{0,2},{1,3},{2,0},{3,1},{4,6},{5,7},{6,4},{7,5},{8,10},{9,11},{10,... | collective-permute-start | bytes 1105928 | tf_op jit(solution)/shard_map/ppermute | solution.py:63
  446.5 9.8 %collective-permute-start.21 = (bf16[96,768]{1,0:T(8,128)(2,1)S(1)}, bf16[96,768]{1,0:T(8,128)(2,1)S(1)}, u32[]{:S(2)}, u32[]{:S(2)}) collective-permute-start(bf16[96,768]{1,0:T(8,128)(2,1)S(1)} %fusion.135), channel_id=1, source_target_pairs={{0,16},{4,20},{8,24},{12,28},{16,0},{20,4},{24,8},{28,12},{1,17},{... | collective-permute-start | bytes 442376 | tf_op jit(solution)/shard_map/ppermute | solution.py:63
  456.4 19.2 %collective-permute-start.22 = (bf16[96,768]{1,0:T(8,128)(2,1)S(1)}, bf16[96,768]{1,0:T(8,128)(2,1)S(1)}, u32[]{:S(2)}, u32[]{:S(2)}) collective-permute-start(bf16[96,768]{1,0:T(8,128)(2,1)S(1)} %fusion.132), channel_id=1, source_target_pairs={{0,16},{4,20},{8,24},{12,28},{16,0},{20,4},{24,8},{28,12},{1,17},{... | collective-permute-start | bytes 442376 | tf_op jit(solution)/shard_map/ppermute | solution.py:63
  460.6 1.3 collective-permute-start.25
  461.9 3.8 collective-permute-start.26
  475.7 20.1 %collective-permute-start.23 = (bf16[2,96,768]{2,1,0:T(8,128)(2,1)S(1)}, bf16[2,96,768]{2,1,0:T(8,128)(2,1)S(1)}, u32[]{:S(2)}, u32[]{:S(2)}) collective-permute-start(bf16[2,96,768]{2,1,0:T(8,128)(2,1)S(1)} %pad_maximum_fusion.17), channel_id=1, source_target_pairs={{0,8},{4,12},{8,0},{12,4},{16,24},{20,28},{24,16},{28,20},{1,9},{5... | collective-permute-start | bytes 884744 | tf_op jit(solution)/shard_map/ppermute | solution.py:63
  475.8 3.9 collective-permute-start.27
  479.7 15.4 %collective-permute-start.28 = (f32[8,768]{1,0:T(8,128)S(1)}, f32[8,768]{1,0:T(8,128)S(1)}, u32[]{:S(2)}, u32[]{:S(2)}) collective-permute-start(f32[8,768]{1,0:T(8,128)S(1)} %fusion.256), channel_id=1, source_target_pairs={{0,8},{4,12},{8,0},{12,4},{16,24},{20,28},{24,16},{28,20},{1,9},{5... | collective-permute-start | bytes 73736 | tf_op jit(solution)/shard_map/ppermute | solution.py:63
  495.1 83.1 %collective-permute-start.29 = (f32[8,768]{1,0:T(8,128)S(1)}, f32[8,768]{1,0:T(8,128)S(1)}, u32[]{:S(2)}, u32[]{:S(2)}) collective-permute-start(f32[8,768]{1,0:T(8,128)S(1)} %add.359), channel_id=1, source_target_pairs={{0,16},{4,20},{8,24},{12,28},{16,0},{20,4},{24,8},{28,12},{1,17},{... | collective-permute-start | bytes 73736 | tf_op jit(solution)/shard_map/ppermute | solution.py:63
  495.9 84.2 %collective-permute-start.24 = (bf16[2,2,96,768]{3,2,1,0:T(8,128)(2,1)S(1)}, bf16[2,2,96,768]{3,2,1,0:T(8,128)(2,1)S(1)}, u32[]{:S(2)}, u32[]{:S(2)}) collective-permute-start(bf16[2,2,96,768]{3,2,1,0:T(8,128)(2,1)S(1)} %pad_maximum_fusion.13), channel_id=1, source_target_pairs={{0,4},{4,0},{8,12},{12,8},{16,20},{20,16},{24,28},{28,24},{1,5},{5... | collective-permute-start | bytes 1769480 | tf_op jit(solution)/shard_map/ppermute | solution.py:63
  (65 other events, 186.5 us)
Sparse Core Ops, SparseCore 0:
  14.2 28.7 all-gather.1
  124.2 43.0 all-reduce.3
  452.0 122.0 all-reduce.5

commit v8 on v6

--- a/solution.py
+++ b/solution.py
@@ -144,7 +144,11 @@
     active = gelu_exact(jnp.dot(normed2, w_fc1, preferred_element_type=jnp.float32)).astype(
         jnp.bfloat16
     )
-    mean_active = jnp.mean(active.astype(jnp.float32).reshape(count, length, -1), 1)
+    pool = (
+        lax.broadcasted_iota(jnp.int32, (count, count * length), 1) // length
+        == lax.broadcasted_iota(jnp.int32, (count, count * length), 0)
+    ).astype(jnp.bfloat16)
+    mean_active = jnp.dot(pool, active, preferred_element_type=jnp.float32) / length
     pooled = jnp.mean(middle.reshape(count, length, D), 1) + jnp.dot(
         mean_active, w_fc2.astype(jnp.float32), precision=lax.Precision.HIGHEST
     )
@@ -287,7 +291,7 @@
         "gd,gf->df", normed2_all, grad_hidden16, preferred_element_type=jnp.float32
     )
     grad_fc1_bias = jnp.sum(grad_hidden16.astype(jnp.float32), 0)
-    fc_sums = reduce_exchanged(jnp.concatenate([grad_fc1, grad_fc2], 0), "dp")
+    fc_sums = lax.psum(jnp.concatenate([grad_fc1, grad_fc2], 0).astype(jnp.bfloat16), "dp")
     grad_normed2 = reduce_exchanged(
         jnp.einsum("gf,df->gd", grad_hidden16, txt_fc1, preferred_element_type=jnp.float32), "mp"
     ).astype(jnp.float32)

time: 623 us -> 615 us (0.987)
  waiting for transfers between devices: 198 us -> 237 us
  local copies, waits for them, and re-layouts: 134 us -> 107 us
  starting transfers between devices: 45.8 us -> 34.3 us
  other arithmetic: 103 us -> 92.5 us
    psum x0 -> x1, waiting for transfers between devices: none -> 76.6 us  [local_body(): lax.psum(jnp.concatenate([grad_fc1, grad_fc2], 0).astype(jnp.bfloat16), '...]
    ppermute x36 -> x30, waiting for transfers between devices: 198 us -> 161 us  [exchange(): return lax.ppermute(values, axis, [(i, i ^ 1 << bit) for i in range(count)])]
    reshape x2 -> x0, local copies, waits for them, and re-layouts: 13 us -> none  [image_ffn(): active.astype(jnp.float32).reshape(count, length, -1)]
    ppermute x36 -> x30, starting transfers between devices: 45.7 us -> 33.7 us  [exchange(): return lax.ppermute(values, axis, [(i, i ^ 1 << bit) for i in range(count)])]
    reduce_sum x2 -> x0, other arithmetic: 8.04 us -> none  [image_ffn(): jnp.mean(active.astype(jnp.float32).reshape(count, length, -1), 1)]
    another operation x18 -> x13, other arithmetic: 9.04 us -> 2.61 us  [gather_ordered(): jnp.stack([jnp.where(upper, other, data), jnp.where(upper, data, other)], 0)]
    unnamed x204 -> x188, local copies, waits for them, and re-layouts: 19.2 us -> 13.6 us
  transfers between devices with their start and end apart: 38 -> 33, of which waited for: 20 -> 19; matrix products, arithmetic and copies ran while one was open for 44% -> 34% of each run, Pallas kernels for 0% -> 0%
where the time goes in v8:
time: 615 us; the launch traced here: 605 us
  waiting for transfers between devices  237 us (39%)
  matrix products  115 us (19%)
  local copies, waits for them, and re-layouts  107 us (17%)
  other arithmetic  92.5 us (15%)
  starting transfers between devices  34.3 us (6%)
  between operations  18.8 us (3%)
    ppermute x30, waiting for transfers between devices, exchange(): return lax.ppermute(values, axis, [(i, i ^ 1 << bit) for i in range(count)])  161 us
    psum x1, waiting for transfers between devices, local_body(): lax.psum(jnp.concatenate([grad_fc1, grad_fc2], 0).astype(jnp.bfloat16), '...  76.6 us
    dot_general x2, matrix products, image_ffn(): jnp.dot(pool, active, preferred_element_type=jnp.float32) / length  36.8 us
    ppermute x30, starting transfers between devices, exchange(): return lax.ppermute(values, axis, [(i, i ^ 1 << bit) for i in range(count)])  33.7 us
    concatenate x8, other arithmetic, gather_stacked(): data = jnp.concatenate([data, exchange(data, axis, count, bit)], 0)  19.8 us
    squeeze x4, local copies, waits for them, and re-layouts, image_attention(): shares, _ = attention_shares(shaped[0], shaped[1], None)  14.7 us
    unnamed x188, local copies, waits for them, and re-layouts  13.6 us
  transfers between devices with their start and end apart: 33, of which 19 were waited for; matrix products, arithmetic and copies ran while one was open for 34% of the time, Pallas kernels for 0%

profile of v8, /device:TPU:0, one launch (start us, length us, event | category | flops | bytes accessed | tf_op | source)
XLA Modules:
  0.0 605.0 jit_solution(18226703920466390221)
XLA Ops:
  8.9 3.1 collective-permute-start.4
  30.1 42.0 %collective-permute-done.2 = bf16[1,192,768]{2,1,0:T(8,128)(2,1)} collective-permute-done((bf16[1,192,768]{2,1,0:T(8,128)(2,1)}, bf16[1,192,768]{2,1,0:T(8,128)(2,1)}, u32[]{:S(2)}, u32[]{:S(2)}) %collective-permute-start.2) | collective-permute-done | bytes 294944 | tf_op jit(solution)/shard_map/ppermute | solution.py:63
  75.8 2.8 pad_maximum_fusion.7
  81.3 2.9 pad_maximum_fusion.3
  84.3 12.1 %collective-permute-done.6 = bf16[1,768,768]{2,1,0:T(8,128)(2,1)S(1)} collective-permute-done((bf16[1,768,768]{2,1,0:T(8,128)(2,1)}, bf16[1,768,768]{2,1,0:T(8,128)(2,1)S(1)}, u32[]{:S(2)}, u32[]{:S(2)}) %collective-permute-start.6) | collective-permute-done | bytes 1179680 | tf_op jit(solution)/shard_map/ppermute | solution.py:63
  102.0 2.5 fusion.123
  105.7 2.5 copy.95
  108.2 6.4 %reshape.297 = bf16[60,16,3,3,64]{4,3,1,0,2:T(4,128)(2,1)} reshape(bf16[960,3,192]{2,0,1:T(8,128)(2,1)} %copy.95) | data formatting | bytes 2211840 | tf_op jit(solution)/shard_map/reshape | solution.py:216
  114.7 3.2 fusion.221
  121.6 2.4 reshape.298
  131.6 3.3 reshape.331
  135.0 3.3 reshape.330
  138.3 3.0 fusion.64
  141.3 3.8 fusion.227
  145.1 2.3 reshape.329
  147.4 4.1 fusion.68
  153.7 4.1 reshape.307
  157.8 3.4 fusion.228
  161.3 2.6 reshape.308
  165.3 4.7 convert_bitcast_fusion
  171.7 4.1 squeeze.70
  175.8 4.0 squeeze.69
  179.8 3.7 fusion.50
  183.5 3.2 fusion.229
  186.6 4.0 squeeze.68
  190.7 4.2 convert_bitcast_fusion.1
  196.7 4.2 reshape.302
  200.9 3.9 fusion.230
  204.9 3.0 reshape.304
  213.7 4.0 fusion.220
  218.9 8.7 %multiply_convert_fusion = (bf16[960,768]{1,0:T(8,128)(2,1)S(1)}, f32[960,768]{1,0:T(8,128)}, f32[960,768]{1,0:T(8,128)}) fusion(f32[768]{0:T(1024)S(1)} %copy-done.85, bf16[768,768]{1,0:T(8,128)(2,1)S(1)} %copy-done, f32[960,768]{1,0:T(8,128)S(1)} %subtract_multiply_fusion, f32[768]{0:T(1024)S(1)} %copy-done.70, f32[768]{0:T(1024)S(1)} %get-tuple-element.46), kind=kOutput, calls=%fused_computation.69 | convolution fusion | flops 1183334400 | bytes 11510784 | tf_op jit(solution)/shard_map/dot_general | solution.py:237
  230.3 4.4 pad_maximum_fusion
  234.8 15.5 %convolution_multiply_fusion = f32[3,3072]{1,0:T(4,128)S(1)} fusion(bf16[768,3072]{0,1:T(8,128)(2,1)} %bitcast.223, f32[435,768]{1,0:T(8,128)S(1)} %copy-done.15, f32[768]{0:T(1024)S(1)} %copy-done.72, f32[435]{0:T(512)S(1)} %add_rsqrt_fusion.4, f32[435]{0:T(512)S(1)} %broadcast_multiply_fusion.5, s32[435]{0:T(512)S(1)} %copy-done.79, ...), kind=kOutput, calls=%fused_computation.59 | convolution fusion | flops 2148814336 | bytes 6102243 | tf_op jit(solution)/shard_map/dot_general | solution.py:151
  250.3 2.6 pad_maximum_fusion.1
  252.9 2.2 copy-done.3
  257.2 21.3 %fusion.30 = f32[12,3072]{1,0:T(8,128)} fusion(bf16[768,3072]{0,1:T(8,128)(2,1)} %bitcast.224, f32[600,768]{1,0:T(8,128)S(1)} %copy-done.13, f32[768]{0:T(1024)} %get-tuple-element.50, f32[600]{0:T(1024)} %add_rsqrt_fusion, f32[600]{0:T(1024)S(1)} %copy-done.58, s32[600]{0:T(1024)} %iota_divide_fusion, s32[600]{0:T(1024)} %broadcast_add_fusion, ...), kind=kOutput, calls=%fused_computation.58 | convolution fusion | flops 2997094400 | bytes 6722520 | tf_op jit(solution)/shard_map/dot_general | solution.py:151
  278.5 4.5 multiply_reduce_fusion.16
  287.5 9.2 %collective-permute-done.9 = f32[120,768]{1,0:T(8,128)S(1)} collective-permute-done((f32[120,768]{1,0:T(8,128)S(1)}, f32[120,768]{1,0:T(8,128)S(1)}, u32[]{:S(2)}, u32[]{:S(2)}) %collective-permute-start.9) | collective-permute-done | bytes 368672 | tf_op jit(solution)/shard_map/ppermute | solution.py:63
  297.2 2.8 collective-permute-start.10
  300.0 8.3 %collective-permute-done.10 = bf16[120,768]{1,0:T(8,128)(2,1)S(1)} collective-permute-done((bf16[120,768]{1,0:T(8,128)(2,1)S(1)}, bf16[120,768]{1,0:T(8,128)(2,1)S(1)}, u32[]{:S(2)}, u32[]{:S(2)}) %collective-permute-start.10) | collective-permute-done | bytes 184352 | tf_op jit(solution)/shard_map/ppermute | solution.py:63
  309.1 8.8 %collective-permute-done.11 = bf16[2,120,768]{2,1,0:T(8,128)(2,1)S(1)} collective-permute-done((bf16[2,120,768]{2,1,0:T(8,128)(2,1)S(1)}, bf16[2,120,768]{2,1,0:T(8,128)(2,1)S(1)}, u32[]{:S(2)}, u32[]{:S(2)}) %collective-permute-start.11) | collective-permute-done | bytes 368672 | tf_op jit(solution)/shard_map/ppermute | solution.py:63
  320.9 15.0 %collective-permute-done.12 = bf16[2,2,120,768]{3,2,1,0:T(8,128)(2,1)S(1)} collective-permute-done((bf16[2,2,120,768]{3,2,1,0:T(8,128)(2,1)}, bf16[2,2,120,768]{3,2,1,0:T(8,128)(2,1)S(1)}, u32[]{:S(2)}, u32[]{:S(2)}) %collective-permute-start.12) | collective-permute-done | bytes 737312 | tf_op jit(solution)/shard_map/ppermute | solution.py:63
  340.1 2.7 select_reduce_fusion
  344.3 2.7 convert_reduce_fusion.1
  350.2 2.3 collective-permute-done.13
  355.8 9.4 %collective-permute-done.14 = bf16[240,768]{1,0:T(8,128)(2,1)} collective-permute-done((bf16[240,768]{1,0:T(8,128)(2,1)S(1)}, bf16[240,768]{1,0:T(8,128)(2,1)}, u32[]{:S(2)}, u32[]{:S(2)}) %collective-permute-start.14) | collective-permute-done | bytes 368672 | tf_op jit(solution)/shard_map/ppermute | solution.py:63
  367.7 8.4 %collective-permute-done.15 = bf16[240,768]{1,0:T(8,128)(2,1)S(1)} collective-permute-done((bf16[240,768]{1,0:T(8,128)(2,1)S(1)}, bf16[240,768]{1,0:T(8,128)(2,1)S(1)}, u32[]{:S(2)}, u32[]{:S(2)}) %collective-permute-start.15) | collective-permute-done | bytes 368672 | tf_op jit(solution)/shard_map/ppermute | solution.py:63
  377.8 4.8 convolution_convert_fusion.2
  383.3 2.3 copy-done.2
  386.4 5.5 bitcast_multiply_fusion
  397.5 2.5 convert_reduce_fusion.4
  413.2 2.3 fusion.122
  415.5 6.1 %dot_general.137 = bf16[2,2,240,3,192]{2,1,0,4,3:T(2,128)(2,1)} reshape(bf16[960,3,192]{0,2,1:T(8,128)(2,1)} %fusion.122) | data formatting | bytes 2211840 | tf_op jit(solution)/shard_map/jgw,jdw->gd/dot_general | solution.py:338
  421.6 3.6 convolution_bitcast_fusion.1
  436.5 10.9 %collective-permute-done.19 = bf16[2,2,96,768]{3,2,1,0:T(8,128)(2,1)S(1)} collective-permute-done((bf16[2,2,96,768]{3,2,1,0:T(8,128)(2,1)S(1)}, bf16[2,2,96,768]{3,2,1,0:T(8,128)(2,1)S(1)}, u32[]{:S(2)}, u32[]{:S(2)}) %collective-permute-start.19) | collective-permute-done | bytes 589856 | tf_op jit(solution)/shard_map/ppermute | solution.py:63
  447.6 2.6 collective-permute-start.20
  452.4 4.5 collective-permute-done.20
  457.1 3.7 collective-permute-start.21
  468.6 2.4 dynamic-slice_reduce_fusion.2
  476.2 9.9 %collective-permute-done.22 = bf16[96,768]{1,0:T(8,128)(2,1)S(1)} collective-permute-done((bf16[96,768]{1,0:T(8,128)(2,1)S(1)}, bf16[96,768]{1,0:T(8,128)(2,1)S(1)}, u32[]{:S(2)}, u32[]{:S(2)}) %collective-permute-start.22) | collective-permute-done | bytes 147488 | tf_op jit(solution)/shard_map/ppermute | solution.py:63
  488.0 2.2 collective-permute-done.27
  494.2 11.4 %collective-permute-done.28 = f32[8,768]{1,0:T(8,128)S(1)} collective-permute-done((f32[8,768]{1,0:T(8,128)S(1)}, f32[8,768]{1,0:T(8,128)S(1)}, u32[]{:S(2)}, u32[]{:S(2)}) %collective-permute-start.28) | collective-permute-done | bytes 24608 | tf_op jit(solution)/shard_map/ppermute | solution.py:63
  508.0 76.6 %all-reduce.6.cloned.1.call-done = bf16[1536,768]{1,0:T(8,128)(2,1)} async-done(((bf16[1536,768]{1,0:T(8,128)(2,1)}), bf16[1536,768]{1,0:T(8,128)(2,1)}) %all-reduce.6.cloned.1.call-update) | async-done | bytes 2359312 | tf_op jit(solution)/shard_map/psum | solution.py:294
  584.6 4.2 slice_convert_fusion
  (416 shorter events, 149.0 us)
Async XLA Ops:
  7.2 211.4 %copy-start = (bf16[768,768]{1,0:T(8,128)(2,1)S(1)}, bf16[768,768]{1,0:T(8,128)(2,1)}, u32[]{:S(2)}) copy-start(bf16[768,768]{1,0:T(8,128)(2,1)} %param.32) | copy-start | bytes 3538948
  7.2 19.0 %copy-start.63 = (s32[60,16]{0,1:T(8,128)S(1)}, s32[60,16]{0,1:T(8,128)}, u32[]{:S(2)}) copy-start(s32[60,16]{0,1:T(8,128)} %param.20) | copy-start | bytes 11524
  7.2 91.0 %all-gather.2.cloned.1.call-start = ((), (), s32[]{:S(2)}) async-start(), calls=%async_computation | async-start | bytes 1843200 | tf_op jit(solution)/shard_map/all_gather | solution.py:208
  8.9 72.3 %copy-start.11 = (bf16[768,768]{0,1:T(8,128)(2,1)}, bf16[768,768]{0,1:T(8,128)(2,1)S(1)}, u32[]{:S(2)}) copy-start(bf16[768,768]{0,1:T(8,128)(2,1)S(1)} %copy.109) | copy-start | bytes 3538948
  8.9 72.3 %collective-permute-start.4 = (bf16[1,768,768]{1,2,0:T(8,128)(2,1)S(1)}, bf16[1,768,768]{1,2,0:T(8,128)(2,1)}, u32[]{:S(2)}, u32[]{:S(2)}) collective-permute-start(bf16[1,768,768]{1,2,0:T(8,128)(2,1)S(1)} %bitcast.214), channel_id=1, source_target_pairs={{0,2},{1,3},{2,0},{3,1},{4,6},{5,7},{6,4},{7,5},{8,10},{9,11},{10,... | collective-permute-start | bytes 3538952 | tf_op jit(solution)/shard_map/ppermute | solution.py:63
  12.0 63.9 %collective-permute-start = (bf16[1,3,768,192]{2,3,0,1:T(8,128)(2,1)}, bf16[1,3,768,192]{2,3,0,1:T(8,128)(2,1)}, u32[]{:S(2)}, u32[]{:S(2)}) collective-permute-start(bf16[1,3,768,192]{2,3,0,1:T(8,128)(2,1)} %bitcast.227), channel_id=1, source_target_pairs={{0,2},{1,3},{2,0},{3,1},{4,6},{5,7},{6,4},{7,5},{8,10},{9,11},{10,... | collective-permute-start | bytes 2654216 | tf_op jit(solution)/shard_map/ppermute | solution.py:63
  12.1 60.0 %collective-permute-start.2 = (bf16[1,192,768]{2,1,0:T(8,128)(2,1)}, bf16[1,192,768]{2,1,0:T(8,128)(2,1)}, u32[]{:S(2)}, u32[]{:S(2)}) collective-permute-start(bf16[1,192,768]{2,1,0:T(8,128)(2,1)} %bitcast.236), channel_id=1, source_target_pairs={{0,2},{1,3},{2,0},{3,1},{4,6},{5,7},{6,4},{7,5},{8,10},{9,11},{10,... | collective-permute-start | bytes 884744 | tf_op jit(solution)/shard_map/ppermute | solution.py:63
  14.0 82.4 %collective-permute-start.6 = (bf16[1,768,768]{2,1,0:T(8,128)(2,1)}, bf16[1,768,768]{2,1,0:T(8,128)(2,1)S(1)}, u32[]{:S(2)}, u32[]{:S(2)}) collective-permute-start(bf16[1,768,768]{2,1,0:T(8,128)(2,1)} %bitcast.220), channel_id=1, source_target_pairs={{0,2},{1,3},{2,0},{3,1},{4,6},{5,7},{6,4},{7,5},{8,10},{9,11},{10,... | collective-permute-start | bytes 3538952 | tf_op jit(solution)/shard_map/ppermute | solution.py:63
  14.1 199.6 %all-reduce.4.cloned.1.call-start = ((), (), s32[]{:S(2)}) async-start(), calls=%async_computation.1 | async-start | bytes 2949120 | tf_op jit(solution)/shard_map/psum | solution.py:229
  14.2 9.0 %copy-start.21 = (bf16[600,768]{1,0:T(8,128)(2,1)S(1)}, bf16[600,768]{1,0:T(8,128)(2,1)}, u32[]{:S(2)}) copy-start(bf16[600,768]{1,0:T(8,128)(2,1)} %param.22) | copy-start | bytes 2764804
  14.2 10.1 %copy-start.65 = (f32[2,768]{1,0:T(2,128)S(1)}, f32[2,768]{1,0:T(2,128)}, u32[]{:S(2)}) copy-start(f32[2,768]{1,0:T(2,128)} %param.37) | copy-start | bytes 18436
  14.2 10.6 %copy-start.66 = (f32[2,768]{1,0:T(2,128)S(1)}, f32[2,768]{1,0:T(2,128)}, u32[]{:S(2)}) copy-start(f32[2,768]{1,0:T(2,128)} %param.36) | copy-start | bytes 18436
  14.2 11.3 %copy-start.78 = (f32[2,192]{1,0:T(2,128)S(1)}, f32[2,192]{1,0:T(2,128)}, u32[]{:S(2)}) copy-start(f32[2,192]{1,0:T(2,128)} %param.30) | copy-start | bytes 4612
  26.8 54.4 %copy-start.50 = (pred[60,16]{0,1:T(8,128)(4,1)}, pred[60,16]{0,1:T(8,128)(4,1)S(1)}, u32[]{:S(2)}) copy-start(pred[60,16]{0,1:T(8,128)(4,1)S(1)} %get-tuple-element.58) | copy-start | bytes 2884
  29.3 49.8 %copy-start.36 = (bf16[192,768]{1,0:T(8,128)(2,1)S(1)}, bf16[192,768]{1,0:T(8,128)(2,1)}, u32[]{:S(2)}) copy-start(bf16[192,768]{1,0:T(8,128)(2,1)} %param.26) | copy-start | bytes 884740
  30.1 71.9 %copy-start.46 = (f32[768]{0:T(1024)}, f32[768]{0:T(1024)S(1)}, u32[]{:S(2)}) copy-start(f32[768]{0:T(1024)S(1)} %get-tuple-element.47) | copy-start | bytes 9220
  73.2 5.9 collective-permute-start.3
  78.6 17.8 %copy-start.16 = (bf16[768,768]{1,0:T(8,128)(2,1)S(1)}, bf16[768,768]{1,0:T(8,128)(2,1)}, u32[]{:S(2)}) copy-start(bf16[768,768]{1,0:T(8,128)(2,1)} %param.28) | copy-start | bytes 3538948
  78.6 47.6 %collective-permute-start.1 = (bf16[2,3,768,192]{2,3,0,1:T(8,128)(2,1)}, bf16[2,3,768,192]{2,3,0,1:T(8,128)(2,1)}, u32[]{:S(2)}, u32[]{:S(2)}) collective-permute-start(bf16[2,3,768,192]{2,3,0,1:T(8,128)(2,1)} %pad_maximum_fusion.7), channel_id=1, source_target_pairs={{0,1},{1,0},{2,3},{3,2},{4,5},{5,4},{6,7},{7,6},{8,9},{9,8},{10,11... | collective-permute-start | bytes 5308424 | tf_op jit(solution)/shard_map/ppermute | solution.py:63
  84.2 146.2 %collective-permute-start.5 = (bf16[2,768,768]{1,2,0:T(8,128)(2,1)}, bf16[2,768,768]{1,2,0:T(8,128)(2,1)}, u32[]{:S(2)}, u32[]{:S(2)}) collective-permute-start(bf16[2,768,768]{1,2,0:T(8,128)(2,1)} %pad_maximum_fusion.3), channel_id=1, source_target_pairs={{0,1},{1,0},{2,3},{3,2},{4,5},{5,4},{6,7},{7,6},{8,9},{9,8},{10,11... | collective-permute-start | bytes 7077896 | tf_op jit(solution)/shard_map/ppermute | solution.py:63
  98.2 152.1 %collective-permute-start.7 = (bf16[2,768,768]{2,1,0:T(8,128)(2,1)}, bf16[2,768,768]{2,1,0:T(8,128)(2,1)}, u32[]{:S(2)}, u32[]{:S(2)}) collective-permute-start(bf16[2,768,768]{2,1,0:T(8,128)(2,1)} %pad_maximum_fusion.4), channel_id=1, source_target_pairs={{0,1},{1,0},{2,3},{3,2},{4,5},{5,4},{6,7},{7,6},{8,9},{9,8},{10,11... | collective-permute-start | bytes 7077896 | tf_op jit(solution)/shard_map/ppermute | solution.py:63
  100.0 113.7 %copy-start.48 = (f32[960]{0:T(1024)}, f32[960]{0:T(1024)S(1)}, u32[]{:S(2)}) copy-start(f32[960]{0:T(1024)S(1)} %broadcast_multiply_fusion.4) | copy-start | bytes 11524
  102.0 111.7 %copy-start.52 = (f32[960]{0:T(1024)}, f32[960]{0:T(1024)S(1)}, u32[]{:S(2)}) copy-start(f32[960]{0:T(1024)S(1)} %add_rsqrt_fusion.3) | copy-start | bytes 11524
  125.7 458.8 %all-reduce.6.cloned.1.call-start = ((), (), s32[]{:S(2)}) async-start(), calls=%async_computation.2 | async-start | bytes 4718592 | tf_op jit(solution)/shard_map/psum | solution.py:294
  217.6 11.3 %copy-start.1 = (f32[960,768]{1,0:T(8,128)}, f32[960,768]{1,0:T(8,128)S(1)}, u32[]{:S(2)}) copy-start(f32[960,768]{1,0:T(8,128)S(1)} %get-tuple-element.62) | copy-start | bytes 8847364
  218.5 9.1 %copy-start.18 = (f32[960,768]{1,0:T(8,128)}, f32[960,768]{1,0:T(8,128)S(1)}, u32[]{:S(2)}) copy-start(f32[960,768]{1,0:T(8,128)S(1)} %subtract_multiply_fusion) | copy-start | bytes 8847364
  218.9 8.7 %copy-start.82 = (bf16[768,768]{1,0:T(8,128)(2,1)S(1)}, bf16[768,768]{1,0:T(8,128)(2,1)}, u32[]{:S(2)}) copy-start(bf16[768,768]{1,0:T(8,128)(2,1)} %param.34) | copy-start | bytes 3538948
  283.0 13.8 %copy-start.54 = (f32[768]{0:T(1024)S(1)}, f32[768]{0:T(1024)}, u32[]{:S(2)}) copy-start(f32[768]{0:T(1024)} %get-tuple-element.44) | copy-start | bytes 9220
  283.0 13.8 %copy-start.67 = (f32[60]{0:T(128)S(1)}, f32[60]{0:T(128)}, u32[]{:S(2)}) copy-start(f32[60]{0:T(128)} %get-tuple-element.57) | copy-start | bytes 724
  283.7 2.0 collective-permute-start.8
  285.8 10.9 %collective-permute-start.9 = (f32[120,768]{1,0:T(8,128)S(1)}, f32[120,768]{1,0:T(8,128)S(1)}, u32[]{:S(2)}, u32[]{:S(2)}) collective-permute-start(f32[120,768]{1,0:T(8,128)S(1)} %fusion.267), channel_id=1, source_target_pairs={{0,2},{1,3},{2,0},{3,1},{4,6},{5,7},{6,4},{7,5},{8,10},{9,11},{10,... | collective-permute-start | bytes 1105928 | tf_op jit(solution)/shard_map/ppermute | solution.py:63
  296.8 23.8 %copy-start.51 = (pred[60,16]{0,1:T(8,128)(4,1)S(1)}, pred[60,16]{0,1:T(8,128)(4,1)}, u32[]{:S(2)}) copy-start(pred[60,16]{0,1:T(8,128)(4,1)} %copy-done.50) | copy-start | bytes 2884
  296.8 24.0 %copy-start.76 = (s32[480]{0:T(512)S(1)}, s32[480]{0:T(512)}, u32[]{:S(2)}) copy-start(s32[480]{0:T(512)} %param.21) | copy-start | bytes 5764
  297.2 11.1 %collective-permute-start.10 = (bf16[120,768]{1,0:T(8,128)(2,1)S(1)}, bf16[120,768]{1,0:T(8,128)(2,1)S(1)}, u32[]{:S(2)}, u32[]{:S(2)}) collective-permute-start(bf16[120,768]{1,0:T(8,128)(2,1)S(1)} %pad_maximum_fusion.18), channel_id=1, source_target_pairs={{0,16},{4,20},{8,24},{12,28},{16,0},{20,4},{24,8},{28,12},{1,17},{... | collective-permute-start | bytes 552968 | tf_op jit(solution)/shard_map/ppermute | solution.py:63
  308.4 9.6 %collective-permute-start.11 = (bf16[2,120,768]{2,1,0:T(8,128)(2,1)S(1)}, bf16[2,120,768]{2,1,0:T(8,128)(2,1)S(1)}, u32[]{:S(2)}, u32[]{:S(2)}) collective-permute-start(bf16[2,120,768]{2,1,0:T(8,128)(2,1)S(1)} %pad_maximum_fusion.16), channel_id=1, source_target_pairs={{0,8},{4,12},{8,0},{12,4},{16,24},{20,28},{24,16},{28,20},{1,9},{5... | collective-permute-start | bytes 1105928 | tf_op jit(solution)/shard_map/ppermute | solution.py:63
  318.9 17.0 %collective-permute-start.12 = (bf16[2,2,120,768]{3,2,1,0:T(8,128)(2,1)}, bf16[2,2,120,768]{3,2,1,0:T(8,128)(2,1)S(1)}, u32[]{:S(2)}, u32[]{:S(2)}) collective-permute-start(bf16[2,2,120,768]{3,2,1,0:T(8,128)(2,1)} %pad_maximum_fusion.10), channel_id=1, source_target_pairs={{0,4},{4,0},{8,12},{12,8},{16,20},{20,16},{24,28},{28,24},{1,5},{5... | collective-permute-start | bytes 2211848 | tf_op jit(solution)/shard_map/ppermute | solution.py:63
  350.2 2.4 collective-permute-start.13
  354.3 22.8 %copy-start.53 = (f32[960]{0:T(1024)S(1)}, f32[960]{0:T(1024)}, u32[]{:S(2)}) copy-start(f32[960]{0:T(1024)} %copy-done.52) | copy-start | bytes 11524
  354.3 23.4 %copy-start.42 = (f32[60,3,16]{2,1,0:T(4,128)S(1)}, f32[60,3,16]{2,1,0:T(4,128)}, u32[]{:S(2)}) copy-start(f32[60,3,16]{2,1,0:T(4,128)} %copy-done.41) | copy-start | bytes 34564
  354.3 23.4 %copy-start.44 = (f32[60,3,16]{2,1,0:T(4,128)S(1)}, f32[60,3,16]{2,1,0:T(4,128)}, u32[]{:S(2)}) copy-start(f32[60,3,16]{2,1,0:T(4,128)} %copy-done.43) | copy-start | bytes 34564
  354.3 23.5 %copy-start.71 = (f32[768]{0:T(1024)S(1)}, f32[768]{0:T(1024)}, u32[]{:S(2)}) copy-start(f32[768]{0:T(1024)} %get-tuple-element.48) | copy-start | bytes 9220
  354.4 10.8 %collective-permute-start.14 = (bf16[240,768]{1,0:T(8,128)(2,1)S(1)}, bf16[240,768]{1,0:T(8,128)(2,1)}, u32[]{:S(2)}, u32[]{:S(2)}) collective-permute-start(bf16[240,768]{1,0:T(8,128)(2,1)S(1)} %fusion.125), channel_id=1, source_target_pairs={{0,2},{1,3},{2,0},{3,1},{4,6},{5,7},{6,4},{7,5},{8,10},{9,11},{10,... | collective-permute-start | bytes 1105928 | tf_op jit(solution)/shard_map/ppermute | solution.py:63
  366.3 9.8 %collective-permute-start.15 = (bf16[240,768]{1,0:T(8,128)(2,1)S(1)}, bf16[240,768]{1,0:T(8,128)(2,1)S(1)}, u32[]{:S(2)}, u32[]{:S(2)}) collective-permute-start(bf16[240,768]{1,0:T(8,128)(2,1)S(1)} %fusion.99), channel_id=1, source_target_pairs={{0,2},{1,3},{2,0},{3,1},{4,6},{5,7},{6,4},{7,5},{8,10},{9,11},{10,... | collective-permute-start | bytes 1105928 | tf_op jit(solution)/shard_map/ppermute | solution.py:63
  377.1 5.5 collective-permute-start.16
  386.4 7.2 %copy-start.35 = (bf16[192,768]{1,0:T(8,128)(2,1)S(1)}, bf16[192,768]{1,0:T(8,128)(2,1)}, u32[]{:S(2)}) copy-start(bf16[192,768]{1,0:T(8,128)(2,1)} %param.31) | copy-start | bytes 884740
  412.2 9.4 %copy-start.10 = (bf16[960,768]{1,0:T(8,128)(2,1)S(1)}, bf16[960,768]{1,0:T(8,128)(2,1)}, u32[]{:S(2)}) copy-start(bf16[960,768]{1,0:T(8,128)(2,1)} %all-gather.2.cloned.1.call-done) | copy-start | bytes 4423684
  412.2 9.4 %copy-start.47 = (f32[768]{0:T(1024)S(1)}, f32[768]{0:T(1024)}, u32[]{:S(2)}) copy-start(f32[768]{0:T(1024)} %copy-done.46) | copy-start | bytes 9220
  412.2 9.4 %copy-start.49 = (f32[960]{0:T(1024)S(1)}, f32[960]{0:T(1024)}, u32[]{:S(2)}) copy-start(f32[960]{0:T(1024)} %copy-done.48) | copy-start | bytes 11524
  412.2 9.4 %copy-start.69 = (f32[768]{0:T(1024)S(1)}, f32[768]{0:T(1024)}, u32[]{:S(2)}) copy-start(f32[768]{0:T(1024)} %get-tuple-element.49) | copy-start | bytes 9220
  413.2 8.4 %copy-start.31 = (bf16[1,960,192]{1,2,0:T(8,128)(2,1)S(1)}, bf16[1,960,192]{1,2,0:T(8,128)(2,1)}, u32[]{:S(2)}) copy-start(bf16[1,960,192]{1,2,0:T(8,128)(2,1)} %copy.131) | copy-start | bytes 1105924
  431.6 15.8 %collective-permute-start.19 = (bf16[2,2,96,768]{3,2,1,0:T(8,128)(2,1)S(1)}, bf16[2,2,96,768]{3,2,1,0:T(8,128)(2,1)S(1)}, u32[]{:S(2)}, u32[]{:S(2)}) collective-permute-start(bf16[2,2,96,768]{3,2,1,0:T(8,128)(2,1)S(1)} %fusion.118), channel_id=1, source_target_pairs={{0,4},{4,0},{8,12},{12,8},{16,20},{20,16},{24,28},{28,24},{1,5},{5... | collective-permute-start | bytes 1769480 | tf_op jit(solution)/shard_map/ppermute | solution.py:63
  434.7 15.4 %collective-permute-start.17 = (bf16[2,240,768]{2,1,0:T(8,128)(2,1)S(1)}, bf16[2,240,768]{2,1,0:T(8,128)(2,1)S(1)}, u32[]{:S(2)}, u32[]{:S(2)}) collective-permute-start(bf16[2,240,768]{2,1,0:T(8,128)(2,1)S(1)} %fusion.98), channel_id=1, source_target_pairs={{0,1},{1,0},{2,3},{3,2},{4,5},{5,4},{6,7},{7,6},{8,9},{9,8},{10,11... | collective-permute-start | bytes 2211848 | tf_op jit(solution)/shard_map/ppermute | solution.py:63
  447.6 13.2 %copy-start.38 = (bf16[768,768]{1,0:T(8,128)(2,1)S(1)}, bf16[768,768]{1,0:T(8,128)(2,1)}, u32[]{:S(2)}) copy-start(bf16[768,768]{1,0:T(8,128)(2,1)} %convolution_convert_fusion.2) | copy-start | bytes 3538948
  447.6 9.4 %collective-permute-start.20 = (bf16[2,96,768]{2,1,0:T(8,128)(2,1)S(1)}, bf16[2,96,768]{2,1,0:T(8,128)(2,1)S(1)}, u32[]{:S(2)}, u32[]{:S(2)}) collective-permute-start(bf16[2,96,768]{2,1,0:T(8,128)(2,1)S(1)} %fusion.127), channel_id=1, source_target_pairs={{0,8},{4,12},{8,0},{12,4},{16,24},{20,28},{24,16},{28,20},{1,9},{5... | collective-permute-start | bytes 884744 | tf_op jit(solution)/shard_map/ppermute | solution.py:63
  451.1 15.9 %collective-permute-start.18 = (bf16[240,768]{1,0:T(8,128)(2,1)}, bf16[240,768]{1,0:T(8,128)(2,1)}, u32[]{:S(2)}, u32[]{:S(2)}) collective-permute-start(bf16[240,768]{1,0:T(8,128)(2,1)} %fusion.126), channel_id=1, source_target_pairs={{0,2},{1,3},{2,0},{3,1},{4,6},{5,7},{6,4},{7,5},{8,10},{9,11},{10,... | collective-permute-start | bytes 1105928 | tf_op jit(solution)/shard_map/ppermute | solution.py:63
  457.1 9.8 %collective-permute-start.21 = (bf16[96,768]{1,0:T(8,128)(2,1)S(1)}, bf16[96,768]{1,0:T(8,128)(2,1)S(1)}, u32[]{:S(2)}, u32[]{:S(2)}) collective-permute-start(bf16[96,768]{1,0:T(8,128)(2,1)S(1)} %fusion.131), channel_id=1, source_target_pairs={{0,16},{4,20},{8,24},{12,28},{16,0},{20,4},{24,8},{28,12},{1,17},{... | collective-permute-start | bytes 442376 | tf_op jit(solution)/shard_map/ppermute | solution.py:63
  466.9 19.2 %collective-permute-start.22 = (bf16[96,768]{1,0:T(8,128)(2,1)S(1)}, bf16[96,768]{1,0:T(8,128)(2,1)S(1)}, u32[]{:S(2)}, u32[]{:S(2)}) collective-permute-start(bf16[96,768]{1,0:T(8,128)(2,1)S(1)} %fusion.128), channel_id=1, source_target_pairs={{0,16},{4,20},{8,24},{12,28},{16,0},{20,4},{24,8},{28,12},{1,17},{... | collective-permute-start | bytes 442376 | tf_op jit(solution)/shard_map/ppermute | solution.py:63
  471.1 1.3 collective-permute-start.25
  472.4 3.8 collective-permute-start.26
  486.2 20.1 %collective-permute-start.23 = (bf16[2,96,768]{2,1,0:T(8,128)(2,1)S(1)}, bf16[2,96,768]{2,1,0:T(8,128)(2,1)S(1)}, u32[]{:S(2)}, u32[]{:S(2)}) collective-permute-start(bf16[2,96,768]{2,1,0:T(8,128)(2,1)S(1)} %pad_maximum_fusion.17), channel_id=1, source_target_pairs={{0,8},{4,12},{8,0},{12,4},{16,24},{20,28},{24,16},{28,20},{1,9},{5... | collective-permute-start | bytes 884744 | tf_op jit(solution)/shard_map/ppermute | solution.py:63
  486.3 3.9 collective-permute-start.27
  490.2 15.4 %collective-permute-start.28 = (f32[8,768]{1,0:T(8,128)S(1)}, f32[8,768]{1,0:T(8,128)S(1)}, u32[]{:S(2)}, u32[]{:S(2)}) collective-permute-start(f32[8,768]{1,0:T(8,128)S(1)} %fusion.266), channel_id=1, source_target_pairs={{0,8},{4,12},{8,0},{12,4},{16,24},{20,28},{24,16},{28,20},{1,9},{5... | collective-permute-start | bytes 73736 | tf_op jit(solution)/shard_map/ppermute | solution.py:63
  505.6 83.1 %collective-permute-start.29 = (f32[8,768]{1,0:T(8,128)S(1)}, f32[8,768]{1,0:T(8,128)S(1)}, u32[]{:S(2)}, u32[]{:S(2)}) collective-permute-start(f32[8,768]{1,0:T(8,128)S(1)} %add.363), channel_id=1, source_target_pairs={{0,16},{4,20},{8,24},{12,28},{16,0},{20,4},{24,8},{28,12},{1,17},{... | collective-permute-start | bytes 73736 | tf_op jit(solution)/shard_map/ppermute | solution.py:63
  506.4 84.2 %collective-permute-start.24 = (bf16[2,2,96,768]{3,2,1,0:T(8,128)(2,1)S(1)}, bf16[2,2,96,768]{3,2,1,0:T(8,128)(2,1)S(1)}, u32[]{:S(2)}, u32[]{:S(2)}) collective-permute-start(bf16[2,2,96,768]{3,2,1,0:T(8,128)(2,1)S(1)} %pad_maximum_fusion.13), channel_id=1, source_target_pairs={{0,4},{4,0},{8,12},{12,8},{16,20},{20,16},{24,28},{28,24},{1,5},{5... | collective-permute-start | bytes 1769480 | tf_op jit(solution)/shard_map/ppermute | solution.py:63
  (62 other events, 189.8 us)
Sparse Core Ops, SparseCore 0:
  14.2 28.7 all-gather.1
  125.8 43.0 all-reduce.3
  462.5 122.0 all-reduce.5

commit v9 on v8

--- a/solution.py
+++ b/solution.py
@@ -179,12 +179,16 @@
     txt_biases,
 ):
     qkv_parts = gather_stacked(img_qkv, "mp")
-    fc1_parts = gather_stacked(img_fc1, "mp")
+    out_parts = gather_stacked(img_out, "mp")
+    qkv_parts, out_parts, fc1_local, fc2_local = lax.optimization_barrier(
+        (qkv_parts, out_parts, img_fc1, img_fc2)
+    )
+    fc1_parts = gather_stacked(fc1_local, "mp")
     weights = (
         qkv_parts.transpose(1, 2, 0, 3).reshape(3, D, -1),
-        gather_stacked(img_out, "mp").reshape(-1, D),
+        out_parts.reshape(-1, D),
         fc1_parts.transpose(1, 0, 2).reshape(D, -1),
-        gather_stacked(img_fc2, "mp").reshape(-1, D),
+        gather_stacked(fc2_local, "mp").reshape(-1, D),
     )
     low_count = image_low.shape[0] // P_LOW
     high_count = image_high.shape[0] // P_HIGH

time: 615 us -> 580 us (0.943)
  waiting for transfers between devices: 237 us -> 203 us
    ppermute x30, waiting for transfers between devices: 161 us -> 126 us  [exchange(): return lax.ppermute(values, axis, [(i, i ^ 1 << bit) for i in range(count)])]
    unnamed x188 -> x149, local copies, waits for them, and re-layouts: 13.6 us -> 12.6 us
  transfers between devices with their start and end apart: 33 -> 33, of which waited for: 19 -> 18; matrix products, arithmetic and copies ran while one was open for 34% -> 36% of each run, Pallas kernels for 0% -> 0%
where the time goes in v9:
time: 580 us; the launch traced here: 570 us
  waiting for transfers between devices  203 us (35%)
  matrix products  117 us (20%)
  local copies, waits for them, and re-layouts  108 us (19%)
  other arithmetic  89 us (15%)
  starting transfers between devices  34.7 us (6%)
  between operations  18.6 us (3%)
    ppermute x30, waiting for transfers between devices, exchange(): return lax.ppermute(values, axis, [(i, i ^ 1 << bit) for i in range(count)])  126 us
    psum x1, waiting for transfers between devices, local_body(): lax.psum(jnp.concatenate([grad_fc1, grad_fc2], 0).astype(jnp.bfloat16), '...  76.6 us
    dot_general x2, matrix products, image_ffn(): jnp.dot(pool, active, preferred_element_type=jnp.float32) / length  36.8 us
    ppermute x30, starting transfers between devices, exchange(): return lax.ppermute(values, axis, [(i, i ^ 1 << bit) for i in range(count)])  34.1 us
    concatenate x8, other arithmetic, gather_stacked(): data = jnp.concatenate([data, exchange(data, axis, count, bit)], 0)  20.1 us
    squeeze x4, local copies, waits for them, and re-layouts, image_attention(): shares, _ = attention_shares(shaped[0], shaped[1], None)  14.7 us
    unnamed x149, local copies, waits for them, and re-layouts  12.6 us
  transfers between devices with their start and end apart: 33, of which 18 were waited for; matrix products, arithmetic and copies ran while one was open for 36% of the time, Pallas kernels for 0%

profile of v9, /device:TPU:0, one launch (start us, length us, event | category | flops | bytes accessed | tf_op | source)
XLA Modules:
  0.0 570.1 jit_solution(16333308636262617385)
XLA Ops:
  7.3 3.1 collective-permute-start
  24.5 20.0 %collective-permute-done.2 = bf16[1,192,768]{2,1,0:T(8,128)(2,1)} collective-permute-done((bf16[1,192,768]{2,1,0:T(8,128)(2,1)}, bf16[1,192,768]{2,1,0:T(8,128)(2,1)}, u32[]{:S(2)}, u32[]{:S(2)}) %collective-permute-start.2) | collective-permute-done | bytes 294944 | tf_op jit(solution)/shard_map/ppermute | solution.py:63
  45.7 2.5 pad_maximum_fusion.7
  54.6 2.4 fusion.123
  58.2 2.5 copy.94
  60.7 6.4 %reshape.297 = bf16[60,16,3,3,64]{4,3,1,0,2:T(4,128)(2,1)} reshape(bf16[960,3,192]{2,0,1:T(8,128)(2,1)} %copy.94) | data formatting | bytes 2211840 | tf_op jit(solution)/shard_map/reshape | solution.py:220
  67.2 3.2 fusion.221
  74.1 2.4 reshape.298
  78.7 3.4 pad_maximum_fusion.2
  82.1 2.4 copy.108
  86.2 4.0 convert_bitcast_fusion.2
  91.4 3.3 reshape.331
  94.7 3.3 reshape.330
  98.0 3.0 fusion.64
  101.0 3.9 fusion.227
  107.1 4.1 fusion.68
  113.4 4.1 reshape.307
  117.5 3.4 fusion.228
  121.4 2.6 reshape.308
  125.4 4.7 convert_bitcast_fusion
  131.7 4.1 squeeze.70
  135.8 4.1 squeeze.69
  139.8 3.7 fusion.50
  143.5 3.1 fusion.229
  146.6 4.1 squeeze.68
  150.7 4.2 convert_bitcast_fusion.1
  156.7 4.2 reshape.302
  160.9 3.9 fusion.230
  164.8 2.9 reshape.304
  173.6 4.0 fusion.220
  181.9 8.6 %multiply_convert_fusion = (bf16[960,768]{1,0:T(8,128)(2,1)S(1)}, f32[960,768]{1,0:T(8,128)}, f32[960,768]{1,0:T(8,128)}) fusion(f32[768]{0:T(1024)S(1)} %copy-done.66, bf16[768,768]{1,0:T(8,128)(2,1)S(1)} %copy-done, f32[960,768]{1,0:T(8,128)S(1)} %subtract_multiply_fusion, f32[768]{0:T(1024)S(1)} %get-tuple-element.56, f32[768]{0:T(1024)S(1)} %get-tuple-element.54), kind=kOutput, calls=%fused_computation.69 | convolution fusion | flops 1183334400 | bytes 11510784 | tf_op jit(solution)/shard_map/dot_general | solution.py:241
  193.2 3.2 pad_maximum_fusion.4
  197.0 3.8 pad_maximum_fusion
  200.8 15.5 %convolution_multiply_fusion = f32[3,3072]{1,0:T(4,128)S(1)} fusion(bf16[768,3072]{0,1:T(8,128)(2,1)} %bitcast.220, f32[435,768]{1,0:T(8,128)S(1)} %copy-done.14, f32[768]{0:T(1024)S(1)} %copy-done.56, f32[435]{0:T(512)S(1)} %add_rsqrt_fusion.4, f32[435]{0:T(512)S(1)} %broadcast_multiply_fusion.5, s32[435]{0:T(512)S(1)} %copy-done.61, ...), kind=kOutput, calls=%fused_computation.59 | convolution fusion | flops 2148814336 | bytes 6102243 | tf_op jit(solution)/shard_map/dot_general | solution.py:151
  216.4 2.6 pad_maximum_fusion.1
  223.3 21.3 %fusion.30 = f32[12,3072]{1,0:T(8,128)} fusion(bf16[768,3072]{0,1:T(8,128)(2,1)} %bitcast.221, f32[600,768]{1,0:T(8,128)S(1)} %copy-done.12, f32[768]{0:T(1024)} %get-tuple-element.58, f32[600]{0:T(1024)} %add_rsqrt_fusion, f32[600]{0:T(1024)} %copy-done.48, s32[600]{0:T(1024)} %iota_divide_fusion, s32[600]{0:T(1024)} %broadcast_add_fusion, ...), kind=kOutput, calls=%fused_computation.58 | convolution fusion | flops 2997094400 | bytes 6722520 | tf_op jit(solution)/shard_map/dot_general | solution.py:151
  244.6 4.5 multiply_reduce_fusion.16
  253.4 8.9 %collective-permute-done.9 = f32[120,768]{1,0:T(8,128)S(1)} collective-permute-done((f32[120,768]{1,0:T(8,128)S(1)}, f32[120,768]{1,0:T(8,128)S(1)}, u32[]{:S(2)}, u32[]{:S(2)}) %collective-permute-start.9) | collective-permute-done | bytes 368672 | tf_op jit(solution)/shard_map/ppermute | solution.py:63
  262.8 2.9 collective-permute-start.10
  265.7 8.0 %collective-permute-done.10 = bf16[120,768]{1,0:T(8,128)(2,1)S(1)} collective-permute-done((bf16[120,768]{1,0:T(8,128)(2,1)S(1)}, bf16[120,768]{1,0:T(8,128)(2,1)S(1)}, u32[]{:S(2)}, u32[]{:S(2)}) %collective-permute-start.10) | collective-permute-done | bytes 184352 | tf_op jit(solution)/shard_map/ppermute | solution.py:63
  274.7 8.8 %collective-permute-done.11 = bf16[2,120,768]{2,1,0:T(8,128)(2,1)S(1)} collective-permute-done((bf16[2,120,768]{2,1,0:T(8,128)(2,1)S(1)}, bf16[2,120,768]{2,1,0:T(8,128)(2,1)S(1)}, u32[]{:S(2)}, u32[]{:S(2)}) %collective-permute-start.11) | collective-permute-done | bytes 368672 | tf_op jit(solution)/shard_map/ppermute | solution.py:63
  286.4 15.1 %collective-permute-done.12 = bf16[2,2,120,768]{3,2,1,0:T(8,128)(2,1)S(1)} collective-permute-done((bf16[2,2,120,768]{3,2,1,0:T(8,128)(2,1)}, bf16[2,2,120,768]{3,2,1,0:T(8,128)(2,1)S(1)}, u32[]{:S(2)}, u32[]{:S(2)}) %collective-permute-start.12) | collective-permute-done | bytes 737312 | tf_op jit(solution)/shard_map/ppermute | solution.py:63
  305.6 2.7 select_reduce_fusion
  309.8 2.7 convert_reduce_fusion.1
  315.7 2.3 collective-permute-done.13
  321.4 9.2 %collective-permute-done.14 = bf16[240,768]{1,0:T(8,128)(2,1)} collective-permute-done((bf16[240,768]{1,0:T(8,128)(2,1)S(1)}, bf16[240,768]{1,0:T(8,128)(2,1)}, u32[]{:S(2)}, u32[]{:S(2)}) %collective-permute-start.14) | collective-permute-done | bytes 368672 | tf_op jit(solution)/shard_map/ppermute | solution.py:63
  333.2 8.3 %collective-permute-done.15 = bf16[240,768]{1,0:T(8,128)(2,1)S(1)} collective-permute-done((bf16[240,768]{1,0:T(8,128)(2,1)S(1)}, bf16[240,768]{1,0:T(8,128)(2,1)S(1)}, u32[]{:S(2)}, u32[]{:S(2)}) %collective-permute-start.15) | collective-permute-done | bytes 368672 | tf_op jit(solution)/shard_map/ppermute | solution.py:63
  343.2 4.7 convolution_convert_fusion.2
  348.7 2.3 copy-done.2
  351.8 5.4 bitcast_multiply_fusion
  362.7 2.5 convert_reduce_fusion.4
  378.4 2.3 fusion.122
  380.7 6.1 %dot_general.137 = bf16[2,2,240,3,192]{2,1,0,4,3:T(2,128)(2,1)} reshape(bf16[960,3,192]{0,2,1:T(8,128)(2,1)} %fusion.122) | data formatting | bytes 2211840 | tf_op jit(solution)/shard_map/jgw,jdw->gd/dot_general | solution.py:342
  386.9 3.6 convolution_bitcast_fusion.1
  401.6 11.0 %collective-permute-done.19 = bf16[2,2,96,768]{3,2,1,0:T(8,128)(2,1)S(1)} collective-permute-done((bf16[2,2,96,768]{3,2,1,0:T(8,128)(2,1)S(1)}, bf16[2,2,96,768]{3,2,1,0:T(8,128)(2,1)S(1)}, u32[]{:S(2)}, u32[]{:S(2)}) %collective-permute-start.19) | collective-permute-done | bytes 589856 | tf_op jit(solution)/shard_map/ppermute | solution.py:63
  412.8 2.6 collective-permute-start.20
  417.8 4.4 collective-permute-done.20
  422.3 3.7 collective-permute-start.21
  433.9 2.4 dynamic-slice_reduce_fusion.2
  441.5 9.9 %collective-permute-done.22 = bf16[96,768]{1,0:T(8,128)(2,1)S(1)} collective-permute-done((bf16[96,768]{1,0:T(8,128)(2,1)S(1)}, bf16[96,768]{1,0:T(8,128)(2,1)S(1)}, u32[]{:S(2)}, u32[]{:S(2)}) %collective-permute-start.22) | collective-permute-done | bytes 147488 | tf_op jit(solution)/shard_map/ppermute | solution.py:63
  453.1 2.3 collective-permute-done.27
  459.4 11.4 %collective-permute-done.28 = f32[8,768]{1,0:T(8,128)S(1)} collective-permute-done((f32[8,768]{1,0:T(8,128)S(1)}, f32[8,768]{1,0:T(8,128)S(1)}, u32[]{:S(2)}, u32[]{:S(2)}) %collective-permute-start.28) | collective-permute-done | bytes 24608 | tf_op jit(solution)/shard_map/ppermute | solution.py:63
  473.1 76.6 %all-reduce.6.cloned.1.call-done = bf16[1536,768]{1,0:T(8,128)(2,1)} async-done(((bf16[1536,768]{1,0:T(8,128)(2,1)}), bf16[1536,768]{1,0:T(8,128)(2,1)}) %all-reduce.6.cloned.1.call-update) | async-done | bytes 2359312 | tf_op jit(solution)/shard_map/psum | solution.py:298
  549.7 4.2 slice_convert_fusion
  (378 shorter events, 144.6 us)
Async XLA Ops:
  7.2 174.7 %copy-start = (bf16[768,768]{1,0:T(8,128)(2,1)S(1)}, bf16[768,768]{1,0:T(8,128)(2,1)}, u32[]{:S(2)}) copy-start(bf16[768,768]{1,0:T(8,128)(2,1)} %param.32) | copy-start | bytes 3538948
  7.2 38.5 %copy-start.19 = (bf16[3,768,192]{1,2,0:T(8,128)(2,1)S(1)}, bf16[3,768,192]{1,2,0:T(8,128)(2,1)}, u32[]{:S(2)}) copy-start(bf16[3,768,192]{1,2,0:T(8,128)(2,1)} %param.25) | copy-start | bytes 2654212
  7.2 37.3 %copy-start.32 = (bf16[192,768]{1,0:T(8,128)(2,1)S(1)}, bf16[192,768]{1,0:T(8,128)(2,1)}, u32[]{:S(2)}) copy-start(bf16[192,768]{1,0:T(8,128)(2,1)} %param.26) | copy-start | bytes 884740
  7.2 16.3 %copy-start.18 = (bf16[600,768]{1,0:T(8,128)(2,1)S(1)}, bf16[600,768]{1,0:T(8,128)(2,1)}, u32[]{:S(2)}) copy-start(bf16[600,768]{1,0:T(8,128)(2,1)} %param.22) | copy-start | bytes 2764804
  7.2 16.7 %copy-start.60 = (f32[2,192]{1,0:T(2,128)S(1)}, f32[2,192]{1,0:T(2,128)}, u32[]{:S(2)}) copy-start(f32[2,192]{1,0:T(2,128)} %param.30) | copy-start | bytes 4612
  7.2 43.6 %all-gather.2.cloned.1.call-start = ((), (), s32[]{:S(2)}) async-start(), calls=%async_computation | async-start | bytes 1843200 | tf_op jit(solution)/shard_map/all_gather | solution.py:212
  7.3 38.4 %collective-permute-start = (bf16[1,3,768,192]{2,3,0,1:T(8,128)(2,1)}, bf16[1,3,768,192]{2,3,0,1:T(8,128)(2,1)}, u32[]{:S(2)}, u32[]{:S(2)}) collective-permute-start(bf16[1,3,768,192]{2,3,0,1:T(8,128)(2,1)} %bitcast.224), channel_id=1, source_target_pairs={{0,2},{1,3},{2,0},{3,1},{4,6},{5,7},{6,4},{7,5},{8,10},{9,11},{10,... | collective-permute-start | bytes 2654216 | tf_op jit(solution)/shard_map/ppermute | solution.py:63
  10.3 34.2 %collective-permute-start.2 = (bf16[1,192,768]{2,1,0:T(8,128)(2,1)}, bf16[1,192,768]{2,1,0:T(8,128)(2,1)}, u32[]{:S(2)}, u32[]{:S(2)}) collective-permute-start(bf16[1,192,768]{2,1,0:T(8,128)(2,1)} %bitcast.233), channel_id=1, source_target_pairs={{0,2},{1,3},{2,0},{3,1},{4,6},{5,7},{6,4},{7,5},{8,10},{9,11},{10,... | collective-permute-start | bytes 884744 | tf_op jit(solution)/shard_map/ppermute | solution.py:63
  10.4 163.2 %all-reduce.4.cloned.1.call-start = ((), (), s32[]{:S(2)}) async-start(), calls=%async_computation.1 | async-start | bytes 2949120 | tf_op jit(solution)/shard_map/psum | solution.py:233
  14.7 33.5 %copy-start.45 = (pred[60,16]{0,1:T(8,128)(4,1)}, pred[60,16]{0,1:T(8,128)(4,1)S(1)}, u32[]{:S(2)}) copy-start(pred[60,16]{0,1:T(8,128)(4,1)S(1)} %get-tuple-element.66) | copy-start | bytes 2884
  21.0 33.5 %copy-start.52 = (f32[768]{0:T(1024)}, f32[768]{0:T(1024)S(1)}, u32[]{:S(2)}) copy-start(f32[768]{0:T(1024)S(1)} %get-tuple-element.57) | copy-start | bytes 9220
  21.0 160.8 %copy-start.54 = (f32[768]{0:T(1024)}, f32[768]{0:T(1024)S(1)}, u32[]{:S(2)}) copy-start(f32[768]{0:T(1024)S(1)} %get-tuple-element.56) | copy-start | bytes 9220
  21.9 32.7 %copy-start.41 = (f32[768]{0:T(1024)}, f32[768]{0:T(1024)S(1)}, u32[]{:S(2)}) copy-start(f32[768]{0:T(1024)S(1)} %get-tuple-element.55) | copy-start | bytes 9220
  45.6 3.2 collective-permute-start.3
  48.2 30.5 %collective-permute-start.1 = (bf16[2,3,768,192]{2,3,0,1:T(8,128)(2,1)}, bf16[2,3,768,192]{2,3,0,1:T(8,128)(2,1)}, u32[]{:S(2)}, u32[]{:S(2)}) collective-permute-start(bf16[2,3,768,192]{2,3,0,1:T(8,128)(2,1)} %pad_maximum_fusion.7), channel_id=1, source_target_pairs={{0,1},{1,0},{2,3},{3,2},{4,5},{5,4},{6,7},{7,6},{8,9},{9,8},{10,11... | collective-permute-start | bytes 5308424 | tf_op jit(solution)/shard_map/ppermute | solution.py:63
  52.6 121.1 %copy-start.43 = (f32[960]{0:T(1024)}, f32[960]{0:T(1024)S(1)}, u32[]{:S(2)}) copy-start(f32[960]{0:T(1024)S(1)} %broadcast_multiply_fusion.4) | copy-start | bytes 11524
  76.5 5.6 copy-start.16
  78.2 471.5 %all-reduce.6.cloned.1.call-start = ((), (), s32[]{:S(2)}) async-start(), calls=%async_computation.2 | async-start | bytes 4718592 | tf_op jit(solution)/shard_map/psum | solution.py:298
  84.4 94.0 %collective-permute-start.4 = (bf16[1,768,768]{1,2,0:T(8,128)(2,1)}, bf16[1,768,768]{1,2,0:T(8,128)(2,1)}, u32[]{:S(2)}, u32[]{:S(2)}) collective-permute-start(bf16[1,768,768]{1,2,0:T(8,128)(2,1)} %bitcast.214), channel_id=1, source_target_pairs={{0,2},{1,3},{2,0},{3,1},{4,6},{5,7},{6,4},{7,5},{8,10},{9,11},{10,... | collective-permute-start | bytes 3538952 | tf_op jit(solution)/shard_map/ppermute | solution.py:63
  111.3 6.3 %copy-start.24 = (bf16[435,768]{1,0:T(8,128)(2,1)S(1)}, bf16[435,768]{1,0:T(8,128)(2,1)}, u32[]{:S(2)}) copy-start(bf16[435,768]{1,0:T(8,128)(2,1)} %param.23) | copy-start | bytes 2004484
  121.0 72.2 %collective-permute-start.6 = (bf16[1,768,768]{2,1,0:T(8,128)(2,1)}, bf16[1,768,768]{2,1,0:T(8,128)(2,1)}, u32[]{:S(2)}, u32[]{:S(2)}) collective-permute-start(bf16[1,768,768]{2,1,0:T(8,128)(2,1)} %bitcast.20), channel_id=1, source_target_pairs={{0,2},{1,3},{2,0},{3,1},{4,6},{5,7},{6,4},{7,5},{8,10},{9,11},{10,... | collective-permute-start | bytes 3538952 | tf_op jit(solution)/shard_map/ppermute | solution.py:63
  164.8 6.3 %copy-start.48 = (f32[600]{0:T(1024)}, f32[600]{0:T(1024)S(1)}, u32[]{:S(2)}) copy-start(f32[600]{0:T(1024)S(1)} %broadcast_multiply_fusion) | copy-start | bytes 7204
  177.6 14.3 %copy-start.1 = (f32[960,768]{1,0:T(8,128)}, f32[960,768]{1,0:T(8,128)S(1)}, u32[]{:S(2)}) copy-start(f32[960,768]{1,0:T(8,128)S(1)} %get-tuple-element.70) | copy-start | bytes 8847364
  178.5 12.1 %copy-start.15 = (f32[960,768]{1,0:T(8,128)}, f32[960,768]{1,0:T(8,128)S(1)}, u32[]{:S(2)}) copy-start(f32[960,768]{1,0:T(8,128)S(1)} %subtract_multiply_fusion) | copy-start | bytes 8847364
  181.8 15.2 %collective-permute-start.5 = (bf16[2,768,768]{1,2,0:T(8,128)(2,1)S(1)}, bf16[2,768,768]{1,2,0:T(8,128)(2,1)S(1)}, u32[]{:S(2)}, u32[]{:S(2)}) collective-permute-start(bf16[2,768,768]{1,2,0:T(8,128)(2,1)S(1)} %pad_maximum_fusion.3), channel_id=1, source_target_pairs={{0,1},{1,0},{2,3},{3,2},{4,5},{5,4},{6,7},{7,6},{8,9},{9,8},{10,11... | collective-permute-start | bytes 7077896 | tf_op jit(solution)/shard_map/ppermute | solution.py:63
  181.9 8.7 %copy-start.63 = (bf16[768,768]{1,0:T(8,128)(2,1)S(1)}, bf16[768,768]{1,0:T(8,128)(2,1)}, u32[]{:S(2)}) copy-start(bf16[768,768]{1,0:T(8,128)(2,1)} %param.34) | copy-start | bytes 3538948
  196.4 19.9 %collective-permute-start.7 = (bf16[2,768,768]{2,1,0:T(8,128)(2,1)}, bf16[2,768,768]{2,1,0:T(8,128)(2,1)}, u32[]{:S(2)}, u32[]{:S(2)}) collective-permute-start(bf16[2,768,768]{2,1,0:T(8,128)(2,1)} %pad_maximum_fusion.4), channel_id=1, source_target_pairs={{0,1},{1,0},{2,3},{3,2},{4,5},{5,4},{6,7},{7,6},{8,9},{9,8},{10,11... | collective-permute-start | bytes 7077896 | tf_op jit(solution)/shard_map/ppermute | solution.py:63
  249.1 13.3 %copy-start.47 = (f32[768]{0:T(1024)S(1)}, f32[768]{0:T(1024)}, u32[]{:S(2)}) copy-start(f32[768]{0:T(1024)} %get-tuple-element.52) | copy-start | bytes 9220
  249.1 13.3 %copy-start.50 = (f32[60]{0:T(128)S(1)}, f32[60]{0:T(128)}, u32[]{:S(2)}) copy-start(f32[60]{0:T(128)} %get-tuple-element.65) | copy-start | bytes 724
  249.8 1.8 collective-permute-start.8
  251.6 10.7 %collective-permute-start.9 = (f32[120,768]{1,0:T(8,128)S(1)}, f32[120,768]{1,0:T(8,128)S(1)}, u32[]{:S(2)}, u32[]{:S(2)}) collective-permute-start(f32[120,768]{1,0:T(8,128)S(1)} %fusion.267), channel_id=1, source_target_pairs={{0,2},{1,3},{2,0},{3,1},{4,6},{5,7},{6,4},{7,5},{8,10},{9,11},{10,... | collective-permute-start | bytes 1105928 | tf_op jit(solution)/shard_map/ppermute | solution.py:63
  262.4 23.7 %copy-start.46 = (pred[60,16]{0,1:T(8,128)(4,1)S(1)}, pred[60,16]{0,1:T(8,128)(4,1)}, u32[]{:S(2)}) copy-start(pred[60,16]{0,1:T(8,128)(4,1)} %copy-done.45) | copy-start | bytes 2884
  262.4 23.8 %copy-start.58 = (s32[480]{0:T(512)S(1)}, s32[480]{0:T(512)}, u32[]{:S(2)}) copy-start(s32[480]{0:T(512)} %param.21) | copy-start | bytes 5764
  262.8 11.0 %collective-permute-start.10 = (bf16[120,768]{1,0:T(8,128)(2,1)S(1)}, bf16[120,768]{1,0:T(8,128)(2,1)S(1)}, u32[]{:S(2)}, u32[]{:S(2)}) collective-permute-start(bf16[120,768]{1,0:T(8,128)(2,1)S(1)} %pad_maximum_fusion.18), channel_id=1, source_target_pairs={{0,16},{4,20},{8,24},{12,28},{16,0},{20,4},{24,8},{28,12},{1,17},{... | collective-permute-start | bytes 552968 | tf_op jit(solution)/shard_map/ppermute | solution.py:63
  273.9 9.6 %collective-permute-start.11 = (bf16[2,120,768]{2,1,0:T(8,128)(2,1)S(1)}, bf16[2,120,768]{2,1,0:T(8,128)(2,1)S(1)}, u32[]{:S(2)}, u32[]{:S(2)}) collective-permute-start(bf16[2,120,768]{2,1,0:T(8,128)(2,1)S(1)} %pad_maximum_fusion.16), channel_id=1, source_target_pairs={{0,8},{4,12},{8,0},{12,4},{16,24},{20,28},{24,16},{28,20},{1,9},{5... | collective-permute-start | bytes 1105928 | tf_op jit(solution)/shard_map/ppermute | solution.py:63
  284.4 17.0 %collective-permute-start.12 = (bf16[2,2,120,768]{3,2,1,0:T(8,128)(2,1)}, bf16[2,2,120,768]{3,2,1,0:T(8,128)(2,1)S(1)}, u32[]{:S(2)}, u32[]{:S(2)}) collective-permute-start(bf16[2,2,120,768]{3,2,1,0:T(8,128)(2,1)} %pad_maximum_fusion.10), channel_id=1, source_target_pairs={{0,4},{4,0},{8,12},{12,8},{16,20},{20,16},{24,28},{28,24},{1,5},{5... | collective-permute-start | bytes 2211848 | tf_op jit(solution)/shard_map/ppermute | solution.py:63
  315.6 2.4 collective-permute-start.13
  319.7 23.4 %copy-start.38 = (f32[60,3,16]{2,1,0:T(4,128)S(1)}, f32[60,3,16]{2,1,0:T(4,128)}, u32[]{:S(2)}) copy-start(f32[60,3,16]{2,1,0:T(4,128)} %copy-done.37) | copy-start | bytes 34564
  319.7 23.4 %copy-start.40 = (f32[60,3,16]{2,1,0:T(4,128)S(1)}, f32[60,3,16]{2,1,0:T(4,128)}, u32[]{:S(2)}) copy-start(f32[60,3,16]{2,1,0:T(4,128)} %copy-done.39) | copy-start | bytes 34564
  319.8 23.4 %copy-start.55 = (f32[768]{0:T(1024)S(1)}, f32[768]{0:T(1024)}, u32[]{:S(2)}) copy-start(f32[768]{0:T(1024)} %copy-done.54) | copy-start | bytes 9220
  319.8 10.8 %collective-permute-start.14 = (bf16[240,768]{1,0:T(8,128)(2,1)S(1)}, bf16[240,768]{1,0:T(8,128)(2,1)}, u32[]{:S(2)}, u32[]{:S(2)}) collective-permute-start(bf16[240,768]{1,0:T(8,128)(2,1)S(1)} %fusion.125), channel_id=1, source_target_pairs={{0,2},{1,3},{2,0},{3,1},{4,6},{5,7},{6,4},{7,5},{8,10},{9,11},{10,... | collective-permute-start | bytes 1105928 | tf_op jit(solution)/shard_map/ppermute | solution.py:63
  331.7 9.8 %collective-permute-start.15 = (bf16[240,768]{1,0:T(8,128)(2,1)S(1)}, bf16[240,768]{1,0:T(8,128)(2,1)S(1)}, u32[]{:S(2)}, u32[]{:S(2)}) collective-permute-start(bf16[240,768]{1,0:T(8,128)(2,1)S(1)} %fusion.99), channel_id=1, source_target_pairs={{0,2},{1,3},{2,0},{3,1},{4,6},{5,7},{6,4},{7,5},{8,10},{9,11},{10,... | collective-permute-start | bytes 1105928 | tf_op jit(solution)/shard_map/ppermute | solution.py:63
  342.5 5.4 collective-permute-start.16
  351.8 7.0 %copy-start.31 = (bf16[192,768]{1,0:T(8,128)(2,1)S(1)}, bf16[192,768]{1,0:T(8,128)(2,1)}, u32[]{:S(2)}) copy-start(bf16[192,768]{1,0:T(8,128)(2,1)} %param.31) | copy-start | bytes 884740
  377.4 9.4 %copy-start.10 = (bf16[960,768]{1,0:T(8,128)(2,1)S(1)}, bf16[960,768]{1,0:T(8,128)(2,1)}, u32[]{:S(2)}) copy-start(bf16[960,768]{1,0:T(8,128)(2,1)} %all-gather.2.cloned.1.call-done) | copy-start | bytes 4423684
  377.4 9.4 %copy-start.42 = (f32[768]{0:T(1024)S(1)}, f32[768]{0:T(1024)}, u32[]{:S(2)}) copy-start(f32[768]{0:T(1024)} %copy-done.41) | copy-start | bytes 9220
  377.5 9.4 %copy-start.44 = (f32[960]{0:T(1024)S(1)}, f32[960]{0:T(1024)}, u32[]{:S(2)}) copy-start(f32[960]{0:T(1024)} %copy-done.43) | copy-start | bytes 11524
  377.5 9.4 %copy-start.53 = (f32[768]{0:T(1024)S(1)}, f32[768]{0:T(1024)}, u32[]{:S(2)}) copy-start(f32[768]{0:T(1024)} %copy-done.52) | copy-start | bytes 9220
  378.4 8.4 %copy-start.27 = (bf16[1,960,192]{1,2,0:T(8,128)(2,1)S(1)}, bf16[1,960,192]{1,2,0:T(8,128)(2,1)}, u32[]{:S(2)}) copy-start(bf16[1,960,192]{1,2,0:T(8,128)(2,1)} %copy.130) | copy-start | bytes 1105924
  396.8 15.8 %collective-permute-start.19 = (bf16[2,2,96,768]{3,2,1,0:T(8,128)(2,1)S(1)}, bf16[2,2,96,768]{3,2,1,0:T(8,128)(2,1)S(1)}, u32[]{:S(2)}, u32[]{:S(2)}) collective-permute-start(bf16[2,2,96,768]{3,2,1,0:T(8,128)(2,1)S(1)} %fusion.118), channel_id=1, source_target_pairs={{0,4},{4,0},{8,12},{12,8},{16,20},{20,16},{24,28},{28,24},{1,5},{5... | collective-permute-start | bytes 1769480 | tf_op jit(solution)/shard_map/ppermute | solution.py:63
  399.9 15.5 %collective-permute-start.17 = (bf16[2,240,768]{2,1,0:T(8,128)(2,1)S(1)}, bf16[2,240,768]{2,1,0:T(8,128)(2,1)S(1)}, u32[]{:S(2)}, u32[]{:S(2)}) collective-permute-start(bf16[2,240,768]{2,1,0:T(8,128)(2,1)S(1)} %fusion.98), channel_id=1, source_target_pairs={{0,1},{1,0},{2,3},{3,2},{4,5},{5,4},{6,7},{7,6},{8,9},{9,8},{10,11... | collective-permute-start | bytes 2211848 | tf_op jit(solution)/shard_map/ppermute | solution.py:63
  412.8 13.2 %copy-start.34 = (bf16[768,768]{1,0:T(8,128)(2,1)S(1)}, bf16[768,768]{1,0:T(8,128)(2,1)}, u32[]{:S(2)}) copy-start(bf16[768,768]{1,0:T(8,128)(2,1)} %convolution_convert_fusion.2) | copy-start | bytes 3538948
  412.8 9.4 %collective-permute-start.20 = (bf16[2,96,768]{2,1,0:T(8,128)(2,1)S(1)}, bf16[2,96,768]{2,1,0:T(8,128)(2,1)S(1)}, u32[]{:S(2)}, u32[]{:S(2)}) collective-permute-start(bf16[2,96,768]{2,1,0:T(8,128)(2,1)S(1)} %fusion.127), channel_id=1, source_target_pairs={{0,8},{4,12},{8,0},{12,4},{16,24},{20,28},{24,16},{28,20},{1,9},{5... | collective-permute-start | bytes 884744 | tf_op jit(solution)/shard_map/ppermute | solution.py:63
  416.3 15.9 %collective-permute-start.18 = (bf16[240,768]{1,0:T(8,128)(2,1)}, bf16[240,768]{1,0:T(8,128)(2,1)}, u32[]{:S(2)}, u32[]{:S(2)}) collective-permute-start(bf16[240,768]{1,0:T(8,128)(2,1)} %fusion.126), channel_id=1, source_target_pairs={{0,2},{1,3},{2,0},{3,1},{4,6},{5,7},{6,4},{7,5},{8,10},{9,11},{10,... | collective-permute-start | bytes 1105928 | tf_op jit(solution)/shard_map/ppermute | solution.py:63
  422.3 9.8 %collective-permute-start.21 = (bf16[96,768]{1,0:T(8,128)(2,1)S(1)}, bf16[96,768]{1,0:T(8,128)(2,1)S(1)}, u32[]{:S(2)}, u32[]{:S(2)}) collective-permute-start(bf16[96,768]{1,0:T(8,128)(2,1)S(1)} %fusion.131), channel_id=1, source_target_pairs={{0,16},{4,20},{8,24},{12,28},{16,0},{20,4},{24,8},{28,12},{1,17},{... | collective-permute-start | bytes 442376 | tf_op jit(solution)/shard_map/ppermute | solution.py:63
  427.6 6.3 %copy-start.51 = (f32[240]{0:T(256)S(1)}, f32[240]{0:T(256)}, u32[]{:S(2)}) copy-start(f32[240]{0:T(256)} %dynamic-slice.3) | copy-start | bytes 2884
  432.2 19.2 %collective-permute-start.22 = (bf16[96,768]{1,0:T(8,128)(2,1)S(1)}, bf16[96,768]{1,0:T(8,128)(2,1)S(1)}, u32[]{:S(2)}, u32[]{:S(2)}) collective-permute-start(bf16[96,768]{1,0:T(8,128)(2,1)S(1)} %fusion.128), channel_id=1, source_target_pairs={{0,16},{4,20},{8,24},{12,28},{16,0},{20,4},{24,8},{28,12},{1,17},{... | collective-permute-start | bytes 442376 | tf_op jit(solution)/shard_map/ppermute | solution.py:63
  436.4 1.3 collective-permute-start.25
  437.7 3.8 collective-permute-start.26
  451.5 20.1 %collective-permute-start.23 = (bf16[2,96,768]{2,1,0:T(8,128)(2,1)S(1)}, bf16[2,96,768]{2,1,0:T(8,128)(2,1)S(1)}, u32[]{:S(2)}, u32[]{:S(2)}) collective-permute-start(bf16[2,96,768]{2,1,0:T(8,128)(2,1)S(1)} %pad_maximum_fusion.17), channel_id=1, source_target_pairs={{0,8},{4,12},{8,0},{12,4},{16,24},{20,28},{24,16},{28,20},{1,9},{5... | collective-permute-start | bytes 884744 | tf_op jit(solution)/shard_map/ppermute | solution.py:63
  451.6 3.9 collective-permute-start.27
  455.5 15.3 %collective-permute-start.28 = (f32[8,768]{1,0:T(8,128)S(1)}, f32[8,768]{1,0:T(8,128)S(1)}, u32[]{:S(2)}, u32[]{:S(2)}) collective-permute-start(f32[8,768]{1,0:T(8,128)S(1)} %fusion.266), channel_id=1, source_target_pairs={{0,8},{4,12},{8,0},{12,4},{16,24},{20,28},{24,16},{28,20},{1,9},{5... | collective-permute-start | bytes 73736 | tf_op jit(solution)/shard_map/ppermute | solution.py:63
  470.8 83.1 %collective-permute-start.29 = (f32[8,768]{1,0:T(8,128)S(1)}, f32[8,768]{1,0:T(8,128)S(1)}, u32[]{:S(2)}, u32[]{:S(2)}) collective-permute-start(f32[8,768]{1,0:T(8,128)S(1)} %add.363), channel_id=1, source_target_pairs={{0,16},{4,20},{8,24},{12,28},{16,0},{20,4},{24,8},{28,12},{1,17},{... | collective-permute-start | bytes 73736 | tf_op jit(solution)/shard_map/ppermute | solution.py:63
  471.7 84.1 %collective-permute-start.24 = (bf16[2,2,96,768]{3,2,1,0:T(8,128)(2,1)S(1)}, bf16[2,2,96,768]{3,2,1,0:T(8,128)(2,1)S(1)}, u32[]{:S(2)}, u32[]{:S(2)}) collective-permute-start(bf16[2,2,96,768]{3,2,1,0:T(8,128)(2,1)S(1)} %pad_maximum_fusion.13), channel_id=1, source_target_pairs={{0,4},{4,0},{8,12},{12,8},{16,20},{20,16},{24,28},{28,24},{1,5},{5... | collective-permute-start | bytes 1769480 | tf_op jit(solution)/shard_map/ppermute | solution.py:63
  (43 other events, 131.3 us)
Sparse Core Ops, SparseCore 0:
  10.6 28.8 all-gather.1
  78.3 66.1 all-reduce.3
  427.7 121.9 all-reduce.5

commit v10 on v9

--- a/solution.py
+++ b/solution.py
@@ -229,13 +229,9 @@
         preferred_element_type=jnp.float32,
     )
     context = context.astype(jnp.bfloat16).reshape(group_rows, width)
-    middle = inputs + (
-        lax.psum(
-            jnp.dot(context, txt_out, preferred_element_type=jnp.float32).astype(jnp.bfloat16),
-            "mp",
-        ).astype(jnp.float32)
-        + txt_biases[0]
-    )
+    attn_part = jnp.dot(context, txt_out, preferred_element_type=jnp.float32).astype(jnp.bfloat16)
+    attn_full = lax.psum(attn_part, "mp")
+    middle = inputs + (attn_full.astype(jnp.float32) + txt_biases[0])
     unit2, inverse2 = layer_stats(middle)
     normed2_all = (unit2 * txt_gains[1] + txt_shifts[1]).astype(jnp.bfloat16)
     hidden = jnp.dot(normed2_all, txt_fc1, preferred_element_type=jnp.float32) + txt_fc1_bias

time: 580 us -> 580 us (level)
  no operation moved by 1% of the time
where the time goes in v10:
time: 580 us; the launch traced here: 570 us
  waiting for transfers between devices  203 us (35%)
  matrix products  117 us (20%)
  local copies, waits for them, and re-layouts  108 us (19%)
  other arithmetic  89 us (15%)
  starting transfers between devices  34.7 us (6%)
  between operations  18.6 us (3%)
    ppermute x30, waiting for transfers between devices, exchange(): return lax.ppermute(values, axis, [(i, i ^ 1 << bit) for i in range(count)])  126 us
    psum x1, waiting for transfers between devices, local_body(): lax.psum(jnp.concatenate([grad_fc1, grad_fc2], 0).astype(jnp.bfloat16), '...  76.6 us
    dot_general x2, matrix products, image_ffn(): jnp.dot(pool, active, preferred_element_type=jnp.float32) / length  36.8 us
    ppermute x30, starting transfers between devices, exchange(): return lax.ppermute(values, axis, [(i, i ^ 1 << bit) for i in range(count)])  34.1 us
    concatenate x8, other arithmetic, gather_stacked(): data = jnp.concatenate([data, exchange(data, axis, count, bit)], 0)  20.1 us
    squeeze x4, local copies, waits for them, and re-layouts, image_attention(): shares, _ = attention_shares(shaped[0], shaped[1], None)  14.7 us
    unnamed x149, local copies, waits for them, and re-layouts  12.6 us
  transfers between devices with their start and end apart: 33, of which 18 were waited for; matrix products, arithmetic and copies ran while one was open for 36% of the time, Pallas kernels for 0%

profile of v10, /device:TPU:0, one launch (start us, length us, event | category | flops | bytes accessed | tf_op | source)
XLA Modules:
  0.0 570.1 jit_solution(16333308636262617385)
XLA Ops:
  7.3 3.1 collective-permute-start
  24.5 20.0 %collective-permute-done.2 = bf16[1,192,768]{2,1,0:T(8,128)(2,1)} collective-permute-done((bf16[1,192,768]{2,1,0:T(8,128)(2,1)}, bf16[1,192,768]{2,1,0:T(8,128)(2,1)}, u32[]{:S(2)}, u32[]{:S(2)}) %collective-permute-start.2) | collective-permute-done | bytes 294944 | tf_op jit(solution)/shard_map/ppermute | solution.py:63
  45.7 2.5 pad_maximum_fusion.7
  54.6 2.4 fusion.123
  58.2 2.5 copy.94
  60.7 6.4 %reshape.297 = bf16[60,16,3,3,64]{4,3,1,0,2:T(4,128)(2,1)} reshape(bf16[960,3,192]{2,0,1:T(8,128)(2,1)} %copy.94) | data formatting | bytes 2211840 | tf_op jit(solution)/shard_map/reshape | solution.py:220
  67.2 3.2 fusion.221
  74.1 2.4 reshape.298
  78.7 3.4 pad_maximum_fusion.2
  82.1 2.4 copy.108
  86.2 4.0 convert_bitcast_fusion.2
  91.4 3.3 reshape.331
  94.7 3.3 reshape.330
  98.0 3.0 fusion.64
  101.0 3.9 fusion.227
  107.1 4.1 fusion.68
  113.4 4.1 reshape.307
  117.5 3.4 fusion.228
  121.4 2.6 reshape.308
  125.4 4.7 convert_bitcast_fusion
  131.7 4.1 squeeze.70
  135.8 4.1 squeeze.69
  139.8 3.7 fusion.50
  143.5 3.1 fusion.229
  146.6 4.1 squeeze.68
  150.7 4.2 convert_bitcast_fusion.1
  156.7 4.2 reshape.302
  160.9 3.9 fusion.230
  164.8 2.9 reshape.304
  173.6 4.0 fusion.220
  181.9 8.6 %multiply_convert_fusion = (bf16[960,768]{1,0:T(8,128)(2,1)S(1)}, f32[960,768]{1,0:T(8,128)}, f32[960,768]{1,0:T(8,128)}) fusion(f32[768]{0:T(1024)S(1)} %copy-done.66, bf16[768,768]{1,0:T(8,128)(2,1)S(1)} %copy-done, f32[960,768]{1,0:T(8,128)S(1)} %subtract_multiply_fusion, f32[768]{0:T(1024)S(1)} %get-tuple-element.56, f32[768]{0:T(1024)S(1)} %get-tuple-element.54), kind=kOutput, calls=%fused_computation.69 | convolution fusion | flops 1183334400 | bytes 11510784 | tf_op jit(solution)/shard_map/dot_general | solution.py:237
  193.2 3.2 pad_maximum_fusion.4
  197.0 3.8 pad_maximum_fusion
  200.8 15.5 %convolution_multiply_fusion = f32[3,3072]{1,0:T(4,128)S(1)} fusion(bf16[768,3072]{0,1:T(8,128)(2,1)} %bitcast.220, f32[435,768]{1,0:T(8,128)S(1)} %copy-done.14, f32[768]{0:T(1024)S(1)} %copy-done.56, f32[435]{0:T(512)S(1)} %add_rsqrt_fusion.4, f32[435]{0:T(512)S(1)} %broadcast_multiply_fusion.5, s32[435]{0:T(512)S(1)} %copy-done.61, ...), kind=kOutput, calls=%fused_computation.59 | convolution fusion | flops 2148814336 | bytes 6102243 | tf_op jit(solution)/shard_map/dot_general | solution.py:151
  216.4 2.6 pad_maximum_fusion.1
  223.3 21.3 %fusion.30 = f32[12,3072]{1,0:T(8,128)} fusion(bf16[768,3072]{0,1:T(8,128)(2,1)} %bitcast.221, f32[600,768]{1,0:T(8,128)S(1)} %copy-done.12, f32[768]{0:T(1024)} %get-tuple-element.58, f32[600]{0:T(1024)} %add_rsqrt_fusion, f32[600]{0:T(1024)} %copy-done.48, s32[600]{0:T(1024)} %iota_divide_fusion, s32[600]{0:T(1024)} %broadcast_add_fusion, ...), kind=kOutput, calls=%fused_computation.58 | convolution fusion | flops 2997094400 | bytes 6722520 | tf_op jit(solution)/shard_map/dot_general | solution.py:151
  244.6 4.5 multiply_reduce_fusion.16
  253.4 8.9 %collective-permute-done.9 = f32[120,768]{1,0:T(8,128)S(1)} collective-permute-done((f32[120,768]{1,0:T(8,128)S(1)}, f32[120,768]{1,0:T(8,128)S(1)}, u32[]{:S(2)}, u32[]{:S(2)}) %collective-permute-start.9) | collective-permute-done | bytes 368672 | tf_op jit(solution)/shard_map/ppermute | solution.py:63
  262.8 2.9 collective-permute-start.10
  265.7 8.0 %collective-permute-done.10 = bf16[120,768]{1,0:T(8,128)(2,1)S(1)} collective-permute-done((bf16[120,768]{1,0:T(8,128)(2,1)S(1)}, bf16[120,768]{1,0:T(8,128)(2,1)S(1)}, u32[]{:S(2)}, u32[]{:S(2)}) %collective-permute-start.10) | collective-permute-done | bytes 184352 | tf_op jit(solution)/shard_map/ppermute | solution.py:63
  274.7 8.8 %collective-permute-done.11 = bf16[2,120,768]{2,1,0:T(8,128)(2,1)S(1)} collective-permute-done((bf16[2,120,768]{2,1,0:T(8,128)(2,1)S(1)}, bf16[2,120,768]{2,1,0:T(8,128)(2,1)S(1)}, u32[]{:S(2)}, u32[]{:S(2)}) %collective-permute-start.11) | collective-permute-done | bytes 368672 | tf_op jit(solution)/shard_map/ppermute | solution.py:63
  286.4 15.1 %collective-permute-done.12 = bf16[2,2,120,768]{3,2,1,0:T(8,128)(2,1)S(1)} collective-permute-done((bf16[2,2,120,768]{3,2,1,0:T(8,128)(2,1)}, bf16[2,2,120,768]{3,2,1,0:T(8,128)(2,1)S(1)}, u32[]{:S(2)}, u32[]{:S(2)}) %collective-permute-start.12) | collective-permute-done | bytes 737312 | tf_op jit(solution)/shard_map/ppermute | solution.py:63
  305.6 2.7 select_reduce_fusion
  309.8 2.7 convert_reduce_fusion.1
  315.7 2.3 collective-permute-done.13
  321.4 9.2 %collective-permute-done.14 = bf16[240,768]{1,0:T(8,128)(2,1)} collective-permute-done((bf16[240,768]{1,0:T(8,128)(2,1)S(1)}, bf16[240,768]{1,0:T(8,128)(2,1)}, u32[]{:S(2)}, u32[]{:S(2)}) %collective-permute-start.14) | collective-permute-done | bytes 368672 | tf_op jit(solution)/shard_map/ppermute | solution.py:63
  333.2 8.3 %collective-permute-done.15 = bf16[240,768]{1,0:T(8,128)(2,1)S(1)} collective-permute-done((bf16[240,768]{1,0:T(8,128)(2,1)S(1)}, bf16[240,768]{1,0:T(8,128)(2,1)S(1)}, u32[]{:S(2)}, u32[]{:S(2)}) %collective-permute-start.15) | collective-permute-done | bytes 368672 | tf_op jit(solution)/shard_map/ppermute | solution.py:63
  343.2 4.7 convolution_convert_fusion.2
  348.7 2.3 copy-done.2
  351.8 5.4 bitcast_multiply_fusion
  362.7 2.5 convert_reduce_fusion.4
  378.4 2.3 fusion.122
  380.7 6.1 %dot_general.137 = bf16[2,2,240,3,192]{2,1,0,4,3:T(2,128)(2,1)} reshape(bf16[960,3,192]{0,2,1:T(8,128)(2,1)} %fusion.122) | data formatting | bytes 2211840 | tf_op jit(solution)/shard_map/jgw,jdw->gd/dot_general | solution.py:338
  386.9 3.6 convolution_bitcast_fusion.1
  401.6 11.0 %collective-permute-done.19 = bf16[2,2,96,768]{3,2,1,0:T(8,128)(2,1)S(1)} collective-permute-done((bf16[2,2,96,768]{3,2,1,0:T(8,128)(2,1)S(1)}, bf16[2,2,96,768]{3,2,1,0:T(8,128)(2,1)S(1)}, u32[]{:S(2)}, u32[]{:S(2)}) %collective-permute-start.19) | collective-permute-done | bytes 589856 | tf_op jit(solution)/shard_map/ppermute | solution.py:63
  412.8 2.6 collective-permute-start.20
  417.8 4.4 collective-permute-done.20
  422.3 3.7 collective-permute-start.21
  433.9 2.4 dynamic-slice_reduce_fusion.2
  441.5 9.9 %collective-permute-done.22 = bf16[96,768]{1,0:T(8,128)(2,1)S(1)} collective-permute-done((bf16[96,768]{1,0:T(8,128)(2,1)S(1)}, bf16[96,768]{1,0:T(8,128)(2,1)S(1)}, u32[]{:S(2)}, u32[]{:S(2)}) %collective-permute-start.22) | collective-permute-done | bytes 147488 | tf_op jit(solution)/shard_map/ppermute | solution.py:63
  453.1 2.3 collective-permute-done.27
  459.4 11.4 %collective-permute-done.28 = f32[8,768]{1,0:T(8,128)S(1)} collective-permute-done((f32[8,768]{1,0:T(8,128)S(1)}, f32[8,768]{1,0:T(8,128)S(1)}, u32[]{:S(2)}, u32[]{:S(2)}) %collective-permute-start.28) | collective-permute-done | bytes 24608 | tf_op jit(solution)/shard_map/ppermute | solution.py:63
  473.1 76.6 %all-reduce.6.cloned.1.call-done = bf16[1536,768]{1,0:T(8,128)(2,1)} async-done(((bf16[1536,768]{1,0:T(8,128)(2,1)}), bf16[1536,768]{1,0:T(8,128)(2,1)}) %all-reduce.6.cloned.1.call-update) | async-done | bytes 2359312 | tf_op jit(solution)/shard_map/psum | solution.py:294
  549.7 4.2 slice_convert_fusion
  (378 shorter events, 144.6 us)
Async XLA Ops:
  7.2 174.7 %copy-start = (bf16[768,768]{1,0:T(8,128)(2,1)S(1)}, bf16[768,768]{1,0:T(8,128)(2,1)}, u32[]{:S(2)}) copy-start(bf16[768,768]{1,0:T(8,128)(2,1)} %param.32) | copy-start | bytes 3538948
  7.2 38.5 %copy-start.19 = (bf16[3,768,192]{1,2,0:T(8,128)(2,1)S(1)}, bf16[3,768,192]{1,2,0:T(8,128)(2,1)}, u32[]{:S(2)}) copy-start(bf16[3,768,192]{1,2,0:T(8,128)(2,1)} %param.25) | copy-start | bytes 2654212
  7.2 37.3 %copy-start.32 = (bf16[192,768]{1,0:T(8,128)(2,1)S(1)}, bf16[192,768]{1,0:T(8,128)(2,1)}, u32[]{:S(2)}) copy-start(bf16[192,768]{1,0:T(8,128)(2,1)} %param.26) | copy-start | bytes 884740
  7.2 16.3 %copy-start.18 = (bf16[600,768]{1,0:T(8,128)(2,1)S(1)}, bf16[600,768]{1,0:T(8,128)(2,1)}, u32[]{:S(2)}) copy-start(bf16[600,768]{1,0:T(8,128)(2,1)} %param.22) | copy-start | bytes 2764804
  7.2 16.7 %copy-start.60 = (f32[2,192]{1,0:T(2,128)S(1)}, f32[2,192]{1,0:T(2,128)}, u32[]{:S(2)}) copy-start(f32[2,192]{1,0:T(2,128)} %param.30) | copy-start | bytes 4612
  7.2 43.6 %all-gather.2.cloned.1.call-start = ((), (), s32[]{:S(2)}) async-start(), calls=%async_computation | async-start | bytes 1843200 | tf_op jit(solution)/shard_map/all_gather | solution.py:212
  7.3 38.4 %collective-permute-start = (bf16[1,3,768,192]{2,3,0,1:T(8,128)(2,1)}, bf16[1,3,768,192]{2,3,0,1:T(8,128)(2,1)}, u32[]{:S(2)}, u32[]{:S(2)}) collective-permute-start(bf16[1,3,768,192]{2,3,0,1:T(8,128)(2,1)} %bitcast.224), channel_id=1, source_target_pairs={{0,2},{1,3},{2,0},{3,1},{4,6},{5,7},{6,4},{7,5},{8,10},{9,11},{10,... | collective-permute-start | bytes 2654216 | tf_op jit(solution)/shard_map/ppermute | solution.py:63
  10.3 34.2 %collective-permute-start.2 = (bf16[1,192,768]{2,1,0:T(8,128)(2,1)}, bf16[1,192,768]{2,1,0:T(8,128)(2,1)}, u32[]{:S(2)}, u32[]{:S(2)}) collective-permute-start(bf16[1,192,768]{2,1,0:T(8,128)(2,1)} %bitcast.233), channel_id=1, source_target_pairs={{0,2},{1,3},{2,0},{3,1},{4,6},{5,7},{6,4},{7,5},{8,10},{9,11},{10,... | collective-permute-start | bytes 884744 | tf_op jit(solution)/shard_map/ppermute | solution.py:63
  10.4 163.2 %all-reduce.4.cloned.1.call-start = ((), (), s32[]{:S(2)}) async-start(), calls=%async_computation.1 | async-start | bytes 2949120 | tf_op jit(solution)/shard_map/psum | solution.py:233
  14.7 33.5 %copy-start.45 = (pred[60,16]{0,1:T(8,128)(4,1)}, pred[60,16]{0,1:T(8,128)(4,1)S(1)}, u32[]{:S(2)}) copy-start(pred[60,16]{0,1:T(8,128)(4,1)S(1)} %get-tuple-element.66) | copy-start | bytes 2884
  21.0 33.5 %copy-start.52 = (f32[768]{0:T(1024)}, f32[768]{0:T(1024)S(1)}, u32[]{:S(2)}) copy-start(f32[768]{0:T(1024)S(1)} %get-tuple-element.57) | copy-start | bytes 9220
  21.0 160.8 %copy-start.54 = (f32[768]{0:T(1024)}, f32[768]{0:T(1024)S(1)}, u32[]{:S(2)}) copy-start(f32[768]{0:T(1024)S(1)} %get-tuple-element.56) | copy-start | bytes 9220
  21.9 32.7 %copy-start.41 = (f32[768]{0:T(1024)}, f32[768]{0:T(1024)S(1)}, u32[]{:S(2)}) copy-start(f32[768]{0:T(1024)S(1)} %get-tuple-element.55) | copy-start | bytes 9220
  45.6 3.2 collective-permute-start.3
  48.2 30.5 %collective-permute-start.1 = (bf16[2,3,768,192]{2,3,0,1:T(8,128)(2,1)}, bf16[2,3,768,192]{2,3,0,1:T(8,128)(2,1)}, u32[]{:S(2)}, u32[]{:S(2)}) collective-permute-start(bf16[2,3,768,192]{2,3,0,1:T(8,128)(2,1)} %pad_maximum_fusion.7), channel_id=1, source_target_pairs={{0,1},{1,0},{2,3},{3,2},{4,5},{5,4},{6,7},{7,6},{8,9},{9,8},{10,11... | collective-permute-start | bytes 5308424 | tf_op jit(solution)/shard_map/ppermute | solution.py:63
  52.6 121.1 %copy-start.43 = (f32[960]{0:T(1024)}, f32[960]{0:T(1024)S(1)}, u32[]{:S(2)}) copy-start(f32[960]{0:T(1024)S(1)} %broadcast_multiply_fusion.4) | copy-start | bytes 11524
  76.5 5.6 copy-start.16
  78.2 471.5 %all-reduce.6.cloned.1.call-start = ((), (), s32[]{:S(2)}) async-start(), calls=%async_computation.2 | async-start | bytes 4718592 | tf_op jit(solution)/shard_map/psum | solution.py:294
  84.4 94.0 %collective-permute-start.4 = (bf16[1,768,768]{1,2,0:T(8,128)(2,1)}, bf16[1,768,768]{1,2,0:T(8,128)(2,1)}, u32[]{:S(2)}, u32[]{:S(2)}) collective-permute-start(bf16[1,768,768]{1,2,0:T(8,128)(2,1)} %bitcast.214), channel_id=1, source_target_pairs={{0,2},{1,3},{2,0},{3,1},{4,6},{5,7},{6,4},{7,5},{8,10},{9,11},{10,... | collective-permute-start | bytes 3538952 | tf_op jit(solution)/shard_map/ppermute | solution.py:63
  111.3 6.3 %copy-start.24 = (bf16[435,768]{1,0:T(8,128)(2,1)S(1)}, bf16[435,768]{1,0:T(8,128)(2,1)}, u32[]{:S(2)}) copy-start(bf16[435,768]{1,0:T(8,128)(2,1)} %param.23) | copy-start | bytes 2004484
  121.0 72.2 %collective-permute-start.6 = (bf16[1,768,768]{2,1,0:T(8,128)(2,1)}, bf16[1,768,768]{2,1,0:T(8,128)(2,1)}, u32[]{:S(2)}, u32[]{:S(2)}) collective-permute-start(bf16[1,768,768]{2,1,0:T(8,128)(2,1)} %bitcast.20), channel_id=1, source_target_pairs={{0,2},{1,3},{2,0},{3,1},{4,6},{5,7},{6,4},{7,5},{8,10},{9,11},{10,... | collective-permute-start | bytes 3538952 | tf_op jit(solution)/shard_map/ppermute | solution.py:63
  164.8 6.3 %copy-start.48 = (f32[600]{0:T(1024)}, f32[600]{0:T(1024)S(1)}, u32[]{:S(2)}) copy-start(f32[600]{0:T(1024)S(1)} %broadcast_multiply_fusion) | copy-start | bytes 7204
  177.6 14.3 %copy-start.1 = (f32[960,768]{1,0:T(8,128)}, f32[960,768]{1,0:T(8,128)S(1)}, u32[]{:S(2)}) copy-start(f32[960,768]{1,0:T(8,128)S(1)} %get-tuple-element.70) | copy-start | bytes 8847364
  178.5 12.1 %copy-start.15 = (f32[960,768]{1,0:T(8,128)}, f32[960,768]{1,0:T(8,128)S(1)}, u32[]{:S(2)}) copy-start(f32[960,768]{1,0:T(8,128)S(1)} %subtract_multiply_fusion) | copy-start | bytes 8847364
  181.8 15.2 %collective-permute-start.5 = (bf16[2,768,768]{1,2,0:T(8,128)(2,1)S(1)}, bf16[2,768,768]{1,2,0:T(8,128)(2,1)S(1)}, u32[]{:S(2)}, u32[]{:S(2)}) collective-permute-start(bf16[2,768,768]{1,2,0:T(8,128)(2,1)S(1)} %pad_maximum_fusion.3), channel_id=1, source_target_pairs={{0,1},{1,0},{2,3},{3,2},{4,5},{5,4},{6,7},{7,6},{8,9},{9,8},{10,11... | collective-permute-start | bytes 7077896 | tf_op jit(solution)/shard_map/ppermute | solution.py:63
  181.9 8.7 %copy-start.63 = (bf16[768,768]{1,0:T(8,128)(2,1)S(1)}, bf16[768,768]{1,0:T(8,128)(2,1)}, u32[]{:S(2)}) copy-start(bf16[768,768]{1,0:T(8,128)(2,1)} %param.34) | copy-start | bytes 3538948
  196.4 19.9 %collective-permute-start.7 = (bf16[2,768,768]{2,1,0:T(8,128)(2,1)}, bf16[2,768,768]{2,1,0:T(8,128)(2,1)}, u32[]{:S(2)}, u32[]{:S(2)}) collective-permute-start(bf16[2,768,768]{2,1,0:T(8,128)(2,1)} %pad_maximum_fusion.4), channel_id=1, source_target_pairs={{0,1},{1,0},{2,3},{3,2},{4,5},{5,4},{6,7},{7,6},{8,9},{9,8},{10,11... | collective-permute-start | bytes 7077896 | tf_op jit(solution)/shard_map/ppermute | solution.py:63
  249.1 13.3 %copy-start.47 = (f32[768]{0:T(1024)S(1)}, f32[768]{0:T(1024)}, u32[]{:S(2)}) copy-start(f32[768]{0:T(1024)} %get-tuple-element.52) | copy-start | bytes 9220
  249.1 13.3 %copy-start.50 = (f32[60]{0:T(128)S(1)}, f32[60]{0:T(128)}, u32[]{:S(2)}) copy-start(f32[60]{0:T(128)} %get-tuple-element.65) | copy-start | bytes 724
  249.8 1.8 collective-permute-start.8
  251.6 10.7 %collective-permute-start.9 = (f32[120,768]{1,0:T(8,128)S(1)}, f32[120,768]{1,0:T(8,128)S(1)}, u32[]{:S(2)}, u32[]{:S(2)}) collective-permute-start(f32[120,768]{1,0:T(8,128)S(1)} %fusion.267), channel_id=1, source_target_pairs={{0,2},{1,3},{2,0},{3,1},{4,6},{5,7},{6,4},{7,5},{8,10},{9,11},{10,... | collective-permute-start | bytes 1105928 | tf_op jit(solution)/shard_map/ppermute | solution.py:63
  262.4 23.7 %copy-start.46 = (pred[60,16]{0,1:T(8,128)(4,1)S(1)}, pred[60,16]{0,1:T(8,128)(4,1)}, u32[]{:S(2)}) copy-start(pred[60,16]{0,1:T(8,128)(4,1)} %copy-done.45) | copy-start | bytes 2884
  262.4 23.8 %copy-start.58 = (s32[480]{0:T(512)S(1)}, s32[480]{0:T(512)}, u32[]{:S(2)}) copy-start(s32[480]{0:T(512)} %param.21) | copy-start | bytes 5764
  262.8 11.0 %collective-permute-start.10 = (bf16[120,768]{1,0:T(8,128)(2,1)S(1)}, bf16[120,768]{1,0:T(8,128)(2,1)S(1)}, u32[]{:S(2)}, u32[]{:S(2)}) collective-permute-start(bf16[120,768]{1,0:T(8,128)(2,1)S(1)} %pad_maximum_fusion.18), channel_id=1, source_target_pairs={{0,16},{4,20},{8,24},{12,28},{16,0},{20,4},{24,8},{28,12},{1,17},{... | collective-permute-start | bytes 552968 | tf_op jit(solution)/shard_map/ppermute | solution.py:63
  273.9 9.6 %collective-permute-start.11 = (bf16[2,120,768]{2,1,0:T(8,128)(2,1)S(1)}, bf16[2,120,768]{2,1,0:T(8,128)(2,1)S(1)}, u32[]{:S(2)}, u32[]{:S(2)}) collective-permute-start(bf16[2,120,768]{2,1,0:T(8,128)(2,1)S(1)} %pad_maximum_fusion.16), channel_id=1, source_target_pairs={{0,8},{4,12},{8,0},{12,4},{16,24},{20,28},{24,16},{28,20},{1,9},{5... | collective-permute-start | bytes 1105928 | tf_op jit(solution)/shard_map/ppermute | solution.py:63
  284.4 17.0 %collective-permute-start.12 = (bf16[2,2,120,768]{3,2,1,0:T(8,128)(2,1)}, bf16[2,2,120,768]{3,2,1,0:T(8,128)(2,1)S(1)}, u32[]{:S(2)}, u32[]{:S(2)}) collective-permute-start(bf16[2,2,120,768]{3,2,1,0:T(8,128)(2,1)} %pad_maximum_fusion.10), channel_id=1, source_target_pairs={{0,4},{4,0},{8,12},{12,8},{16,20},{20,16},{24,28},{28,24},{1,5},{5... | collective-permute-start | bytes 2211848 | tf_op jit(solution)/shard_map/ppermute | solution.py:63
  315.6 2.4 collective-permute-start.13
  319.7 23.4 %copy-start.38 = (f32[60,3,16]{2,1,0:T(4,128)S(1)}, f32[60,3,16]{2,1,0:T(4,128)}, u32[]{:S(2)}) copy-start(f32[60,3,16]{2,1,0:T(4,128)} %copy-done.37) | copy-start | bytes 34564
  319.7 23.4 %copy-start.40 = (f32[60,3,16]{2,1,0:T(4,128)S(1)}, f32[60,3,16]{2,1,0:T(4,128)}, u32[]{:S(2)}) copy-start(f32[60,3,16]{2,1,0:T(4,128)} %copy-done.39) | copy-start | bytes 34564
  319.8 23.4 %copy-start.55 = (f32[768]{0:T(1024)S(1)}, f32[768]{0:T(1024)}, u32[]{:S(2)}) copy-start(f32[768]{0:T(1024)} %copy-done.54) | copy-start | bytes 9220
  319.8 10.8 %collective-permute-start.14 = (bf16[240,768]{1,0:T(8,128)(2,1)S(1)}, bf16[240,768]{1,0:T(8,128)(2,1)}, u32[]{:S(2)}, u32[]{:S(2)}) collective-permute-start(bf16[240,768]{1,0:T(8,128)(2,1)S(1)} %fusion.125), channel_id=1, source_target_pairs={{0,2},{1,3},{2,0},{3,1},{4,6},{5,7},{6,4},{7,5},{8,10},{9,11},{10,... | collective-permute-start | bytes 1105928 | tf_op jit(solution)/shard_map/ppermute | solution.py:63
  331.7 9.8 %collective-permute-start.15 = (bf16[240,768]{1,0:T(8,128)(2,1)S(1)}, bf16[240,768]{1,0:T(8,128)(2,1)S(1)}, u32[]{:S(2)}, u32[]{:S(2)}) collective-permute-start(bf16[240,768]{1,0:T(8,128)(2,1)S(1)} %fusion.99), channel_id=1, source_target_pairs={{0,2},{1,3},{2,0},{3,1},{4,6},{5,7},{6,4},{7,5},{8,10},{9,11},{10,... | collective-permute-start | bytes 1105928 | tf_op jit(solution)/shard_map/ppermute | solution.py:63
  342.5 5.4 collective-permute-start.16
  351.8 7.0 %copy-start.31 = (bf16[192,768]{1,0:T(8,128)(2,1)S(1)}, bf16[192,768]{1,0:T(8,128)(2,1)}, u32[]{:S(2)}) copy-start(bf16[192,768]{1,0:T(8,128)(2,1)} %param.31) | copy-start | bytes 884740
  377.4 9.4 %copy-start.10 = (bf16[960,768]{1,0:T(8,128)(2,1)S(1)}, bf16[960,768]{1,0:T(8,128)(2,1)}, u32[]{:S(2)}) copy-start(bf16[960,768]{1,0:T(8,128)(2,1)} %all-gather.2.cloned.1.call-done) | copy-start | bytes 4423684
  377.4 9.4 %copy-start.42 = (f32[768]{0:T(1024)S(1)}, f32[768]{0:T(1024)}, u32[]{:S(2)}) copy-start(f32[768]{0:T(1024)} %copy-done.41) | copy-start | bytes 9220
  377.5 9.4 %copy-start.44 = (f32[960]{0:T(1024)S(1)}, f32[960]{0:T(1024)}, u32[]{:S(2)}) copy-start(f32[960]{0:T(1024)} %copy-done.43) | copy-start | bytes 11524
  377.5 9.4 %copy-start.53 = (f32[768]{0:T(1024)S(1)}, f32[768]{0:T(1024)}, u32[]{:S(2)}) copy-start(f32[768]{0:T(1024)} %copy-done.52) | copy-start | bytes 9220
  378.4 8.4 %copy-start.27 = (bf16[1,960,192]{1,2,0:T(8,128)(2,1)S(1)}, bf16[1,960,192]{1,2,0:T(8,128)(2,1)}, u32[]{:S(2)}) copy-start(bf16[1,960,192]{1,2,0:T(8,128)(2,1)} %copy.130) | copy-start | bytes 1105924
  396.8 15.8 %collective-permute-start.19 = (bf16[2,2,96,768]{3,2,1,0:T(8,128)(2,1)S(1)}, bf16[2,2,96,768]{3,2,1,0:T(8,128)(2,1)S(1)}, u32[]{:S(2)}, u32[]{:S(2)}) collective-permute-start(bf16[2,2,96,768]{3,2,1,0:T(8,128)(2,1)S(1)} %fusion.118), channel_id=1, source_target_pairs={{0,4},{4,0},{8,12},{12,8},{16,20},{20,16},{24,28},{28,24},{1,5},{5... | collective-permute-start | bytes 1769480 | tf_op jit(solution)/shard_map/ppermute | solution.py:63
  399.9 15.5 %collective-permute-start.17 = (bf16[2,240,768]{2,1,0:T(8,128)(2,1)S(1)}, bf16[2,240,768]{2,1,0:T(8,128)(2,1)S(1)}, u32[]{:S(2)}, u32[]{:S(2)}) collective-permute-start(bf16[2,240,768]{2,1,0:T(8,128)(2,1)S(1)} %fusion.98), channel_id=1, source_target_pairs={{0,1},{1,0},{2,3},{3,2},{4,5},{5,4},{6,7},{7,6},{8,9},{9,8},{10,11... | collective-permute-start | bytes 2211848 | tf_op jit(solution)/shard_map/ppermute | solution.py:63
  412.8 13.2 %copy-start.34 = (bf16[768,768]{1,0:T(8,128)(2,1)S(1)}, bf16[768,768]{1,0:T(8,128)(2,1)}, u32[]{:S(2)}) copy-start(bf16[768,768]{1,0:T(8,128)(2,1)} %convolution_convert_fusion.2) | copy-start | bytes 3538948
  412.8 9.4 %collective-permute-start.20 = (bf16[2,96,768]{2,1,0:T(8,128)(2,1)S(1)}, bf16[2,96,768]{2,1,0:T(8,128)(2,1)S(1)}, u32[]{:S(2)}, u32[]{:S(2)}) collective-permute-start(bf16[2,96,768]{2,1,0:T(8,128)(2,1)S(1)} %fusion.127), channel_id=1, source_target_pairs={{0,8},{4,12},{8,0},{12,4},{16,24},{20,28},{24,16},{28,20},{1,9},{5... | collective-permute-start | bytes 884744 | tf_op jit(solution)/shard_map/ppermute | solution.py:63
  416.3 15.9 %collective-permute-start.18 = (bf16[240,768]{1,0:T(8,128)(2,1)}, bf16[240,768]{1,0:T(8,128)(2,1)}, u32[]{:S(2)}, u32[]{:S(2)}) collective-permute-start(bf16[240,768]{1,0:T(8,128)(2,1)} %fusion.126), channel_id=1, source_target_pairs={{0,2},{1,3},{2,0},{3,1},{4,6},{5,7},{6,4},{7,5},{8,10},{9,11},{10,... | collective-permute-start | bytes 1105928 | tf_op jit(solution)/shard_map/ppermute | solution.py:63
  422.3 9.8 %collective-permute-start.21 = (bf16[96,768]{1,0:T(8,128)(2,1)S(1)}, bf16[96,768]{1,0:T(8,128)(2,1)S(1)}, u32[]{:S(2)}, u32[]{:S(2)}) collective-permute-start(bf16[96,768]{1,0:T(8,128)(2,1)S(1)} %fusion.131), channel_id=1, source_target_pairs={{0,16},{4,20},{8,24},{12,28},{16,0},{20,4},{24,8},{28,12},{1,17},{... | collective-permute-start | bytes 442376 | tf_op jit(solution)/shard_map/ppermute | solution.py:63
  427.6 6.3 %copy-start.51 = (f32[240]{0:T(256)S(1)}, f32[240]{0:T(256)}, u32[]{:S(2)}) copy-start(f32[240]{0:T(256)} %dynamic-slice.3) | copy-start | bytes 2884
  432.2 19.2 %collective-permute-start.22 = (bf16[96,768]{1,0:T(8,128)(2,1)S(1)}, bf16[96,768]{1,0:T(8,128)(2,1)S(1)}, u32[]{:S(2)}, u32[]{:S(2)}) collective-permute-start(bf16[96,768]{1,0:T(8,128)(2,1)S(1)} %fusion.128), channel_id=1, source_target_pairs={{0,16},{4,20},{8,24},{12,28},{16,0},{20,4},{24,8},{28,12},{1,17},{... | collective-permute-start | bytes 442376 | tf_op jit(solution)/shard_map/ppermute | solution.py:63
  436.4 1.3 collective-permute-start.25
  437.7 3.8 collective-permute-start.26
  451.5 20.1 %collective-permute-start.23 = (bf16[2,96,768]{2,1,0:T(8,128)(2,1)S(1)}, bf16[2,96,768]{2,1,0:T(8,128)(2,1)S(1)}, u32[]{:S(2)}, u32[]{:S(2)}) collective-permute-start(bf16[2,96,768]{2,1,0:T(8,128)(2,1)S(1)} %pad_maximum_fusion.17), channel_id=1, source_target_pairs={{0,8},{4,12},{8,0},{12,4},{16,24},{20,28},{24,16},{28,20},{1,9},{5... | collective-permute-start | bytes 884744 | tf_op jit(solution)/shard_map/ppermute | solution.py:63
  451.6 3.9 collective-permute-start.27
  455.5 15.3 %collective-permute-start.28 = (f32[8,768]{1,0:T(8,128)S(1)}, f32[8,768]{1,0:T(8,128)S(1)}, u32[]{:S(2)}, u32[]{:S(2)}) collective-permute-start(f32[8,768]{1,0:T(8,128)S(1)} %fusion.266), channel_id=1, source_target_pairs={{0,8},{4,12},{8,0},{12,4},{16,24},{20,28},{24,16},{28,20},{1,9},{5... | collective-permute-start | bytes 73736 | tf_op jit(solution)/shard_map/ppermute | solution.py:63
  470.8 83.1 %collective-permute-start.29 = (f32[8,768]{1,0:T(8,128)S(1)}, f32[8,768]{1,0:T(8,128)S(1)}, u32[]{:S(2)}, u32[]{:S(2)}) collective-permute-start(f32[8,768]{1,0:T(8,128)S(1)} %add.363), channel_id=1, source_target_pairs={{0,16},{4,20},{8,24},{12,28},{16,0},{20,4},{24,8},{28,12},{1,17},{... | collective-permute-start | bytes 73736 | tf_op jit(solution)/shard_map/ppermute | solution.py:63
  471.7 84.1 %collective-permute-start.24 = (bf16[2,2,96,768]{3,2,1,0:T(8,128)(2,1)S(1)}, bf16[2,2,96,768]{3,2,1,0:T(8,128)(2,1)S(1)}, u32[]{:S(2)}, u32[]{:S(2)}) collective-permute-start(bf16[2,2,96,768]{3,2,1,0:T(8,128)(2,1)S(1)} %pad_maximum_fusion.13), channel_id=1, source_target_pairs={{0,4},{4,0},{8,12},{12,8},{16,20},{20,16},{24,28},{28,24},{1,5},{5... | collective-permute-start | bytes 1769480 | tf_op jit(solution)/shard_map/ppermute | solution.py:63
  (43 other events, 131.3 us)
Sparse Core Ops, SparseCore 0:
  10.6 28.8 all-gather.1
  78.3 66.1 all-reduce.3
  427.7 121.9 all-reduce.5

commit v11 on v7

--- a/solution.py
+++ b/solution.py
@@ -63,12 +63,12 @@
     return lax.ppermute(values, axis, [(i, i ^ (1 << bit)) for i in range(count)])
 
 
-def gather_stacked(values, axis):
+def gather_chunks(values, axis):
     count, bits = axis_bits(axis)
-    data = values[None]
+    chunks = [values]
     for bit in bits:
-        data = jnp.concatenate([data, exchange(data, axis, count, bit)], 0)
-    return data
+        chunks = chunks + [exchange(chunk, axis, count, bit) for chunk in chunks]
+    return chunks
 
 
 def gather_ordered(values, axis):
@@ -112,16 +112,29 @@
 
 
 def image_tower(tokens, count, length, gains, weights):
-    w_qkv, w_out, w_fc1, w_fc2 = weights
-    _, middle = image_attention(tokens, count, length, gains, w_qkv, w_out)
-    return image_ffn(middle, count, length, gains, w_fc1, w_fc2)
-
-
-def image_attention(tokens, count, length, gains, w_qkv, w_out):
-    head_count = D // HEAD
+    qkv_chunks, out_chunks, fc1_chunks, fc2_chunks = weights
     inputs = tokens.astype(jnp.float32)
     unit, _ = layer_stats(inputs)
     normed = (unit * gains[0]).astype(jnp.bfloat16)
+    middle = inputs
+    for w_qkv, w_out in zip(qkv_chunks, out_chunks):
+        middle = middle + image_heads(normed, count, length, w_qkv, w_out)
+    unit2, _ = layer_stats(middle)
+    normed2 = (unit2 * gains[1]).astype(jnp.bfloat16)
+    result = middle
+    for w_fc1, w_fc2 in zip(fc1_chunks, fc2_chunks):
+        active = gelu_exact(jnp.dot(normed2, w_fc1, preferred_element_type=jnp.float32)).astype(
+            jnp.bfloat16
+        )
+        result = result + jnp.dot(active, w_fc2, preferred_element_type=jnp.float32)
+    pooled = jnp.mean(result.reshape(count, length, D), 1)
+    return (pooled * lax.rsqrt(jnp.sum(pooled * pooled, -1, keepdims=True) + EPS)).astype(
+        jnp.bfloat16
+    )
+
+
+def image_heads(normed, count, length, w_qkv, w_out):
+    head_count = w_qkv.shape[2] // HEAD
     projected = jnp.einsum("rd,jdw->jrw", normed, w_qkv, preferred_element_type=jnp.float32).astype(
         jnp.bfloat16
     )
@@ -133,22 +146,8 @@
         shaped[2],
         preferred_element_type=jnp.float32,
     )
-    context = context.astype(jnp.bfloat16).reshape(count * length, D)
-    middle = inputs + jnp.dot(context, w_out, preferred_element_type=jnp.float32)
-    return inputs, middle
-
-
-def image_ffn(middle, count, length, gains, w_fc1, w_fc2):
-    unit2, _ = layer_stats(middle)
-    normed2 = (unit2 * gains[1]).astype(jnp.bfloat16)
-    active = gelu_exact(jnp.dot(normed2, w_fc1, preferred_element_type=jnp.float32)).astype(
-        jnp.bfloat16
-    )
-    result = middle + jnp.dot(active, w_fc2, preferred_element_type=jnp.float32)
-    pooled = jnp.mean(result.reshape(count, length, D), 1)
-    return (pooled * lax.rsqrt(jnp.sum(pooled * pooled, -1, keepdims=True) + EPS)).astype(
-        jnp.bfloat16
-    )
+    context = context.astype(jnp.bfloat16).reshape(count * length, head_count * HEAD)
+    return jnp.dot(context, w_out, preferred_element_type=jnp.float32)
 
 
 def local_body(
@@ -172,13 +171,11 @@
     txt_shifts,
     txt_biases,
 ):
-    qkv_parts = gather_stacked(img_qkv, "mp")
-    fc1_parts = gather_stacked(img_fc1, "mp")
     weights = (
-        qkv_parts.transpose(1, 2, 0, 3).reshape(3, D, -1),
-        gather_stacked(img_out, "mp").reshape(-1, D),
-        fc1_parts.transpose(1, 0, 2).reshape(D, -1),
-        gather_stacked(img_fc2, "mp").reshape(-1, D),
+        gather_chunks(img_qkv, "mp"),
+        gather_chunks(img_out, "mp"),
+        gather_chunks(img_fc1, "mp"),
+        gather_chunks(img_fc2, "mp"),
     )
     low_count = image_low.shape[0] // P_LOW
     high_count = image_high.shape[0] // P_HIGH

time: 604 us -> 639 us (1.058)
  matrix products: 113 us -> 188 us
  waiting for transfers between devices: 236 us -> 199 us
  local copies, waits for them, and re-layouts: 105 us -> 123 us
  other arithmetic: 86 us -> 69.7 us
  starting transfers between devices: 35.2 us -> 28.5 us
    ppermute x30 -> x34, waiting for transfers between devices: 159 us -> 109 us  [exchange(): return lax.ppermute(values, axis, [(i, i ^ 1 << bit) for i in range(count)])]
    dot_general x8 -> x24, matrix products: 64.6 us -> 103 us  [the longest x8 65.2 us: image_tower(): result = result + jnp.dot(active, w_fc2, preferred_element_type=jnp.float32)]
    concatenate x8 -> x0, other arithmetic: 21 us -> none  [gather_stacked(): data = jnp.concatenate([data, exchange(data, axis, count, bit)], 0)]
    unnamed x1 -> x9, matrix products: 2.45 us -> 22.9 us
    psum x1, waiting for transfers between devices: 0.02 us -> 14.5 us  [local_body(): lax.psum(jnp.dot(context, txt_out, preferred_element_type=jnp.float32).as...]
    squeeze x6 -> x24, local copies, waits for them, and re-layouts: 21.1 us -> 33.5 us  [the longest x16 22.4 us: image_heads(): shares, _ = attention_shares(shaped[0], shaped[1], None)]
    sub x0 -> x4, matrix products: none -> 11.2 us  [attention_shares(): raised = jnp.exp(scores - highest)]
    ppermute x30 -> x34, starting transfers between devices: 34.6 us -> 28.2 us  [exchange(): return lax.ppermute(values, axis, [(i, i ^ 1 << bit) for i in range(count)])]
  transfers between devices with their start and end apart: 33 -> 37, of which waited for: 20 -> 18; matrix products, arithmetic and copies ran while one was open for 29% -> 43% of each run, Pallas kernels for 0% -> 0%
where the time goes in v11:
time: 639 us; the launch traced here: 627 us
  waiting for transfers between devices  199 us (31%)
  matrix products  188 us (29%)
  local copies, waits for them, and re-layouts  123 us (19%)
  other arithmetic  69.7 us (11%)
  starting transfers between devices  28.5 us (4%)
  between operations  19 us (3%)
    ppermute x34, waiting for transfers between devices, exchange(): return lax.ppermute(values, axis, [(i, i ^ 1 << bit) for i in range(count)])  109 us
    psum x1, waiting for transfers between devices, local_body(): lax.psum(jnp.concatenate([grad_fc1, grad_fc2], 0).astype(jnp.bfloat16), '...  75.6 us
    dot_general x8, matrix products, image_tower(): result = result + jnp.dot(active, w_fc2, preferred_element_type=jnp.float32)  65.2 us
    ppermute x34, starting transfers between devices, exchange(): return lax.ppermute(values, axis, [(i, i ^ 1 << bit) for i in range(count)])  28.2 us
    unnamed x9, matrix products  22.9 us
    squeeze x16, local copies, waits for them, and re-layouts, image_heads(): shares, _ = attention_shares(shaped[0], shaped[1], None)  22.4 us
    dot_general x8, matrix products, image_heads(): return jnp.dot(context, w_out, preferred_element_type=jnp.float32)  18.9 us
    dot_general x8, matrix products, image_heads(): jnp.einsum('nhqk,nkhe->nqhe', shares.astype(jnp.bfloat16), shaped[2], pre...  18.5 us
  transfers between devices with their start and end apart: 37, of which 18 were waited for; matrix products, arithmetic and copies ran while one was open for 43% of the time, Pallas kernels for 0%

profile of v11, /device:TPU:0, one launch (start us, length us, event | category | flops | bytes accessed | tf_op | source)
XLA Modules:
  0.0 627.2 jit_solution(8859282732337010121)
XLA Ops:
  7.3 3.1 collective-permute-start.1
  24.1 2.8 fusion.663
  40.6 3.2 fusion.135
  47.0 2.6 convert_add_fusion.2
  53.3 3.3 fusion.637
  56.9 3.0 fusion.629
  60.0 3.7 fusion.639
  91.5 2.7 fusion.658
  94.2 3.1 fusion.137
  97.3 2.9 fusion.668
  100.2 2.4 fusion.142
  102.6 3.1 fusion.136
  112.3 2.5 fusion.141
  115.1 2.6 fusion.704
  123.0 2.7 fusion.703
  125.7 2.5 fusion.82
  131.0 3.3 fusion.635
  143.2 2.8 fusion.673
  151.2 2.2 fusion.138
  156.9 3.3 fusion.683
  161.9 8.7 %fusion.179 = f32[600,768]{1,0:T(8,128)} fusion(bf16[768,768]{1,0:T(8,128)(2,1)} %param.28, bf16[600,768]{1,0:T(8,128)(2,1)S(1)} %multiply_convert_fusion.1, bf16[768,768]{1,0:T(8,128)(2,1)} %param.27), kind=kOutput, calls=%fused_computation.351 | convolution fusion | flops 1445529600 | bytes 5124096 | tf_op jit(solution)/shard_map/dot_general | solution.py:129
  170.9 6.8 %convolution_add_fusion.2 = f32[435,768]{1,0:T(8,128)} fusion(f32[435,768]{1,0:T(8,128)S(1)} %get-tuple-element.133, bf16[768,768]{1,0:T(8,128)(2,1)} %param.28, bf16[768,768]{1,0:T(8,128)(2,1)} %param.27, f32[768]{0:T(1024)S(1)} %get-tuple-element.50, f32[435]{0:T(512)S(1)} %add_rsqrt_fusion.4, f32[435]{0:T(512)S(1)} %broadcast_multiply_fusion.5), kind=kOutput, calls=%fused_computation.186 | convolution fusion | flops 1049679360 | bytes 5038488 | tf_op jit(solution)/shard_map/dot_general | solution.py:129
  177.7 6.8 %fusion.287 = f32[435,768]{1,0:T(8,128)} fusion(bf16[768,768]{1,0:T(8,128)(2,1)} %collective-permute-done.9, bf16[768,768]{1,0:T(8,128)(2,1)} %collective-permute-done.8, f32[435,768]{1,0:T(8,128)S(1)} %get-tuple-element.133, f32[768]{0:T(1024)S(1)} %get-tuple-element.50, f32[435]{0:T(512)S(1)} %add_rsqrt_fusion.4, f32[435]{0:T(512)S(1)} %broadcast_multiply_fusion.5), kind=kOutput, calls=%fused_computation.479 | convolution fusion | flops 1049345280 | bytes 5038488 | tf_op jit(solution)/shard_map/dot_general | solution.py:129
  184.4 8.6 %fusion.175 = f32[600,768]{1,0:T(8,128)} fusion(bf16[768,768]{1,0:T(8,128)(2,1)} %collective-permute-done.9, bf16[600,768]{1,0:T(8,128)(2,1)S(1)} %multiply_convert_fusion.1, bf16[768,768]{1,0:T(8,128)(2,1)} %collective-permute-done.8), kind=kOutput, calls=%fused_computation.349 | convolution fusion | flops 1445529600 | bytes 5124096 | tf_op jit(solution)/shard_map/dot_general | solution.py:129
  193.0 7.6 %fusion.81 = f32[435,768]{1,0:T(8,128)} fusion(f32[435,768]{1,0:T(8,128)} %fusion.287, f32[435,768]{1,0:T(8,128)} %convolution_add_fusion.2, bf16[768,768]{1,0:T(8,128)(2,1)} %collective-permute-done.7, bf16[768,768]{1,0:T(8,128)(2,1)} %collective-permute-done.6, f32[435,768]{1,0:T(8,128)S(1)} %get-tuple-element.133, f32[768]{0:T(1024)S(1)} %get-tuple-element.50, ...), kind=kOutput, calls=%fused_computation.185 | convolution fusion | flops 1050013440 | bytes 7711128 | tf_op jit(solution)/shard_map/dot_general | solution.py:129
  200.6 8.3 %fusion.177 = f32[600,768]{1,0:T(8,128)} fusion(bf16[768,768]{1,0:T(8,128)(2,1)} %collective-permute-done.7, bf16[600,768]{1,0:T(8,128)(2,1)S(1)} %multiply_convert_fusion.1, bf16[768,768]{1,0:T(8,128)(2,1)} %collective-permute-done.6), kind=kOutput, calls=%fused_computation.350 | convolution fusion | flops 1445529600 | bytes 5124096 | tf_op jit(solution)/shard_map/dot_general | solution.py:129
  215.9 3.0 reshape.357
  218.9 3.2 fusion.646
  226.1 2.4 reshape.358
  230.5 7.6 %convolution_add_fusion = f32[435,768]{1,0:T(8,128)} fusion(f32[435,768]{1,0:T(8,128)} %fusion.81, bf16[768,768]{1,0:T(8,128)(2,1)} %collective-permute-done.11, bf16[768,768]{1,0:T(8,128)(2,1)} %collective-permute-done.10, f32[435,768]{1,0:T(8,128)} %copy-done.13, f32[768]{0:T(1024)S(1)} %get-tuple-element.50, f32[435]{0:T(512)S(1)} %add_rsqrt_fusion.4, ...), kind=kOutput, calls=%fused_computation.183 | convolution fusion | flops 1049679360 | bytes 6374808 | tf_op jit(solution)/shard_map/dot_general | solution.py:129
  238.1 2.6 reshape.370
  242.2 10.9 %add_add_fusion = f32[600,768]{1,0:T(8,128)} fusion(f32[600,768]{1,0:T(8,128)} %fusion.175, f32[600,768]{1,0:T(8,128)} %fusion.177, f32[600,768]{1,0:T(8,128)} %copy-done.5, f32[600,768]{1,0:T(8,128)} %fusion.179, bf16[768,768]{1,0:T(8,128)(2,1)} %collective-permute-done.11, bf16[600,768]{1,0:T(8,128)(2,1)} %copy-done.52, ...), kind=kOutput, calls=%fused_computation.93 | convolution fusion | flops 1447372800 | bytes 12496896 | tf_op jit(solution)/shard_map/dot_general | solution.py:129
  253.1 3.1 reshape.365
  258.8 14.5 %all-reduce.4.cloned.1.call-done = bf16[960,768]{1,0:T(8,128)(2,1)} async-done(((bf16[960,768]{1,0:T(8,128)(2,1)}), bf16[960,768]{1,0:T(8,128)(2,1)}) %all-reduce.4.cloned.1.call-update) | async-done | bytes 1474576 | tf_op jit(solution)/shard_map/psum | solution.py:220
  273.3 4.5 fusion.645
  279.3 8.7 %multiply_convert_fusion = (bf16[960,768]{1,0:T(8,128)(2,1)S(1)}, f32[960,768]{1,0:T(8,128)}, f32[960,768]{1,0:T(8,128)}) fusion(f32[768]{0:T(1024)S(1)} %copy-done.102, bf16[768,768]{1,0:T(8,128)(2,1)S(1)} %copy-done, f32[960,768]{1,0:T(8,128)S(1)} %subtract_multiply_fusion, f32[768]{0:T(1024)S(1)} %copy-done.87, f32[768]{0:T(1024)S(1)} %copy-done.62), kind=kOutput, calls=%fused_computation.23 | convolution fusion | flops 1183334400 | bytes 11510784 | tf_op jit(solution)/shard_map/dot_general | solution.py:228
  292.9 10.2 %collective-permute-done.13 = f32[120,768]{1,0:T(8,128)S(1)} collective-permute-done((f32[120,768]{1,0:T(8,128)S(1)}, f32[120,768]{1,0:T(8,128)S(1)}, u32[]{:S(2)}, u32[]{:S(2)}) %collective-permute-start.13) | collective-permute-done | bytes 368672 | tf_op jit(solution)/shard_map/ppermute | solution.py:63
  304.9 2.4 collective-permute-start.14
  307.3 8.5 %collective-permute-done.14 = bf16[120,768]{1,0:T(8,128)(2,1)S(1)} collective-permute-done((bf16[120,768]{1,0:T(8,128)(2,1)}, bf16[120,768]{1,0:T(8,128)(2,1)S(1)}, u32[]{:S(2)}, u32[]{:S(2)}) %collective-permute-start.14) | collective-permute-done | bytes 184352 | tf_op jit(solution)/shard_map/ppermute | solution.py:63
  317.3 9.0 %collective-permute-done.15 = bf16[2,120,768]{2,1,0:T(8,128)(2,1)} collective-permute-done((bf16[2,120,768]{2,1,0:T(8,128)(2,1)S(1)}, bf16[2,120,768]{2,1,0:T(8,128)(2,1)}, u32[]{:S(2)}, u32[]{:S(2)}) %collective-permute-start.15) | collective-permute-done | bytes 368672 | tf_op jit(solution)/shard_map/ppermute | solution.py:63
  334.3 11.8 %collective-permute-done.16 = bf16[2,2,120,768]{3,2,1,0:T(8,128)(2,1)} collective-permute-done((bf16[2,2,120,768]{3,2,1,0:T(8,128)(2,1)}, bf16[2,2,120,768]{3,2,1,0:T(8,128)(2,1)}, u32[]{:S(2)}, u32[]{:S(2)}) %collective-permute-start.16) | collective-permute-done | bytes 737312 | tf_op jit(solution)/shard_map/ppermute | solution.py:63
  353.3 3.0 select_reduce_fusion
  359.3 5.1 convert_reduce_fusion.1
  368.3 2.6 collective-permute-done.17
  374.4 10.1 %collective-permute-done.18 = bf16[240,768]{1,0:T(8,128)(2,1)} collective-permute-done((bf16[240,768]{1,0:T(8,128)(2,1)S(1)}, bf16[240,768]{1,0:T(8,128)(2,1)}, u32[]{:S(2)}, u32[]{:S(2)}) %collective-permute-start.18) | collective-permute-done | bytes 368672 | tf_op jit(solution)/shard_map/ppermute | solution.py:63
  386.6 9.2 %collective-permute-done.19 = bf16[240,768]{1,0:T(8,128)(2,1)} collective-permute-done((bf16[240,768]{1,0:T(8,128)(2,1)S(1)}, bf16[240,768]{1,0:T(8,128)(2,1)}, u32[]{:S(2)}, u32[]{:S(2)}) %collective-permute-start.19) | collective-permute-done | bytes 368672 | tf_op jit(solution)/shard_map/ppermute | solution.py:63
  400.9 4.8 convolution_convert_fusion.2
  409.2 3.6 multiply_reduce_fusion
  413.6 2.6 bitcast_multiply_fusion
  422.1 2.3 multiply_reduce_fusion.6
  438.3 6.2 dot_general.273
  444.6 3.6 convolution_bitcast_fusion.1
  448.2 2.2 copy.230
  460.4 10.0 %collective-permute-done.23 = bf16[2,2,96,768]{3,2,1,0:T(8,128)(2,1)S(1)} collective-permute-done((bf16[2,2,96,768]{3,2,1,0:T(8,128)(2,1)S(1)}, bf16[2,2,96,768]{3,2,1,0:T(8,128)(2,1)S(1)}, u32[]{:S(2)}, u32[]{:S(2)}) %collective-permute-start.23) | collective-permute-done | bytes 589856 | tf_op jit(solution)/shard_map/ppermute | solution.py:63
  470.5 2.6 collective-permute-start.24
  474.7 5.2 collective-permute-done.24
  480.0 3.6 collective-permute-start.25
  491.5 2.4 dynamic-slice_reduce_fusion.2
  496.1 3.0 collective-permute-done.30
  499.1 9.6 %collective-permute-done.26 = bf16[96,768]{1,0:T(8,128)(2,1)S(1)} collective-permute-done((bf16[96,768]{1,0:T(8,128)(2,1)S(1)}, bf16[96,768]{1,0:T(8,128)(2,1)S(1)}, u32[]{:S(2)}, u32[]{:S(2)}) %collective-permute-start.26) | collective-permute-done | bytes 147488 | tf_op jit(solution)/shard_map/ppermute | solution.py:63
  510.3 2.5 collective-permute-done.31
  516.8 12.5 %collective-permute-done.32 = f32[8,768]{1,0:T(8,128)S(1)} collective-permute-done((f32[8,768]{1,0:T(8,128)S(1)}, f32[8,768]{1,0:T(8,128)S(1)}, u32[]{:S(2)}, u32[]{:S(2)}) %collective-permute-start.32) | collective-permute-done | bytes 24608 | tf_op jit(solution)/shard_map/ppermute | solution.py:63
  531.0 75.6 %all-reduce.6.cloned.1.call-done = bf16[1536,768]{1,0:T(8,128)(2,1)} async-done(((bf16[1536,768]{1,0:T(8,128)(2,1)}), bf16[1536,768]{1,0:T(8,128)(2,1)}) %all-reduce.6.cloned.1.call-update) | async-done | bytes 2359312 | tf_op jit(solution)/shard_map/psum | solution.py:285
  606.5 4.2 slice_convert_fusion
  (520 shorter events, 214.7 us)
Async XLA Ops:
  7.2 272.1 %copy-start = (bf16[768,768]{1,0:T(8,128)(2,1)S(1)}, bf16[768,768]{1,0:T(8,128)(2,1)}, u32[]{:S(2)}) copy-start(bf16[768,768]{1,0:T(8,128)(2,1)} %param.32) | copy-start | bytes 3538948
  7.2 8.2 %copy-start.11 = (bf16[435,768]{1,0:T(8,128)(2,1)S(1)}, bf16[435,768]{1,0:T(8,128)(2,1)}, u32[]{:S(2)}) copy-start(bf16[435,768]{1,0:T(8,128)(2,1)} %param.23) | copy-start | bytes 2004484
  7.2 8.5 %copy-start.94 = (f32[2,192]{1,0:T(2,128)S(1)}, f32[2,192]{1,0:T(2,128)}, u32[]{:S(2)}) copy-start(f32[2,192]{1,0:T(2,128)} %param.30) | copy-start | bytes 4612
  7.2 9.1 %copy-start.8 = (bf16[600,768]{1,0:T(8,128)(2,1)S(1)}, bf16[600,768]{1,0:T(8,128)(2,1)}, u32[]{:S(2)}) copy-start(bf16[600,768]{1,0:T(8,128)(2,1)} %param.22) | copy-start | bytes 2764804
  7.2 201.8 %all-gather.2.cloned.1.call-start = ((), (), s32[]{:S(2)}) async-start(), calls=%async_computation | async-start | bytes 1843200 | tf_op jit(solution)/shard_map/all_gather | solution.py:199
  7.3 115.3 %collective-permute-start.1 = (bf16[192,768]{1,0:T(8,128)(2,1)}, bf16[192,768]{1,0:T(8,128)(2,1)}, u32[]{:S(2)}, u32[]{:S(2)}) collective-permute-start(bf16[192,768]{1,0:T(8,128)(2,1)} %param.26), channel_id=1, source_target_pairs={{0,2},{1,3},{2,0},{3,1},{4,6},{5,7},{6,4},{7,5},{8,10},{9,11},{10,... | collective-permute-start | bytes 884744 | tf_op jit(solution)/shard_map/ppermute | solution.py:63
  10.3 104.5 %collective-permute-start.3 = (bf16[192,768]{1,0:T(8,128)(2,1)}, bf16[192,768]{1,0:T(8,128)(2,1)}, u32[]{:S(2)}, u32[]{:S(2)}) collective-permute-start(bf16[192,768]{1,0:T(8,128)(2,1)} %param.26), channel_id=1, source_target_pairs={{0,1},{1,0},{2,3},{3,2},{4,5},{5,4},{6,7},{7,6},{8,9},{9,8},{10,11... | collective-permute-start | bytes 884744 | tf_op jit(solution)/shard_map/ppermute | solution.py:63
  10.3 46.3 %collective-permute-start = (bf16[3,768,192]{1,2,0:T(8,128)(2,1)}, bf16[3,768,192]{1,2,0:T(8,128)(2,1)}, u32[]{:S(2)}, u32[]{:S(2)}) collective-permute-start(bf16[3,768,192]{1,2,0:T(8,128)(2,1)} %param.25), channel_id=1, source_target_pairs={{0,2},{1,3},{2,0},{3,1},{4,6},{5,7},{6,4},{7,5},{8,10},{9,11},{10,... | collective-permute-start | bytes 2654216 | tf_op jit(solution)/shard_map/ppermute | solution.py:63
  10.5 40.8 %collective-permute-start.2 = (bf16[3,768,192]{1,2,0:T(8,128)(2,1)}, bf16[3,768,192]{1,2,0:T(8,128)(2,1)}, u32[]{:S(2)}, u32[]{:S(2)}) collective-permute-start(bf16[3,768,192]{1,2,0:T(8,128)(2,1)} %param.25), channel_id=1, source_target_pairs={{0,1},{1,0},{2,3},{3,2},{4,5},{5,4},{6,7},{7,6},{8,9},{9,8},{10,11... | collective-permute-start | bytes 2654216 | tf_op jit(solution)/shard_map/ppermute | solution.py:63
  10.9 262.4 %all-reduce.4.cloned.1.call-start = ((), (), s32[]{:S(2)}) async-start(), calls=%async_computation.1 | async-start | bytes 2949120 | tf_op jit(solution)/shard_map/psum | solution.py:220
  10.9 117.2 %collective-permute-start.6 = (bf16[768,768]{1,0:T(8,128)(2,1)}, bf16[768,768]{1,0:T(8,128)(2,1)}, u32[]{:S(2)}, u32[]{:S(2)}) collective-permute-start(bf16[768,768]{1,0:T(8,128)(2,1)} %param.27), channel_id=1, source_target_pairs={{0,2},{1,3},{2,0},{3,1},{4,6},{5,7},{6,4},{7,5},{8,10},{9,11},{10,... | collective-permute-start | bytes 3538952 | tf_op jit(solution)/shard_map/ppermute | solution.py:63
  15.8 5.3 copy-start.95
  17.7 193.8 %copy-start.66 = (f32[768]{0:T(1024)}, f32[768]{0:T(1024)S(1)}, u32[]{:S(2)}) copy-start(f32[768]{0:T(1024)S(1)} %get-tuple-element.47) | copy-start | bytes 9220
  18.3 193.2 %copy-start.85 = (f32[768]{0:T(1024)}, f32[768]{0:T(1024)S(1)}, u32[]{:S(2)}) copy-start(f32[768]{0:T(1024)S(1)} %get-tuple-element.49) | copy-start | bytes 9220
  51.3 126.4 %collective-permute-start.8 = (bf16[768,768]{1,0:T(8,128)(2,1)}, bf16[768,768]{1,0:T(8,128)(2,1)}, u32[]{:S(2)}, u32[]{:S(2)}) collective-permute-start(bf16[768,768]{1,0:T(8,128)(2,1)} %param.27), channel_id=1, source_target_pairs={{0,1},{1,0},{2,3},{3,2},{4,5},{5,4},{6,7},{7,6},{8,9},{9,8},{10,11... | collective-permute-start | bytes 3538952 | tf_op jit(solution)/shard_map/ppermute | solution.py:63
  56.6 71.8 %collective-permute-start.7 = (bf16[768,768]{1,0:T(8,128)(2,1)}, bf16[768,768]{1,0:T(8,128)(2,1)}, u32[]{:S(2)}, u32[]{:S(2)}) collective-permute-start(bf16[768,768]{1,0:T(8,128)(2,1)} %param.28), channel_id=1, source_target_pairs={{0,2},{1,3},{2,0},{3,1},{4,6},{5,7},{6,4},{7,5},{8,10},{9,11},{10,... | collective-permute-start | bytes 3538952 | tf_op jit(solution)/shard_map/ppermute | solution.py:63
  114.8 13.8 %collective-permute-start.4 = (bf16[3,768,192]{1,2,0:T(8,128)(2,1)}, bf16[3,768,192]{1,2,0:T(8,128)(2,1)}, u32[]{:S(2)}, u32[]{:S(2)}) collective-permute-start(bf16[3,768,192]{1,2,0:T(8,128)(2,1)} %collective-permute-done), channel_id=1, source_target_pairs={{0,1},{1,0},{2,3},{3,2},{4,5},{5,4},{6,7},{7,6},{8,9},{9,8},{10,11... | collective-permute-start | bytes 2654216 | tf_op jit(solution)/shard_map/ppermute | solution.py:63
  122.6 55.1 %collective-permute-start.9 = (bf16[768,768]{1,0:T(8,128)(2,1)}, bf16[768,768]{1,0:T(8,128)(2,1)}, u32[]{:S(2)}, u32[]{:S(2)}) collective-permute-start(bf16[768,768]{1,0:T(8,128)(2,1)} %param.28), channel_id=1, source_target_pairs={{0,1},{1,0},{2,3},{3,2},{4,5},{5,4},{6,7},{7,6},{8,9},{9,8},{10,11... | collective-permute-start | bytes 3538952 | tf_op jit(solution)/shard_map/ppermute | solution.py:63
  128.1 26.6 %collective-permute-start.5 = (bf16[192,768]{1,0:T(8,128)(2,1)}, bf16[192,768]{1,0:T(8,128)(2,1)}, u32[]{:S(2)}, u32[]{:S(2)}) collective-permute-start(bf16[192,768]{1,0:T(8,128)(2,1)} %collective-permute-done.1), channel_id=1, source_target_pairs={{0,1},{1,0},{2,3},{3,2},{4,5},{5,4},{6,7},{7,6},{8,9},{9,8},{10,11... | collective-permute-start | bytes 884744 | tf_op jit(solution)/shard_map/ppermute | solution.py:63
  128.4 102.0 %collective-permute-start.10 = (bf16[768,768]{1,0:T(8,128)(2,1)}, bf16[768,768]{1,0:T(8,128)(2,1)}, u32[]{:S(2)}, u32[]{:S(2)}) collective-permute-start(bf16[768,768]{1,0:T(8,128)(2,1)} %collective-permute-done.6), channel_id=1, source_target_pairs={{0,1},{1,0},{2,3},{3,2},{4,5},{5,4},{6,7},{7,6},{8,9},{9,8},{10,11... | collective-permute-start | bytes 3538952 | tf_op jit(solution)/shard_map/ppermute | solution.py:63
  128.6 101.8 %collective-permute-start.11 = (bf16[768,768]{1,0:T(8,128)(2,1)}, bf16[768,768]{1,0:T(8,128)(2,1)}, u32[]{:S(2)}, u32[]{:S(2)}) collective-permute-start(bf16[768,768]{1,0:T(8,128)(2,1)} %collective-permute-done.7), channel_id=1, source_target_pairs={{0,1},{1,0},{2,3},{3,2},{4,5},{5,4},{6,7},{7,6},{8,9},{9,8},{10,11... | collective-permute-start | bytes 3538952 | tf_op jit(solution)/shard_map/ppermute | solution.py:63
  156.9 36.1 %copy-start.13 = (f32[435,768]{1,0:T(8,128)}, f32[435,768]{1,0:T(8,128)S(1)}, u32[]{:S(2)}) copy-start(f32[435,768]{1,0:T(8,128)S(1)} %get-tuple-element.133) | copy-start | bytes 4008964
  161.9 38.8 %copy-start.52 = (bf16[600,768]{1,0:T(8,128)(2,1)}, bf16[600,768]{1,0:T(8,128)(2,1)S(1)}, u32[]{:S(2)}) copy-start(bf16[600,768]{1,0:T(8,128)(2,1)S(1)} %multiply_convert_fusion.1) | copy-start | bytes 2764804
  210.8 62.5 %copy-start.68 = (f32[960]{0:T(1024)}, f32[960]{0:T(1024)S(1)}, u32[]{:S(2)}) copy-start(f32[960]{0:T(1024)S(1)} %broadcast_multiply_fusion.4) | copy-start | bytes 11524
  211.4 61.8 %copy-start.72 = (f32[960]{0:T(1024)}, f32[960]{0:T(1024)S(1)}, u32[]{:S(2)}) copy-start(f32[960]{0:T(1024)S(1)} %add_rsqrt_fusion.3) | copy-start | bytes 11524
  230.2 376.4 %all-reduce.6.cloned.1.call-start = ((), (), s32[]{:S(2)}) async-start(), calls=%async_computation.2 | async-start | bytes 4718592 | tf_op jit(solution)/shard_map/psum | solution.py:285
  256.2 17.1 %copy-start.75 = (f32[768]{0:T(1024)S(1)}, f32[768]{0:T(1024)}, u32[]{:S(2)}) copy-start(f32[768]{0:T(1024)} %get-tuple-element.45) | copy-start | bytes 9220
  277.8 11.6 %copy-start.1 = (f32[960,768]{1,0:T(8,128)}, f32[960,768]{1,0:T(8,128)S(1)}, u32[]{:S(2)}) copy-start(f32[960,768]{1,0:T(8,128)S(1)} %get-tuple-element.62) | copy-start | bytes 8847364
  279.3 8.7 %copy-start.14 = (f32[960,768]{1,0:T(8,128)}, f32[960,768]{1,0:T(8,128)S(1)}, u32[]{:S(2)}) copy-start(f32[960,768]{1,0:T(8,128)S(1)} %subtract_multiply_fusion) | copy-start | bytes 8847364
  279.3 8.7 %copy-start.98 = (bf16[768,768]{1,0:T(8,128)(2,1)S(1)}, bf16[768,768]{1,0:T(8,128)(2,1)}, u32[]{:S(2)}) copy-start(bf16[768,768]{1,0:T(8,128)(2,1)} %param.34) | copy-start | bytes 3538948
  290.6 12.6 %copy-start.74 = (f32[768]{0:T(1024)S(1)}, f32[768]{0:T(1024)}, u32[]{:S(2)}) copy-start(f32[768]{0:T(1024)} %get-tuple-element.44) | copy-start | bytes 9220
  290.6 12.6 %copy-start.83 = (f32[60]{0:T(128)S(1)}, f32[60]{0:T(128)}, u32[]{:S(2)}) copy-start(f32[60]{0:T(128)} %get-tuple-element.57) | copy-start | bytes 724
  290.6 1.8 collective-permute-start.12
  292.5 10.7 %collective-permute-start.13 = (f32[120,768]{1,0:T(8,128)S(1)}, f32[120,768]{1,0:T(8,128)S(1)}, u32[]{:S(2)}, u32[]{:S(2)}) collective-permute-start(f32[120,768]{1,0:T(8,128)S(1)} %fusion.784), channel_id=1, source_target_pairs={{0,2},{1,3},{2,0},{3,1},{4,6},{5,7},{6,4},{7,5},{8,10},{9,11},{10,... | collective-permute-start | bytes 1105928 | tf_op jit(solution)/shard_map/ppermute | solution.py:63
  304.9 10.9 %collective-permute-start.14 = (bf16[120,768]{1,0:T(8,128)(2,1)}, bf16[120,768]{1,0:T(8,128)(2,1)S(1)}, u32[]{:S(2)}, u32[]{:S(2)}) collective-permute-start(bf16[120,768]{1,0:T(8,128)(2,1)} %pad_maximum_fusion.10), channel_id=1, source_target_pairs={{0,16},{4,20},{8,24},{12,28},{16,0},{20,4},{24,8},{28,12},{1,17},{... | collective-permute-start | bytes 552968 | tf_op jit(solution)/shard_map/ppermute | solution.py:63
  316.6 9.7 %collective-permute-start.15 = (bf16[2,120,768]{2,1,0:T(8,128)(2,1)S(1)}, bf16[2,120,768]{2,1,0:T(8,128)(2,1)}, u32[]{:S(2)}, u32[]{:S(2)}) collective-permute-start(bf16[2,120,768]{2,1,0:T(8,128)(2,1)S(1)} %pad_maximum_fusion.8), channel_id=1, source_target_pairs={{0,8},{4,12},{8,0},{12,4},{16,24},{20,28},{24,16},{28,20},{1,9},{5... | collective-permute-start | bytes 1105928 | tf_op jit(solution)/shard_map/ppermute | solution.py:63
  317.3 13.4 %copy-start.71 = (pred[60,16]{0,1:T(8,128)(4,1)S(1)}, pred[60,16]{0,1:T(8,128)(4,1)}, u32[]{:S(2)}) copy-start(pred[60,16]{0,1:T(8,128)(4,1)} %copy-done.70) | copy-start | bytes 2884
  329.2 16.9 %collective-permute-start.16 = (bf16[2,2,120,768]{3,2,1,0:T(8,128)(2,1)}, bf16[2,2,120,768]{3,2,1,0:T(8,128)(2,1)}, u32[]{:S(2)}, u32[]{:S(2)}) collective-permute-start(bf16[2,2,120,768]{3,2,1,0:T(8,128)(2,1)} %pad_maximum_fusion.3), channel_id=1, source_target_pairs={{0,4},{4,0},{8,12},{12,8},{16,20},{20,16},{24,28},{28,24},{1,5},{5... | collective-permute-start | bytes 2211848 | tf_op jit(solution)/shard_map/ppermute | solution.py:63
  353.3 6.1 copy-start.109
  368.3 2.6 collective-permute-start.17
  373.8 10.8 %collective-permute-start.18 = (bf16[240,768]{1,0:T(8,128)(2,1)S(1)}, bf16[240,768]{1,0:T(8,128)(2,1)}, u32[]{:S(2)}, u32[]{:S(2)}) collective-permute-start(bf16[240,768]{1,0:T(8,128)(2,1)S(1)} %fusion.312), channel_id=1, source_target_pairs={{0,2},{1,3},{2,0},{3,1},{4,6},{5,7},{6,4},{7,5},{8,10},{9,11},{10,... | collective-permute-start | bytes 1105928 | tf_op jit(solution)/shard_map/ppermute | solution.py:63
  385.9 9.9 %collective-permute-start.19 = (bf16[240,768]{1,0:T(8,128)(2,1)S(1)}, bf16[240,768]{1,0:T(8,128)(2,1)}, u32[]{:S(2)}, u32[]{:S(2)}) collective-permute-start(bf16[240,768]{1,0:T(8,128)(2,1)S(1)} %fusion.187), channel_id=1, source_target_pairs={{0,2},{1,3},{2,0},{3,1},{4,6},{5,7},{6,4},{7,5},{8,10},{9,11},{10,... | collective-permute-start | bytes 1105928 | tf_op jit(solution)/shard_map/ppermute | solution.py:63
  386.6 12.0 %copy-start.73 = (f32[960]{0:T(1024)S(1)}, f32[960]{0:T(1024)}, u32[]{:S(2)}) copy-start(f32[960]{0:T(1024)} %copy-done.72) | copy-start | bytes 11524
  386.6 14.3 %copy-start.88 = (f32[768]{0:T(1024)S(1)}, f32[768]{0:T(1024)}, u32[]{:S(2)}) copy-start(f32[768]{0:T(1024)} %get-tuple-element.48) | copy-start | bytes 9220
  398.6 7.1 %collective-permute-start.20 = (bf16[2,240,768]{2,1,0:T(8,128)(2,1)}, bf16[2,240,768]{2,1,0:T(8,128)(2,1)}, u32[]{:S(2)}, u32[]{:S(2)}) collective-permute-start(bf16[2,240,768]{2,1,0:T(8,128)(2,1)} %pad_maximum_fusion.4), channel_id=1, source_target_pairs={{0,1},{1,0},{2,3},{3,2},{4,5},{5,4},{6,7},{7,6},{8,9},{9,8},{10,11... | collective-permute-start | bytes 2211848 | tf_op jit(solution)/shard_map/ppermute | solution.py:63
  407.3 5.5 copy-start.27
  438.3 6.2 copy-start.7
  438.3 6.2 copy-start.67
  438.3 6.2 copy-start.69
  438.3 6.2 copy-start.86
  454.6 15.8 %collective-permute-start.23 = (bf16[2,2,96,768]{3,2,1,0:T(8,128)(2,1)S(1)}, bf16[2,2,96,768]{3,2,1,0:T(8,128)(2,1)S(1)}, u32[]{:S(2)}, u32[]{:S(2)}) collective-permute-start(bf16[2,2,96,768]{3,2,1,0:T(8,128)(2,1)S(1)} %fusion.289), channel_id=1, source_target_pairs={{0,4},{4,0},{8,12},{12,8},{16,20},{20,16},{24,28},{28,24},{1,5},{5... | collective-permute-start | bytes 1769480 | tf_op jit(solution)/shard_map/ppermute | solution.py:63
  457.6 15.5 %collective-permute-start.21 = (bf16[2,240,768]{2,1,0:T(8,128)(2,1)S(1)}, bf16[2,240,768]{2,1,0:T(8,128)(2,1)S(1)}, u32[]{:S(2)}, u32[]{:S(2)}) collective-permute-start(bf16[2,240,768]{2,1,0:T(8,128)(2,1)S(1)} %fusion.186), channel_id=1, source_target_pairs={{0,1},{1,0},{2,3},{3,2},{4,5},{5,4},{6,7},{7,6},{8,9},{9,8},{10,11... | collective-permute-start | bytes 2211848 | tf_op jit(solution)/shard_map/ppermute | solution.py:63
  470.5 9.4 %collective-permute-start.24 = (bf16[2,96,768]{2,1,0:T(8,128)(2,1)S(1)}, bf16[2,96,768]{2,1,0:T(8,128)(2,1)S(1)}, u32[]{:S(2)}, u32[]{:S(2)}) collective-permute-start(bf16[2,96,768]{2,1,0:T(8,128)(2,1)S(1)} %fusion.314), channel_id=1, source_target_pairs={{0,8},{4,12},{8,0},{12,4},{16,24},{20,28},{24,16},{28,20},{1,9},{5... | collective-permute-start | bytes 884744 | tf_op jit(solution)/shard_map/ppermute | solution.py:63
  473.3 10.4 %copy-start.45 = (bf16[768,768]{1,0:T(8,128)(2,1)S(1)}, bf16[768,768]{1,0:T(8,128)(2,1)}, u32[]{:S(2)}) copy-start(bf16[768,768]{1,0:T(8,128)(2,1)} %convolution_convert_fusion.2) | copy-start | bytes 3538948
  474.1 15.8 %collective-permute-start.22 = (bf16[240,768]{1,0:T(8,128)(2,1)}, bf16[240,768]{1,0:T(8,128)(2,1)}, u32[]{:S(2)}, u32[]{:S(2)}) collective-permute-start(bf16[240,768]{1,0:T(8,128)(2,1)} %fusion.313), channel_id=1, source_target_pairs={{0,2},{1,3},{2,0},{3,1},{4,6},{5,7},{6,4},{7,5},{8,10},{9,11},{10,... | collective-permute-start | bytes 1105928 | tf_op jit(solution)/shard_map/ppermute | solution.py:63
  480.0 9.7 %collective-permute-start.25 = (bf16[96,768]{1,0:T(8,128)(2,1)S(1)}, bf16[96,768]{1,0:T(8,128)(2,1)S(1)}, u32[]{:S(2)}, u32[]{:S(2)}) collective-permute-start(bf16[96,768]{1,0:T(8,128)(2,1)S(1)} %fusion.330), channel_id=1, source_target_pairs={{0,16},{4,20},{8,24},{12,28},{16,0},{20,4},{24,8},{28,12},{1,17},{... | collective-permute-start | bytes 442376 | tf_op jit(solution)/shard_map/ppermute | solution.py:63
  489.8 19.0 %collective-permute-start.26 = (bf16[96,768]{1,0:T(8,128)(2,1)S(1)}, bf16[96,768]{1,0:T(8,128)(2,1)S(1)}, u32[]{:S(2)}, u32[]{:S(2)}) collective-permute-start(bf16[96,768]{1,0:T(8,128)(2,1)S(1)} %fusion.315), channel_id=1, source_target_pairs={{0,16},{4,20},{8,24},{12,28},{16,0},{20,4},{24,8},{28,12},{1,17},{... | collective-permute-start | bytes 442376 | tf_op jit(solution)/shard_map/ppermute | solution.py:63
  494.0 1.3 collective-permute-start.29
  495.2 3.8 collective-permute-start.30
  508.8 20.5 %collective-permute-start.27 = (bf16[2,96,768]{2,1,0:T(8,128)(2,1)S(1)}, bf16[2,96,768]{2,1,0:T(8,128)(2,1)S(1)}, u32[]{:S(2)}, u32[]{:S(2)}) collective-permute-start(bf16[2,96,768]{2,1,0:T(8,128)(2,1)S(1)} %pad_maximum_fusion.9), channel_id=1, source_target_pairs={{0,8},{4,12},{8,0},{12,4},{16,24},{20,28},{24,16},{28,20},{1,9},{5... | collective-permute-start | bytes 884744 | tf_op jit(solution)/shard_map/ppermute | solution.py:63
  508.9 3.9 collective-permute-start.31
  512.8 16.5 %collective-permute-start.32 = (f32[8,768]{1,0:T(8,128)S(1)}, f32[8,768]{1,0:T(8,128)S(1)}, u32[]{:S(2)}, u32[]{:S(2)}) collective-permute-start(f32[8,768]{1,0:T(8,128)S(1)} %fusion.783), channel_id=1, source_target_pairs={{0,8},{4,12},{8,0},{12,4},{16,24},{20,28},{24,16},{28,20},{1,9},{5... | collective-permute-start | bytes 73736 | tf_op jit(solution)/shard_map/ppermute | solution.py:63
  529.3 81.4 %collective-permute-start.33 = (f32[8,768]{1,0:T(8,128)S(1)}, f32[8,768]{1,0:T(8,128)S(1)}, u32[]{:S(2)}, u32[]{:S(2)}) collective-permute-start(f32[8,768]{1,0:T(8,128)S(1)} %add.407), channel_id=1, source_target_pairs={{0,16},{4,20},{8,24},{12,28},{16,0},{20,4},{24,8},{28,12},{1,17},{... | collective-permute-start | bytes 73736 | tf_op jit(solution)/shard_map/ppermute | solution.py:63
  529.4 83.2 %collective-permute-start.28 = (bf16[2,2,96,768]{3,2,1,0:T(8,128)(2,1)S(1)}, bf16[2,2,96,768]{3,2,1,0:T(8,128)(2,1)S(1)}, u32[]{:S(2)}, u32[]{:S(2)}) collective-permute-start(bf16[2,2,96,768]{3,2,1,0:T(8,128)(2,1)S(1)} %pad_maximum_fusion.5), channel_id=1, source_target_pairs={{0,4},{4,0},{8,12},{12,8},{16,20},{20,16},{24,28},{28,24},{1,5},{5... | collective-permute-start | bytes 1769480 | tf_op jit(solution)/shard_map/ppermute | solution.py:63
  (83 other events, 185.1 us)
Sparse Core Ops, SparseCore 0:
  11.0 28.5 all-gather.1
  230.3 42.9 all-reduce.3
  485.4 121.1 all-reduce.5

commit v12 on v9

--- a/solution.py
+++ b/solution.py
@@ -144,14 +144,8 @@
     active = gelu_exact(jnp.dot(normed2, w_fc1, preferred_element_type=jnp.float32)).astype(
         jnp.bfloat16
     )
-    pool = (
-        lax.broadcasted_iota(jnp.int32, (count, count * length), 1) // length
-        == lax.broadcasted_iota(jnp.int32, (count, count * length), 0)
-    ).astype(jnp.bfloat16)
-    mean_active = jnp.dot(pool, active, preferred_element_type=jnp.float32) / length
-    pooled = jnp.mean(middle.reshape(count, length, D), 1) + jnp.dot(
-        mean_active, w_fc2.astype(jnp.float32), precision=lax.Precision.HIGHEST
-    )
+    result = middle + jnp.dot(active, w_fc2, preferred_element_type=jnp.float32)
+    pooled = jnp.mean(result.reshape(count, length, D), 1)
     return (pooled * lax.rsqrt(jnp.sum(pooled * pooled, -1, keepdims=True) + EPS)).astype(
         jnp.bfloat16
     )

time: 580 us -> 571 us (0.984)
  waiting for transfers between devices: 203 us -> 221 us
  other arithmetic: 89 us -> 78.9 us
  starting transfers between devices: 34.7 us -> 27.1 us
    ppermute x30, waiting for transfers between devices: 126 us -> 145 us  [exchange(): return lax.ppermute(values, axis, [(i, i ^ 1 << bit) for i in range(count)])]
    ppermute x30, starting transfers between devices: 34.1 us -> 26.5 us  [exchange(): return lax.ppermute(values, axis, [(i, i ^ 1 << bit) for i in range(count)])]
    dot_general x4 -> x2, matrix products: 43.4 us -> 45.5 us  [image_ffn(): result = middle + jnp.dot(active, w_fc2, preferred_element_type=jnp.float32)]
    unnamed x149 -> x169, local copies, waits for them, and re-layouts: 12.6 us -> 10.9 us
  transfers between devices with their start and end apart: 33 -> 33, of which waited for: 18 -> 19; matrix products, arithmetic and copies ran while one was open for 36% -> 29% of each run, Pallas kernels for 0% -> 0%
where the time goes in v12:
time: 571 us; the launch traced here: 562 us
  waiting for transfers between devices  221 us (39%)
  matrix products  113 us (20%)
  local copies, waits for them, and re-layouts  103 us (18%)
  other arithmetic  78.9 us (14%)
  starting transfers between devices  27.1 us (5%)
  between operations  18.8 us (3%)
    ppermute x30, waiting for transfers between devices, exchange(): return lax.ppermute(values, axis, [(i, i ^ 1 << bit) for i in range(count)])  145 us
    psum x1, waiting for transfers between devices, local_body(): lax.psum(jnp.concatenate([grad_fc1, grad_fc2], 0).astype(jnp.bfloat16), '...  75.9 us
    dot_general x2, matrix products, image_ffn(): result = middle + jnp.dot(active, w_fc2, preferred_element_type=jnp.float32)  45.5 us
    ppermute x30, starting transfers between devices, exchange(): return lax.ppermute(values, axis, [(i, i ^ 1 << bit) for i in range(count)])  26.5 us
    concatenate x8, other arithmetic, gather_stacked(): data = jnp.concatenate([data, exchange(data, axis, count, bit)], 0)  18.8 us
    squeeze x4, local copies, waits for them, and re-layouts, image_attention(): shares, _ = attention_shares(shaped[0], shaped[1], None)  14.7 us
  transfers between devices with their start and end apart: 33, of which 19 were waited for; matrix products, arithmetic and copies ran while one was open for 29% of the time, Pallas kernels for 0%

profile of v12, /device:TPU:0, one launch (start us, length us, event | category | flops | bytes accessed | tf_op | source)
XLA Modules:
  0.0 562.2 jit_solution(2187794574474158872)
XLA Ops:
  7.3 3.1 collective-permute-start
  19.7 24.8 %collective-permute-done.2 = bf16[1,192,768]{2,1,0:T(8,128)(2,1)} collective-permute-done((bf16[1,192,768]{2,1,0:T(8,128)(2,1)}, bf16[1,192,768]{2,1,0:T(8,128)(2,1)}, u32[]{:S(2)}, u32[]{:S(2)}) %collective-permute-start.2) | collective-permute-done | bytes 294944 | tf_op jit(solution)/shard_map/ppermute | solution.py:63
  45.7 2.5 pad_maximum_fusion.7
  54.6 2.4 fusion.127
  58.3 2.5 copy.94
  60.8 6.4 %reshape.297 = bf16[60,16,3,3,64]{4,3,1,0,2:T(4,128)(2,1)} reshape(bf16[960,3,192]{2,0,1:T(8,128)(2,1)} %copy.94) | data formatting | bytes 2211840 | tf_op jit(solution)/shard_map/reshape | solution.py:214
  67.2 3.2 fusion.213
  74.1 2.4 reshape.298
  78.7 2.2 pad_maximum_fusion.2
  84.1 3.3 reshape.331
  87.4 3.3 reshape.330
  90.7 3.0 fusion.68
  93.7 3.9 fusion.219
  97.6 2.3 reshape.329
  99.9 4.1 fusion.72
  106.1 4.1 reshape.307
  111.9 2.5 copy.108
  114.8 3.5 fusion.220
  118.3 2.5 convert_bitcast_fusion
  122.4 4.1 squeeze.70
  126.4 4.1 squeeze.69
  130.5 3.7 fusion.48
  134.1 3.1 fusion.221
  137.3 4.1 squeeze.68
  141.3 4.2 convert_bitcast_fusion.1
  147.4 4.4 reshape.302
  151.8 2.9 fusion.222
  156.3 4.0 fusion.212
  164.8 6.8 %collective-permute-done.4 = bf16[1,768,768]{1,2,0:T(8,128)(2,1)} collective-permute-done((bf16[1,768,768]{1,2,0:T(8,128)(2,1)}, bf16[1,768,768]{1,2,0:T(8,128)(2,1)}, u32[]{:S(2)}, u32[]{:S(2)}) %collective-permute-start.4) | collective-permute-done | bytes 1179680 | tf_op jit(solution)/shard_map/ppermute | solution.py:63
  173.2 8.6 %multiply_convert_fusion = (bf16[960,768]{1,0:T(8,128)(2,1)S(1)}, f32[960,768]{1,0:T(8,128)}, f32[960,768]{1,0:T(8,128)}) fusion(f32[768]{0:T(1024)S(1)} %copy-done.77, bf16[768,768]{1,0:T(8,128)(2,1)S(1)} %copy-done, f32[960,768]{1,0:T(8,128)S(1)} %subtract_multiply_fusion, f32[768]{0:T(1024)S(1)} %get-tuple-element.56, f32[768]{0:T(1024)S(1)} %get-tuple-element.54), kind=kOutput, calls=%fused_computation.67 | convolution fusion | flops 1183334400 | bytes 11510784 | tf_op jit(solution)/shard_map/dot_general | solution.py:235
  185.2 3.4 pad_maximum_fusion.1
  188.6 4.0 pad_maximum_fusion
  192.5 19.5 %fusion.65 = f32[435,768]{1,0:T(8,128)} fusion(f32[435,768]{1,0:T(8,128)S(1)} %copy-done.34, bf16[3072,768]{1,0:T(8,128)(2,1)} %bitcast.219, bf16[768,3072]{0,1:T(8,128)(2,1)} %bitcast.221, f32[768]{0:T(1024)S(1)} %get-tuple-element.58, f32[435]{0:T(512)S(1)} %add_rsqrt_fusion.4, f32[435]{0:T(512)S(1)} %broadcast_multiply_fusion.5), kind=kOutput, calls=%fused_computation.145 | convolution fusion | flops 4193706240 | bytes 12116376 | tf_op jit(solution)/shard_map/dot_general | solution.py:147
  213.8 26.0 %fusion.61 = f32[600,768]{1,0:T(8,128)} fusion(f32[600,768]{1,0:T(8,128)} %copy-done.27, bf16[3072,768]{1,0:T(8,128)(2,1)} %bitcast.220, bf16[768,3072]{0,1:T(8,128)(2,1)} %bitcast.222, f32[768]{0:T(1024)S(1)} %get-tuple-element.58, f32[600]{0:T(1024)S(1)} %add_rsqrt_fusion, f32[600]{0:T(1024)S(1)} %broadcast_multiply_fusion), kind=kOutput, calls=%fused_computation.127 | convolution fusion | flops 5784422400 | bytes 13131456 | tf_op jit(solution)/shard_map/dot_general | solution.py:147
  245.1 10.5 %collective-permute-done.9 = f32[120,768]{1,0:T(8,128)S(1)} collective-permute-done((f32[120,768]{1,0:T(8,128)S(1)}, f32[120,768]{1,0:T(8,128)S(1)}, u32[]{:S(2)}, u32[]{:S(2)}) %collective-permute-start.9) | collective-permute-done | bytes 368672 | tf_op jit(solution)/shard_map/ppermute | solution.py:63
  256.1 2.5 collective-permute-start.10
  258.6 8.5 %collective-permute-done.10 = bf16[120,768]{1,0:T(8,128)(2,1)S(1)} collective-permute-done((bf16[120,768]{1,0:T(8,128)(2,1)S(1)}, bf16[120,768]{1,0:T(8,128)(2,1)S(1)}, u32[]{:S(2)}, u32[]{:S(2)}) %collective-permute-start.10) | collective-permute-done | bytes 184352 | tf_op jit(solution)/shard_map/ppermute | solution.py:63
  267.8 9.1 %collective-permute-done.11 = bf16[2,120,768]{2,1,0:T(8,128)(2,1)S(1)} collective-permute-done((bf16[2,120,768]{2,1,0:T(8,128)(2,1)S(1)}, bf16[2,120,768]{2,1,0:T(8,128)(2,1)S(1)}, u32[]{:S(2)}, u32[]{:S(2)}) %collective-permute-start.11) | collective-permute-done | bytes 368672 | tf_op jit(solution)/shard_map/ppermute | solution.py:63
  279.6 15.0 %collective-permute-done.12 = bf16[2,2,120,768]{3,2,1,0:T(8,128)(2,1)S(1)} collective-permute-done((bf16[2,2,120,768]{3,2,1,0:T(8,128)(2,1)}, bf16[2,2,120,768]{3,2,1,0:T(8,128)(2,1)S(1)}, u32[]{:S(2)}, u32[]{:S(2)}) %collective-permute-start.12) | collective-permute-done | bytes 737312 | tf_op jit(solution)/shard_map/ppermute | solution.py:63
  298.4 2.7 select_reduce_fusion
  302.7 2.7 convert_reduce_fusion.1
  308.6 2.3 collective-permute-done.13
  313.2 10.4 %collective-permute-done.14 = bf16[240,768]{1,0:T(8,128)(2,1)} collective-permute-done((bf16[240,768]{1,0:T(8,128)(2,1)S(1)}, bf16[240,768]{1,0:T(8,128)(2,1)}, u32[]{:S(2)}, u32[]{:S(2)}) %collective-permute-start.14) | collective-permute-done | bytes 368672 | tf_op jit(solution)/shard_map/ppermute | solution.py:63
  325.1 9.4 %collective-permute-done.15 = bf16[240,768]{1,0:T(8,128)(2,1)S(1)} collective-permute-done((bf16[240,768]{1,0:T(8,128)(2,1)S(1)}, bf16[240,768]{1,0:T(8,128)(2,1)S(1)}, u32[]{:S(2)}, u32[]{:S(2)}) %collective-permute-start.15) | collective-permute-done | bytes 368672 | tf_op jit(solution)/shard_map/ppermute | solution.py:63
  336.1 4.7 convolution_convert_fusion.2
  341.6 2.3 copy-done.2
  344.7 5.4 bitcast_multiply_fusion
  355.7 2.5 convert_reduce_fusion.4
  371.3 2.3 fusion.126
  373.7 6.1 %dot_general.129 = bf16[2,2,240,3,192]{2,1,0,4,3:T(2,128)(2,1)} reshape(bf16[960,3,192]{0,2,1:T(8,128)(2,1)} %fusion.126) | data formatting | bytes 2211840 | tf_op jit(solution)/shard_map/jgw,jdw->gd/dot_general | solution.py:336
  379.8 3.6 convolution_bitcast_fusion.1
  385.5 2.2 reshape.314
  394.5 11.0 %collective-permute-done.19 = bf16[2,2,96,768]{3,2,1,0:T(8,128)(2,1)S(1)} collective-permute-done((bf16[2,2,96,768]{3,2,1,0:T(8,128)(2,1)S(1)}, bf16[2,2,96,768]{3,2,1,0:T(8,128)(2,1)S(1)}, u32[]{:S(2)}, u32[]{:S(2)}) %collective-permute-start.19) | collective-permute-done | bytes 589856 | tf_op jit(solution)/shard_map/ppermute | solution.py:63
  405.8 2.4 collective-permute-start.20
  409.6 5.4 collective-permute-done.20
  415.1 3.7 collective-permute-start.21
  426.6 2.4 dynamic-slice_reduce_fusion.2
  431.2 3.1 collective-permute-done.26
  434.2 9.7 %collective-permute-done.22 = bf16[96,768]{1,0:T(8,128)(2,1)S(1)} collective-permute-done((bf16[96,768]{1,0:T(8,128)(2,1)S(1)}, bf16[96,768]{1,0:T(8,128)(2,1)S(1)}, u32[]{:S(2)}, u32[]{:S(2)}) %collective-permute-start.22) | collective-permute-done | bytes 147488 | tf_op jit(solution)/shard_map/ppermute | solution.py:63
  445.5 2.5 collective-permute-done.27
  452.0 12.4 %collective-permute-done.28 = f32[8,768]{1,0:T(8,128)S(1)} collective-permute-done((f32[8,768]{1,0:T(8,128)S(1)}, f32[8,768]{1,0:T(8,128)S(1)}, u32[]{:S(2)}, u32[]{:S(2)}) %collective-permute-start.28) | collective-permute-done | bytes 24608 | tf_op jit(solution)/shard_map/ppermute | solution.py:63
  465.9 75.9 %all-reduce.6.cloned.1.call-done = bf16[1536,768]{1,0:T(8,128)(2,1)} async-done(((bf16[1536,768]{1,0:T(8,128)(2,1)}), bf16[1536,768]{1,0:T(8,128)(2,1)}) %all-reduce.6.cloned.1.call-update) | async-done | bytes 2359312 | tf_op jit(solution)/shard_map/psum | solution.py:292
  541.8 4.2 slice_convert_fusion
  550.3 2.2 reshape.321
  (392 shorter events, 121.6 us)
Async XLA Ops:
  7.2 166.0 %copy-start = (bf16[768,768]{1,0:T(8,128)(2,1)S(1)}, bf16[768,768]{1,0:T(8,128)(2,1)}, u32[]{:S(2)}) copy-start(bf16[768,768]{1,0:T(8,128)(2,1)} %param.32) | copy-start | bytes 3538948
  7.2 38.5 %copy-start.18 = (bf16[3,768,192]{1,2,0:T(8,128)(2,1)S(1)}, bf16[3,768,192]{1,2,0:T(8,128)(2,1)}, u32[]{:S(2)}) copy-start(bf16[3,768,192]{1,2,0:T(8,128)(2,1)} %param.25) | copy-start | bytes 2654212
  7.2 37.3 %copy-start.37 = (bf16[192,768]{1,0:T(8,128)(2,1)S(1)}, bf16[192,768]{1,0:T(8,128)(2,1)}, u32[]{:S(2)}) copy-start(bf16[192,768]{1,0:T(8,128)(2,1)} %param.26) | copy-start | bytes 884740
  7.2 11.9 %copy-start.16 = (bf16[600,768]{1,0:T(8,128)(2,1)S(1)}, bf16[600,768]{1,0:T(8,128)(2,1)}, u32[]{:S(2)}) copy-start(bf16[600,768]{1,0:T(8,128)(2,1)} %param.22) | copy-start | bytes 2764804
  7.2 12.3 %copy-start.73 = (f32[2,192]{1,0:T(2,128)S(1)}, f32[2,192]{1,0:T(2,128)}, u32[]{:S(2)}) copy-start(f32[2,192]{1,0:T(2,128)} %param.30) | copy-start | bytes 4612
  7.2 12.3 %copy-start.63 = (f32[2,768]{1,0:T(2,128)S(1)}, f32[2,768]{1,0:T(2,128)}, u32[]{:S(2)}) copy-start(f32[2,768]{1,0:T(2,128)} %param.35) | copy-start | bytes 18436
  7.2 43.6 %all-gather.2.cloned.1.call-start = ((), (), s32[]{:S(2)}) async-start(), calls=%async_computation | async-start | bytes 1843200 | tf_op jit(solution)/shard_map/all_gather | solution.py:206
  7.3 38.4 %collective-permute-start = (bf16[1,3,768,192]{2,3,0,1:T(8,128)(2,1)}, bf16[1,3,768,192]{2,3,0,1:T(8,128)(2,1)}, u32[]{:S(2)}, u32[]{:S(2)}) collective-permute-start(bf16[1,3,768,192]{2,3,0,1:T(8,128)(2,1)} %bitcast.225), channel_id=1, source_target_pairs={{0,2},{1,3},{2,0},{3,1},{4,6},{5,7},{6,4},{7,5},{8,10},{9,11},{10,... | collective-permute-start | bytes 2654216 | tf_op jit(solution)/shard_map/ppermute | solution.py:63
  10.4 34.2 %collective-permute-start.2 = (bf16[1,192,768]{2,1,0:T(8,128)(2,1)}, bf16[1,192,768]{2,1,0:T(8,128)(2,1)}, u32[]{:S(2)}, u32[]{:S(2)}) collective-permute-start(bf16[1,192,768]{2,1,0:T(8,128)(2,1)} %bitcast.234), channel_id=1, source_target_pairs={{0,2},{1,3},{2,0},{3,1},{4,6},{5,7},{6,4},{7,5},{8,10},{9,11},{10,... | collective-permute-start | bytes 884744 | tf_op jit(solution)/shard_map/ppermute | solution.py:63
  10.5 145.8 %all-reduce.4.cloned.1.call-start = ((), (), s32[]{:S(2)}) async-start(), calls=%async_computation.1 | async-start | bytes 2949120 | tf_op jit(solution)/shard_map/psum | solution.py:227
  11.7 36.5 %copy-start.57 = (pred[60,16]{0,1:T(8,128)(4,1)}, pred[60,16]{0,1:T(8,128)(4,1)S(1)}, u32[]{:S(2)}) copy-start(pred[60,16]{0,1:T(8,128)(4,1)S(1)} %get-tuple-element.66) | copy-start | bytes 2884
  17.5 37.1 %copy-start.66 = (f32[768]{0:T(1024)}, f32[768]{0:T(1024)S(1)}, u32[]{:S(2)}) copy-start(f32[768]{0:T(1024)S(1)} %get-tuple-element.57) | copy-start | bytes 9220
  17.5 155.7 %copy-start.68 = (f32[768]{0:T(1024)}, f32[768]{0:T(1024)S(1)}, u32[]{:S(2)}) copy-start(f32[768]{0:T(1024)S(1)} %get-tuple-element.56) | copy-start | bytes 9220
  19.6 35.0 %copy-start.53 = (f32[768]{0:T(1024)}, f32[768]{0:T(1024)S(1)}, u32[]{:S(2)}) copy-start(f32[768]{0:T(1024)S(1)} %get-tuple-element.55) | copy-start | bytes 9220
  19.6 153.6 %copy-start.49 = (f32[768]{0:T(1024)}, f32[768]{0:T(1024)S(1)}, u32[]{:S(2)}) copy-start(f32[768]{0:T(1024)S(1)} %get-tuple-element.54) | copy-start | bytes 9220
  45.6 3.2 collective-permute-start.3
  48.2 30.5 %collective-permute-start.1 = (bf16[2,3,768,192]{2,3,0,1:T(8,128)(2,1)}, bf16[2,3,768,192]{2,3,0,1:T(8,128)(2,1)}, u32[]{:S(2)}, u32[]{:S(2)}) collective-permute-start(bf16[2,3,768,192]{2,3,0,1:T(8,128)(2,1)} %pad_maximum_fusion.7), channel_id=1, source_target_pairs={{0,1},{1,0},{2,3},{3,2},{4,5},{5,4},{6,7},{7,6},{8,9},{9,8},{10,11... | collective-permute-start | bytes 5308424 | tf_op jit(solution)/shard_map/ppermute | solution.py:63
  52.6 103.7 %copy-start.55 = (f32[960]{0:T(1024)}, f32[960]{0:T(1024)S(1)}, u32[]{:S(2)}) copy-start(f32[960]{0:T(1024)S(1)} %broadcast_multiply_fusion.4) | copy-start | bytes 11524
  54.6 101.7 %copy-start.59 = (f32[960]{0:T(1024)}, f32[960]{0:T(1024)S(1)}, u32[]{:S(2)}) copy-start(f32[960]{0:T(1024)S(1)} %add_rsqrt_fusion.3) | copy-start | bytes 11524
  78.2 463.5 %all-reduce.6.cloned.1.call-start = ((), (), s32[]{:S(2)}) async-start(), calls=%async_computation.2 | async-start | bytes 4718592 | tf_op jit(solution)/shard_map/psum | solution.py:292
  110.2 51.6 %collective-permute-start.6 = (bf16[1,768,768]{2,1,0:T(8,128)(2,1)}, bf16[1,768,768]{2,1,0:T(8,128)(2,1)}, u32[]{:S(2)}, u32[]{:S(2)}) collective-permute-start(bf16[1,768,768]{2,1,0:T(8,128)(2,1)} %bitcast.216), channel_id=1, source_target_pairs={{0,2},{1,3},{2,0},{3,1},{4,6},{5,7},{6,4},{7,5},{8,10},{9,11},{10,... | collective-permute-start | bytes 3538952 | tf_op jit(solution)/shard_map/ppermute | solution.py:63
  114.4 57.2 %collective-permute-start.4 = (bf16[1,768,768]{1,2,0:T(8,128)(2,1)}, bf16[1,768,768]{1,2,0:T(8,128)(2,1)}, u32[]{:S(2)}, u32[]{:S(2)}) collective-permute-start(bf16[1,768,768]{1,2,0:T(8,128)(2,1)} %bitcast.210), channel_id=1, source_target_pairs={{0,2},{1,3},{2,0},{3,1},{4,6},{5,7},{6,4},{7,5},{8,10},{9,11},{10,... | collective-permute-start | bytes 3538952 | tf_op jit(solution)/shard_map/ppermute | solution.py:63
  160.3 22.9 %copy-start.1 = (f32[960,768]{1,0:T(8,128)}, f32[960,768]{1,0:T(8,128)S(1)}, u32[]{:S(2)}) copy-start(f32[960,768]{1,0:T(8,128)S(1)} %get-tuple-element.70) | copy-start | bytes 8847364
  161.8 11.4 %copy-start.13 = (f32[960,768]{1,0:T(8,128)}, f32[960,768]{1,0:T(8,128)S(1)}, u32[]{:S(2)}) copy-start(f32[960,768]{1,0:T(8,128)S(1)} %subtract_multiply_fusion) | copy-start | bytes 8847364
  161.8 9.8 %copy-start.10 = (bf16[768,768]{0,1:T(8,128)(2,1)S(1)}, bf16[768,768]{0,1:T(8,128)(2,1)}, u32[]{:S(2)}) copy-start(bf16[768,768]{0,1:T(8,128)(2,1)} %copy.108) | copy-start | bytes 3538948
  164.7 20.4 %collective-permute-start.7 = (bf16[2,768,768]{2,1,0:T(8,128)(2,1)S(1)}, bf16[2,768,768]{2,1,0:T(8,128)(2,1)S(1)}, u32[]{:S(2)}, u32[]{:S(2)}) collective-permute-start(bf16[2,768,768]{2,1,0:T(8,128)(2,1)S(1)} %pad_maximum_fusion.4), channel_id=1, source_target_pairs={{0,1},{1,0},{2,3},{3,2},{4,5},{5,4},{6,7},{7,6},{8,9},{9,8},{10,11... | collective-permute-start | bytes 7077896 | tf_op jit(solution)/shard_map/ppermute | solution.py:63
  173.1 15.5 %collective-permute-start.5 = (bf16[2,768,768]{1,2,0:T(8,128)(2,1)S(1)}, bf16[2,768,768]{1,2,0:T(8,128)(2,1)S(1)}, u32[]{:S(2)}, u32[]{:S(2)}) collective-permute-start(bf16[2,768,768]{1,2,0:T(8,128)(2,1)S(1)} %pad_maximum_fusion.3), channel_id=1, source_target_pairs={{0,1},{1,0},{2,3},{3,2},{4,5},{5,4},{6,7},{7,6},{8,9},{9,8},{10,11... | collective-permute-start | bytes 7077896 | tf_op jit(solution)/shard_map/ppermute | solution.py:63
  241.4 14.3 %copy-start.61 = (f32[768]{0:T(1024)S(1)}, f32[768]{0:T(1024)}, u32[]{:S(2)}) copy-start(f32[768]{0:T(1024)} %get-tuple-element.52) | copy-start | bytes 9220
  241.4 14.3 %copy-start.64 = (f32[60]{0:T(128)S(1)}, f32[60]{0:T(128)}, u32[]{:S(2)}) copy-start(f32[60]{0:T(128)} %get-tuple-element.65) | copy-start | bytes 724
  241.6 14.1 %copy-start.42 = (f32[60,768]{1,0:T(8,128)S(1)}, f32[60,768]{1,0:T(8,128)}, u32[]{:S(2)}) copy-start(f32[60,768]{1,0:T(8,128)} %get-tuple-element.50) | copy-start | bytes 552964
  242.8 1.8 collective-permute-start.8
  244.7 10.9 %collective-permute-start.9 = (f32[120,768]{1,0:T(8,128)S(1)}, f32[120,768]{1,0:T(8,128)S(1)}, u32[]{:S(2)}, u32[]{:S(2)}) collective-permute-start(f32[120,768]{1,0:T(8,128)S(1)} %fusion.257), channel_id=1, source_target_pairs={{0,2},{1,3},{2,0},{3,1},{4,6},{5,7},{6,4},{7,5},{8,10},{9,11},{10,... | collective-permute-start | bytes 1105928 | tf_op jit(solution)/shard_map/ppermute | solution.py:63
  255.7 23.6 %copy-start.58 = (pred[60,16]{0,1:T(8,128)(4,1)S(1)}, pred[60,16]{0,1:T(8,128)(4,1)}, u32[]{:S(2)}) copy-start(pred[60,16]{0,1:T(8,128)(4,1)} %copy-done.57) | copy-start | bytes 2884
  255.7 23.8 %copy-start.71 = (s32[480]{0:T(512)S(1)}, s32[480]{0:T(512)}, u32[]{:S(2)}) copy-start(s32[480]{0:T(512)} %param.21) | copy-start | bytes 5764
  256.1 11.0 %collective-permute-start.10 = (bf16[120,768]{1,0:T(8,128)(2,1)S(1)}, bf16[120,768]{1,0:T(8,128)(2,1)S(1)}, u32[]{:S(2)}, u32[]{:S(2)}) collective-permute-start(bf16[120,768]{1,0:T(8,128)(2,1)S(1)} %pad_maximum_fusion.18), channel_id=1, source_target_pairs={{0,16},{4,20},{8,24},{12,28},{16,0},{20,4},{24,8},{28,12},{1,17},{... | collective-permute-start | bytes 552968 | tf_op jit(solution)/shard_map/ppermute | solution.py:63
  267.2 9.7 %collective-permute-start.11 = (bf16[2,120,768]{2,1,0:T(8,128)(2,1)S(1)}, bf16[2,120,768]{2,1,0:T(8,128)(2,1)S(1)}, u32[]{:S(2)}, u32[]{:S(2)}) collective-permute-start(bf16[2,120,768]{2,1,0:T(8,128)(2,1)S(1)} %pad_maximum_fusion.16), channel_id=1, source_target_pairs={{0,8},{4,12},{8,0},{12,4},{16,24},{20,28},{24,16},{28,20},{1,9},{5... | collective-permute-start | bytes 1105928 | tf_op jit(solution)/shard_map/ppermute | solution.py:63
  277.8 16.8 %collective-permute-start.12 = (bf16[2,2,120,768]{3,2,1,0:T(8,128)(2,1)}, bf16[2,2,120,768]{3,2,1,0:T(8,128)(2,1)S(1)}, u32[]{:S(2)}, u32[]{:S(2)}) collective-permute-start(bf16[2,2,120,768]{3,2,1,0:T(8,128)(2,1)} %pad_maximum_fusion.10), channel_id=1, source_target_pairs={{0,4},{4,0},{8,12},{12,8},{16,20},{20,16},{24,28},{28,24},{1,5},{5... | collective-permute-start | bytes 2211848 | tf_op jit(solution)/shard_map/ppermute | solution.py:63
  308.5 2.4 collective-permute-start.13
  312.7 22.8 %copy-start.60 = (f32[960]{0:T(1024)S(1)}, f32[960]{0:T(1024)}, u32[]{:S(2)}) copy-start(f32[960]{0:T(1024)} %copy-done.59) | copy-start | bytes 11524
  312.7 23.4 %copy-start.44 = (f32[60,3,16]{2,1,0:T(4,128)S(1)}, f32[60,3,16]{2,1,0:T(4,128)}, u32[]{:S(2)}) copy-start(f32[60,3,16]{2,1,0:T(4,128)} %copy-done.43) | copy-start | bytes 34564
  312.7 23.4 %copy-start.46 = (f32[60,3,16]{2,1,0:T(4,128)S(1)}, f32[60,3,16]{2,1,0:T(4,128)}, u32[]{:S(2)}) copy-start(f32[60,3,16]{2,1,0:T(4,128)} %copy-done.45) | copy-start | bytes 34564
  312.7 23.4 %copy-start.50 = (f32[768]{0:T(1024)S(1)}, f32[768]{0:T(1024)}, u32[]{:S(2)}) copy-start(f32[768]{0:T(1024)} %copy-done.49) | copy-start | bytes 9220
  312.7 23.4 %copy-start.69 = (f32[768]{0:T(1024)S(1)}, f32[768]{0:T(1024)}, u32[]{:S(2)}) copy-start(f32[768]{0:T(1024)} %copy-done.68) | copy-start | bytes 9220
  312.8 10.8 %collective-permute-start.14 = (bf16[240,768]{1,0:T(8,128)(2,1)S(1)}, bf16[240,768]{1,0:T(8,128)(2,1)}, u32[]{:S(2)}, u32[]{:S(2)}) collective-permute-start(bf16[240,768]{1,0:T(8,128)(2,1)S(1)} %fusion.129), channel_id=1, source_target_pairs={{0,2},{1,3},{2,0},{3,1},{4,6},{5,7},{6,4},{7,5},{8,10},{9,11},{10,... | collective-permute-start | bytes 1105928 | tf_op jit(solution)/shard_map/ppermute | solution.py:63
  324.6 9.8 %collective-permute-start.15 = (bf16[240,768]{1,0:T(8,128)(2,1)S(1)}, bf16[240,768]{1,0:T(8,128)(2,1)S(1)}, u32[]{:S(2)}, u32[]{:S(2)}) collective-permute-start(bf16[240,768]{1,0:T(8,128)(2,1)S(1)} %fusion.103), channel_id=1, source_target_pairs={{0,2},{1,3},{2,0},{3,1},{4,6},{5,7},{6,4},{7,5},{8,10},{9,11},{10,... | collective-permute-start | bytes 1105928 | tf_op jit(solution)/shard_map/ppermute | solution.py:63
  335.5 5.4 collective-permute-start.16
  370.4 9.4 %copy-start.9 = (bf16[960,768]{1,0:T(8,128)(2,1)S(1)}, bf16[960,768]{1,0:T(8,128)(2,1)}, u32[]{:S(2)}) copy-start(bf16[960,768]{1,0:T(8,128)(2,1)} %all-gather.2.cloned.1.call-done) | copy-start | bytes 4423684
  370.4 9.4 %copy-start.54 = (f32[768]{0:T(1024)S(1)}, f32[768]{0:T(1024)}, u32[]{:S(2)}) copy-start(f32[768]{0:T(1024)} %copy-done.53) | copy-start | bytes 9220
  370.4 9.4 %copy-start.56 = (f32[960]{0:T(1024)S(1)}, f32[960]{0:T(1024)}, u32[]{:S(2)}) copy-start(f32[960]{0:T(1024)} %copy-done.55) | copy-start | bytes 11524
  370.4 9.4 %copy-start.67 = (f32[768]{0:T(1024)S(1)}, f32[768]{0:T(1024)}, u32[]{:S(2)}) copy-start(f32[768]{0:T(1024)} %copy-done.66) | copy-start | bytes 9220
  389.8 15.8 %collective-permute-start.19 = (bf16[2,2,96,768]{3,2,1,0:T(8,128)(2,1)S(1)}, bf16[2,2,96,768]{3,2,1,0:T(8,128)(2,1)S(1)}, u32[]{:S(2)}, u32[]{:S(2)}) collective-permute-start(bf16[2,2,96,768]{3,2,1,0:T(8,128)(2,1)S(1)} %fusion.122), channel_id=1, source_target_pairs={{0,4},{4,0},{8,12},{12,8},{16,20},{20,16},{24,28},{28,24},{1,5},{5... | collective-permute-start | bytes 1769480 | tf_op jit(solution)/shard_map/ppermute | solution.py:63
  392.8 15.4 %collective-permute-start.17 = (bf16[2,240,768]{2,1,0:T(8,128)(2,1)S(1)}, bf16[2,240,768]{2,1,0:T(8,128)(2,1)S(1)}, u32[]{:S(2)}, u32[]{:S(2)}) collective-permute-start(bf16[2,240,768]{2,1,0:T(8,128)(2,1)S(1)} %fusion.102), channel_id=1, source_target_pairs={{0,1},{1,0},{2,3},{3,2},{4,5},{5,4},{6,7},{7,6},{8,9},{9,8},{10,11... | collective-permute-start | bytes 2211848 | tf_op jit(solution)/shard_map/ppermute | solution.py:63
  405.8 13.1 %copy-start.39 = (bf16[768,768]{1,0:T(8,128)(2,1)S(1)}, bf16[768,768]{1,0:T(8,128)(2,1)}, u32[]{:S(2)}) copy-start(bf16[768,768]{1,0:T(8,128)(2,1)} %convolution_convert_fusion.2) | copy-start | bytes 3538948
  405.8 9.2 %collective-permute-start.20 = (bf16[2,96,768]{2,1,0:T(8,128)(2,1)S(1)}, bf16[2,96,768]{2,1,0:T(8,128)(2,1)S(1)}, u32[]{:S(2)}, u32[]{:S(2)}) collective-permute-start(bf16[2,96,768]{2,1,0:T(8,128)(2,1)S(1)} %fusion.131), channel_id=1, source_target_pairs={{0,8},{4,12},{8,0},{12,4},{16,24},{20,28},{24,16},{28,20},{1,9},{5... | collective-permute-start | bytes 884744 | tf_op jit(solution)/shard_map/ppermute | solution.py:63
  409.1 15.9 %collective-permute-start.18 = (bf16[240,768]{1,0:T(8,128)(2,1)}, bf16[240,768]{1,0:T(8,128)(2,1)}, u32[]{:S(2)}, u32[]{:S(2)}) collective-permute-start(bf16[240,768]{1,0:T(8,128)(2,1)} %fusion.130), channel_id=1, source_target_pairs={{0,2},{1,3},{2,0},{3,1},{4,6},{5,7},{6,4},{7,5},{8,10},{9,11},{10,... | collective-permute-start | bytes 1105928 | tf_op jit(solution)/shard_map/ppermute | solution.py:63
  415.1 9.8 %collective-permute-start.21 = (bf16[96,768]{1,0:T(8,128)(2,1)S(1)}, bf16[96,768]{1,0:T(8,128)(2,1)S(1)}, u32[]{:S(2)}, u32[]{:S(2)}) collective-permute-start(bf16[96,768]{1,0:T(8,128)(2,1)S(1)} %fusion.135), channel_id=1, source_target_pairs={{0,16},{4,20},{8,24},{12,28},{16,0},{20,4},{24,8},{28,12},{1,17},{... | collective-permute-start | bytes 442376 | tf_op jit(solution)/shard_map/ppermute | solution.py:63
  425.0 18.9 %collective-permute-start.22 = (bf16[96,768]{1,0:T(8,128)(2,1)S(1)}, bf16[96,768]{1,0:T(8,128)(2,1)S(1)}, u32[]{:S(2)}, u32[]{:S(2)}) collective-permute-start(bf16[96,768]{1,0:T(8,128)(2,1)S(1)} %fusion.132), channel_id=1, source_target_pairs={{0,16},{4,20},{8,24},{12,28},{16,0},{20,4},{24,8},{28,12},{1,17},{... | collective-permute-start | bytes 442376 | tf_op jit(solution)/shard_map/ppermute | solution.py:63
  429.1 1.3 collective-permute-start.25
  430.4 3.8 collective-permute-start.26
  444.0 20.5 %collective-permute-start.23 = (bf16[2,96,768]{2,1,0:T(8,128)(2,1)S(1)}, bf16[2,96,768]{2,1,0:T(8,128)(2,1)S(1)}, u32[]{:S(2)}, u32[]{:S(2)}) collective-permute-start(bf16[2,96,768]{2,1,0:T(8,128)(2,1)S(1)} %pad_maximum_fusion.17), channel_id=1, source_target_pairs={{0,8},{4,12},{8,0},{12,4},{16,24},{20,28},{24,16},{28,20},{1,9},{5... | collective-permute-start | bytes 884744 | tf_op jit(solution)/shard_map/ppermute | solution.py:63
  444.1 3.9 collective-permute-start.27
  448.0 16.4 %collective-permute-start.28 = (f32[8,768]{1,0:T(8,128)S(1)}, f32[8,768]{1,0:T(8,128)S(1)}, u32[]{:S(2)}, u32[]{:S(2)}) collective-permute-start(f32[8,768]{1,0:T(8,128)S(1)} %fusion.256), channel_id=1, source_target_pairs={{0,8},{4,12},{8,0},{12,4},{16,24},{20,28},{24,16},{28,20},{1,9},{5... | collective-permute-start | bytes 73736 | tf_op jit(solution)/shard_map/ppermute | solution.py:63
  464.4 81.5 %collective-permute-start.29 = (f32[8,768]{1,0:T(8,128)S(1)}, f32[8,768]{1,0:T(8,128)S(1)}, u32[]{:S(2)}, u32[]{:S(2)}) collective-permute-start(f32[8,768]{1,0:T(8,128)S(1)} %add.359), channel_id=1, source_target_pairs={{0,16},{4,20},{8,24},{12,28},{16,0},{20,4},{24,8},{28,12},{1,17},{... | collective-permute-start | bytes 73736 | tf_op jit(solution)/shard_map/ppermute | solution.py:63
  464.5 83.3 %collective-permute-start.24 = (bf16[2,2,96,768]{3,2,1,0:T(8,128)(2,1)S(1)}, bf16[2,2,96,768]{3,2,1,0:T(8,128)(2,1)S(1)}, u32[]{:S(2)}, u32[]{:S(2)}) collective-permute-start(bf16[2,2,96,768]{3,2,1,0:T(8,128)(2,1)S(1)} %pad_maximum_fusion.13), channel_id=1, source_target_pairs={{0,4},{4,0},{8,12},{12,8},{16,20},{20,16},{24,28},{28,24},{1,5},{5... | collective-permute-start | bytes 1769480 | tf_op jit(solution)/shard_map/ppermute | solution.py:63
  (53 other events, 178.3 us)
Sparse Core Ops, SparseCore 0:
  10.6 28.8 all-gather.1
  78.3 50.8 all-reduce.3
  420.5 121.1 all-reduce.5

commit v13 on v7

--- a/solution.py
+++ b/solution.py
@@ -199,7 +199,7 @@
     present = (caption_ids > 0).astype(jnp.float32)
     keep = (caption_ids > 0)[:, None, None, :]
     counts = jnp.sum(present, 1, keepdims=True)
-    inputs = lax.all_gather(text_in, "mp", axis=0, tiled=True).astype(jnp.float32)
+    inputs = gather_ordered(text_in, "mp").reshape(-1, D).astype(jnp.float32)
     unit1, inverse1 = layer_stats(inputs)
     normed1_all = (unit1 * txt_gains[0] + txt_shifts[0]).astype(jnp.bfloat16)
     bias_rows = jnp.stack([txt_qv_bias[0], jnp.zeros_like(txt_qv_bias[0]), txt_qv_bias[1]])
@@ -239,17 +239,16 @@
         mp_index * own_caps,
         0,
     )
-    both = sum_exchanged(jnp.concatenate([ffn_pooled, image_slots], 0), "mp")
+    images_all = gather_ordered(
+        sum_exchanged(image_slots.astype(jnp.bfloat16), "mp"), "dp"
+    ).reshape(-1, D)
+    ffn_sum = sum_exchanged(ffn_pooled, "mp")
     mid_pooled = jnp.sum(middle.reshape(group_caps, L, D) * present[:, :, None], 1)
-    pooled = (mid_pooled + both[:group_caps]) / counts + txt_biases[1]
+    pooled = (mid_pooled + ffn_sum) / counts + txt_biases[1]
     inverse_len = lax.rsqrt(jnp.sum(pooled * pooled, -1, keepdims=True) + EPS)
     captions_unit = pooled * inverse_len
     captions16 = captions_unit.astype(jnp.bfloat16)
-    gathered = gather_ordered(
-        jnp.concatenate([captions16, both[group_caps:].astype(jnp.bfloat16)], 0), "dp"
-    )
-    arrived = gathered[:, :group_caps].reshape(-1, D)
-    images_all = gathered[:, group_caps:].reshape(-1, D)
+    arrived = gather_ordered(captions16, "dp").reshape(-1, D)
     total_pairs = pairing.shape[0]
     first_pair = lax.axis_index("dp") * group_caps
     logits = SCALE * jnp.einsum("id,jd->ij", images_all, arrived, preferred_element_type=jnp.float32)

time: 604 us -> 593 us (0.982)
    ppermute x30 -> x37, waiting for transfers between devices: 159 us -> 101 us  [exchange(): return lax.ppermute(values, axis, [(i, i ^ 1 << bit) for i in range(count)])]
    psum x1, waiting for transfers between devices: 0.02 us -> 55.1 us  [local_body(): lax.psum(jnp.dot(context, txt_out, preferred_element_type=jnp.float32).as...]
    ppermute x30 -> x37, starting transfers between devices: 34.6 us -> 29.6 us  [exchange(): return lax.ppermute(values, axis, [(i, i ^ 1 << bit) for i in range(count)])]
    unnamed x194 -> x208, local copies, waits for them, and re-layouts: 12.2 us -> 11.8 us
  transfers between devices with their start and end apart: 33 -> 39, of which waited for: 20 -> 22; matrix products, arithmetic and copies ran while one was open for 29% -> 40% of each run, Pallas kernels for 0% -> 0%
where the time goes in v13:
time: 593 us; the launch traced here: 582 us
  waiting for transfers between devices  233 us (39%)
  matrix products  108 us (18%)
  local copies, waits for them, and re-layouts  100 us (17%)
  other arithmetic  91.8 us (15%)
  starting transfers between devices  29.7 us (5%)
  between operations  19.4 us (3%)
    ppermute x37, waiting for transfers between devices, exchange(): return lax.ppermute(values, axis, [(i, i ^ 1 << bit) for i in range(count)])  101 us
    psum x1, waiting for transfers between devices, local_body(): lax.psum(jnp.concatenate([grad_fc1, grad_fc2], 0).astype(jnp.bfloat16), '...  76.8 us
    psum x1, waiting for transfers between devices, local_body(): lax.psum(jnp.dot(context, txt_out, preferred_element_type=jnp.float32).as...  55.1 us
    dot_general x2, matrix products, image_ffn(): result = middle + jnp.dot(active, w_fc2, preferred_element_type=jnp.float32)  46.6 us
    ppermute x37, starting transfers between devices, exchange(): return lax.ppermute(values, axis, [(i, i ^ 1 << bit) for i in range(count)])  29.6 us
    concatenate x8, other arithmetic, gather_stacked(): data = jnp.concatenate([data, exchange(data, axis, count, bit)], 0)  21.7 us
    squeeze x4, local copies, waits for them, and re-layouts, image_attention(): shares, _ = attention_shares(shaped[0], shaped[1], None)  15.1 us
  transfers between devices with their start and end apart: 39, of which 22 were waited for; matrix products, arithmetic and copies ran while one was open for 40% of the time, Pallas kernels for 0%

profile of v13, /device:TPU:0, one launch (start us, length us, event | category | flops | bytes accessed | tf_op | source)
XLA Modules:
  0.0 582.3 jit_solution(1307783137501861214)
XLA Ops:
  7.3 3.1 collective-permute-start.2
  20.7 5.7 collective-permute-done.13
  39.9 6.5 %reshape.318 = bf16[60,16,3,3,64]{4,3,1,0,2:T(4,128)(2,1)} reshape(bf16[960,3,192]{2,0,1:T(8,128)(2,1)} %copy.214) | data formatting | bytes 2211840 | tf_op jit(solution)/shard_map/reshape | solution.py:210
  46.4 3.2 fusion.207
  53.2 2.5 reshape.319
  55.7 2.8 convolution_convert_fusion
  60.9 2.8 pad_maximum_fusion.7
  64.0 55.1 %all-reduce.4.cloned.1.call-done = bf16[960,768]{1,0:T(8,128)(2,1)} async-done(((bf16[960,768]{1,0:T(8,128)(2,1)}), bf16[960,768]{1,0:T(8,128)(2,1)}) %all-reduce.4.cloned.1.call-update) | async-done | bytes 1474576 | tf_op jit(solution)/shard_map/psum | solution.py:223
  119.2 4.2 add_add_fusion
  125.4 2.4 multiply_reduce_fusion.4
  128.8 8.8 %multiply_convert_fusion = (bf16[960,768]{1,0:T(8,128)(2,1)S(1)}, f32[960,768]{1,0:T(8,128)}, f32[960,768]{1,0:T(8,128)}) fusion(f32[768]{0:T(1024)S(1)} %copy-done.94, bf16[768,768]{1,0:T(8,128)(2,1)S(1)} %copy-done, f32[960,768]{1,0:T(8,128)S(1)} %subtract_multiply_fusion.1, f32[768]{0:T(1024)S(1)} %copy-done.81, f32[768]{0:T(1024)S(1)} %get-tuple-element.68), kind=kOutput, calls=%fused_computation.64 | convolution fusion | flops 1183334400 | bytes 11510784 | tf_op jit(solution)/shard_map/dot_general | solution.py:231
  145.1 2.3 pad_maximum_fusion.10
  147.4 3.0 pad_maximum_fusion.3
  150.7 2.7 collective-permute-start.17
  153.5 2.9 pad_maximum_fusion.4
  156.5 2.5 collective-permute-done.17
  164.6 2.5 convert_bitcast_fusion.2
  170.0 3.3 reshape.340
  173.3 4.0 squeeze.65
  177.3 3.3 reshape.342
  180.6 3.7 reshape.341
  184.3 2.9 fusion.67
  187.3 4.5 fusion.212
  191.8 4.0 squeeze.67
  195.8 4.1 squeeze.66
  199.9 3.9 fusion.46
  203.8 6.8 %fusion.214 = (f32[12,12,50]{2,1,0:T(8,128)S(1)}, f32[12,12,50,50]{2,3,1,0:T(8,128)S(1)}) fusion(f32[12,12,50,50]{2,3,1,0:T(8,128)S(1)} %fusion.46), kind=kOutput, calls=%fused_computation.407 | output fusion | flops 1440049 | bytes 2908800 | tf_op jit(solution)/shard_map/sub | solution.py:50
  212.3 2.7 convert_bitcast_fusion.3
  217.2 3.9 reshape.316
  221.1 3.4 copy.199
  224.6 4.2 reshape.311
  228.8 2.7 fusion.213
  236.1 3.8 pad_maximum_fusion
  239.8 4.0 pad_maximum_fusion.1
  243.8 20.3 %fusion.64 = f32[435,768]{1,0:T(8,128)} fusion(f32[435,768]{1,0:T(8,128)} %copy-done.34, bf16[3072,768]{1,0:T(8,128)(2,1)} %bitcast.251, bf16[768,3072]{0,1:T(8,128)(2,1)} %bitcast.249, f32[768]{0:T(1024)S(1)} %get-tuple-element.72, f32[435]{0:T(512)S(1)} %copy-done.89, f32[435]{0:T(512)S(1)} %broadcast_multiply_fusion.5), kind=kOutput, calls=%fused_computation.146 | convolution fusion | flops 4193706240 | bytes 12116376 | tf_op jit(solution)/shard_map/dot_general | solution.py:147
  265.9 26.3 %fusion.59 = f32[600,768]{1,0:T(8,128)} fusion(f32[600,768]{1,0:T(8,128)} %copy-done.27, bf16[3072,768]{1,0:T(8,128)(2,1)} %bitcast.252, bf16[768,3072]{0,1:T(8,128)(2,1)} %bitcast.250, f32[768]{0:T(1024)S(1)} %get-tuple-element.72, f32[600]{0:T(1024)S(1)} %add_rsqrt_fusion.2, f32[600]{0:T(1024)S(1)} %broadcast_multiply_fusion.3), kind=kOutput, calls=%fused_computation.127 | convolution fusion | flops 5784422400 | bytes 13131456 | tf_op jit(solution)/shard_map/dot_general | solution.py:147
  297.5 3.5 collective-permute-done.9
  301.1 3.3 collective-permute-start.10
  306.0 2.8 collective-permute-done.10
  309.1 6.4 %collective-permute-done.11 = bf16[2,60,768]{2,1,0:T(8,128)(2,1)S(1)} collective-permute-done((bf16[2,60,768]{2,1,0:T(8,128)(2,1)S(1)}, bf16[2,60,768]{2,1,0:T(8,128)(2,1)S(1)}, u32[]{:S(2)}, u32[]{:S(2)}) %collective-permute-start.11) | collective-permute-done | bytes 184352 | tf_op jit(solution)/shard_map/ppermute | solution.py:63
  318.3 7.3 %collective-permute-done.12 = bf16[2,2,60,768]{3,2,1,0:T(8,128)(2,1)} collective-permute-done((bf16[2,2,60,768]{3,2,1,0:T(8,128)(2,1)S(1)}, bf16[2,2,60,768]{3,2,1,0:T(8,128)(2,1)}, u32[]{:S(2)}, u32[]{:S(2)}) %collective-permute-start.12) | collective-permute-done | bytes 368672 | tf_op jit(solution)/shard_map/ppermute | solution.py:63
  327.1 2.7 select_reduce_fusion
  332.1 2.7 convert_reduce_fusion
  338.0 2.3 collective-permute-done.20
  342.5 10.4 %collective-permute-done.21 = bf16[240,768]{1,0:T(8,128)(2,1)} collective-permute-done((bf16[240,768]{1,0:T(8,128)(2,1)S(1)}, bf16[240,768]{1,0:T(8,128)(2,1)}, u32[]{:S(2)}, u32[]{:S(2)}) %collective-permute-start.21) | collective-permute-done | bytes 368672 | tf_op jit(solution)/shard_map/ppermute | solution.py:63
  354.5 9.4 %collective-permute-done.22 = bf16[240,768]{1,0:T(8,128)(2,1)S(1)} collective-permute-done((bf16[240,768]{1,0:T(8,128)(2,1)S(1)}, bf16[240,768]{1,0:T(8,128)(2,1)S(1)}, u32[]{:S(2)}, u32[]{:S(2)}) %collective-permute-start.22) | collective-permute-done | bytes 368672 | tf_op jit(solution)/shard_map/ppermute | solution.py:63
  365.7 3.9 convolution_convert_fusion.2
  372.0 2.2 copy.225
  375.8 2.7 bitcast_multiply_fusion
  384.2 2.3 multiply_reduce_fusion.8
  399.5 4.3 convolution_bitcast_fusion.1
  405.9 2.2 copy.240
  408.1 2.2 reshape.324
  417.1 11.0 %collective-permute-done.26 = bf16[2,2,96,768]{3,2,1,0:T(8,128)(2,1)S(1)} collective-permute-done((bf16[2,2,96,768]{3,2,1,0:T(8,128)(2,1)S(1)}, bf16[2,2,96,768]{3,2,1,0:T(8,128)(2,1)S(1)}, u32[]{:S(2)}, u32[]{:S(2)}) %collective-permute-start.26) | collective-permute-done | bytes 589856 | tf_op jit(solution)/shard_map/ppermute | solution.py:63
  430.2 6.7 %collective-permute-done.27 = bf16[2,96,768]{2,1,0:T(8,128)(2,1)S(1)} collective-permute-done((bf16[2,96,768]{2,1,0:T(8,128)(2,1)S(1)}, bf16[2,96,768]{2,1,0:T(8,128)(2,1)S(1)}, u32[]{:S(2)}, u32[]{:S(2)}) %collective-permute-start.27) | collective-permute-done | bytes 294944 | tf_op jit(solution)/shard_map/ppermute | solution.py:63
  441.4 4.4 collective-permute-done.28
  447.5 2.4 dynamic-slice_reduce_fusion.2
  451.7 3.4 collective-permute-done.33
  455.1 7.4 %collective-permute-done.29 = bf16[96,768]{1,0:T(8,128)(2,1)S(1)} collective-permute-done((bf16[96,768]{1,0:T(8,128)(2,1)S(1)}, bf16[96,768]{1,0:T(8,128)(2,1)S(1)}, u32[]{:S(2)}, u32[]{:S(2)}) %collective-permute-start.29) | collective-permute-done | bytes 147488 | tf_op jit(solution)/shard_map/ppermute | solution.py:63
  464.3 2.3 collective-permute-done.34
  470.5 12.3 %collective-permute-done.35 = f32[8,768]{1,0:T(8,128)S(1)} collective-permute-done((f32[8,768]{1,0:T(8,128)S(1)}, f32[8,768]{1,0:T(8,128)S(1)}, u32[]{:S(2)}, u32[]{:S(2)}) %collective-permute-start.35) | collective-permute-done | bytes 24608 | tf_op jit(solution)/shard_map/ppermute | solution.py:63
  484.5 76.8 %all-reduce.6.cloned.1.call-done = bf16[1536,768]{1,0:T(8,128)(2,1)} async-done(((bf16[1536,768]{1,0:T(8,128)(2,1)}), bf16[1536,768]{1,0:T(8,128)(2,1)}) %all-reduce.6.cloned.1.call-update) | async-done | bytes 2359312 | tf_op jit(solution)/shard_map/psum | solution.py:287
  561.3 4.2 slice_convert_fusion
  569.9 2.2 reshape.332
  (459 shorter events, 134.5 us)
Async XLA Ops:
  7.2 121.5 %copy-start = (bf16[768,768]{1,0:T(8,128)(2,1)S(1)}, bf16[768,768]{1,0:T(8,128)(2,1)}, u32[]{:S(2)}) copy-start(bf16[768,768]{1,0:T(8,128)(2,1)} %param.32) | copy-start | bytes 3538948
  7.2 12.1 %copy-start.17 = (bf16[600,768]{1,0:T(8,128)(2,1)S(1)}, bf16[600,768]{1,0:T(8,128)(2,1)}, u32[]{:S(2)}) copy-start(bf16[600,768]{1,0:T(8,128)(2,1)} %param.22) | copy-start | bytes 2764804
  7.2 12.3 %copy-start.72 = (f32[2,768]{1,0:T(2,128)S(1)}, f32[2,768]{1,0:T(2,128)}, u32[]{:S(2)}) copy-start(f32[2,768]{1,0:T(2,128)} %param.35) | copy-start | bytes 18436
  7.2 111.9 %all-reduce.4.cloned.1.call-start = ((), (), s32[]{:S(2)}) async-start(), calls=%async_computation | async-start | bytes 2949120 | tf_op jit(solution)/shard_map/psum | solution.py:223
  7.3 52.3 %collective-permute-start.2 = (bf16[1,192,768]{2,1,0:T(8,128)(2,1)}, bf16[1,192,768]{2,1,0:T(8,128)(2,1)}, u32[]{:S(2)}, u32[]{:S(2)}) collective-permute-start(bf16[1,192,768]{2,1,0:T(8,128)(2,1)} %bitcast.264), channel_id=1, source_target_pairs={{0,2},{1,3},{2,0},{3,1},{4,6},{5,7},{6,4},{7,5},{8,10},{9,11},{10,... | collective-permute-start | bytes 884744 | tf_op jit(solution)/shard_map/ppermute | solution.py:63
  10.3 16.1 %collective-permute-start.13 = (bf16[240,768]{1,0:T(8,128)(2,1)}, bf16[240,768]{1,0:T(8,128)(2,1)}, u32[]{:S(2)}, u32[]{:S(2)}) collective-permute-start(bf16[240,768]{1,0:T(8,128)(2,1)} %param.19), channel_id=1, source_target_pairs={{0,2},{1,3},{2,0},{3,1},{4,6},{5,7},{6,4},{7,5},{8,10},{9,11},{10,... | collective-permute-start | bytes 1105928 | tf_op jit(solution)/shard_map/ppermute | solution.py:63
  10.4 50.5 %collective-permute-start = (bf16[1,3,768,192]{2,3,0,1:T(8,128)(2,1)}, bf16[1,3,768,192]{2,3,0,1:T(8,128)(2,1)}, u32[]{:S(2)}, u32[]{:S(2)}) collective-permute-start(bf16[1,3,768,192]{2,3,0,1:T(8,128)(2,1)} %bitcast.255), channel_id=1, source_target_pairs={{0,2},{1,3},{2,0},{3,1},{4,6},{5,7},{6,4},{7,5},{8,10},{9,11},{10,... | collective-permute-start | bytes 2654216 | tf_op jit(solution)/shard_map/ppermute | solution.py:63
  13.9 13.8 %copy-start.73 = (f32[2,768]{1,0:T(2,128)S(1)}, f32[2,768]{1,0:T(2,128)}, u32[]{:S(2)}) copy-start(f32[2,768]{1,0:T(2,128)} %param.36) | copy-start | bytes 18436
  13.9 15.0 %copy-start.87 = (f32[2,192]{1,0:T(2,128)S(1)}, f32[2,192]{1,0:T(2,128)}, u32[]{:S(2)}) copy-start(f32[2,192]{1,0:T(2,128)} %param.30) | copy-start | bytes 4612
  13.9 133.4 %collective-permute-start.4 = (bf16[1,768,768]{1,2,0:T(8,128)(2,1)S(1)}, bf16[1,768,768]{1,2,0:T(8,128)(2,1)}, u32[]{:S(2)}, u32[]{:S(2)}) collective-permute-start(bf16[1,768,768]{1,2,0:T(8,128)(2,1)S(1)} %bitcast.239), channel_id=1, source_target_pairs={{0,2},{1,3},{2,0},{3,1},{4,6},{5,7},{6,4},{7,5},{8,10},{9,11},{10,... | collective-permute-start | bytes 3538952 | tf_op jit(solution)/shard_map/ppermute | solution.py:63
  14.1 139.4 %collective-permute-start.6 = (bf16[1,768,768]{2,1,0:T(8,128)(2,1)}, bf16[1,768,768]{2,1,0:T(8,128)(2,1)}, u32[]{:S(2)}, u32[]{:S(2)}) collective-permute-start(bf16[1,768,768]{2,1,0:T(8,128)(2,1)} %bitcast.246), channel_id=1, source_target_pairs={{0,2},{1,3},{2,0},{3,1},{4,6},{5,7},{6,4},{7,5},{8,10},{9,11},{10,... | collective-permute-start | bytes 3538952 | tf_op jit(solution)/shard_map/ppermute | solution.py:63
  19.5 17.1 %copy-start.59 = (f32[768]{0:T(1024)}, f32[768]{0:T(1024)S(1)}, u32[]{:S(2)}) copy-start(f32[768]{0:T(1024)S(1)} %get-tuple-element.69) | copy-start | bytes 9220
  19.5 109.2 %copy-start.54 = (f32[768]{0:T(1024)}, f32[768]{0:T(1024)S(1)}, u32[]{:S(2)}) copy-start(f32[768]{0:T(1024)S(1)} %get-tuple-element.68) | copy-start | bytes 9220
  27.6 2.3 collective-permute-start.14
  28.3 8.2 %copy-start.79 = (f32[768]{0:T(1024)}, f32[768]{0:T(1024)S(1)}, u32[]{:S(2)}) copy-start(f32[768]{0:T(1024)S(1)} %get-tuple-element.71) | copy-start | bytes 9220
  55.7 8.0 %copy-start.15 = (bf16[960,192]{1,0:T(8,128)(2,1)}, bf16[960,192]{1,0:T(8,128)(2,1)S(1)}, u32[]{:S(2)}) copy-start(bf16[960,192]{1,0:T(8,128)(2,1)S(1)} %reshape.319) | copy-start | bytes 1105924
  58.5 502.8 %all-reduce.6.cloned.1.call-start = ((), (), s32[]{:S(2)}) async-start(), calls=%async_computation.1 | async-start | bytes 4718592 | tf_op jit(solution)/shard_map/psum | solution.py:287
  60.7 84.4 %collective-permute-start.3 = (bf16[2,192,768]{2,1,0:T(8,128)(2,1)S(1)}, bf16[2,192,768]{2,1,0:T(8,128)(2,1)}, u32[]{:S(2)}, u32[]{:S(2)}) collective-permute-start(bf16[2,192,768]{2,1,0:T(8,128)(2,1)S(1)} %pad_maximum_fusion.14), channel_id=1, source_target_pairs={{0,1},{1,0},{2,3},{3,2},{4,5},{5,4},{6,7},{7,6},{8,9},{9,8},{10,11... | collective-permute-start | bytes 1769480 | tf_op jit(solution)/shard_map/ppermute | solution.py:63
  63.7 97.0 %collective-permute-start.1 = (bf16[2,3,768,192]{2,3,0,1:T(8,128)(2,1)}, bf16[2,3,768,192]{2,3,0,1:T(8,128)(2,1)}, u32[]{:S(2)}, u32[]{:S(2)}) collective-permute-start(bf16[2,3,768,192]{2,3,0,1:T(8,128)(2,1)} %pad_maximum_fusion.7), channel_id=1, source_target_pairs={{0,1},{1,0},{2,3},{3,2},{4,5},{5,4},{6,7},{7,6},{8,9},{9,8},{10,11... | collective-permute-start | bytes 5308424 | tf_op jit(solution)/shard_map/ppermute | solution.py:63
  128.7 8.9 %copy-start.13 = (f32[960,768]{1,0:T(8,128)}, f32[960,768]{1,0:T(8,128)S(1)}, u32[]{:S(2)}) copy-start(f32[960,768]{1,0:T(8,128)S(1)} %subtract_multiply_fusion.1) | copy-start | bytes 8847364
  128.8 8.8 %copy-start.90 = (bf16[768,768]{1,0:T(8,128)(2,1)S(1)}, bf16[768,768]{1,0:T(8,128)(2,1)}, u32[]{:S(2)}) copy-start(bf16[768,768]{1,0:T(8,128)(2,1)} %param.34) | copy-start | bytes 3538948
  140.9 1.6 collective-permute-start.15
  143.4 7.0 %collective-permute-start.16 = (f32[60,768]{1,0:T(8,128)S(1)}, f32[60,768]{1,0:T(8,128)S(1)}, u32[]{:S(2)}, u32[]{:S(2)}) collective-permute-start(f32[60,768]{1,0:T(8,128)S(1)} %add.331), channel_id=1, source_target_pairs={{0,2},{1,3},{2,0},{3,1},{4,6},{5,7},{6,4},{7,5},{8,10},{9,11},{10,... | collective-permute-start | bytes 552968 | tf_op jit(solution)/shard_map/ppermute | solution.py:63
  150.4 85.7 %collective-permute-start.5 = (bf16[2,768,768]{1,2,0:T(8,128)(2,1)}, bf16[2,768,768]{1,2,0:T(8,128)(2,1)}, u32[]{:S(2)}, u32[]{:S(2)}) collective-permute-start(bf16[2,768,768]{1,2,0:T(8,128)(2,1)} %pad_maximum_fusion.3), channel_id=1, source_target_pairs={{0,1},{1,0},{2,3},{3,2},{4,5},{5,4},{6,7},{7,6},{8,9},{9,8},{10,11... | collective-permute-start | bytes 7077896 | tf_op jit(solution)/shard_map/ppermute | solution.py:63
  150.6 9.3 %copy-start.10 = (f32[60,768]{1,0:T(8,128)}, f32[60,768]{1,0:T(8,128)S(1)}, u32[]{:S(2)}) copy-start(f32[60,768]{1,0:T(8,128)S(1)} %get-tuple-element.78) | copy-start | bytes 552964
  150.6 9.2 %copy-start.66 = (f32[60]{0:T(128)}, f32[60]{0:T(128)S(1)}, u32[]{:S(2)}) copy-start(f32[60]{0:T(128)S(1)} %add_rsqrt_fusion.6) | copy-start | bytes 724
  150.6 10.0 %copy-start.20 = (bf16[3,768,192]{1,2,0:T(8,128)(2,1)S(1)}, bf16[3,768,192]{1,2,0:T(8,128)(2,1)}, u32[]{:S(2)}) copy-start(bf16[3,768,192]{1,2,0:T(8,128)(2,1)} %param.25) | copy-start | bytes 2654212
  150.7 8.3 %collective-permute-start.17 = (bf16[60,768]{1,0:T(8,128)(2,1)S(1)}, bf16[60,768]{1,0:T(8,128)(2,1)S(1)}, u32[]{:S(2)}, u32[]{:S(2)}) collective-permute-start(bf16[60,768]{1,0:T(8,128)(2,1)S(1)} %multiply_convert_fusion.16), channel_id=1, source_target_pairs={{0,16},{4,20},{8,24},{12,28},{16,0},{20,4},{24,8},{28,12},{1,17},{... | collective-permute-start | bytes 276488 | tf_op jit(solution)/shard_map/ppermute | solution.py:63
  156.4 83.5 %collective-permute-start.7 = (bf16[2,768,768]{2,1,0:T(8,128)(2,1)}, bf16[2,768,768]{2,1,0:T(8,128)(2,1)}, u32[]{:S(2)}, u32[]{:S(2)}) collective-permute-start(bf16[2,768,768]{2,1,0:T(8,128)(2,1)} %pad_maximum_fusion.4), channel_id=1, source_target_pairs={{0,1},{1,0},{2,3},{3,2},{4,5},{5,4},{6,7},{7,6},{8,9},{9,8},{10,11... | collective-permute-start | bytes 7077896 | tf_op jit(solution)/shard_map/ppermute | solution.py:63
  159.9 136.7 %collective-permute-start.18 = (bf16[2,60,768]{2,1,0:T(8,128)(2,1)}, bf16[2,60,768]{2,1,0:T(8,128)(2,1)}, u32[]{:S(2)}, u32[]{:S(2)}) collective-permute-start(bf16[2,60,768]{2,1,0:T(8,128)(2,1)} %pad_maximum_fusion.21), channel_id=1, source_target_pairs={{0,8},{4,12},{8,0},{12,4},{16,24},{20,28},{24,16},{28,20},{1,9},{5... | collective-permute-start | bytes 552968 | tf_op jit(solution)/shard_map/ppermute | solution.py:63
  199.9 10.7 %slice-start = ((s8[5603328]{0:T(1024)(128)(4,1)}), s8[4194304]{0:T(1024)(128)(4,1)S(1)}, s32[]{:S(2)}) async-start(s8[5603328]{0:T(1024)(128)(4,1)} %bitcast.244), calls=%async_computation.2 | async-start | bytes 8388608
  203.8 6.8 %slice-start.1 = ((s8[5603328]{0:T(1024)(128)(4,1)}), s8[1409024]{0:T(1024)(128)(4,1)S(1)}, s32[]{:S(2)}) async-start(s8[5603328]{0:T(1024)(128)(4,1)} %bitcast.244), calls=%async_computation.3 | async-start | bytes 2818048
  293.8 15.1 %copy-start.64 = (pred[60,16]{0,1:T(8,128)(4,1)S(1)}, pred[60,16]{0,1:T(8,128)(4,1)}, u32[]{:S(2)}) copy-start(pred[60,16]{0,1:T(8,128)(4,1)} %copy-done.63) | copy-start | bytes 2884
  293.8 15.1 %copy-start.77 = (f32[60]{0:T(128)S(1)}, f32[60]{0:T(128)}, u32[]{:S(2)}) copy-start(f32[60]{0:T(128)} %get-tuple-element.79) | copy-start | bytes 724
  294.7 1.4 collective-permute-start.8
  296.1 4.9 collective-permute-start.9
  301.1 7.7 %collective-permute-start.10 = (bf16[60,768]{1,0:T(8,128)(2,1)S(1)}, bf16[60,768]{1,0:T(8,128)(2,1)S(1)}, u32[]{:S(2)}, u32[]{:S(2)}) collective-permute-start(bf16[60,768]{1,0:T(8,128)(2,1)S(1)} %add.314), channel_id=1, source_target_pairs={{0,16},{4,20},{8,24},{12,28},{16,0},{20,4},{24,8},{28,12},{1,17},{... | collective-permute-start | bytes 276488 | tf_op jit(solution)/shard_map/ppermute | solution.py:63
  304.4 12.7 %collective-permute-start.19 = (bf16[2,2,60,768]{3,2,1,0:T(8,128)(2,1)S(1)}, bf16[2,2,60,768]{3,2,1,0:T(8,128)(2,1)S(1)}, u32[]{:S(2)}, u32[]{:S(2)}) collective-permute-start(bf16[2,2,60,768]{3,2,1,0:T(8,128)(2,1)S(1)} %pad_maximum_fusion.18), channel_id=1, source_target_pairs={{0,4},{4,0},{8,12},{12,8},{16,20},{20,16},{24,28},{28,24},{1,5},{5... | collective-permute-start | bytes 1105928 | tf_op jit(solution)/shard_map/ppermute | solution.py:63
  308.8 6.6 %collective-permute-start.11 = (bf16[2,60,768]{2,1,0:T(8,128)(2,1)S(1)}, bf16[2,60,768]{2,1,0:T(8,128)(2,1)S(1)}, u32[]{:S(2)}, u32[]{:S(2)}) collective-permute-start(bf16[2,60,768]{2,1,0:T(8,128)(2,1)S(1)} %pad_maximum_fusion.20), channel_id=1, source_target_pairs={{0,8},{4,12},{8,0},{12,4},{16,24},{20,28},{24,16},{28,20},{1,9},{5... | collective-permute-start | bytes 552968 | tf_op jit(solution)/shard_map/ppermute | solution.py:63
  315.5 10.1 %collective-permute-start.12 = (bf16[2,2,60,768]{3,2,1,0:T(8,128)(2,1)S(1)}, bf16[2,2,60,768]{3,2,1,0:T(8,128)(2,1)}, u32[]{:S(2)}, u32[]{:S(2)}) collective-permute-start(bf16[2,2,60,768]{3,2,1,0:T(8,128)(2,1)S(1)} %pad_maximum_fusion.17), channel_id=1, source_target_pairs={{0,4},{4,0},{8,12},{12,8},{16,20},{20,16},{24,28},{28,24},{1,5},{5... | collective-permute-start | bytes 1105928 | tf_op jit(solution)/shard_map/ppermute | solution.py:63
  337.9 2.4 collective-permute-start.20
  338.0 16.4 %copy-start.62 = (f32[2,2,240]{2,1,0:T(2,128)S(1)}, f32[2,2,240]{2,1,0:T(2,128)}, u32[]{:S(2)}) copy-start(f32[2,2,240]{2,1,0:T(2,128)} %copy-done.61) | copy-start | bytes 11524
  342.1 22.7 %copy-start.49 = (f32[60,3,16]{2,1,0:T(4,128)S(1)}, f32[60,3,16]{2,1,0:T(4,128)}, u32[]{:S(2)}) copy-start(f32[60,3,16]{2,1,0:T(4,128)} %copy-done.48) | copy-start | bytes 34564
  342.1 23.6 %copy-start.55 = (f32[768]{0:T(1024)S(1)}, f32[768]{0:T(1024)}, u32[]{:S(2)}) copy-start(f32[768]{0:T(1024)} %copy-done.54) | copy-start | bytes 9220
  342.1 23.6 %copy-start.82 = (f32[768]{0:T(1024)S(1)}, f32[768]{0:T(1024)}, u32[]{:S(2)}) copy-start(f32[768]{0:T(1024)} %get-tuple-element.70) | copy-start | bytes 9220
  342.1 10.8 %collective-permute-start.21 = (bf16[240,768]{1,0:T(8,128)(2,1)S(1)}, bf16[240,768]{1,0:T(8,128)(2,1)}, u32[]{:S(2)}, u32[]{:S(2)}) collective-permute-start(bf16[240,768]{1,0:T(8,128)(2,1)S(1)} %fusion.128), channel_id=1, source_target_pairs={{0,2},{1,3},{2,0},{3,1},{4,6},{5,7},{6,4},{7,5},{8,10},{9,11},{10,... | collective-permute-start | bytes 1105928 | tf_op jit(solution)/shard_map/ppermute | solution.py:63
  354.0 9.8 %collective-permute-start.22 = (bf16[240,768]{1,0:T(8,128)(2,1)S(1)}, bf16[240,768]{1,0:T(8,128)(2,1)S(1)}, u32[]{:S(2)}, u32[]{:S(2)}) collective-permute-start(bf16[240,768]{1,0:T(8,128)(2,1)S(1)} %fusion.102), channel_id=1, source_target_pairs={{0,2},{1,3},{2,0},{3,1},{4,6},{5,7},{6,4},{7,5},{8,10},{9,11},{10,... | collective-permute-start | bytes 1105928 | tf_op jit(solution)/shard_map/ppermute | solution.py:63
  354.5 11.2 %copy-start.14 = (f32[960,768]{1,0:T(8,128)S(1)}, f32[960,768]{1,0:T(8,128)}, u32[]{:S(2)}) copy-start(f32[960,768]{1,0:T(8,128)} %copy-done.13) | copy-start | bytes 8847364
  364.0 5.6 collective-permute-start.23
  412.3 15.8 %collective-permute-start.26 = (bf16[2,2,96,768]{3,2,1,0:T(8,128)(2,1)S(1)}, bf16[2,2,96,768]{3,2,1,0:T(8,128)(2,1)S(1)}, u32[]{:S(2)}, u32[]{:S(2)}) collective-permute-start(bf16[2,2,96,768]{3,2,1,0:T(8,128)(2,1)S(1)} %fusion.121), channel_id=1, source_target_pairs={{0,4},{4,0},{8,12},{12,8},{16,20},{20,16},{24,28},{28,24},{1,5},{5... | collective-permute-start | bytes 1769480 | tf_op jit(solution)/shard_map/ppermute | solution.py:63
  415.4 13.6 %collective-permute-start.24 = (bf16[2,240,768]{2,1,0:T(8,128)(2,1)S(1)}, bf16[2,240,768]{2,1,0:T(8,128)(2,1)S(1)}, u32[]{:S(2)}, u32[]{:S(2)}) collective-permute-start(bf16[2,240,768]{2,1,0:T(8,128)(2,1)S(1)} %fusion.101), channel_id=1, source_target_pairs={{0,1},{1,0},{2,3},{3,2},{4,5},{5,4},{6,7},{7,6},{8,9},{9,8},{10,11... | collective-permute-start | bytes 2211848 | tf_op jit(solution)/shard_map/ppermute | solution.py:63
  428.3 8.8 %copy-start.39 = (bf16[768,768]{1,0:T(8,128)(2,1)S(1)}, bf16[768,768]{1,0:T(8,128)(2,1)}, u32[]{:S(2)}) copy-start(bf16[768,768]{1,0:T(8,128)(2,1)} %convolution_convert_fusion.2) | copy-start | bytes 3538948
  428.3 8.6 %collective-permute-start.27 = (bf16[2,96,768]{2,1,0:T(8,128)(2,1)S(1)}, bf16[2,96,768]{2,1,0:T(8,128)(2,1)S(1)}, u32[]{:S(2)}, u32[]{:S(2)}) collective-permute-start(bf16[2,96,768]{2,1,0:T(8,128)(2,1)S(1)} %fusion.130), channel_id=1, source_target_pairs={{0,8},{4,12},{8,0},{12,4},{16,24},{20,28},{24,16},{28,20},{1,9},{5... | collective-permute-start | bytes 884744 | tf_op jit(solution)/shard_map/ppermute | solution.py:63
  429.9 16.0 %collective-permute-start.25 = (bf16[240,768]{1,0:T(8,128)(2,1)}, bf16[240,768]{1,0:T(8,128)(2,1)}, u32[]{:S(2)}, u32[]{:S(2)}) collective-permute-start(bf16[240,768]{1,0:T(8,128)(2,1)} %fusion.129), channel_id=1, source_target_pairs={{0,2},{1,3},{2,0},{3,1},{4,6},{5,7},{6,4},{7,5},{8,10},{9,11},{10,... | collective-permute-start | bytes 1105928 | tf_op jit(solution)/shard_map/ppermute | solution.py:63
  437.0 8.8 %collective-permute-start.28 = (bf16[96,768]{1,0:T(8,128)(2,1)S(1)}, bf16[96,768]{1,0:T(8,128)(2,1)S(1)}, u32[]{:S(2)}, u32[]{:S(2)}) collective-permute-start(bf16[96,768]{1,0:T(8,128)(2,1)S(1)} %fusion.132), channel_id=1, source_target_pairs={{0,16},{4,20},{8,24},{12,28},{16,0},{20,4},{24,8},{28,12},{1,17},{... | collective-permute-start | bytes 442376 | tf_op jit(solution)/shard_map/ppermute | solution.py:63
  438.7 8.8 %copy-start.78 = (f32[240,1]{0,1:T(1,128)S(1)}, f32[240,1]{0,1:T(1,128)}, u32[]{:S(2)}) copy-start(f32[240,1]{0,1:T(1,128)} %constant_dynamic-slice_fusion) | copy-start | bytes 2884
  445.9 16.7 %collective-permute-start.29 = (bf16[96,768]{1,0:T(8,128)(2,1)S(1)}, bf16[96,768]{1,0:T(8,128)(2,1)S(1)}, u32[]{:S(2)}, u32[]{:S(2)}) collective-permute-start(bf16[96,768]{1,0:T(8,128)(2,1)S(1)} %fusion.131), channel_id=1, source_target_pairs={{0,16},{4,20},{8,24},{12,28},{16,0},{20,4},{24,8},{28,12},{1,17},{... | collective-permute-start | bytes 442376 | tf_op jit(solution)/shard_map/ppermute | solution.py:63
  450.0 1.3 collective-permute-start.32
  451.3 3.8 collective-permute-start.33
  462.6 20.3 %collective-permute-start.30 = (bf16[2,96,768]{2,1,0:T(8,128)(2,1)S(1)}, bf16[2,96,768]{2,1,0:T(8,128)(2,1)S(1)}, u32[]{:S(2)}, u32[]{:S(2)}) collective-permute-start(bf16[2,96,768]{2,1,0:T(8,128)(2,1)S(1)} %pad_maximum_fusion.19), channel_id=1, source_target_pairs={{0,8},{4,12},{8,0},{12,4},{16,24},{20,28},{24,16},{28,20},{1,9},{5... | collective-permute-start | bytes 884744 | tf_op jit(solution)/shard_map/ppermute | solution.py:63
  462.7 3.9 collective-permute-start.34
  466.6 16.3 %collective-permute-start.35 = (f32[8,768]{1,0:T(8,128)S(1)}, f32[8,768]{1,0:T(8,128)S(1)}, u32[]{:S(2)}, u32[]{:S(2)}) collective-permute-start(f32[8,768]{1,0:T(8,128)S(1)} %fusion.249), channel_id=1, source_target_pairs={{0,8},{4,12},{8,0},{12,4},{16,24},{20,28},{24,16},{28,20},{1,9},{5... | collective-permute-start | bytes 73736 | tf_op jit(solution)/shard_map/ppermute | solution.py:63
  482.9 82.6 %collective-permute-start.36 = (f32[8,768]{1,0:T(8,128)S(1)}, f32[8,768]{1,0:T(8,128)S(1)}, u32[]{:S(2)}, u32[]{:S(2)}) collective-permute-start(f32[8,768]{1,0:T(8,128)S(1)} %add.368), channel_id=1, source_target_pairs={{0,16},{4,20},{8,24},{12,28},{16,0},{20,4},{24,8},{28,12},{1,17},{... | collective-permute-start | bytes 73736 | tf_op jit(solution)/shard_map/ppermute | solution.py:63
  483.0 84.4 %collective-permute-start.31 = (bf16[2,2,96,768]{3,2,1,0:T(8,128)(2,1)S(1)}, bf16[2,2,96,768]{3,2,1,0:T(8,128)(2,1)S(1)}, u32[]{:S(2)}, u32[]{:S(2)}) collective-permute-start(bf16[2,2,96,768]{3,2,1,0:T(8,128)(2,1)S(1)} %pad_maximum_fusion.15), channel_id=1, source_target_pairs={{0,4},{4,0},{8,12},{12,8},{16,20},{20,16},{24,28},{28,24},{1,5},{5... | collective-permute-start | bytes 1769480 | tf_op jit(solution)/shard_map/ppermute | solution.py:63
  (78 other events, 228.9 us)
Sparse Core Ops, SparseCore 0:
  58.6 60.4 all-reduce.3
  438.8 122.4 all-reduce.5

commit v14 on v13

--- a/solution.py
+++ b/solution.py
@@ -199,7 +199,7 @@
     present = (caption_ids > 0).astype(jnp.float32)
     keep = (caption_ids > 0)[:, None, None, :]
     counts = jnp.sum(present, 1, keepdims=True)
-    inputs = gather_ordered(text_in, "mp").reshape(-1, D).astype(jnp.float32)
+    inputs = lax.all_gather(text_in, "mp", axis=0, tiled=True).astype(jnp.float32)
     unit1, inverse1 = layer_stats(inputs)
     normed1_all = (unit1 * txt_gains[0] + txt_shifts[0]).astype(jnp.bfloat16)
     bias_rows = jnp.stack([txt_qv_bias[0], jnp.zeros_like(txt_qv_bias[0]), txt_qv_bias[1]])
@@ -291,6 +291,7 @@
     grad_middle = grad_result + norm_back(grad_normed2, unit2, inverse2, txt_gains[1])
     grad_mid_all = grad_middle.astype(jnp.bfloat16)
     grad_out = jnp.einsum("gw,gd->wd", context, grad_mid_all, preferred_element_type=jnp.float32)
+    out_sums = reduce_exchanged(grad_out, "dp")
     grad_context = jnp.einsum(
         "gd,wd->gw", grad_mid_all, txt_out, preferred_element_type=jnp.float32
     )
@@ -326,7 +327,7 @@
             jnp.sum(grad_triple[2].astype(jnp.float32), 0),
         ]
     )
-    attn_sums = reduce_exchanged(jnp.concatenate([grad_qkv.reshape(-1, D), grad_out], 0), "dp")
+    qkv_sums = reduce_exchanged(grad_qkv.reshape(-1, D), "dp")
     grad_normed1 = scatter_exchanged(
         jnp.einsum("jgw,jdw->gd", grad_triple, txt_qkv, preferred_element_type=jnp.float32), "mp"
     )
@@ -358,9 +359,9 @@
     return (
         loss,
         grad_inputs,
-        attn_sums[: grad_qkv.size // D].astype(jnp.float32).reshape(grad_qkv.shape),
+        qkv_sums.astype(jnp.float32).reshape(grad_qkv.shape),
         shared[6, :qv_count].reshape(grad_qv_bias.shape),
-        attn_sums[grad_qkv.size // D :].astype(jnp.float32),
+        out_sums.astype(jnp.float32),
         fc_sums[:fc1_rows].astype(jnp.float32),
         shared[7],
         fc_sums[fc1_rows:].astype(jnp.float32),

time: 593 us -> 550 us (0.927)
  waiting for transfers between devices: 233 us -> 174 us
  starting transfers between devices: 29.7 us -> 44.8 us
  other arithmetic: 91.8 us -> 83.7 us
  local copies, waits for them, and re-layouts: 100 us -> 106 us
    psum x1, waiting for transfers between devices: 55.1 us -> 0.01 us  [local_body(): lax.psum(jnp.dot(context, txt_out, preferred_element_type=jnp.float32).as...]
    psum x1, waiting for transfers between devices: 76.8 us -> 49.3 us  [local_body(): lax.psum(jnp.concatenate([grad_fc1, grad_fc2], 0).astype(jnp.bfloat16), '...]
    ppermute x37 -> x41, waiting for transfers between devices: 101 us -> 125 us  [exchange(): return lax.ppermute(values, axis, [(i, i ^ 1 << bit) for i in range(count)])]
    ppermute x37 -> x41, starting transfers between devices: 29.6 us -> 44.5 us  [exchange(): return lax.ppermute(values, axis, [(i, i ^ 1 << bit) for i in range(count)])]
    unnamed x208 -> x190, local copies, waits for them, and re-layouts: 11.8 us -> 13.5 us
  transfers between devices with their start and end apart: 39 -> 44, of which waited for: 22 -> 28; matrix products, arithmetic and copies ran while one was open for 40% -> 50% of each run, Pallas kernels for 0% -> 0%
where the time goes in v14:
time: 550 us; the launch traced here: 540 us
  waiting for transfers between devices  174 us (32%)
  matrix products  113 us (21%)
  local copies, waits for them, and re-layouts  106 us (19%)
  other arithmetic  83.7 us (15%)
  starting transfers between devices  44.8 us (8%)
  between operations  19 us (3%)
    ppermute x41, waiting for transfers between devices, exchange(): return lax.ppermute(values, axis, [(i, i ^ 1 << bit) for i in range(count)])  125 us
    psum x1, waiting for transfers between devices, local_body(): lax.psum(jnp.concatenate([grad_fc1, grad_fc2], 0).astype(jnp.bfloat16), '...  49.3 us
    dot_general x2, matrix products, image_ffn(): result = middle + jnp.dot(active, w_fc2, preferred_element_type=jnp.float32)  45.8 us
    ppermute x41, starting transfers between devices, exchange(): return lax.ppermute(values, axis, [(i, i ^ 1 << bit) for i in range(count)])  44.5 us
    concatenate x8, other arithmetic, gather_stacked(): data = jnp.concatenate([data, exchange(data, axis, count, bit)], 0)  20.6 us
    squeeze x4, local copies, waits for them, and re-layouts, image_attention(): shares, _ = attention_shares(shaped[0], shaped[1], None)  15 us
    unnamed x190, local copies, waits for them, and re-layouts  13.5 us
  transfers between devices with their start and end apart: 44, of which 28 were waited for; matrix products, arithmetic and copies ran while one was open for 50% of the time, Pallas kernels for 0%

profile of v14, /device:TPU:0, one launch (start us, length us, event | category | flops | bytes accessed | tf_op | source)
XLA Modules:
  0.0 539.9 jit_solution(15807846978332187121)
XLA Ops:
  7.2 3.1 collective-permute-start
  29.5 15.9 %collective-permute-done.2 = bf16[1,192,768]{2,1,0:T(8,128)(2,1)} collective-permute-done((bf16[1,192,768]{2,1,0:T(8,128)(2,1)}, bf16[1,192,768]{2,1,0:T(8,128)(2,1)}, u32[]{:S(2)}, u32[]{:S(2)}) %collective-permute-start.2) | collective-permute-done | bytes 294944 | tf_op jit(solution)/shard_map/ppermute | solution.py:63
  48.4 2.9 pad_maximum_fusion.6
  53.9 16.7 %collective-permute-done.6 = bf16[1,768,768]{2,1,0:T(8,128)(2,1)} collective-permute-done((bf16[1,768,768]{2,1,0:T(8,128)(2,1)}, bf16[1,768,768]{2,1,0:T(8,128)(2,1)}, u32[]{:S(2)}, u32[]{:S(2)}) %collective-permute-start.6) | collective-permute-done | bytes 1179680 | tf_op jit(solution)/shard_map/ppermute | solution.py:63
  70.6 2.9 pad_maximum_fusion.4
  73.5 21.4 %collective-permute-done.4 = bf16[1,768,768]{1,2,0:T(8,128)(2,1)S(1)} collective-permute-done((bf16[1,768,768]{1,2,0:T(8,128)(2,1)S(1)}, bf16[1,768,768]{1,2,0:T(8,128)(2,1)S(1)}, u32[]{:S(2)}, u32[]{:S(2)}) %collective-permute-start.4) | collective-permute-done | bytes 1179680 | tf_op jit(solution)/shard_map/ppermute | solution.py:63
  100.5 2.5 fusion.128
  104.2 2.5 copy.114
  106.8 6.5 %reshape.295 = bf16[60,16,3,3,64]{4,3,1,0,2:T(4,128)(2,1)} reshape(bf16[960,3,192]{2,0,1:T(8,128)(2,1)} %copy.114) | data formatting | bytes 2211840 | tf_op jit(solution)/shard_map/reshape | solution.py:210
  113.3 3.2 fusion.215
  120.1 2.4 reshape.296
  124.5 2.2 pad_maximum_fusion.2
  129.9 3.3 reshape.315
  133.2 3.3 reshape.314
  136.4 3.0 fusion.70
  139.4 3.9 fusion.220
  143.3 2.3 reshape.313
  145.6 4.1 fusion.74
  149.8 2.2 copy.112
  151.9 3.1 reshape.293
  155.0 4.7 convert_bitcast_fusion
  161.4 4.4 squeeze.82
  165.8 4.0 squeeze.81
  169.8 3.8 fusion.48
  173.6 3.1 fusion.222
  176.8 4.1 squeeze.80
  180.8 4.2 convert_bitcast_fusion.1
  186.9 4.2 reshape.288
  191.1 2.9 fusion.223
  197.6 4.0 fusion.214
  203.1 8.7 %multiply_convert_fusion = (bf16[960,768]{1,0:T(8,128)(2,1)S(1)}, f32[960,768]{1,0:T(8,128)}, f32[960,768]{1,0:T(8,128)}) fusion(f32[768]{0:T(1024)S(1)} %copy-done.87, bf16[768,768]{1,0:T(8,128)(2,1)S(1)} %copy-done, f32[960,768]{1,0:T(8,128)S(1)} %subtract_multiply_fusion, f32[768]{0:T(1024)S(1)} %copy-done.78, f32[768]{0:T(1024)S(1)} %get-tuple-element.46), kind=kOutput, calls=%fused_computation.67 | convolution fusion | flops 1183334400 | bytes 11510784 | tf_op jit(solution)/shard_map/dot_general | solution.py:231
  218.1 5.1 collective-permute-done.14
  223.6 2.8 collective-permute-start.15
  226.4 4.7 collective-permute-done.15
  232.5 3.8 pad_maximum_fusion.1
  236.3 3.9 pad_maximum_fusion
  240.2 19.6 %fusion.67 = f32[435,768]{1,0:T(8,128)} fusion(f32[435,768]{1,0:T(8,128)S(1)} %copy-done.41, bf16[3072,768]{1,0:T(8,128)(2,1)} %bitcast.265, bf16[768,3072]{0,1:T(8,128)(2,1)} %bitcast.267, f32[768]{0:T(1024)S(1)} %copy-done.80, f32[435]{0:T(512)S(1)} %add_rsqrt_fusion.4, f32[435]{0:T(512)S(1)} %broadcast_multiply_fusion.5), kind=kOutput, calls=%fused_computation.146 | convolution fusion | flops 4193706240 | bytes 12116376 | tf_op jit(solution)/shard_map/dot_general | solution.py:147
  261.6 26.2 %fusion.61 = f32[600,768]{1,0:T(8,128)} fusion(f32[600,768]{1,0:T(8,128)} %copy-done.32, bf16[3072,768]{1,0:T(8,128)(2,1)} %bitcast.266, bf16[768,3072]{0,1:T(8,128)(2,1)} %bitcast.268, f32[768]{0:T(1024)S(1)} %copy-done.80, f32[600]{0:T(1024)S(1)} %add_rsqrt_fusion.2, f32[600]{0:T(1024)S(1)} %broadcast_multiply_fusion.3), kind=kOutput, calls=%fused_computation.127 | convolution fusion | flops 5784422400 | bytes 13131456 | tf_op jit(solution)/shard_map/dot_general | solution.py:147
  294.3 2.3 collective-permute-done.9
  296.6 3.4 collective-permute-start.10
  301.6 2.8 collective-permute-done.10
  304.7 6.4 %collective-permute-done.11 = bf16[2,60,768]{2,1,0:T(8,128)(2,1)S(1)} collective-permute-done((bf16[2,60,768]{2,1,0:T(8,128)(2,1)S(1)}, bf16[2,60,768]{2,1,0:T(8,128)(2,1)S(1)}, u32[]{:S(2)}, u32[]{:S(2)}) %collective-permute-start.11) | collective-permute-done | bytes 184352 | tf_op jit(solution)/shard_map/ppermute | solution.py:63
  313.9 7.4 %collective-permute-done.12 = bf16[2,2,60,768]{3,2,1,0:T(8,128)(2,1)} collective-permute-done((bf16[2,2,60,768]{3,2,1,0:T(8,128)(2,1)S(1)}, bf16[2,2,60,768]{3,2,1,0:T(8,128)(2,1)}, u32[]{:S(2)}, u32[]{:S(2)}) %collective-permute-start.12) | collective-permute-done | bytes 368672 | tf_op jit(solution)/shard_map/ppermute | solution.py:63
  322.7 2.7 select_reduce_fusion
  333.0 2.3 collective-permute-done.18
  341.4 7.3 %collective-permute-done.19 = bf16[240,768]{1,0:T(8,128)(2,1)} collective-permute-done((bf16[240,768]{1,0:T(8,128)(2,1)}, bf16[240,768]{1,0:T(8,128)(2,1)}, u32[]{:S(2)}, u32[]{:S(2)}) %collective-permute-start.19) | collective-permute-done | bytes 368672 | tf_op jit(solution)/shard_map/ppermute | solution.py:63
  351.4 3.4 convolution_convert_fusion.1
  354.8 4.8 collective-permute-done.20
  367.5 2.5 copy-done.2
  370.8 5.7 %bitcast_multiply_fusion = (f32[960,768]{1,0:T(8,128)}, f32[960,768]{1,0:T(8,128)S(1)}) fusion(f32[960]{0:T(1024)S(1)} %mul.488, f32[60,768]{1,0:T(8,128)S(1)} %subtract_multiply_fusion.1, f32[960]{0:T(1024)S(1)} %broadcast_multiply_fusion, f32[960]{0:T(1024)S(1)} %div.136, f32[768]{0:T(1024)S(1)} %copy-done.54, f32[2,2,240,768]{3,2,0,1:T(8,128)} %copy-done.5, ...), kind=kLoop, calls=%fused_computation.60 | loop fusion | flops 6635520 | bytes 12003072 | tf_op jit(solution)/shard_map/mul | solution.py:278
  398.1 3.0 convolution_bitcast_fusion
  406.2 2.6 convolution_bitcast_fusion.1
  408.8 2.2 copy.138
  411.0 2.2 reshape_reshape.14
  424.9 49.3 %all-reduce.6.cloned.1.call-done = bf16[1536,768]{1,0:T(8,128)(2,1)} async-done(((bf16[1536,768]{1,0:T(8,128)(2,1)}), bf16[1536,768]{1,0:T(8,128)(2,1)}) %all-reduce.6.cloned.1.call-update) | async-done | bytes 2359312 | tf_op jit(solution)/shard_map/psum | solution.py:287
  474.2 4.2 slice_convert_fusion
  480.7 2.9 collective-permute-done.39
  494.6 4.6 collective-permute-done.23
  499.6 2.2 dynamic-slice_reduce_fusion.2
  504.7 2.3 collective-permute-done.31
  512.5 2.6 collective-permute-done.28
  517.4 2.7 collective-permute-done.34
  522.0 4.3 collective-permute-done.29
  527.9 2.2 reshape.303
  (449 shorter events, 161.2 us)
Async XLA Ops:
  7.2 195.9 %copy-start = (bf16[768,768]{1,0:T(8,128)(2,1)S(1)}, bf16[768,768]{1,0:T(8,128)(2,1)}, u32[]{:S(2)}) copy-start(bf16[768,768]{1,0:T(8,128)(2,1)} %param.32) | copy-start | bytes 3538948
  7.2 89.6 %all-gather.2.cloned.1.call-start = ((), (), s32[]{:S(2)}) async-start(), calls=%async_computation | async-start | bytes 1843200 | tf_op jit(solution)/shard_map/all_gather | solution.py:202
  7.2 41.2 %collective-permute-start = (bf16[1,3,768,192]{2,3,0,1:T(8,128)(2,1)}, bf16[1,3,768,192]{2,3,0,1:T(8,128)(2,1)}, u32[]{:S(2)}, u32[]{:S(2)}) collective-permute-start(bf16[1,3,768,192]{2,3,0,1:T(8,128)(2,1)} %bitcast.270), channel_id=1, source_target_pairs={{0,2},{1,3},{2,0},{3,1},{4,6},{5,7},{6,4},{7,5},{8,10},{9,11},{10,... | collective-permute-start | bytes 2654216 | tf_op jit(solution)/shard_map/ppermute | solution.py:63
  10.3 35.0 %collective-permute-start.2 = (bf16[1,192,768]{2,1,0:T(8,128)(2,1)}, bf16[1,192,768]{2,1,0:T(8,128)(2,1)}, u32[]{:S(2)}, u32[]{:S(2)}) collective-permute-start(bf16[1,192,768]{2,1,0:T(8,128)(2,1)} %bitcast.280), channel_id=1, source_target_pairs={{0,2},{1,3},{2,0},{3,1},{4,6},{5,7},{6,4},{7,5},{8,10},{9,11},{10,... | collective-permute-start | bytes 884744 | tf_op jit(solution)/shard_map/ppermute | solution.py:63
  10.4 13.5 %copy-start.75 = (s32[60,16]{0,1:T(8,128)S(1)}, s32[60,16]{0,1:T(8,128)}, u32[]{:S(2)}) copy-start(s32[60,16]{0,1:T(8,128)} %param.20) | copy-start | bytes 11524
  10.4 60.2 %collective-permute-start.6 = (bf16[1,768,768]{2,1,0:T(8,128)(2,1)}, bf16[1,768,768]{2,1,0:T(8,128)(2,1)}, u32[]{:S(2)}, u32[]{:S(2)}) collective-permute-start(bf16[1,768,768]{2,1,0:T(8,128)(2,1)} %bitcast.262), channel_id=1, source_target_pairs={{0,2},{1,3},{2,0},{3,1},{4,6},{5,7},{6,4},{7,5},{8,10},{9,11},{10,... | collective-permute-start | bytes 3538952 | tf_op jit(solution)/shard_map/ppermute | solution.py:63
  13.9 81.0 %copy-start.10 = (bf16[768,768]{0,1:T(8,128)(2,1)}, bf16[768,768]{0,1:T(8,128)(2,1)S(1)}, u32[]{:S(2)}) copy-start(bf16[768,768]{0,1:T(8,128)(2,1)S(1)} %copy.103) | copy-start | bytes 3538948
  13.9 81.0 %collective-permute-start.4 = (bf16[1,768,768]{1,2,0:T(8,128)(2,1)S(1)}, bf16[1,768,768]{1,2,0:T(8,128)(2,1)S(1)}, u32[]{:S(2)}, u32[]{:S(2)}) collective-permute-start(bf16[1,768,768]{1,2,0:T(8,128)(2,1)S(1)} %bitcast.259), channel_id=1, source_target_pairs={{0,2},{1,3},{2,0},{3,1},{4,6},{5,7},{6,4},{7,5},{8,10},{9,11},{10,... | collective-permute-start | bytes 3538952 | tf_op jit(solution)/shard_map/ppermute | solution.py:63
  14.1 183.5 %all-reduce.4.cloned.1.call-start = ((), (), s32[]{:S(2)}) async-start(), calls=%async_computation.1 | async-start | bytes 2949120 | tf_op jit(solution)/shard_map/psum | solution.py:223
  24.4 29.4 %copy-start.61 = (pred[60,16]{0,1:T(8,128)(4,1)}, pred[60,16]{0,1:T(8,128)(4,1)S(1)}, u32[]{:S(2)}) copy-start(pred[60,16]{0,1:T(8,128)(4,1)S(1)} %get-tuple-element.58) | copy-start | bytes 2884
  28.6 23.2 %copy-start.44 = (bf16[192,768]{1,0:T(8,128)(2,1)S(1)}, bf16[192,768]{1,0:T(8,128)(2,1)}, u32[]{:S(2)}) copy-start(bf16[192,768]{1,0:T(8,128)(2,1)} %param.26) | copy-start | bytes 884740
  29.4 71.1 %copy-start.57 = (f32[768]{0:T(1024)}, f32[768]{0:T(1024)S(1)}, u32[]{:S(2)}) copy-start(f32[768]{0:T(1024)S(1)} %get-tuple-element.47) | copy-start | bytes 9220
  29.4 173.6 %copy-start.53 = (f32[768]{0:T(1024)}, f32[768]{0:T(1024)S(1)}, u32[]{:S(2)}) copy-start(f32[768]{0:T(1024)S(1)} %get-tuple-element.46) | copy-start | bytes 9220
  46.4 5.4 collective-permute-start.3
  48.4 22.2 %copy-start.17 = (bf16[768,768]{1,0:T(8,128)(2,1)S(1)}, bf16[768,768]{1,0:T(8,128)(2,1)}, u32[]{:S(2)}) copy-start(bf16[768,768]{1,0:T(8,128)(2,1)} %param.28) | copy-start | bytes 3538948
  51.3 73.2 %collective-permute-start.1 = (bf16[2,3,768,192]{2,3,0,1:T(8,128)(2,1)}, bf16[2,3,768,192]{2,3,0,1:T(8,128)(2,1)}, u32[]{:S(2)}, u32[]{:S(2)}) collective-permute-start(bf16[2,3,768,192]{2,3,0,1:T(8,128)(2,1)} %pad_maximum_fusion.6), channel_id=1, source_target_pairs={{0,1},{1,0},{2,3},{3,2},{4,5},{5,4},{6,7},{7,6},{8,9},{9,8},{10,11... | collective-permute-start | bytes 5308424 | tf_op jit(solution)/shard_map/ppermute | solution.py:63
  73.5 158.9 %collective-permute-start.7 = (bf16[2,768,768]{2,1,0:T(8,128)(2,1)}, bf16[2,768,768]{2,1,0:T(8,128)(2,1)}, u32[]{:S(2)}, u32[]{:S(2)}) collective-permute-start(bf16[2,768,768]{2,1,0:T(8,128)(2,1)} %pad_maximum_fusion.4), channel_id=1, source_target_pairs={{0,1},{1,0},{2,3},{3,2},{4,5},{5,4},{6,7},{7,6},{8,9},{9,8},{10,11... | collective-permute-start | bytes 7077896 | tf_op jit(solution)/shard_map/ppermute | solution.py:63
  96.7 139.6 %collective-permute-start.5 = (bf16[2,768,768]{1,2,0:T(8,128)(2,1)}, bf16[2,768,768]{1,2,0:T(8,128)(2,1)}, u32[]{:S(2)}, u32[]{:S(2)}) collective-permute-start(bf16[2,768,768]{1,2,0:T(8,128)(2,1)} %pad_maximum_fusion.3), channel_id=1, source_target_pairs={{0,1},{1,0},{2,3},{3,2},{4,5},{5,4},{6,7},{7,6},{8,9},{9,8},{10,11... | collective-permute-start | bytes 7077896 | tf_op jit(solution)/shard_map/ppermute | solution.py:63
  98.5 99.0 %copy-start.59 = (f32[960]{0:T(1024)}, f32[960]{0:T(1024)S(1)}, u32[]{:S(2)}) copy-start(f32[960]{0:T(1024)S(1)} %broadcast_multiply_fusion.2) | copy-start | bytes 11524
  100.5 97.1 %copy-start.63 = (f32[960]{0:T(1024)}, f32[960]{0:T(1024)S(1)}, u32[]{:S(2)}) copy-start(f32[960]{0:T(1024)S(1)} %add_rsqrt_fusion.1) | copy-start | bytes 11524
  124.2 350.0 %all-reduce.6.cloned.1.call-start = ((), (), s32[]{:S(2)}) async-start(), calls=%async_computation.2 | async-start | bytes 4718592 | tf_op jit(solution)/shard_map/psum | solution.py:287
  201.6 11.5 %copy-start.1 = (f32[960,768]{1,0:T(8,128)}, f32[960,768]{1,0:T(8,128)S(1)}, u32[]{:S(2)}) copy-start(f32[960,768]{1,0:T(8,128)S(1)} %get-tuple-element.62) | copy-start | bytes 8847364
  213.1 10.1 %copy-start.65 = (f32[768]{0:T(1024)S(1)}, f32[768]{0:T(1024)}, u32[]{:S(2)}) copy-start(f32[768]{0:T(1024)} %get-tuple-element.44) | copy-start | bytes 9220
  213.1 10.1 %copy-start.76 = (f32[60]{0:T(128)S(1)}, f32[60]{0:T(128)}, u32[]{:S(2)}) copy-start(f32[60]{0:T(128)} %get-tuple-element.57) | copy-start | bytes 724
  214.4 18.1 %copy-start.18 = (bf16[768,768]{1,0:T(8,128)(2,1)S(1)}, bf16[768,768]{1,0:T(8,128)(2,1)}, u32[]{:S(2)}) copy-start(bf16[768,768]{1,0:T(8,128)(2,1)} %param.28) | copy-start | bytes 3538948
  214.4 1.6 collective-permute-start.13
  216.0 7.3 %collective-permute-start.14 = (f32[60,768]{1,0:T(8,128)S(1)}, f32[60,768]{1,0:T(8,128)S(1)}, u32[]{:S(2)}, u32[]{:S(2)}) collective-permute-start(f32[60,768]{1,0:T(8,128)S(1)} %add.348), channel_id=1, source_target_pairs={{0,2},{1,3},{2,0},{3,1},{4,6},{5,7},{6,4},{7,5},{8,10},{9,11},{10,... | collective-permute-start | bytes 552968 | tf_op jit(solution)/shard_map/ppermute | solution.py:63
  223.5 12.8 %copy-start.70 = (f32[60]{0:T(128)}, f32[60]{0:T(128)S(1)}, u32[]{:S(2)}) copy-start(f32[60]{0:T(128)S(1)} %add_rsqrt_fusion.6) | copy-start | bytes 724
  223.6 7.4 %collective-permute-start.15 = (bf16[60,768]{1,0:T(8,128)(2,1)S(1)}, bf16[60,768]{1,0:T(8,128)(2,1)S(1)}, u32[]{:S(2)}, u32[]{:S(2)}) collective-permute-start(bf16[60,768]{1,0:T(8,128)(2,1)S(1)} %multiply_convert_fusion.16), channel_id=1, source_target_pairs={{0,16},{4,20},{8,24},{12,28},{16,0},{20,4},{24,8},{28,12},{1,17},{... | collective-permute-start | bytes 276488 | tf_op jit(solution)/shard_map/ppermute | solution.py:63
  231.8 61.5 %collective-permute-start.16 = (bf16[2,60,768]{2,1,0:T(8,128)(2,1)}, bf16[2,60,768]{2,1,0:T(8,128)(2,1)}, u32[]{:S(2)}, u32[]{:S(2)}) collective-permute-start(bf16[2,60,768]{2,1,0:T(8,128)(2,1)} %pad_maximum_fusion.17), channel_id=1, source_target_pairs={{0,8},{4,12},{8,0},{12,4},{16,24},{20,28},{24,16},{28,20},{1,9},{5... | collective-permute-start | bytes 552968 | tf_op jit(solution)/shard_map/ppermute | solution.py:63
  289.3 15.2 %copy-start.62 = (pred[60,16]{0,1:T(8,128)(4,1)S(1)}, pred[60,16]{0,1:T(8,128)(4,1)}, u32[]{:S(2)}) copy-start(pred[60,16]{0,1:T(8,128)(4,1)} %copy-done.61) | copy-start | bytes 2884
  290.3 1.4 collective-permute-start.8
  291.7 4.9 collective-permute-start.9
  296.6 7.8 %collective-permute-start.10 = (bf16[60,768]{1,0:T(8,128)(2,1)S(1)}, bf16[60,768]{1,0:T(8,128)(2,1)S(1)}, u32[]{:S(2)}, u32[]{:S(2)}) collective-permute-start(bf16[60,768]{1,0:T(8,128)(2,1)S(1)} %add.331), channel_id=1, source_target_pairs={{0,16},{4,20},{8,24},{12,28},{16,0},{20,4},{24,8},{28,12},{1,17},{... | collective-permute-start | bytes 276488 | tf_op jit(solution)/shard_map/ppermute | solution.py:63
  300.0 12.6 %collective-permute-start.17 = (bf16[2,2,60,768]{3,2,1,0:T(8,128)(2,1)S(1)}, bf16[2,2,60,768]{3,2,1,0:T(8,128)(2,1)S(1)}, u32[]{:S(2)}, u32[]{:S(2)}) collective-permute-start(bf16[2,2,60,768]{3,2,1,0:T(8,128)(2,1)S(1)} %pad_maximum_fusion.14), channel_id=1, source_target_pairs={{0,4},{4,0},{8,12},{12,8},{16,20},{20,16},{24,28},{28,24},{1,5},{5... | collective-permute-start | bytes 1105928 | tf_op jit(solution)/shard_map/ppermute | solution.py:63
  304.4 6.6 %collective-permute-start.11 = (bf16[2,60,768]{2,1,0:T(8,128)(2,1)S(1)}, bf16[2,60,768]{2,1,0:T(8,128)(2,1)S(1)}, u32[]{:S(2)}, u32[]{:S(2)}) collective-permute-start(bf16[2,60,768]{2,1,0:T(8,128)(2,1)S(1)} %pad_maximum_fusion.16), channel_id=1, source_target_pairs={{0,8},{4,12},{8,0},{12,4},{16,24},{20,28},{24,16},{28,20},{1,9},{5... | collective-permute-start | bytes 552968 | tf_op jit(solution)/shard_map/ppermute | solution.py:63
  311.1 10.1 %collective-permute-start.12 = (bf16[2,2,60,768]{3,2,1,0:T(8,128)(2,1)S(1)}, bf16[2,2,60,768]{3,2,1,0:T(8,128)(2,1)}, u32[]{:S(2)}, u32[]{:S(2)}) collective-permute-start(bf16[2,2,60,768]{3,2,1,0:T(8,128)(2,1)S(1)} %pad_maximum_fusion.13), channel_id=1, source_target_pairs={{0,4},{4,0},{8,12},{12,8},{16,20},{20,16},{24,28},{28,24},{1,5},{5... | collective-permute-start | bytes 1105928 | tf_op jit(solution)/shard_map/ppermute | solution.py:63
  332.9 2.4 collective-permute-start.18
  337.8 10.9 %collective-permute-start.19 = (bf16[240,768]{1,0:T(8,128)(2,1)}, bf16[240,768]{1,0:T(8,128)(2,1)}, u32[]{:S(2)}, u32[]{:S(2)}) collective-permute-start(bf16[240,768]{1,0:T(8,128)(2,1)} %fusion.130), channel_id=1, source_target_pairs={{0,2},{1,3},{2,0},{3,1},{4,6},{5,7},{6,4},{7,5},{8,10},{9,11},{10,... | collective-permute-start | bytes 1105928 | tf_op jit(solution)/shard_map/ppermute | solution.py:63
  349.8 9.8 %collective-permute-start.20 = (bf16[240,768]{1,0:T(8,128)(2,1)S(1)}, bf16[240,768]{1,0:T(8,128)(2,1)S(1)}, u32[]{:S(2)}, u32[]{:S(2)}) collective-permute-start(bf16[240,768]{1,0:T(8,128)(2,1)S(1)} %fusion.105), channel_id=1, source_target_pairs={{0,2},{1,3},{2,0},{3,1},{4,6},{5,7},{6,4},{7,5},{8,10},{9,11},{10,... | collective-permute-start | bytes 1105928 | tf_op jit(solution)/shard_map/ppermute | solution.py:63
  351.4 9.2 %copy-start.91 = (bf16[960,768]{1,0:T(8,128)(2,1)S(1)}, bf16[960,768]{1,0:T(8,128)(2,1)}, u32[]{:S(2)}) copy-start(bf16[960,768]{1,0:T(8,128)(2,1)} %copy-done.90) | copy-start | bytes 4423684
  360.6 5.1 collective-permute-start.21
  402.2 86.6 %collective-permute-start.22 = (bf16[2,240,768]{2,1,0:T(8,128)(2,1)}, bf16[2,240,768]{2,1,0:T(8,128)(2,1)}, u32[]{:S(2)}, u32[]{:S(2)}) collective-permute-start(bf16[2,240,768]{2,1,0:T(8,128)(2,1)} %fusion.104), channel_id=1, source_target_pairs={{0,1},{1,0},{2,3},{3,2},{4,5},{5,4},{6,7},{7,6},{8,9},{9,8},{10,11... | collective-permute-start | bytes 2211848 | tf_op jit(solution)/shard_map/ppermute | solution.py:63
  404.7 8.5 %collective-permute-start.35 = (bf16[2,2,24,768]{3,2,1,0:T(8,128)(2,1)}, bf16[2,2,24,768]{3,2,1,0:T(8,128)(2,1)}, u32[]{:S(2)}, u32[]{:S(2)}) collective-permute-start(bf16[2,2,24,768]{3,2,1,0:T(8,128)(2,1)} %fusion.134), channel_id=1, source_target_pairs={{0,4},{4,0},{8,12},{12,8},{16,20},{20,16},{24,28},{28,24},{1,5},{5... | collective-permute-start | bytes 442376 | tf_op jit(solution)/shard_map/ppermute | solution.py:63
  414.3 4.5 collective-permute-start.36
  416.8 62.6 %collective-permute-start.24 = (bf16[2,2,72,768]{3,2,1,0:T(8,128)(2,1)}, bf16[2,2,72,768]{3,2,1,0:T(8,128)(2,1)S(1)}, u32[]{:S(2)}, u32[]{:S(2)}) collective-permute-start(bf16[2,2,72,768]{3,2,1,0:T(8,128)(2,1)} %fusion.127), channel_id=1, source_target_pairs={{0,4},{4,0},{8,12},{12,8},{16,20},{20,16},{24,28},{28,24},{1,5},{5... | collective-permute-start | bytes 1327112 | tf_op jit(solution)/shard_map/ppermute | solution.py:63
  418.8 4.9 collective-permute-start.37
  423.8 55.6 %copy-start.14 = (f32[2,2,2,72,768]{4,3,2,1,0:T(8,128)S(1)}, f32[2,2,2,72,768]{4,3,2,1,0:T(8,128)}, u32[]{:S(2)}) copy-start(f32[2,2,2,72,768]{4,3,2,1,0:T(8,128)} %reshape_reshape.14) | copy-start | bytes 5308420
  423.8 54.6 %collective-permute-start.38 = (bf16[24,768]{1,0:T(8,128)(2,1)S(1)}, bf16[24,768]{1,0:T(8,128)(2,1)S(1)}, u32[]{:S(2)}, u32[]{:S(2)}) collective-permute-start(bf16[24,768]{1,0:T(8,128)(2,1)S(1)} %fusion.137), channel_id=1, source_target_pairs={{0,16},{4,20},{8,24},{12,28},{16,0},{20,4},{24,8},{28,12},{1,17},{... | collective-permute-start | bytes 110600 | tf_op jit(solution)/shard_map/ppermute | solution.py:63
  478.4 10.4 %copy-start.35 = (f32[2,2,240,768]{3,2,1,0:T(8,128)S(1)}, f32[2,2,240,768]{3,2,1,0:T(8,128)}, u32[]{:S(2)}) copy-start(f32[2,2,240,768]{3,2,1,0:T(8,128)} %copy-done.34) | copy-start | bytes 8847364
  478.4 5.2 collective-permute-start.39
  479.5 7.2 %collective-permute-start.25 = (bf16[2,72,768]{2,1,0:T(8,128)(2,1)S(1)}, bf16[2,72,768]{2,1,0:T(8,128)(2,1)S(1)}, u32[]{:S(2)}, u32[]{:S(2)}) collective-permute-start(bf16[2,72,768]{2,1,0:T(8,128)(2,1)S(1)} %fusion.132), channel_id=1, source_target_pairs={{0,8},{4,12},{8,0},{12,4},{16,24},{20,28},{24,16},{28,20},{1,9},{5... | collective-permute-start | bytes 663560 | tf_op jit(solution)/shard_map/ppermute | solution.py:63
  483.6 8.0 %collective-permute-start.40 = (bf16[2,2,24,768]{3,2,1,0:T(8,128)(2,1)S(1)}, bf16[2,2,24,768]{3,2,1,0:T(8,128)(2,1)S(1)}, u32[]{:S(2)}, u32[]{:S(2)}) collective-permute-start(bf16[2,2,24,768]{3,2,1,0:T(8,128)(2,1)S(1)} %pad_maximum_fusion.18), channel_id=1, source_target_pairs={{0,4},{4,0},{8,12},{12,8},{16,20},{20,16},{24,28},{28,24},{1,5},{5... | collective-permute-start | bytes 442376 | tf_op jit(solution)/shard_map/ppermute | solution.py:63
  486.8 12.5 %copy-start.12 = (f32[960,768]{1,0:T(8,128)S(1)}, f32[960,768]{1,0:T(8,128)}, u32[]{:S(2)}) copy-start(f32[960,768]{1,0:T(8,128)} %get-tuple-element.76) | copy-start | bytes 8847364
  486.8 6.9 %collective-permute-start.26 = (bf16[72,768]{1,0:T(8,128)(2,1)S(1)}, bf16[72,768]{1,0:T(8,128)(2,1)S(1)}, u32[]{:S(2)}, u32[]{:S(2)}) collective-permute-start(bf16[72,768]{1,0:T(8,128)(2,1)S(1)} %fusion.135), channel_id=1, source_target_pairs={{0,16},{4,20},{8,24},{12,28},{16,0},{20,4},{24,8},{28,12},{1,17},{... | collective-permute-start | bytes 331784 | tf_op jit(solution)/shard_map/ppermute | solution.py:63
  490.1 9.1 %collective-permute-start.23 = (bf16[240,768]{1,0:T(8,128)(2,1)S(1)}, bf16[240,768]{1,0:T(8,128)(2,1)S(1)}, u32[]{:S(2)}, u32[]{:S(2)}) collective-permute-start(bf16[240,768]{1,0:T(8,128)(2,1)S(1)} %fusion.131), channel_id=1, source_target_pairs={{0,2},{1,3},{2,0},{3,1},{4,6},{5,7},{6,4},{7,5},{8,10},{9,11},{10,... | collective-permute-start | bytes 1105928 | tf_op jit(solution)/shard_map/ppermute | solution.py:63
  493.7 10.9 %collective-permute-start.27 = (bf16[72,768]{1,0:T(8,128)(2,1)S(1)}, bf16[72,768]{1,0:T(8,128)(2,1)S(1)}, u32[]{:S(2)}, u32[]{:S(2)}) collective-permute-start(bf16[72,768]{1,0:T(8,128)(2,1)S(1)} %fusion.133), channel_id=1, source_target_pairs={{0,16},{4,20},{8,24},{12,28},{16,0},{20,4},{24,8},{28,12},{1,17},{... | collective-permute-start | bytes 331784 | tf_op jit(solution)/shard_map/ppermute | solution.py:63
  501.9 1.3 collective-permute-start.30
  503.2 3.8 collective-permute-start.31
  507.0 3.9 collective-permute-start.32
  508.6 6.5 %collective-permute-start.28 = (bf16[2,72,768]{2,1,0:T(8,128)(2,1)S(1)}, bf16[2,72,768]{2,1,0:T(8,128)(2,1)S(1)}, u32[]{:S(2)}, u32[]{:S(2)}) collective-permute-start(bf16[2,72,768]{2,1,0:T(8,128)(2,1)S(1)} %pad_maximum_fusion.15), channel_id=1, source_target_pairs={{0,8},{4,12},{8,0},{12,4},{16,24},{20,28},{24,16},{28,20},{1,9},{5... | collective-permute-start | bytes 663560 | tf_op jit(solution)/shard_map/ppermute | solution.py:63
  510.9 4.4 collective-permute-start.33
  515.4 4.7 collective-permute-start.34
  516.4 9.9 %collective-permute-start.29 = (bf16[2,2,72,768]{3,2,1,0:T(8,128)(2,1)S(1)}, bf16[2,2,72,768]{3,2,1,0:T(8,128)(2,1)S(1)}, u32[]{:S(2)}, u32[]{:S(2)}) collective-permute-start(bf16[2,2,72,768]{3,2,1,0:T(8,128)(2,1)S(1)} %pad_maximum_fusion.12), channel_id=1, source_target_pairs={{0,4},{4,0},{8,12},{12,8},{16,20},{20,16},{24,28},{28,24},{1,5},{5... | collective-permute-start | bytes 1327112 | tf_op jit(solution)/shard_map/ppermute | solution.py:63
  (74 other events, 260.7 us)
Sparse Core Ops, SparseCore 0:
  14.2 28.7 all-gather.1
  124.3 43.0 all-reduce.3
  363.9 110.2 all-reduce.5

commit v15 on v14

--- a/solution.py
+++ b/solution.py
@@ -328,9 +328,8 @@
         ]
     )
     qkv_sums = reduce_exchanged(grad_qkv.reshape(-1, D), "dp")
-    grad_normed1 = scatter_exchanged(
-        jnp.einsum("jgw,jdw->gd", grad_triple, txt_qkv, preferred_element_type=jnp.float32), "mp"
-    )
+    normed1_part = jnp.einsum("jgw,jdw->gd", grad_triple, txt_qkv, preferred_element_type=jnp.float32)
+    grad_normed1 = scatter_exchanged(normed1_part, "mp")
 
     def own(values):
         return lax.dynamic_slice_in_dim(values, mp_index * own_rows, own_rows, 0)
@@ -342,9 +341,9 @@
     grad_inputs = grad_middle_own + norm_back(grad_normed1, unit1_own, own(inverse1), txt_gains[0])
     small_parts = jnp.stack(
         [
-            jnp.sum(grad_normed1 * unit1_own, 0),
+            jnp.sum(normed1_part * unit1, 0),
             jnp.sum(grad_normed2_own * unit2_own, 0),
-            jnp.sum(grad_normed1, 0),
+            jnp.sum(normed1_part, 0),
             jnp.sum(grad_normed2_own, 0),
             jnp.sum(grad_middle_own, 0),
             jnp.sum(own(grad_result), 0),

time: 550 us -> 548 us (level)
  waiting for transfers between devices: 174 us -> 167 us
    psum x1, waiting for transfers between devices: 49.3 us -> 43.2 us  [local_body(): lax.psum(jnp.concatenate([grad_fc1, grad_fc2], 0).astype(jnp.bfloat16), '...]
    unnamed x190 -> x200, local copies, waits for them, and re-layouts: 13.5 us -> 13.5 us
  transfers between devices with their start and end apart: 44 -> 44, of which waited for: 28 -> 28; matrix products, arithmetic and copies ran while one was open for 50% -> 52% of each run, Pallas kernels for 0% -> 0%
where the time goes in v15:
time: 548 us; the launch traced here: 538 us
  waiting for transfers between devices  167 us (30%)
  matrix products  115 us (21%)
  local copies, waits for them, and re-layouts  111 us (20%)
  other arithmetic  81.8 us (15%)
  starting transfers between devices  43.4 us (8%)
  between operations  19 us (3%)
    ppermute x41, waiting for transfers between devices, exchange(): return lax.ppermute(values, axis, [(i, i ^ 1 << bit) for i in range(count)])  124 us
    dot_general x2, matrix products, image_ffn(): result = middle + jnp.dot(active, w_fc2, preferred_element_type=jnp.float32)  45.8 us
    psum x1, waiting for transfers between devices, local_body(): lax.psum(jnp.concatenate([grad_fc1, grad_fc2], 0).astype(jnp.bfloat16), '...  43.2 us
    ppermute x41, starting transfers between devices, exchange(): return lax.ppermute(values, axis, [(i, i ^ 1 << bit) for i in range(count)])  43.1 us
    concatenate x8, other arithmetic, gather_stacked(): data = jnp.concatenate([data, exchange(data, axis, count, bit)], 0)  20.7 us
    squeeze x4, local copies, waits for them, and re-layouts, image_attention(): shares, _ = attention_shares(shaped[0], shaped[1], None)  15 us
    unnamed x200, local copies, waits for them, and re-layouts  13.5 us
  transfers between devices with their start and end apart: 44, of which 28 were waited for; matrix products, arithmetic and copies ran while one was open for 52% of the time, Pallas kernels for 0%

profile of v15, /device:TPU:0, one launch (start us, length us, event | category | flops | bytes accessed | tf_op | source)
XLA Modules:
  0.0 537.5 jit_solution(10646046617930516037)
XLA Ops:
  7.2 3.1 collective-permute-start
  20.8 2.2 fusion.56
  29.3 16.1 %collective-permute-done.2 = bf16[1,192,768]{2,1,0:T(8,128)(2,1)} collective-permute-done((bf16[1,192,768]{2,1,0:T(8,128)(2,1)}, bf16[1,192,768]{2,1,0:T(8,128)(2,1)}, u32[]{:S(2)}, u32[]{:S(2)}) %collective-permute-start.2) | collective-permute-done | bytes 294944 | tf_op jit(solution)/shard_map/ppermute | solution.py:63
  49.1 2.9 pad_maximum_fusion.6
  54.6 16.0 %collective-permute-done.6 = bf16[1,768,768]{2,1,0:T(8,128)(2,1)} collective-permute-done((bf16[1,768,768]{2,1,0:T(8,128)(2,1)}, bf16[1,768,768]{2,1,0:T(8,128)(2,1)}, u32[]{:S(2)}, u32[]{:S(2)}) %collective-permute-start.6) | collective-permute-done | bytes 1179680 | tf_op jit(solution)/shard_map/ppermute | solution.py:63
  70.6 2.9 pad_maximum_fusion.4
  73.5 21.4 %collective-permute-done.4 = bf16[1,768,768]{1,2,0:T(8,128)(2,1)S(1)} collective-permute-done((bf16[1,768,768]{1,2,0:T(8,128)(2,1)S(1)}, bf16[1,768,768]{1,2,0:T(8,128)(2,1)S(1)}, u32[]{:S(2)}, u32[]{:S(2)}) %collective-permute-start.4) | collective-permute-done | bytes 1179680 | tf_op jit(solution)/shard_map/ppermute | solution.py:63
  100.6 2.5 fusion.128
  104.4 2.5 copy.112
  106.9 6.5 %reshape.296 = bf16[60,16,3,3,64]{4,3,1,0,2:T(4,128)(2,1)} reshape(bf16[960,3,192]{2,0,1:T(8,128)(2,1)} %copy.112) | data formatting | bytes 2211840 | tf_op jit(solution)/shard_map/reshape | solution.py:210
  113.3 3.2 fusion.217
  120.2 2.4 reshape.297
  124.6 2.2 pad_maximum_fusion.2
  130.0 3.3 reshape.316
  133.3 3.3 reshape.315
  136.6 3.0 fusion.71
  139.6 3.9 fusion.222
  143.5 2.3 reshape.314
  145.8 4.1 fusion.75
  152.1 3.1 reshape.294
  155.2 4.7 convert_bitcast_fusion
  161.5 4.4 squeeze.82
  166.0 4.0 squeeze.81
  170.0 3.8 fusion.49
  173.8 3.1 fusion.224
  176.9 4.1 squeeze.80
  181.0 4.2 convert_bitcast_fusion.1
  187.1 4.2 reshape.289
  191.3 2.9 fusion.225
  201.0 8.7 %multiply_convert_fusion = (bf16[960,768]{1,0:T(8,128)(2,1)S(1)}, f32[960,768]{1,0:T(8,128)}, f32[960,768]{1,0:T(8,128)}) fusion(f32[768]{0:T(1024)S(1)} %copy-done.92, bf16[768,768]{1,0:T(8,128)(2,1)S(1)} %copy-done, f32[960,768]{1,0:T(8,128)S(1)} %subtract_multiply_fusion, f32[768]{0:T(1024)S(1)} %copy-done.81, f32[768]{0:T(1024)S(1)} %get-tuple-element.46), kind=kOutput, calls=%fused_computation.70 | convolution fusion | flops 1183334400 | bytes 11510784 | tf_op jit(solution)/shard_map/dot_general | solution.py:231
  215.9 5.1 collective-permute-done.14
  221.4 2.8 collective-permute-start.15
  224.2 4.7 collective-permute-done.15
  230.4 3.9 pad_maximum_fusion.1
  234.2 3.9 pad_maximum_fusion
  238.1 19.6 %fusion.68 = f32[435,768]{1,0:T(8,128)} fusion(f32[435,768]{1,0:T(8,128)S(1)} %copy-done.38, bf16[3072,768]{1,0:T(8,128)(2,1)} %bitcast.268, bf16[768,3072]{0,1:T(8,128)(2,1)} %bitcast.270, f32[768]{0:T(1024)S(1)} %copy-done.83, f32[435]{0:T(512)S(1)} %add_rsqrt_fusion.4, f32[435]{0:T(512)S(1)} %broadcast_multiply_fusion.5), kind=kOutput, calls=%fused_computation.148 | convolution fusion | flops 4193706240 | bytes 12116376 | tf_op jit(solution)/shard_map/dot_general | solution.py:147
  259.5 26.2 %fusion.62 = f32[600,768]{1,0:T(8,128)} fusion(f32[600,768]{1,0:T(8,128)} %copy-done.31, bf16[3072,768]{1,0:T(8,128)(2,1)} %bitcast.269, bf16[768,3072]{0,1:T(8,128)(2,1)} %bitcast.271, f32[768]{0:T(1024)S(1)} %copy-done.83, f32[600]{0:T(1024)S(1)} %add_rsqrt_fusion.2, f32[600]{0:T(1024)S(1)} %broadcast_multiply_fusion.3), kind=kOutput, calls=%fused_computation.129 | convolution fusion | flops 5784422400 | bytes 13131456 | tf_op jit(solution)/shard_map/dot_general | solution.py:147
  292.2 2.3 collective-permute-done.9
  294.5 3.4 collective-permute-start.10
  299.7 2.6 collective-permute-done.10
  302.6 6.4 %collective-permute-done.11 = bf16[2,60,768]{2,1,0:T(8,128)(2,1)S(1)} collective-permute-done((bf16[2,60,768]{2,1,0:T(8,128)(2,1)S(1)}, bf16[2,60,768]{2,1,0:T(8,128)(2,1)S(1)}, u32[]{:S(2)}, u32[]{:S(2)}) %collective-permute-start.11) | collective-permute-done | bytes 184352 | tf_op jit(solution)/shard_map/ppermute | solution.py:63
  312.0 7.2 %collective-permute-done.12 = bf16[2,2,60,768]{3,2,1,0:T(8,128)(2,1)} collective-permute-done((bf16[2,2,60,768]{3,2,1,0:T(8,128)(2,1)S(1)}, bf16[2,2,60,768]{3,2,1,0:T(8,128)(2,1)}, u32[]{:S(2)}, u32[]{:S(2)}) %collective-permute-start.12) | collective-permute-done | bytes 368672 | tf_op jit(solution)/shard_map/ppermute | solution.py:63
  320.6 2.7 select_reduce_fusion
  330.9 2.3 collective-permute-done.18
  340.6 6.1 %collective-permute-done.19 = bf16[240,768]{1,0:T(8,128)(2,1)} collective-permute-done((bf16[240,768]{1,0:T(8,128)(2,1)}, bf16[240,768]{1,0:T(8,128)(2,1)}, u32[]{:S(2)}, u32[]{:S(2)}) %collective-permute-start.19) | collective-permute-done | bytes 368672 | tf_op jit(solution)/shard_map/ppermute | solution.py:63
  349.4 3.4 convolution_convert_fusion.1
  352.8 4.8 collective-permute-done.20
  365.5 2.5 copy-done.2
  368.8 5.7 %bitcast_multiply_fusion.1 = (f32[960,768]{1,0:T(8,128)}, f32[960,768]{1,0:T(8,128)S(1)}) fusion(f32[960]{0:T(1024)S(1)} %mul.488, f32[60,768]{1,0:T(8,128)S(1)} %subtract_multiply_fusion.1, f32[960]{0:T(1024)S(1)} %broadcast_multiply_fusion, f32[960]{0:T(1024)S(1)} %div.136, f32[768]{0:T(1024)S(1)} %copy-done.55, f32[2,2,240,768]{3,2,0,1:T(8,128)} %copy-done.5, ...), kind=kLoop, calls=%fused_computation.63 | loop fusion | flops 6635520 | bytes 12003072 | tf_op jit(solution)/shard_map/mul | solution.py:278
  389.6 2.5 stack.203
  393.1 2.6 copy.127
  395.7 2.4 stack.202
  399.1 5.3 bitcast_reduce_fusion
  409.6 2.6 convolution_bitcast_fusion
  425.7 2.5 collective-permute-done.37
  428.7 43.2 %all-reduce.6.cloned.1.call-done = bf16[1536,768]{1,0:T(8,128)(2,1)} async-done(((bf16[1536,768]{1,0:T(8,128)(2,1)}), bf16[1536,768]{1,0:T(8,128)(2,1)}) %all-reduce.6.cloned.1.call-update) | async-done | bytes 2359312 | tf_op jit(solution)/shard_map/psum | solution.py:287
  471.9 4.2 slice_convert_fusion
  478.4 2.9 collective-permute-done.39
  492.3 4.6 collective-permute-done.23
  497.2 2.3 dynamic-slice_reduce_fusion.2
  502.3 2.3 collective-permute-done.31
  510.1 2.6 collective-permute-done.28
  515.0 2.7 collective-permute-done.34
  519.6 4.3 collective-permute-done.29
  (457 shorter events, 164.9 us)
Async XLA Ops:
  7.2 193.8 %copy-start = (bf16[768,768]{1,0:T(8,128)(2,1)S(1)}, bf16[768,768]{1,0:T(8,128)(2,1)}, u32[]{:S(2)}) copy-start(bf16[768,768]{1,0:T(8,128)(2,1)} %param.32) | copy-start | bytes 3538948
  7.2 89.6 %all-gather.2.cloned.1.call-start = ((), (), s32[]{:S(2)}) async-start(), calls=%async_computation | async-start | bytes 1843200 | tf_op jit(solution)/shard_map/all_gather | solution.py:202
  7.2 41.9 %collective-permute-start = (bf16[1,3,768,192]{2,3,0,1:T(8,128)(2,1)}, bf16[1,3,768,192]{2,3,0,1:T(8,128)(2,1)}, u32[]{:S(2)}, u32[]{:S(2)}) collective-permute-start(bf16[1,3,768,192]{2,3,0,1:T(8,128)(2,1)} %bitcast.273), channel_id=1, source_target_pairs={{0,2},{1,3},{2,0},{3,1},{4,6},{5,7},{6,4},{7,5},{8,10},{9,11},{10,... | collective-permute-start | bytes 2654216 | tf_op jit(solution)/shard_map/ppermute | solution.py:63
  10.3 35.0 %collective-permute-start.2 = (bf16[1,192,768]{2,1,0:T(8,128)(2,1)}, bf16[1,192,768]{2,1,0:T(8,128)(2,1)}, u32[]{:S(2)}, u32[]{:S(2)}) collective-permute-start(bf16[1,192,768]{2,1,0:T(8,128)(2,1)} %bitcast.285), channel_id=1, source_target_pairs={{0,2},{1,3},{2,0},{3,1},{4,6},{5,7},{6,4},{7,5},{8,10},{9,11},{10,... | collective-permute-start | bytes 884744 | tf_op jit(solution)/shard_map/ppermute | solution.py:63
  10.4 12.7 %copy-start.88 = (f32[2,192]{1,0:T(2,128)S(1)}, f32[2,192]{1,0:T(2,128)}, u32[]{:S(2)}) copy-start(f32[2,192]{1,0:T(2,128)} %param.30) | copy-start | bytes 4612
  10.4 13.4 %copy-start.73 = (s32[60,16]{0,1:T(8,128)S(1)}, s32[60,16]{0,1:T(8,128)}, u32[]{:S(2)}) copy-start(s32[60,16]{0,1:T(8,128)} %param.20) | copy-start | bytes 11524
  10.4 60.2 %collective-permute-start.6 = (bf16[1,768,768]{2,1,0:T(8,128)(2,1)}, bf16[1,768,768]{2,1,0:T(8,128)(2,1)}, u32[]{:S(2)}, u32[]{:S(2)}) collective-permute-start(bf16[1,768,768]{2,1,0:T(8,128)(2,1)} %bitcast.265), channel_id=1, source_target_pairs={{0,2},{1,3},{2,0},{3,1},{4,6},{5,7},{6,4},{7,5},{8,10},{9,11},{10,... | collective-permute-start | bytes 3538952 | tf_op jit(solution)/shard_map/ppermute | solution.py:63
  13.9 81.0 %copy-start.10 = (bf16[768,768]{0,1:T(8,128)(2,1)}, bf16[768,768]{0,1:T(8,128)(2,1)S(1)}, u32[]{:S(2)}) copy-start(bf16[768,768]{0,1:T(8,128)(2,1)S(1)} %copy.101) | copy-start | bytes 3538948
  13.9 81.0 %collective-permute-start.4 = (bf16[1,768,768]{1,2,0:T(8,128)(2,1)S(1)}, bf16[1,768,768]{1,2,0:T(8,128)(2,1)S(1)}, u32[]{:S(2)}, u32[]{:S(2)}) collective-permute-start(bf16[1,768,768]{1,2,0:T(8,128)(2,1)S(1)} %bitcast.262), channel_id=1, source_target_pairs={{0,2},{1,3},{2,0},{3,1},{4,6},{5,7},{6,4},{7,5},{8,10},{9,11},{10,... | collective-permute-start | bytes 3538952 | tf_op jit(solution)/shard_map/ppermute | solution.py:63
  14.1 183.5 %all-reduce.4.cloned.1.call-start = ((), (), s32[]{:S(2)}) async-start(), calls=%async_computation.1 | async-start | bytes 2949120 | tf_op jit(solution)/shard_map/psum | solution.py:223
  24.3 30.3 %copy-start.60 = (pred[60,16]{0,1:T(8,128)(4,1)}, pred[60,16]{0,1:T(8,128)(4,1)S(1)}, u32[]{:S(2)}) copy-start(pred[60,16]{0,1:T(8,128)(4,1)S(1)} %get-tuple-element.57) | copy-start | bytes 2884
  28.5 24.0 %copy-start.41 = (bf16[192,768]{1,0:T(8,128)(2,1)S(1)}, bf16[192,768]{1,0:T(8,128)(2,1)}, u32[]{:S(2)}) copy-start(bf16[192,768]{1,0:T(8,128)(2,1)} %param.26) | copy-start | bytes 884740
  29.3 71.3 %copy-start.58 = (f32[768]{0:T(1024)}, f32[768]{0:T(1024)S(1)}, u32[]{:S(2)}) copy-start(f32[768]{0:T(1024)S(1)} %get-tuple-element.47) | copy-start | bytes 9220
  29.3 171.7 %copy-start.54 = (f32[768]{0:T(1024)}, f32[768]{0:T(1024)S(1)}, u32[]{:S(2)}) copy-start(f32[768]{0:T(1024)S(1)} %get-tuple-element.46) | copy-start | bytes 9220
  46.4 6.0 %collective-permute-start.3 = (bf16[2,192,768]{2,1,0:T(8,128)(2,1)S(1)}, bf16[2,192,768]{2,1,0:T(8,128)(2,1)S(1)}, u32[]{:S(2)}, u32[]{:S(2)}) collective-permute-start(bf16[2,192,768]{2,1,0:T(8,128)(2,1)S(1)} %pad_maximum_fusion.10), channel_id=1, source_target_pairs={{0,1},{1,0},{2,3},{3,2},{4,5},{5,4},{6,7},{7,6},{8,9},{9,8},{10,11... | collective-permute-start | bytes 1769480 | tf_op jit(solution)/shard_map/ppermute | solution.py:63
  49.1 21.5 %copy-start.16 = (bf16[768,768]{1,0:T(8,128)(2,1)S(1)}, bf16[768,768]{1,0:T(8,128)(2,1)}, u32[]{:S(2)}) copy-start(bf16[768,768]{1,0:T(8,128)(2,1)} %param.28) | copy-start | bytes 3538948
  52.0 72.6 %collective-permute-start.1 = (bf16[2,3,768,192]{2,3,0,1:T(8,128)(2,1)}, bf16[2,3,768,192]{2,3,0,1:T(8,128)(2,1)}, u32[]{:S(2)}, u32[]{:S(2)}) collective-permute-start(bf16[2,3,768,192]{2,3,0,1:T(8,128)(2,1)} %pad_maximum_fusion.6), channel_id=1, source_target_pairs={{0,1},{1,0},{2,3},{3,2},{4,5},{5,4},{6,7},{7,6},{8,9},{9,8},{10,11... | collective-permute-start | bytes 5308424 | tf_op jit(solution)/shard_map/ppermute | solution.py:63
  73.5 156.8 %collective-permute-start.7 = (bf16[2,768,768]{2,1,0:T(8,128)(2,1)}, bf16[2,768,768]{2,1,0:T(8,128)(2,1)}, u32[]{:S(2)}, u32[]{:S(2)}) collective-permute-start(bf16[2,768,768]{2,1,0:T(8,128)(2,1)} %pad_maximum_fusion.4), channel_id=1, source_target_pairs={{0,1},{1,0},{2,3},{3,2},{4,5},{5,4},{6,7},{7,6},{8,9},{9,8},{10,11... | collective-permute-start | bytes 7077896 | tf_op jit(solution)/shard_map/ppermute | solution.py:63
  96.8 137.5 %collective-permute-start.5 = (bf16[2,768,768]{1,2,0:T(8,128)(2,1)}, bf16[2,768,768]{1,2,0:T(8,128)(2,1)}, u32[]{:S(2)}, u32[]{:S(2)}) collective-permute-start(bf16[2,768,768]{1,2,0:T(8,128)(2,1)} %pad_maximum_fusion.3), channel_id=1, source_target_pairs={{0,1},{1,0},{2,3},{3,2},{4,5},{5,4},{6,7},{7,6},{8,9},{9,8},{10,11... | collective-permute-start | bytes 7077896 | tf_op jit(solution)/shard_map/ppermute | solution.py:63
  124.4 347.5 %all-reduce.6.cloned.1.call-start = ((), (), s32[]{:S(2)}) async-start(), calls=%async_computation.2 | async-start | bytes 4718592 | tf_op jit(solution)/shard_map/psum | solution.py:287
  199.5 11.6 %copy-start.1 = (f32[960,768]{1,0:T(8,128)}, f32[960,768]{1,0:T(8,128)S(1)}, u32[]{:S(2)}) copy-start(f32[960,768]{1,0:T(8,128)S(1)} %get-tuple-element.61) | copy-start | bytes 8847364
  211.1 10.0 %copy-start.77 = (f32[60]{0:T(128)S(1)}, f32[60]{0:T(128)}, u32[]{:S(2)}) copy-start(f32[60]{0:T(128)} %get-tuple-element.56) | copy-start | bytes 724
  212.3 18.0 %copy-start.17 = (bf16[768,768]{1,0:T(8,128)(2,1)S(1)}, bf16[768,768]{1,0:T(8,128)(2,1)}, u32[]{:S(2)}) copy-start(bf16[768,768]{1,0:T(8,128)(2,1)} %param.28) | copy-start | bytes 3538948
  212.3 1.5 collective-permute-start.13
  213.9 7.2 %collective-permute-start.14 = (f32[60,768]{1,0:T(8,128)S(1)}, f32[60,768]{1,0:T(8,128)S(1)}, u32[]{:S(2)}, u32[]{:S(2)}) collective-permute-start(f32[60,768]{1,0:T(8,128)S(1)} %add.348), channel_id=1, source_target_pairs={{0,2},{1,3},{2,0},{3,1},{4,6},{5,7},{6,4},{7,5},{8,10},{9,11},{10,... | collective-permute-start | bytes 552968 | tf_op jit(solution)/shard_map/ppermute | solution.py:63
  221.3 12.9 %copy-start.68 = (f32[60]{0:T(128)}, f32[60]{0:T(128)S(1)}, u32[]{:S(2)}) copy-start(f32[60]{0:T(128)S(1)} %add_rsqrt_fusion.6) | copy-start | bytes 724
  221.4 7.5 %collective-permute-start.15 = (bf16[60,768]{1,0:T(8,128)(2,1)S(1)}, bf16[60,768]{1,0:T(8,128)(2,1)S(1)}, u32[]{:S(2)}, u32[]{:S(2)}) collective-permute-start(bf16[60,768]{1,0:T(8,128)(2,1)S(1)} %multiply_convert_fusion.16), channel_id=1, source_target_pairs={{0,16},{4,20},{8,24},{12,28},{16,0},{20,4},{24,8},{28,12},{1,17},{... | collective-permute-start | bytes 276488 | tf_op jit(solution)/shard_map/ppermute | solution.py:63
  229.7 61.5 %collective-permute-start.16 = (bf16[2,60,768]{2,1,0:T(8,128)(2,1)}, bf16[2,60,768]{2,1,0:T(8,128)(2,1)}, u32[]{:S(2)}, u32[]{:S(2)}) collective-permute-start(bf16[2,60,768]{2,1,0:T(8,128)(2,1)} %pad_maximum_fusion.18), channel_id=1, source_target_pairs={{0,8},{4,12},{8,0},{12,4},{16,24},{20,28},{24,16},{28,20},{1,9},{5... | collective-permute-start | bytes 552968 | tf_op jit(solution)/shard_map/ppermute | solution.py:63
  287.3 15.2 %copy-start.61 = (pred[60,16]{0,1:T(8,128)(4,1)S(1)}, pred[60,16]{0,1:T(8,128)(4,1)}, u32[]{:S(2)}) copy-start(pred[60,16]{0,1:T(8,128)(4,1)} %copy-done.60) | copy-start | bytes 2884
  287.3 15.2 %copy-start.78 = (f32[60]{0:T(128)S(1)}, f32[60]{0:T(128)}, u32[]{:S(2)}) copy-start(f32[60]{0:T(128)} %get-tuple-element.56) | copy-start | bytes 724
  288.2 1.4 collective-permute-start.8
  289.6 4.9 collective-permute-start.9
  294.5 7.8 %collective-permute-start.10 = (bf16[60,768]{1,0:T(8,128)(2,1)S(1)}, bf16[60,768]{1,0:T(8,128)(2,1)S(1)}, u32[]{:S(2)}, u32[]{:S(2)}) collective-permute-start(bf16[60,768]{1,0:T(8,128)(2,1)S(1)} %add.331), channel_id=1, source_target_pairs={{0,16},{4,20},{8,24},{12,28},{16,0},{20,4},{24,8},{28,12},{1,17},{... | collective-permute-start | bytes 276488 | tf_op jit(solution)/shard_map/ppermute | solution.py:63
  298.0 12.8 %collective-permute-start.17 = (bf16[2,2,60,768]{3,2,1,0:T(8,128)(2,1)S(1)}, bf16[2,2,60,768]{3,2,1,0:T(8,128)(2,1)S(1)}, u32[]{:S(2)}, u32[]{:S(2)}) collective-permute-start(bf16[2,2,60,768]{3,2,1,0:T(8,128)(2,1)S(1)} %pad_maximum_fusion.15), channel_id=1, source_target_pairs={{0,4},{4,0},{8,12},{12,8},{16,20},{20,16},{24,28},{28,24},{1,5},{5... | collective-permute-start | bytes 1105928 | tf_op jit(solution)/shard_map/ppermute | solution.py:63
  302.4 6.6 %collective-permute-start.11 = (bf16[2,60,768]{2,1,0:T(8,128)(2,1)S(1)}, bf16[2,60,768]{2,1,0:T(8,128)(2,1)S(1)}, u32[]{:S(2)}, u32[]{:S(2)}) collective-permute-start(bf16[2,60,768]{2,1,0:T(8,128)(2,1)S(1)} %pad_maximum_fusion.17), channel_id=1, source_target_pairs={{0,8},{4,12},{8,0},{12,4},{16,24},{20,28},{24,16},{28,20},{1,9},{5... | collective-permute-start | bytes 552968 | tf_op jit(solution)/shard_map/ppermute | solution.py:63
  309.1 10.1 %collective-permute-start.12 = (bf16[2,2,60,768]{3,2,1,0:T(8,128)(2,1)S(1)}, bf16[2,2,60,768]{3,2,1,0:T(8,128)(2,1)}, u32[]{:S(2)}, u32[]{:S(2)}) collective-permute-start(bf16[2,2,60,768]{3,2,1,0:T(8,128)(2,1)S(1)} %pad_maximum_fusion.14), channel_id=1, source_target_pairs={{0,4},{4,0},{8,12},{12,8},{16,20},{20,16},{24,28},{28,24},{1,5},{5... | collective-permute-start | bytes 1105928 | tf_op jit(solution)/shard_map/ppermute | solution.py:63
  330.8 2.4 collective-permute-start.18
  335.7 10.9 %collective-permute-start.19 = (bf16[240,768]{1,0:T(8,128)(2,1)}, bf16[240,768]{1,0:T(8,128)(2,1)}, u32[]{:S(2)}, u32[]{:S(2)}) collective-permute-start(bf16[240,768]{1,0:T(8,128)(2,1)} %fusion.130), channel_id=1, source_target_pairs={{0,2},{1,3},{2,0},{3,1},{4,6},{5,7},{6,4},{7,5},{8,10},{9,11},{10,... | collective-permute-start | bytes 1105928 | tf_op jit(solution)/shard_map/ppermute | solution.py:63
  347.7 9.8 %collective-permute-start.20 = (bf16[240,768]{1,0:T(8,128)(2,1)S(1)}, bf16[240,768]{1,0:T(8,128)(2,1)S(1)}, u32[]{:S(2)}, u32[]{:S(2)}) collective-permute-start(bf16[240,768]{1,0:T(8,128)(2,1)S(1)} %fusion.105), channel_id=1, source_target_pairs={{0,2},{1,3},{2,0},{3,1},{4,6},{5,7},{6,4},{7,5},{8,10},{9,11},{10,... | collective-permute-start | bytes 1105928 | tf_op jit(solution)/shard_map/ppermute | solution.py:63
  358.6 5.1 collective-permute-start.21
  405.4 81.1 %collective-permute-start.22 = (bf16[2,240,768]{2,1,0:T(8,128)(2,1)}, bf16[2,240,768]{2,1,0:T(8,128)(2,1)}, u32[]{:S(2)}, u32[]{:S(2)}) collective-permute-start(bf16[2,240,768]{2,1,0:T(8,128)(2,1)} %fusion.103), channel_id=1, source_target_pairs={{0,1},{1,0},{2,3},{3,2},{4,5},{5,4},{6,7},{7,6},{8,9},{9,8},{10,11... | collective-permute-start | bytes 2211848 | tf_op jit(solution)/shard_map/ppermute | solution.py:63
  407.9 8.6 %collective-permute-start.35 = (bf16[2,2,24,768]{3,2,1,0:T(8,128)(2,1)}, bf16[2,2,24,768]{3,2,1,0:T(8,128)(2,1)}, u32[]{:S(2)}, u32[]{:S(2)}) collective-permute-start(bf16[2,2,24,768]{3,2,1,0:T(8,128)(2,1)} %fusion.134), channel_id=1, source_target_pairs={{0,4},{4,0},{8,12},{12,8},{16,20},{20,16},{24,28},{28,24},{1,5},{5... | collective-permute-start | bytes 442376 | tf_op jit(solution)/shard_map/ppermute | solution.py:63
  414.3 10.1 %copy-start.85 = (f32[768]{0:T(1024)S(1)}, f32[768]{0:T(1024)}, u32[]{:S(2)}) copy-start(f32[768]{0:T(1024)} %get-tuple-element.35) | copy-start | bytes 9220
  417.6 4.4 collective-permute-start.36
  420.2 56.8 %collective-permute-start.24 = (bf16[2,2,72,768]{3,2,1,0:T(8,128)(2,1)}, bf16[2,2,72,768]{3,2,1,0:T(8,128)(2,1)S(1)}, u32[]{:S(2)}, u32[]{:S(2)}) collective-permute-start(bf16[2,2,72,768]{3,2,1,0:T(8,128)(2,1)} %fusion.127), channel_id=1, source_target_pairs={{0,4},{4,0},{8,12},{12,8},{16,20},{20,16},{24,28},{28,24},{1,5},{5... | collective-permute-start | bytes 1327112 | tf_op jit(solution)/shard_map/ppermute | solution.py:63
  422.1 6.1 %collective-permute-start.37 = (bf16[24,768]{1,0:T(8,128)(2,1)S(1)}, bf16[24,768]{1,0:T(8,128)(2,1)S(1)}, u32[]{:S(2)}, u32[]{:S(2)}) collective-permute-start(bf16[24,768]{1,0:T(8,128)(2,1)S(1)} %fusion.143), channel_id=1, source_target_pairs={{0,16},{4,20},{8,24},{12,28},{16,0},{20,4},{24,8},{28,12},{1,17},{... | collective-permute-start | bytes 110600 | tf_op jit(solution)/shard_map/ppermute | solution.py:63
  428.2 48.8 %copy-start.13 = (f32[2,2,2,72,768]{4,3,2,1,0:T(8,128)S(1)}, f32[2,2,2,72,768]{4,3,2,1,0:T(8,128)}, u32[]{:S(2)}) copy-start(f32[2,2,2,72,768]{4,3,2,1,0:T(8,128)} %reshape_reshape.14) | copy-start | bytes 5308420
  428.2 47.8 %collective-permute-start.38 = (bf16[24,768]{1,0:T(8,128)(2,1)S(1)}, bf16[24,768]{1,0:T(8,128)(2,1)S(1)}, u32[]{:S(2)}, u32[]{:S(2)}) collective-permute-start(bf16[24,768]{1,0:T(8,128)(2,1)S(1)} %fusion.138), channel_id=1, source_target_pairs={{0,16},{4,20},{8,24},{12,28},{16,0},{20,4},{24,8},{28,12},{1,17},{... | collective-permute-start | bytes 110600 | tf_op jit(solution)/shard_map/ppermute | solution.py:63
  476.0 10.4 %copy-start.34 = (f32[960,768,1]{1,0,2:T(8,128)S(1)}, f32[960,768,1]{1,0,2:T(8,128)}, u32[]{:S(2)}) copy-start(f32[960,768,1]{1,0,2:T(8,128)} %copy-done.33) | copy-start | bytes 8847364
  476.1 5.2 collective-permute-start.39
  477.2 7.2 %collective-permute-start.25 = (bf16[2,72,768]{2,1,0:T(8,128)(2,1)S(1)}, bf16[2,72,768]{2,1,0:T(8,128)(2,1)S(1)}, u32[]{:S(2)}, u32[]{:S(2)}) collective-permute-start(bf16[2,72,768]{2,1,0:T(8,128)(2,1)S(1)} %fusion.132), channel_id=1, source_target_pairs={{0,8},{4,12},{8,0},{12,4},{16,24},{20,28},{24,16},{28,20},{1,9},{5... | collective-permute-start | bytes 663560 | tf_op jit(solution)/shard_map/ppermute | solution.py:63
  481.3 8.0 %collective-permute-start.40 = (bf16[2,2,24,768]{3,2,1,0:T(8,128)(2,1)S(1)}, bf16[2,2,24,768]{3,2,1,0:T(8,128)(2,1)S(1)}, u32[]{:S(2)}, u32[]{:S(2)}) collective-permute-start(bf16[2,2,24,768]{3,2,1,0:T(8,128)(2,1)S(1)} %pad_maximum_fusion.19), channel_id=1, source_target_pairs={{0,4},{4,0},{8,12},{12,8},{16,20},{20,16},{24,28},{28,24},{1,5},{5... | collective-permute-start | bytes 442376 | tf_op jit(solution)/shard_map/ppermute | solution.py:63
  484.4 12.5 %copy-start.45 = (f32[960,768]{1,0:T(8,128)S(1)}, f32[960,768]{1,0:T(8,128)}, u32[]{:S(2)}) copy-start(f32[960,768]{1,0:T(8,128)} %get-tuple-element.75) | copy-start | bytes 8847364
  484.5 12.7 %copy-start.79 = (f32[240]{0:T(256)S(1)}, f32[240]{0:T(256)}, u32[]{:S(2)}) copy-start(f32[240]{0:T(256)} %dynamic-slice.3) | copy-start | bytes 2884
  484.5 6.9 %collective-permute-start.26 = (bf16[72,768]{1,0:T(8,128)(2,1)S(1)}, bf16[72,768]{1,0:T(8,128)(2,1)S(1)}, u32[]{:S(2)}, u32[]{:S(2)}) collective-permute-start(bf16[72,768]{1,0:T(8,128)(2,1)S(1)} %fusion.135), channel_id=1, source_target_pairs={{0,16},{4,20},{8,24},{12,28},{16,0},{20,4},{24,8},{28,12},{1,17},{... | collective-permute-start | bytes 331784 | tf_op jit(solution)/shard_map/ppermute | solution.py:63
  487.8 9.1 %collective-permute-start.23 = (bf16[240,768]{1,0:T(8,128)(2,1)S(1)}, bf16[240,768]{1,0:T(8,128)(2,1)S(1)}, u32[]{:S(2)}, u32[]{:S(2)}) collective-permute-start(bf16[240,768]{1,0:T(8,128)(2,1)S(1)} %fusion.131), channel_id=1, source_target_pairs={{0,2},{1,3},{2,0},{3,1},{4,6},{5,7},{6,4},{7,5},{8,10},{9,11},{10,... | collective-permute-start | bytes 1105928 | tf_op jit(solution)/shard_map/ppermute | solution.py:63
  491.4 10.8 %collective-permute-start.27 = (bf16[72,768]{1,0:T(8,128)(2,1)S(1)}, bf16[72,768]{1,0:T(8,128)(2,1)S(1)}, u32[]{:S(2)}, u32[]{:S(2)}) collective-permute-start(bf16[72,768]{1,0:T(8,128)(2,1)S(1)} %fusion.133), channel_id=1, source_target_pairs={{0,16},{4,20},{8,24},{12,28},{16,0},{20,4},{24,8},{28,12},{1,17},{... | collective-permute-start | bytes 331784 | tf_op jit(solution)/shard_map/ppermute | solution.py:63
  499.5 1.3 collective-permute-start.30
  500.8 3.8 collective-permute-start.31
  504.6 3.9 collective-permute-start.32
  506.2 6.5 %collective-permute-start.28 = (bf16[2,72,768]{2,1,0:T(8,128)(2,1)S(1)}, bf16[2,72,768]{2,1,0:T(8,128)(2,1)S(1)}, u32[]{:S(2)}, u32[]{:S(2)}) collective-permute-start(bf16[2,72,768]{2,1,0:T(8,128)(2,1)S(1)} %pad_maximum_fusion.16), channel_id=1, source_target_pairs={{0,8},{4,12},{8,0},{12,4},{16,24},{20,28},{24,16},{28,20},{1,9},{5... | collective-permute-start | bytes 663560 | tf_op jit(solution)/shard_map/ppermute | solution.py:63
  508.5 4.4 collective-permute-start.33
  513.0 4.7 collective-permute-start.34
  514.0 9.9 %collective-permute-start.29 = (bf16[2,2,72,768]{3,2,1,0:T(8,128)(2,1)S(1)}, bf16[2,2,72,768]{3,2,1,0:T(8,128)(2,1)S(1)}, u32[]{:S(2)}, u32[]{:S(2)}) collective-permute-start(bf16[2,2,72,768]{3,2,1,0:T(8,128)(2,1)S(1)} %pad_maximum_fusion.13), channel_id=1, source_target_pairs={{0,4},{4,0},{8,12},{12,8},{16,20},{20,16},{24,28},{28,24},{1,5},{5... | collective-permute-start | bytes 1327112 | tf_op jit(solution)/shard_map/ppermute | solution.py:63
  (79 other events, 310.9 us)
Sparse Core Ops, SparseCore 0:
  14.2 28.7 all-gather.1
  124.5 43.0 all-reduce.3
  361.8 110.0 all-reduce.5

commit v16 on v15

--- a/solution.py
+++ b/solution.py
@@ -93,12 +93,17 @@
     return values
 
 
-def scatter_exchanged(values, axis):
+def scatter_exchanged(values, axis, swap_first=False):
     count, bits = axis_bits(axis)
     index = lax.axis_index(axis)
     data = values.reshape((2,) * len(bits) + (values.shape[0] // count,) + values.shape[1:])
-    for bit in reversed(bits):
-        place = len(bits) - 1 - bit
+    order = list(reversed(bits))
+    if swap_first and len(order) > 1:
+        order[0], order[1] = order[1], order[0]
+    left = list(bits)
+    for bit in order:
+        place = left.index(bit)
+        left.remove(bit)
         mine = (index >> bit) & 1
         kept = lax.dynamic_index_in_dim(data, mine, place, keepdims=False)
         sent = lax.dynamic_index_in_dim(data, 1 - mine, place, keepdims=False)
@@ -106,8 +111,8 @@
     return data
 
 
-def reduce_exchanged(values, axis):
-    part = scatter_exchanged(values, axis).astype(jnp.bfloat16)
+def reduce_exchanged(values, axis, swap_first=False):
+    part = scatter_exchanged(values, axis, swap_first).astype(jnp.bfloat16)
     return gather_ordered(part, axis).reshape(values.shape)
 
 
@@ -327,7 +332,7 @@
             jnp.sum(grad_triple[2].astype(jnp.float32), 0),
         ]
     )
-    qkv_sums = reduce_exchanged(grad_qkv.reshape(-1, D), "dp")
+    qkv_sums = reduce_exchanged(grad_qkv.reshape(-1, D), "dp", swap_first=True)
     normed1_part = jnp.einsum("jgw,jdw->gd", grad_triple, txt_qkv, preferred_element_type=jnp.float32)
     grad_normed1 = scatter_exchanged(normed1_part, "mp")
 

time: 548 us -> 546 us (level)
  waiting for transfers between devices: 167 us -> 161 us
    psum x1, waiting for transfers between devices: 43.2 us -> 30.2 us  [local_body(): lax.psum(jnp.concatenate([grad_fc1, grad_fc2], 0).astype(jnp.bfloat16), '...]
    ppermute x41, waiting for transfers between devices: 124 us -> 131 us  [exchange(): return lax.ppermute(values, axis, [(i, i ^ 1 << bit) for i in range(count)])]
  transfers between devices with their start and end apart: 44 -> 44, of which waited for: 28 -> 27; matrix products, arithmetic and copies ran while one was open for 52% -> 52% of each run, Pallas kernels for 0% -> 0%
where the time goes in v16:
time: 546 us; the launch traced here: 536 us
  waiting for transfers between devices  161 us (29%)
  matrix products  115 us (21%)
  local copies, waits for them, and re-layouts  111 us (20%)
  other arithmetic  81.8 us (15%)
  starting transfers between devices  47.6 us (9%)
  between operations  19 us (3%)
    ppermute x41, waiting for transfers between devices, exchange(): return lax.ppermute(values, axis, [(i, i ^ 1 << bit) for i in range(count)])  131 us
    ppermute x41, starting transfers between devices, exchange(): return lax.ppermute(values, axis, [(i, i ^ 1 << bit) for i in range(count)])  47.3 us
    dot_general x2, matrix products, image_ffn(): result = middle + jnp.dot(active, w_fc2, preferred_element_type=jnp.float32)  45.8 us
    psum x1, waiting for transfers between devices, local_body(): lax.psum(jnp.concatenate([grad_fc1, grad_fc2], 0).astype(jnp.bfloat16), '...  30.2 us
    concatenate x8, other arithmetic, gather_stacked(): data = jnp.concatenate([data, exchange(data, axis, count, bit)], 0)  20.7 us
    squeeze x4, local copies, waits for them, and re-layouts, image_attention(): shares, _ = attention_shares(shaped[0], shaped[1], None)  15 us
    unnamed x200, local copies, waits for them, and re-layouts  13.5 us
  transfers between devices with their start and end apart: 44, of which 27 were waited for; matrix products, arithmetic and copies ran while one was open for 52% of the time, Pallas kernels for 0%

profile of v16, /device:TPU:0, one launch (start us, length us, event | category | flops | bytes accessed | tf_op | source)
XLA Modules:
  0.0 535.9 jit_solution(12149659181684489518)
XLA Ops:
  7.2 3.1 collective-permute-start
  20.8 2.2 fusion.56
  29.3 16.1 %collective-permute-done.2 = bf16[1,192,768]{2,1,0:T(8,128)(2,1)} collective-permute-done((bf16[1,192,768]{2,1,0:T(8,128)(2,1)}, bf16[1,192,768]{2,1,0:T(8,128)(2,1)}, u32[]{:S(2)}, u32[]{:S(2)}) %collective-permute-start.2) | collective-permute-done | bytes 294944 | tf_op jit(solution)/shard_map/ppermute | solution.py:63
  49.1 2.9 pad_maximum_fusion.6
  54.6 16.0 %collective-permute-done.6 = bf16[1,768,768]{2,1,0:T(8,128)(2,1)} collective-permute-done((bf16[1,768,768]{2,1,0:T(8,128)(2,1)}, bf16[1,768,768]{2,1,0:T(8,128)(2,1)}, u32[]{:S(2)}, u32[]{:S(2)}) %collective-permute-start.6) | collective-permute-done | bytes 1179680 | tf_op jit(solution)/shard_map/ppermute | solution.py:63
  70.6 2.9 pad_maximum_fusion.4
  73.5 21.4 %collective-permute-done.4 = bf16[1,768,768]{1,2,0:T(8,128)(2,1)S(1)} collective-permute-done((bf16[1,768,768]{1,2,0:T(8,128)(2,1)S(1)}, bf16[1,768,768]{1,2,0:T(8,128)(2,1)S(1)}, u32[]{:S(2)}, u32[]{:S(2)}) %collective-permute-start.4) | collective-permute-done | bytes 1179680 | tf_op jit(solution)/shard_map/ppermute | solution.py:63
  100.6 2.5 fusion.128
  104.4 2.5 copy.112
  106.9 6.5 %reshape.296 = bf16[60,16,3,3,64]{4,3,1,0,2:T(4,128)(2,1)} reshape(bf16[960,3,192]{2,0,1:T(8,128)(2,1)} %copy.112) | data formatting | bytes 2211840 | tf_op jit(solution)/shard_map/reshape | solution.py:215
  113.3 3.2 fusion.217
  120.2 2.4 reshape.297
  124.6 2.2 pad_maximum_fusion.2
  130.0 3.3 reshape.316
  133.3 3.3 reshape.315
  136.6 3.0 fusion.71
  139.6 3.9 fusion.222
  143.5 2.3 reshape.314
  145.8 4.1 fusion.75
  152.1 3.1 reshape.294
  155.2 4.7 convert_bitcast_fusion
  161.5 4.4 squeeze.82
  166.0 4.0 squeeze.81
  170.0 3.8 fusion.49
  173.8 3.1 fusion.224
  176.9 4.1 squeeze.80
  181.0 4.2 convert_bitcast_fusion.1
  187.1 4.2 reshape.289
  191.3 2.9 fusion.225
  201.0 8.7 %multiply_convert_fusion = (bf16[960,768]{1,0:T(8,128)(2,1)S(1)}, f32[960,768]{1,0:T(8,128)}, f32[960,768]{1,0:T(8,128)}) fusion(f32[768]{0:T(1024)S(1)} %copy-done.92, bf16[768,768]{1,0:T(8,128)(2,1)S(1)} %copy-done, f32[960,768]{1,0:T(8,128)S(1)} %subtract_multiply_fusion, f32[768]{0:T(1024)S(1)} %copy-done.81, f32[768]{0:T(1024)S(1)} %get-tuple-element.46), kind=kOutput, calls=%fused_computation.70 | convolution fusion | flops 1183334400 | bytes 11510784 | tf_op jit(solution)/shard_map/dot_general | solution.py:236
  215.9 5.1 collective-permute-done.14
  221.4 2.8 collective-permute-start.15
  224.2 4.7 collective-permute-done.15
  230.4 3.9 pad_maximum_fusion.1
  234.2 3.9 pad_maximum_fusion
  238.1 19.6 %fusion.68 = f32[435,768]{1,0:T(8,128)} fusion(f32[435,768]{1,0:T(8,128)S(1)} %copy-done.38, bf16[3072,768]{1,0:T(8,128)(2,1)} %bitcast.268, bf16[768,3072]{0,1:T(8,128)(2,1)} %bitcast.270, f32[768]{0:T(1024)S(1)} %copy-done.83, f32[435]{0:T(512)S(1)} %add_rsqrt_fusion.4, f32[435]{0:T(512)S(1)} %broadcast_multiply_fusion.5), kind=kOutput, calls=%fused_computation.148 | convolution fusion | flops 4193706240 | bytes 12116376 | tf_op jit(solution)/shard_map/dot_general | solution.py:152
  259.5 26.2 %fusion.62 = f32[600,768]{1,0:T(8,128)} fusion(f32[600,768]{1,0:T(8,128)} %copy-done.31, bf16[3072,768]{1,0:T(8,128)(2,1)} %bitcast.269, bf16[768,3072]{0,1:T(8,128)(2,1)} %bitcast.271, f32[768]{0:T(1024)S(1)} %copy-done.83, f32[600]{0:T(1024)S(1)} %add_rsqrt_fusion.2, f32[600]{0:T(1024)S(1)} %broadcast_multiply_fusion.3), kind=kOutput, calls=%fused_computation.129 | convolution fusion | flops 5784422400 | bytes 13131456 | tf_op jit(solution)/shard_map/dot_general | solution.py:152
  292.2 2.3 collective-permute-done.9
  294.5 3.4 collective-permute-start.10
  299.7 2.6 collective-permute-done.10
  302.6 6.4 %collective-permute-done.11 = bf16[2,60,768]{2,1,0:T(8,128)(2,1)S(1)} collective-permute-done((bf16[2,60,768]{2,1,0:T(8,128)(2,1)S(1)}, bf16[2,60,768]{2,1,0:T(8,128)(2,1)S(1)}, u32[]{:S(2)}, u32[]{:S(2)}) %collective-permute-start.11) | collective-permute-done | bytes 184352 | tf_op jit(solution)/shard_map/ppermute | solution.py:63
  312.0 7.2 %collective-permute-done.12 = bf16[2,2,60,768]{3,2,1,0:T(8,128)(2,1)} collective-permute-done((bf16[2,2,60,768]{3,2,1,0:T(8,128)(2,1)S(1)}, bf16[2,2,60,768]{3,2,1,0:T(8,128)(2,1)}, u32[]{:S(2)}, u32[]{:S(2)}) %collective-permute-start.12) | collective-permute-done | bytes 368672 | tf_op jit(solution)/shard_map/ppermute | solution.py:63
  320.6 2.7 select_reduce_fusion
  330.9 2.3 collective-permute-done.18
  340.6 6.1 %collective-permute-done.19 = bf16[240,768]{1,0:T(8,128)(2,1)} collective-permute-done((bf16[240,768]{1,0:T(8,128)(2,1)}, bf16[240,768]{1,0:T(8,128)(2,1)}, u32[]{:S(2)}, u32[]{:S(2)}) %collective-permute-start.19) | collective-permute-done | bytes 368672 | tf_op jit(solution)/shard_map/ppermute | solution.py:63
  349.4 3.4 convolution_convert_fusion.1
  352.8 4.8 collective-permute-done.20
  365.5 2.5 copy-done.2
  368.8 5.7 %bitcast_multiply_fusion.1 = (f32[960,768]{1,0:T(8,128)}, f32[960,768]{1,0:T(8,128)S(1)}) fusion(f32[960]{0:T(1024)S(1)} %mul.488, f32[60,768]{1,0:T(8,128)S(1)} %subtract_multiply_fusion.1, f32[960]{0:T(1024)S(1)} %broadcast_multiply_fusion, f32[960]{0:T(1024)S(1)} %div.136, f32[768]{0:T(1024)S(1)} %copy-done.55, f32[2,2,240,768]{3,2,0,1:T(8,128)} %copy-done.5, ...), kind=kLoop, calls=%fused_computation.63 | loop fusion | flops 6635520 | bytes 12003072 | tf_op jit(solution)/shard_map/mul | solution.py:283
  389.6 2.5 stack.203
  393.1 2.6 copy.127
  395.7 2.4 stack.202
  399.1 5.3 bitcast_reduce_fusion
  409.6 2.6 convolution_bitcast_fusion
  426.2 11.0 %collective-permute-done.37 = bf16[24,768]{1,0:T(8,128)(2,1)S(1)} collective-permute-done((bf16[24,768]{1,0:T(8,128)(2,1)S(1)}, bf16[24,768]{1,0:T(8,128)(2,1)S(1)}, u32[]{:S(2)}, u32[]{:S(2)}) %collective-permute-start.37) | collective-permute-done | bytes 36896 | tf_op jit(solution)/shard_map/ppermute | solution.py:63
  437.2 3.5 collective-permute-start.38
  440.8 30.2 %all-reduce.6.cloned.1.call-done = bf16[1536,768]{1,0:T(8,128)(2,1)} async-done(((bf16[1536,768]{1,0:T(8,128)(2,1)}), bf16[1536,768]{1,0:T(8,128)(2,1)}) %all-reduce.6.cloned.1.call-update) | async-done | bytes 2359312 | tf_op jit(solution)/shard_map/psum | solution.py:292
  470.9 4.2 slice_convert_fusion
  481.1 3.1 collective-permute-done.25
  488.9 4.3 collective-permute-done.26
  495.3 2.3 dynamic-slice_reduce_fusion.2
  508.3 2.6 collective-permute-done.28
  513.3 2.6 collective-permute-done.34
  517.8 4.4 collective-permute-done.29
  (457 shorter events, 166.8 us)
Async XLA Ops:
  7.2 193.8 %copy-start = (bf16[768,768]{1,0:T(8,128)(2,1)S(1)}, bf16[768,768]{1,0:T(8,128)(2,1)}, u32[]{:S(2)}) copy-start(bf16[768,768]{1,0:T(8,128)(2,1)} %param.32) | copy-start | bytes 3538948
  7.2 89.6 %all-gather.2.cloned.1.call-start = ((), (), s32[]{:S(2)}) async-start(), calls=%async_computation | async-start | bytes 1843200 | tf_op jit(solution)/shard_map/all_gather | solution.py:207
  7.2 41.9 %collective-permute-start = (bf16[1,3,768,192]{2,3,0,1:T(8,128)(2,1)}, bf16[1,3,768,192]{2,3,0,1:T(8,128)(2,1)}, u32[]{:S(2)}, u32[]{:S(2)}) collective-permute-start(bf16[1,3,768,192]{2,3,0,1:T(8,128)(2,1)} %bitcast.273), channel_id=1, source_target_pairs={{0,2},{1,3},{2,0},{3,1},{4,6},{5,7},{6,4},{7,5},{8,10},{9,11},{10,... | collective-permute-start | bytes 2654216 | tf_op jit(solution)/shard_map/ppermute | solution.py:63
  10.3 35.0 %collective-permute-start.2 = (bf16[1,192,768]{2,1,0:T(8,128)(2,1)}, bf16[1,192,768]{2,1,0:T(8,128)(2,1)}, u32[]{:S(2)}, u32[]{:S(2)}) collective-permute-start(bf16[1,192,768]{2,1,0:T(8,128)(2,1)} %bitcast.285), channel_id=1, source_target_pairs={{0,2},{1,3},{2,0},{3,1},{4,6},{5,7},{6,4},{7,5},{8,10},{9,11},{10,... | collective-permute-start | bytes 884744 | tf_op jit(solution)/shard_map/ppermute | solution.py:63
  10.4 12.7 %copy-start.88 = (f32[2,192]{1,0:T(2,128)S(1)}, f32[2,192]{1,0:T(2,128)}, u32[]{:S(2)}) copy-start(f32[2,192]{1,0:T(2,128)} %param.30) | copy-start | bytes 4612
  10.4 13.4 %copy-start.73 = (s32[60,16]{0,1:T(8,128)S(1)}, s32[60,16]{0,1:T(8,128)}, u32[]{:S(2)}) copy-start(s32[60,16]{0,1:T(8,128)} %param.20) | copy-start | bytes 11524
  10.4 60.2 %collective-permute-start.6 = (bf16[1,768,768]{2,1,0:T(8,128)(2,1)}, bf16[1,768,768]{2,1,0:T(8,128)(2,1)}, u32[]{:S(2)}, u32[]{:S(2)}) collective-permute-start(bf16[1,768,768]{2,1,0:T(8,128)(2,1)} %bitcast.265), channel_id=1, source_target_pairs={{0,2},{1,3},{2,0},{3,1},{4,6},{5,7},{6,4},{7,5},{8,10},{9,11},{10,... | collective-permute-start | bytes 3538952 | tf_op jit(solution)/shard_map/ppermute | solution.py:63
  13.9 81.0 %copy-start.10 = (bf16[768,768]{0,1:T(8,128)(2,1)}, bf16[768,768]{0,1:T(8,128)(2,1)S(1)}, u32[]{:S(2)}) copy-start(bf16[768,768]{0,1:T(8,128)(2,1)S(1)} %copy.101) | copy-start | bytes 3538948
  13.9 81.0 %collective-permute-start.4 = (bf16[1,768,768]{1,2,0:T(8,128)(2,1)S(1)}, bf16[1,768,768]{1,2,0:T(8,128)(2,1)S(1)}, u32[]{:S(2)}, u32[]{:S(2)}) collective-permute-start(bf16[1,768,768]{1,2,0:T(8,128)(2,1)S(1)} %bitcast.262), channel_id=1, source_target_pairs={{0,2},{1,3},{2,0},{3,1},{4,6},{5,7},{6,4},{7,5},{8,10},{9,11},{10,... | collective-permute-start | bytes 3538952 | tf_op jit(solution)/shard_map/ppermute | solution.py:63
  14.1 183.5 %all-reduce.4.cloned.1.call-start = ((), (), s32[]{:S(2)}) async-start(), calls=%async_computation.1 | async-start | bytes 2949120 | tf_op jit(solution)/shard_map/psum | solution.py:228
  24.3 30.3 %copy-start.60 = (pred[60,16]{0,1:T(8,128)(4,1)}, pred[60,16]{0,1:T(8,128)(4,1)S(1)}, u32[]{:S(2)}) copy-start(pred[60,16]{0,1:T(8,128)(4,1)S(1)} %get-tuple-element.57) | copy-start | bytes 2884
  28.5 24.0 %copy-start.41 = (bf16[192,768]{1,0:T(8,128)(2,1)S(1)}, bf16[192,768]{1,0:T(8,128)(2,1)}, u32[]{:S(2)}) copy-start(bf16[192,768]{1,0:T(8,128)(2,1)} %param.26) | copy-start | bytes 884740
  29.3 71.3 %copy-start.58 = (f32[768]{0:T(1024)}, f32[768]{0:T(1024)S(1)}, u32[]{:S(2)}) copy-start(f32[768]{0:T(1024)S(1)} %get-tuple-element.47) | copy-start | bytes 9220
  29.3 171.7 %copy-start.54 = (f32[768]{0:T(1024)}, f32[768]{0:T(1024)S(1)}, u32[]{:S(2)}) copy-start(f32[768]{0:T(1024)S(1)} %get-tuple-element.46) | copy-start | bytes 9220
  46.4 6.0 %collective-permute-start.3 = (bf16[2,192,768]{2,1,0:T(8,128)(2,1)S(1)}, bf16[2,192,768]{2,1,0:T(8,128)(2,1)S(1)}, u32[]{:S(2)}, u32[]{:S(2)}) collective-permute-start(bf16[2,192,768]{2,1,0:T(8,128)(2,1)S(1)} %pad_maximum_fusion.10), channel_id=1, source_target_pairs={{0,1},{1,0},{2,3},{3,2},{4,5},{5,4},{6,7},{7,6},{8,9},{9,8},{10,11... | collective-permute-start | bytes 1769480 | tf_op jit(solution)/shard_map/ppermute | solution.py:63
  49.1 21.5 %copy-start.16 = (bf16[768,768]{1,0:T(8,128)(2,1)S(1)}, bf16[768,768]{1,0:T(8,128)(2,1)}, u32[]{:S(2)}) copy-start(bf16[768,768]{1,0:T(8,128)(2,1)} %param.28) | copy-start | bytes 3538948
  52.0 72.6 %collective-permute-start.1 = (bf16[2,3,768,192]{2,3,0,1:T(8,128)(2,1)}, bf16[2,3,768,192]{2,3,0,1:T(8,128)(2,1)}, u32[]{:S(2)}, u32[]{:S(2)}) collective-permute-start(bf16[2,3,768,192]{2,3,0,1:T(8,128)(2,1)} %pad_maximum_fusion.6), channel_id=1, source_target_pairs={{0,1},{1,0},{2,3},{3,2},{4,5},{5,4},{6,7},{7,6},{8,9},{9,8},{10,11... | collective-permute-start | bytes 5308424 | tf_op jit(solution)/shard_map/ppermute | solution.py:63
  73.5 156.8 %collective-permute-start.7 = (bf16[2,768,768]{2,1,0:T(8,128)(2,1)}, bf16[2,768,768]{2,1,0:T(8,128)(2,1)}, u32[]{:S(2)}, u32[]{:S(2)}) collective-permute-start(bf16[2,768,768]{2,1,0:T(8,128)(2,1)} %pad_maximum_fusion.4), channel_id=1, source_target_pairs={{0,1},{1,0},{2,3},{3,2},{4,5},{5,4},{6,7},{7,6},{8,9},{9,8},{10,11... | collective-permute-start | bytes 7077896 | tf_op jit(solution)/shard_map/ppermute | solution.py:63
  96.8 137.5 %collective-permute-start.5 = (bf16[2,768,768]{1,2,0:T(8,128)(2,1)}, bf16[2,768,768]{1,2,0:T(8,128)(2,1)}, u32[]{:S(2)}, u32[]{:S(2)}) collective-permute-start(bf16[2,768,768]{1,2,0:T(8,128)(2,1)} %pad_maximum_fusion.3), channel_id=1, source_target_pairs={{0,1},{1,0},{2,3},{3,2},{4,5},{5,4},{6,7},{7,6},{8,9},{9,8},{10,11... | collective-permute-start | bytes 7077896 | tf_op jit(solution)/shard_map/ppermute | solution.py:63
  124.4 346.5 %all-reduce.6.cloned.1.call-start = ((), (), s32[]{:S(2)}) async-start(), calls=%async_computation.2 | async-start | bytes 4718592 | tf_op jit(solution)/shard_map/psum | solution.py:292
  199.5 11.6 %copy-start.1 = (f32[960,768]{1,0:T(8,128)}, f32[960,768]{1,0:T(8,128)S(1)}, u32[]{:S(2)}) copy-start(f32[960,768]{1,0:T(8,128)S(1)} %get-tuple-element.61) | copy-start | bytes 8847364
  211.1 10.0 %copy-start.77 = (f32[60]{0:T(128)S(1)}, f32[60]{0:T(128)}, u32[]{:S(2)}) copy-start(f32[60]{0:T(128)} %get-tuple-element.56) | copy-start | bytes 724
  212.3 18.0 %copy-start.17 = (bf16[768,768]{1,0:T(8,128)(2,1)S(1)}, bf16[768,768]{1,0:T(8,128)(2,1)}, u32[]{:S(2)}) copy-start(bf16[768,768]{1,0:T(8,128)(2,1)} %param.28) | copy-start | bytes 3538948
  212.3 1.5 collective-permute-start.13
  213.9 7.2 %collective-permute-start.14 = (f32[60,768]{1,0:T(8,128)S(1)}, f32[60,768]{1,0:T(8,128)S(1)}, u32[]{:S(2)}, u32[]{:S(2)}) collective-permute-start(f32[60,768]{1,0:T(8,128)S(1)} %add.348), channel_id=1, source_target_pairs={{0,2},{1,3},{2,0},{3,1},{4,6},{5,7},{6,4},{7,5},{8,10},{9,11},{10,... | collective-permute-start | bytes 552968 | tf_op jit(solution)/shard_map/ppermute | solution.py:63
  221.3 12.9 %copy-start.68 = (f32[60]{0:T(128)}, f32[60]{0:T(128)S(1)}, u32[]{:S(2)}) copy-start(f32[60]{0:T(128)S(1)} %add_rsqrt_fusion.6) | copy-start | bytes 724
  221.4 7.5 %collective-permute-start.15 = (bf16[60,768]{1,0:T(8,128)(2,1)S(1)}, bf16[60,768]{1,0:T(8,128)(2,1)S(1)}, u32[]{:S(2)}, u32[]{:S(2)}) collective-permute-start(bf16[60,768]{1,0:T(8,128)(2,1)S(1)} %multiply_convert_fusion.16), channel_id=1, source_target_pairs={{0,16},{4,20},{8,24},{12,28},{16,0},{20,4},{24,8},{28,12},{1,17},{... | collective-permute-start | bytes 276488 | tf_op jit(solution)/shard_map/ppermute | solution.py:63
  229.7 61.5 %collective-permute-start.16 = (bf16[2,60,768]{2,1,0:T(8,128)(2,1)}, bf16[2,60,768]{2,1,0:T(8,128)(2,1)}, u32[]{:S(2)}, u32[]{:S(2)}) collective-permute-start(bf16[2,60,768]{2,1,0:T(8,128)(2,1)} %pad_maximum_fusion.18), channel_id=1, source_target_pairs={{0,8},{4,12},{8,0},{12,4},{16,24},{20,28},{24,16},{28,20},{1,9},{5... | collective-permute-start | bytes 552968 | tf_op jit(solution)/shard_map/ppermute | solution.py:63
  287.3 15.2 %copy-start.61 = (pred[60,16]{0,1:T(8,128)(4,1)S(1)}, pred[60,16]{0,1:T(8,128)(4,1)}, u32[]{:S(2)}) copy-start(pred[60,16]{0,1:T(8,128)(4,1)} %copy-done.60) | copy-start | bytes 2884
  287.3 15.2 %copy-start.78 = (f32[60]{0:T(128)S(1)}, f32[60]{0:T(128)}, u32[]{:S(2)}) copy-start(f32[60]{0:T(128)} %get-tuple-element.56) | copy-start | bytes 724
  288.2 1.4 collective-permute-start.8
  289.6 4.9 collective-permute-start.9
  294.5 7.8 %collective-permute-start.10 = (bf16[60,768]{1,0:T(8,128)(2,1)S(1)}, bf16[60,768]{1,0:T(8,128)(2,1)S(1)}, u32[]{:S(2)}, u32[]{:S(2)}) collective-permute-start(bf16[60,768]{1,0:T(8,128)(2,1)S(1)} %add.331), channel_id=1, source_target_pairs={{0,16},{4,20},{8,24},{12,28},{16,0},{20,4},{24,8},{28,12},{1,17},{... | collective-permute-start | bytes 276488 | tf_op jit(solution)/shard_map/ppermute | solution.py:63
  298.0 12.8 %collective-permute-start.17 = (bf16[2,2,60,768]{3,2,1,0:T(8,128)(2,1)S(1)}, bf16[2,2,60,768]{3,2,1,0:T(8,128)(2,1)S(1)}, u32[]{:S(2)}, u32[]{:S(2)}) collective-permute-start(bf16[2,2,60,768]{3,2,1,0:T(8,128)(2,1)S(1)} %pad_maximum_fusion.15), channel_id=1, source_target_pairs={{0,4},{4,0},{8,12},{12,8},{16,20},{20,16},{24,28},{28,24},{1,5},{5... | collective-permute-start | bytes 1105928 | tf_op jit(solution)/shard_map/ppermute | solution.py:63
  302.4 6.6 %collective-permute-start.11 = (bf16[2,60,768]{2,1,0:T(8,128)(2,1)S(1)}, bf16[2,60,768]{2,1,0:T(8,128)(2,1)S(1)}, u32[]{:S(2)}, u32[]{:S(2)}) collective-permute-start(bf16[2,60,768]{2,1,0:T(8,128)(2,1)S(1)} %pad_maximum_fusion.17), channel_id=1, source_target_pairs={{0,8},{4,12},{8,0},{12,4},{16,24},{20,28},{24,16},{28,20},{1,9},{5... | collective-permute-start | bytes 552968 | tf_op jit(solution)/shard_map/ppermute | solution.py:63
  309.1 10.1 %collective-permute-start.12 = (bf16[2,2,60,768]{3,2,1,0:T(8,128)(2,1)S(1)}, bf16[2,2,60,768]{3,2,1,0:T(8,128)(2,1)}, u32[]{:S(2)}, u32[]{:S(2)}) collective-permute-start(bf16[2,2,60,768]{3,2,1,0:T(8,128)(2,1)S(1)} %pad_maximum_fusion.14), channel_id=1, source_target_pairs={{0,4},{4,0},{8,12},{12,8},{16,20},{20,16},{24,28},{28,24},{1,5},{5... | collective-permute-start | bytes 1105928 | tf_op jit(solution)/shard_map/ppermute | solution.py:63
  330.8 2.4 collective-permute-start.18
  335.7 10.9 %collective-permute-start.19 = (bf16[240,768]{1,0:T(8,128)(2,1)}, bf16[240,768]{1,0:T(8,128)(2,1)}, u32[]{:S(2)}, u32[]{:S(2)}) collective-permute-start(bf16[240,768]{1,0:T(8,128)(2,1)} %fusion.130), channel_id=1, source_target_pairs={{0,2},{1,3},{2,0},{3,1},{4,6},{5,7},{6,4},{7,5},{8,10},{9,11},{10,... | collective-permute-start | bytes 1105928 | tf_op jit(solution)/shard_map/ppermute | solution.py:63
  347.7 9.8 %collective-permute-start.20 = (bf16[240,768]{1,0:T(8,128)(2,1)S(1)}, bf16[240,768]{1,0:T(8,128)(2,1)S(1)}, u32[]{:S(2)}, u32[]{:S(2)}) collective-permute-start(bf16[240,768]{1,0:T(8,128)(2,1)S(1)} %fusion.105), channel_id=1, source_target_pairs={{0,2},{1,3},{2,0},{3,1},{4,6},{5,7},{6,4},{7,5},{8,10},{9,11},{10,... | collective-permute-start | bytes 1105928 | tf_op jit(solution)/shard_map/ppermute | solution.py:63
  358.6 5.1 collective-permute-start.21
  405.4 80.6 %collective-permute-start.22 = (bf16[2,240,768]{2,1,0:T(8,128)(2,1)}, bf16[2,240,768]{2,1,0:T(8,128)(2,1)}, u32[]{:S(2)}, u32[]{:S(2)}) collective-permute-start(bf16[2,240,768]{2,1,0:T(8,128)(2,1)} %fusion.103), channel_id=1, source_target_pairs={{0,1},{1,0},{2,3},{3,2},{4,5},{5,4},{6,7},{7,6},{8,9},{9,8},{10,11... | collective-permute-start | bytes 2211848 | tf_op jit(solution)/shard_map/ppermute | solution.py:63
  407.9 8.6 %collective-permute-start.35 = (bf16[2,2,24,768]{3,2,1,0:T(8,128)(2,1)}, bf16[2,2,24,768]{3,2,1,0:T(8,128)(2,1)}, u32[]{:S(2)}, u32[]{:S(2)}) collective-permute-start(bf16[2,2,24,768]{3,2,1,0:T(8,128)(2,1)} %fusion.134), channel_id=1, source_target_pairs={{0,4},{4,0},{8,12},{12,8},{16,20},{20,16},{24,28},{28,24},{1,5},{5... | collective-permute-start | bytes 442376 | tf_op jit(solution)/shard_map/ppermute | solution.py:63
  414.3 10.6 %copy-start.85 = (f32[768]{0:T(1024)S(1)}, f32[768]{0:T(1024)}, u32[]{:S(2)}) copy-start(f32[768]{0:T(1024)} %get-tuple-element.35) | copy-start | bytes 9220
  417.6 4.9 collective-permute-start.36
  420.2 55.9 %collective-permute-start.24 = (bf16[2,2,72,768]{3,2,1,0:T(8,128)(2,1)}, bf16[2,2,72,768]{3,2,1,0:T(8,128)(2,1)S(1)}, u32[]{:S(2)}, u32[]{:S(2)}) collective-permute-start(bf16[2,2,72,768]{3,2,1,0:T(8,128)(2,1)} %fusion.127), channel_id=1, source_target_pairs={{0,8},{4,12},{8,0},{12,4},{16,24},{20,28},{24,16},{28,20},{1,9},{5... | collective-permute-start | bytes 1327112 | tf_op jit(solution)/shard_map/ppermute | solution.py:63
  422.6 14.6 %collective-permute-start.37 = (bf16[24,768]{1,0:T(8,128)(2,1)S(1)}, bf16[24,768]{1,0:T(8,128)(2,1)S(1)}, u32[]{:S(2)}, u32[]{:S(2)}) collective-permute-start(bf16[24,768]{1,0:T(8,128)(2,1)S(1)} %fusion.143), channel_id=1, source_target_pairs={{0,16},{4,20},{8,24},{12,28},{16,0},{20,4},{24,8},{28,12},{1,17},{... | collective-permute-start | bytes 110600 | tf_op jit(solution)/shard_map/ppermute | solution.py:63
  437.2 38.9 %copy-start.13 = (f32[2,2,2,72,768]{4,3,2,1,0:T(8,128)S(1)}, f32[2,2,2,72,768]{4,3,2,1,0:T(8,128)}, u32[]{:S(2)}) copy-start(f32[2,2,2,72,768]{4,3,2,1,0:T(8,128)} %reshape_reshape.14) | copy-start | bytes 5308420
  437.2 37.9 %collective-permute-start.38 = (bf16[24,768]{1,0:T(8,128)(2,1)S(1)}, bf16[24,768]{1,0:T(8,128)(2,1)S(1)}, u32[]{:S(2)}, u32[]{:S(2)}) collective-permute-start(bf16[24,768]{1,0:T(8,128)(2,1)S(1)} %fusion.138), channel_id=1, source_target_pairs={{0,16},{4,20},{8,24},{12,28},{16,0},{20,4},{24,8},{28,12},{1,17},{... | collective-permute-start | bytes 110600 | tf_op jit(solution)/shard_map/ppermute | solution.py:63
  475.1 10.9 %copy-start.34 = (f32[960,768,1]{1,0,2:T(8,128)S(1)}, f32[960,768,1]{1,0,2:T(8,128)}, u32[]{:S(2)}) copy-start(f32[960,768,1]{1,0,2:T(8,128)} %copy-done.33) | copy-start | bytes 8847364
  475.1 4.4 collective-permute-start.39
  476.2 8.0 %collective-permute-start.25 = (bf16[2,72,768]{2,1,0:T(8,128)(2,1)S(1)}, bf16[2,72,768]{2,1,0:T(8,128)(2,1)S(1)}, u32[]{:S(2)}, u32[]{:S(2)}) collective-permute-start(bf16[2,72,768]{2,1,0:T(8,128)(2,1)S(1)} %fusion.132), channel_id=1, source_target_pairs={{0,4},{4,0},{8,12},{12,8},{16,20},{20,16},{24,28},{28,24},{1,5},{5... | collective-permute-start | bytes 663560 | tf_op jit(solution)/shard_map/ppermute | solution.py:63
  479.6 9.3 %collective-permute-start.40 = (bf16[2,2,24,768]{3,2,1,0:T(8,128)(2,1)S(1)}, bf16[2,2,24,768]{3,2,1,0:T(8,128)(2,1)S(1)}, u32[]{:S(2)}, u32[]{:S(2)}) collective-permute-start(bf16[2,2,24,768]{3,2,1,0:T(8,128)(2,1)S(1)} %pad_maximum_fusion.19), channel_id=1, source_target_pairs={{0,4},{4,0},{8,12},{12,8},{16,20},{20,16},{24,28},{28,24},{1,5},{5... | collective-permute-start | bytes 442376 | tf_op jit(solution)/shard_map/ppermute | solution.py:63
  484.3 10.7 %copy-start.45 = (f32[960,768]{1,0:T(8,128)S(1)}, f32[960,768]{1,0:T(8,128)}, u32[]{:S(2)}) copy-start(f32[960,768]{1,0:T(8,128)} %get-tuple-element.75) | copy-start | bytes 8847364
  484.3 10.9 %copy-start.79 = (f32[240]{0:T(256)S(1)}, f32[240]{0:T(256)}, u32[]{:S(2)}) copy-start(f32[240]{0:T(256)} %dynamic-slice.3) | copy-start | bytes 2884
  484.3 8.8 %collective-permute-start.26 = (bf16[72,768]{1,0:T(8,128)(2,1)S(1)}, bf16[72,768]{1,0:T(8,128)(2,1)S(1)}, u32[]{:S(2)}, u32[]{:S(2)}) collective-permute-start(bf16[72,768]{1,0:T(8,128)(2,1)S(1)} %fusion.135), channel_id=1, source_target_pairs={{0,16},{4,20},{8,24},{12,28},{16,0},{20,4},{24,8},{28,12},{1,17},{... | collective-permute-start | bytes 331784 | tf_op jit(solution)/shard_map/ppermute | solution.py:63
  487.3 7.6 %collective-permute-start.23 = (bf16[240,768]{1,0:T(8,128)(2,1)S(1)}, bf16[240,768]{1,0:T(8,128)(2,1)S(1)}, u32[]{:S(2)}, u32[]{:S(2)}) collective-permute-start(bf16[240,768]{1,0:T(8,128)(2,1)S(1)} %fusion.131), channel_id=1, source_target_pairs={{0,2},{1,3},{2,0},{3,1},{4,6},{5,7},{6,4},{7,5},{8,10},{9,11},{10,... | collective-permute-start | bytes 1105928 | tf_op jit(solution)/shard_map/ppermute | solution.py:63
  493.2 7.4 %collective-permute-start.27 = (bf16[72,768]{1,0:T(8,128)(2,1)S(1)}, bf16[72,768]{1,0:T(8,128)(2,1)S(1)}, u32[]{:S(2)}, u32[]{:S(2)}) collective-permute-start(bf16[72,768]{1,0:T(8,128)(2,1)S(1)} %fusion.133), channel_id=1, source_target_pairs={{0,16},{4,20},{8,24},{12,28},{16,0},{20,4},{24,8},{28,12},{1,17},{... | collective-permute-start | bytes 331784 | tf_op jit(solution)/shard_map/ppermute | solution.py:63
  497.6 1.3 collective-permute-start.30
  498.8 3.8 collective-permute-start.31
  502.7 3.9 collective-permute-start.32
  504.4 6.5 %collective-permute-start.28 = (bf16[2,72,768]{2,1,0:T(8,128)(2,1)S(1)}, bf16[2,72,768]{2,1,0:T(8,128)(2,1)S(1)}, u32[]{:S(2)}, u32[]{:S(2)}) collective-permute-start(bf16[2,72,768]{2,1,0:T(8,128)(2,1)S(1)} %pad_maximum_fusion.16), channel_id=1, source_target_pairs={{0,8},{4,12},{8,0},{12,4},{16,24},{20,28},{24,16},{28,20},{1,9},{5... | collective-permute-start | bytes 663560 | tf_op jit(solution)/shard_map/ppermute | solution.py:63
  506.6 4.6 collective-permute-start.33
  511.2 4.7 collective-permute-start.34
  512.3 9.9 %collective-permute-start.29 = (bf16[2,2,72,768]{3,2,1,0:T(8,128)(2,1)S(1)}, bf16[2,2,72,768]{3,2,1,0:T(8,128)(2,1)S(1)}, u32[]{:S(2)}, u32[]{:S(2)}) collective-permute-start(bf16[2,2,72,768]{3,2,1,0:T(8,128)(2,1)S(1)} %pad_maximum_fusion.13), channel_id=1, source_target_pairs={{0,4},{4,0},{8,12},{12,8},{16,20},{20,16},{24,28},{28,24},{1,5},{5... | collective-permute-start | bytes 1327112 | tf_op jit(solution)/shard_map/ppermute | solution.py:63
  (79 other events, 310.9 us)
Sparse Core Ops, SparseCore 0:
  14.2 28.7 all-gather.1
  124.5 43.0 all-reduce.3
  361.8 109.0 all-reduce.5
